TPU v7x, 512 devices: a whole 4x8x8 slice. The times are simulated.
512 devices in a mesh: gz: 8 (over y), row: 4 (over x), col: 16 (over z, core).
Axes of the slice: x: 4, y: 8, z: 8, core: 2. Of those that a mesh axis runs over, the one named last changes fastest.
Arguments:
- anc_lower: bfloat16 [17, 1024, 1024], P(None, 'col', 'row'), may hold values from -0.125 to 0.125
- anc_upper: bfloat16 [17, 1024, 1024], P(None, 'col', 'row'), may hold values from -0.125 to 0.125
- sub_lower: bfloat16 [112, 1024, 1024], P('gz', 'col', 'row'), may hold values from -0.125 to 0.125
- sub_upper: bfloat16 [112, 1024, 1024], P('gz', 'col', 'row'), may hold values from -0.125 to 0.125
- anc_rhs: bfloat16 [7, 1024, 64], P(None, 'col'), may hold values from -6 to 6
- sub_rhs: bfloat16 [24, 1024, 64], P('gz', 'col'), may hold values from -6 to 6
- layer_subtree: int32 [8], replicated, may hold values from 0 to 7, each once
- sub_pattern: int32 [88, 2], P('gz'), may hold values 0 or 1
Outputs:
- anc_solution: float32 [7, 1024, 64], P(None, ('row', 'col'))
- sub_solution: float32 [24, 1024, 64], P('gz', ('row', 'col'))
Inputs may be any that keep to these rules, and one draw needn't show every extreme that they name: `layer_subtree`: each subtree is held by exactly one layer.
All inputs are finite; a program needn't handle non-finite values. No bound on the sum of `sub_pattern` on one device may be relied on, other than what follows from the above.
Results may differ from a plain program's by a relative error of at most 0.018.
Values may be sent and summed in bfloat16 or wider, within the bound.
No kernel may reach another device: no remote copies, remote signals or barrier semaphores. Data moves between devices by JAX's collectives and lax.ppermute only.
A program may use at most 64 MiB of HBM per device.

v0:
```python
import jax
import jax.numpy as jnp
import numpy as np
from jax import lax
from jax.sharding import PartitionSpec as P

R = 64
SUB_LEVELS = 2
SUB_NODES = 3


def cut_along(array, dim, size):
    before, after = (array.shape[:dim], array.shape[dim + 1 :])
    return jnp.moveaxis(array.reshape(*before, size, -1, *after), dim, 0)


def sent_and_summed(array, axis, dim):
    size = lax.axis_size(axis)
    tiles = lax.all_to_all(cut_along(array, dim, size), axis, 0, 0, tiled=True)
    return jnp.sum(tiles, axis=0)


def in_order(tiles, dim):
    lengths = list(tiles.shape[1:])
    lengths[dim] *= tiles.shape[0]
    return jnp.moveaxis(tiles, 0, dim).reshape(lengths)


def from_everyone(array, axis):
    copies = jnp.broadcast_to(array, (lax.axis_size(axis), *array.shape))
    return lax.all_to_all(copies, axis, split_axis=0, concat_axis=0, tiled=True)


def gathered_copies(array, axis, dim):
    return in_order(from_everyone(array, axis), dim)


def of_everyone(array, axis):
    everything = from_everyone(array, axis)
    return jnp.sum(everything, axis=0)


def level_span(depth_now):
    return (2**depth_now - 1, 2 ** (depth_now + 1) - 1)


def local_routes(first_id, stop_id, depth_now, target_count):
    table = np.zeros((target_count, (stop_id - first_id) * depth_now), np.float32)
    for offset, member in enumerate(range(first_id, stop_id)):
        for local_level in range(depth_now):
            target = (member + 1 >> depth_now - local_level) - 1
            table[target, offset * depth_now + local_level] = 1.0
    return table


def solve_diagonal(residual, blocks):
    partial_rows = jnp.einsum("nki,nkr->nir", blocks, residual, preferred_element_type=jnp.float32)
    owned = sent_and_summed(partial_rows, "col", 1)
    rows_full = gathered_copies(owned.astype(jnp.bfloat16), "col", 1)
    return (owned, rows_full)


def upper_sum(values):
    return of_everyone(values, "row")


def local(anc_lower, anc_upper, sub_lower, sub_upper, anc_rhs, sub_rhs, layer_subtree, sub_pattern):
    layers = lax.axis_size("gz")
    levels = layers.bit_length() - 1
    anc_count = layers - 1
    row_count = lax.axis_size("row")
    col_count = lax.axis_size("col")
    rows_here = anc_lower.shape[2]
    cols_here = anc_lower.shape[1]
    sub_start = [0]
    for member in range(SUB_NODES):
        sub_start.append(sub_start[-1] + levels + (member + 1).bit_length() - 1)
    anc_start = [0]
    for member in range(anc_count):
        anc_start.append(anc_start[-1] + (member + 1).bit_length() - 1)
    low_pattern = sub_pattern[:, 0].astype(jnp.float32)
    up_pattern = sub_pattern[:, 1].astype(jnp.float32)
    layer_here = lax.axis_index("gz")
    subtree = jnp.sum(
        jnp.where(jnp.arange(layers, dtype=jnp.int32) == layer_here, layer_subtree, 0)
    )
    powers = jnp.asarray(2 ** (levels - np.arange(levels)), jnp.int32)
    heap_ids = (subtree + layers) // powers - 1
    choose = (heap_ids[:, None] == jnp.arange(anc_count, dtype=jnp.int32)[None, :]).astype(
        jnp.float32
    )
    row_index = lax.axis_index("row")
    col_index = lax.axis_index("col")
    holds_piece = (row_index == col_index * row_count // col_count).astype(jnp.float32)
    piece_start = jnp.clip(col_index * cols_here - row_index * rows_here, 0, rows_here - cols_here)

    def own_piece(rows_block):
        return holds_piece * lax.dynamic_slice_in_dim(rows_block, piece_start, cols_here, 1).astype(
            jnp.float32
        )

    sub_acc = jnp.zeros((SUB_NODES, cols_here, R), jnp.float32)
    to_anc = jnp.zeros((anc_count, cols_here, R), jnp.float32)
    sub_rows = {}
    for depth_now in reversed(range(SUB_LEVELS)):
        first_id, stop_id = level_span(depth_now)
        node_count = stop_id - first_id
        given = sub_rhs[first_id:stop_id].astype(jnp.float32)
        if depth_now + 1 < SUB_LEVELS:
            given = given - of_everyone(sub_acc[first_id:stop_id], "row")
        unused, solved = solve_diagonal(given.astype(jnp.bfloat16), sub_lower[first_id:stop_id])
        sub_rows[depth_now] = solved
        per_node = levels + depth_now
        opening = SUB_NODES + sub_start[first_id]
        blocks = sub_lower[opening : opening + node_count * per_node].reshape(
            node_count, per_node, cols_here, rows_here
        )
        weights = low_pattern[sub_start[first_id] : sub_start[stop_id]].reshape(
            node_count, per_node
        )
        updates = jnp.einsum("npik,nkr->npir", blocks, solved, preferred_element_type=jnp.float32)
        updates = updates * weights[:, :, None, None]
        to_anc = to_anc + jnp.einsum("ea,eir->air", choose, jnp.sum(updates[:, :levels], 0))
        if depth_now > 0:
            table = jnp.asarray(local_routes(first_id, stop_id, depth_now, SUB_NODES))
            sub_acc = sub_acc + jnp.einsum(
                "tq,qir->tir", table, updates[:, levels:].reshape(-1, cols_here, R)
            )
    to_anc = of_everyone(to_anc, ("gz", "row"))
    anc_acc = jnp.zeros((anc_count, cols_here, R), jnp.float32)
    anc_rows = {}
    for depth_now in reversed(range(levels)):
        first_id, stop_id = level_span(depth_now)
        node_count = stop_id - first_id
        reached = to_anc[first_id:stop_id]
        if depth_now + 1 < levels:
            reached = reached + of_everyone(anc_acc[first_id:stop_id], "row")
        given = anc_rhs[first_id:stop_id].astype(jnp.float32) - reached
        unused, solved = solve_diagonal(given.astype(jnp.bfloat16), anc_lower[first_id:stop_id])
        anc_rows[depth_now] = solved
        if depth_now > 0:
            opening = anc_count + anc_start[first_id]
            blocks = anc_lower[opening : opening + node_count * depth_now].reshape(
                node_count, depth_now, cols_here, rows_here
            )
            updates = jnp.einsum(
                "npik,nkr->npir", blocks, solved, preferred_element_type=jnp.float32
            )
            table = jnp.asarray(local_routes(first_id, stop_id, depth_now, anc_count))
            anc_acc = anc_acc + jnp.einsum("tq,qir->tir", table, updates.reshape(-1, cols_here, R))
    anc_z_parts = []
    anc_out_parts = []
    for depth_now in range(levels):
        first_id, stop_id = level_span(depth_now)
        node_count = stop_id - first_id
        given = own_piece(anc_rows[depth_now])
        if depth_now > 0:
            z_sofar = jnp.concatenate(anc_z_parts, 0)
            table = local_routes(first_id, stop_id, depth_now, anc_count)[:first_id].T
            sources = jnp.einsum(
                "qa,akr->qkr",
                jnp.asarray(table, jnp.bfloat16),
                z_sofar,
                preferred_element_type=jnp.float32,
            )
            sources = sources.astype(jnp.bfloat16).reshape(node_count, depth_now, rows_here, R)
            opening = anc_count + anc_start[first_id]
            blocks = anc_upper[opening : opening + node_count * depth_now].reshape(
                node_count, depth_now, cols_here, rows_here
            )
            updates = jnp.einsum(
                "npik,npkr->npir", blocks, sources, preferred_element_type=jnp.float32
            )
            given = given - jnp.sum(updates, 1)
        summed = upper_sum(given)
        owned, solved = solve_diagonal(summed.astype(jnp.bfloat16), anc_upper[first_id:stop_id])
        anc_out_parts.append(owned)
        anc_z_parts.append(solved)
    anc_z_all = jnp.concatenate(anc_z_parts, 0)
    selected = jnp.einsum(
        "ea,akr->ekr", choose.astype(jnp.bfloat16), anc_z_all, preferred_element_type=jnp.float32
    )
    selected = selected.astype(jnp.bfloat16)
    sub_z_parts = []
    sub_out_parts = []
    for depth_now in range(SUB_LEVELS):
        first_id, stop_id = level_span(depth_now)
        node_count = stop_id - first_id
        per_node = levels + depth_now
        opening = SUB_NODES + sub_start[first_id]
        blocks = sub_upper[opening : opening + node_count * per_node].reshape(
            node_count, per_node, cols_here, rows_here
        )
        weights = up_pattern[sub_start[first_id] : sub_start[stop_id]].reshape(node_count, per_node)
        updates = jnp.einsum(
            "npik,pkr->npir", blocks[:, :levels], selected, preferred_element_type=jnp.float32
        )
        if depth_now > 0:
            z_sofar = sub_z_parts[0]
            table = local_routes(first_id, stop_id, depth_now, SUB_NODES)[:first_id].T
            sources = jnp.einsum(
                "qa,akr->qkr",
                jnp.asarray(table, jnp.bfloat16),
                z_sofar,
                preferred_element_type=jnp.float32,
            )
            sources = sources.astype(jnp.bfloat16).reshape(node_count, depth_now, rows_here, R)
            local_updates = jnp.einsum(
                "npik,npkr->npir", blocks[:, levels:], sources, preferred_element_type=jnp.float32
            )
            updates = jnp.concatenate([updates, local_updates], 1)
        change = jnp.sum(updates * weights[:, :, None, None], 1)
        summed = upper_sum(own_piece(sub_rows[depth_now]) - change)
        owned, solved = solve_diagonal(summed.astype(jnp.bfloat16), sub_upper[first_id:stop_id])
        sub_out_parts.append(owned)
        sub_z_parts.append(solved)
    return (jnp.concatenate(anc_out_parts, 0), jnp.concatenate(sub_out_parts, 0))


def solution(mesh):
    in_specs = (
        P(None, "col", "row"),
        P(None, "col", "row"),
        P("gz", "col", "row"),
        P("gz", "col", "row"),
        P(None, "col", None),
        P("gz", "col", None),
        P(),
        P("gz", None),
    )
    out_specs = (P(None, ("row", "col"), None), P("gz", ("row", "col"), None))
    return jax.shard_map(local, mesh=mesh, in_specs=in_specs, out_specs=out_specs, check_vma=False)
```

profile of v0, /device:TPU:1, one launch (start us, length us, event | category | flops | bytes accessed | tf_op | source)
XLA Modules:
  0.0 479.2 jit_solution(7709073914604668162)
XLA Ops:
  2.7 11.8 %all-to-all-start = ((f32[16,1,2048]{2,1,0:T(1,128)}), f32[16,1,2048]{2,1,0:T(1,128)S(1)}, u32[]{:S(2)}, u32[]{:S(2)}) async-start(f32[16,1,2048]{2,1,0:T(1,128)} %reshape.296), calls=%async_computation | async-start | bytes 262144 | tf_op jit(solution)/shard_map/all_to_all | solution.py:19
  16.2 7.2 %all-to-all-done = f32[16,1,2048]{2,1,0:T(1,128)S(1)} async-done(((f32[16,1,2048]{2,1,0:T(1,128)}), f32[16,1,2048]{2,1,0:T(1,128)S(1)}, u32[]{:S(2)}, u32[]{:S(2)}) %all-to-all-start) | async-done | bytes 131104 | tf_op jit(solution)/shard_map/all_to_all | solution.py:19
  29.2 7.4 %all-to-all-done.1 = bf16[16,2,1024]{2,1,0:T(2,128)(2,1)S(1)} async-done(((bf16[16,2,1024]{2,1,0:T(2,128)(2,1)}), bf16[16,2,1024]{2,1,0:T(2,128)(2,1)S(1)}, u32[]{:S(2)}, u32[]{:S(2)}) %all-to-all-start.1) | async-done | bytes 65568 | tf_op jit(solution)/shard_map/all_to_all | solution.py:31
  49.3 5.0 %all-to-all-start.3 = ((f32[16,1,1024]{2,1,0:T(1,128)}), f32[16,1,1024]{2,1,0:T(1,128)S(1)}, u32[]{:S(2)}, u32[]{:S(2)}) async-start(f32[16,1,1024]{2,1,0:T(1,128)} %reshape.302), calls=%async_computation.3 | async-start | bytes 131072 | tf_op jit(solution)/shard_map/all_to_all | solution.py:19
  54.5 7.5 %all-to-all-done.3 = f32[16,1,1024]{2,1,0:T(1,128)S(1)} async-done(((f32[16,1,1024]{2,1,0:T(1,128)}), f32[16,1,1024]{2,1,0:T(1,128)S(1)}, u32[]{:S(2)}, u32[]{:S(2)}) %all-to-all-start.3) | async-done | bytes 65568 | tf_op jit(solution)/shard_map/all_to_all | solution.py:19
  67.5 7.2 %all-to-all-done.4 = bf16[16,2,512]{2,1,0:T(2,128)(2,1)S(1)} async-done(((bf16[16,2,512]{2,1,0:T(2,128)(2,1)}), bf16[16,2,512]{2,1,0:T(2,128)(2,1)S(1)}, u32[]{:S(2)}, u32[]{:S(2)}) %all-to-all-start.4) | async-done | bytes 32800 | tf_op jit(solution)/shard_map/all_to_all | solution.py:31
  79.3 8.3 %reshape.306 = f32[32,1,28672]{2,1,0:T(1,128)} reshape(f32[32,7,64,64]{3,2,1,0:T(8,128)} %broadcast_in_dim.64) | data formatting | bytes 7340032
  87.6 91.7 %all_to_all.140 = f32[32,1,28672]{2,1,0:T(1,128)} all-to-all(f32[32,1,28672]{2,1,0:T(1,128)} %reshape.306), channel_id=1, replica_groups=mesh['gz'=8,'row'=4,'col'=16] {'gz','row'}, dimensions={0} | all-to-all | bytes 7340032 | tf_op jit(solution)/shard_map/all_to_all | solution.py:31
  179.3 12.9 %reduce.22 = f32[32,28672]{1,0:T(8,128)} reduce(f32[32,1,28672]{2,1,0:T(1,128)} %all_to_all.140, f32[]{:T(128)} %broadcast.89), dimensions={1}, to_apply=%all_to_all.89.reduce_sub_computation | reduce | bytes 7340036 | tf_op jit(solution)/shard_map/all_to_all | solution.py:31
  192.2 6.8 %reshape.307 = f32[32,7,64,64]{3,2,1,0:T(8,128)} reshape(f32[32,28672]{1,0:T(8,128)} %reduce.22) | data formatting | bytes 7340032
  203.9 16.5 %all_to_all.141 = f32[16,1,4096]{2,1,0:T(1,128)S(1)} all-to-all(f32[16,1,4096]{2,1,0:T(1,128)S(1)} %reshape.308), channel_id=1, replica_groups=mesh['gz'=8,'row'=4,'col'=16] {'col'}, dimensions={0} | all-to-all | bytes 524288 | tf_op jit(solution)/shard_map/all_to_all | solution.py:19
  226.5 8.2 %all-to-all-done.7 = bf16[16,2,2048]{2,1,0:T(2,128)(2,1)S(1)} async-done(((bf16[16,2,2048]{2,1,0:T(2,128)(2,1)}), bf16[16,2,2048]{2,1,0:T(2,128)(2,1)S(1)}, u32[]{:S(2)}, u32[]{:S(2)}) %all-to-all-start.7) | async-done | bytes 131104 | tf_op jit(solution)/shard_map/all_to_all | solution.py:31
  235.8 8.0 %all_to_all.142 = f32[4,1,8192]{2,1,0:T(1,128)S(1)} all-to-all(f32[4,1,8192]{2,1,0:T(1,128)S(1)} %reshape.312), channel_id=1, replica_groups=mesh['gz'=8,'row'=4,'col'=16] {'row'}, dimensions={0} | all-to-all | bytes 262144 | tf_op jit(solution)/shard_map/all_to_all | solution.py:31
  245.6 12.9 %all_to_all.143 = f32[16,1,2048]{2,1,0:T(1,128)S(1)} all-to-all(f32[16,1,2048]{2,1,0:T(1,128)S(1)} %reshape.314), channel_id=1, replica_groups=mesh['gz'=8,'row'=4,'col'=16] {'col'}, dimensions={0} | all-to-all | bytes 262144 | tf_op jit(solution)/shard_map/all_to_all | solution.py:19
  259.7 10.4 %all_to_all.144 = bf16[16,2,1024]{2,1,0:T(2,128)(2,1)S(1)} all-to-all(bf16[16,2,1024]{2,1,0:T(2,128)(2,1)S(1)} %reshape.316), channel_id=1, replica_groups=mesh['gz'=8,'row'=4,'col'=16] {'col'}, dimensions={0} | all-to-all | bytes 131072 | tf_op jit(solution)/shard_map/all_to_all | solution.py:31
  275.1 4.3 all-to-all-done.11
  280.7 11.5 %all_to_all.145 = f32[16,1,1024]{2,1,0:T(1,128)S(1)} all-to-all(f32[16,1,1024]{2,1,0:T(1,128)S(1)} %reshape.320), channel_id=1, replica_groups=mesh['gz'=8,'row'=4,'col'=16] {'col'}, dimensions={0} | all-to-all | bytes 131072 | tf_op jit(solution)/shard_map/all_to_all | solution.py:19
  297.3 7.5 %all-to-all-done.13 = bf16[16,2,512]{2,1,0:T(2,128)(2,1)S(1)} async-done(((bf16[16,2,512]{2,1,0:T(2,128)(2,1)}), bf16[16,2,512]{2,1,0:T(2,128)(2,1)S(1)}, u32[]{:S(2)}, u32[]{:S(2)}) %all-to-all-start.13) | async-done | bytes 32800 | tf_op jit(solution)/shard_map/all_to_all | solution.py:31
  314.8 11.8 %all_to_all.146 = f32[16,1,1024]{2,1,0:T(1,128)S(1)} all-to-all(f32[16,1,1024]{2,1,0:T(1,128)S(1)} %reshape.326), channel_id=1, replica_groups=mesh['gz'=8,'row'=4,'col'=16] {'col'}, dimensions={0} | all-to-all | bytes 131072 | tf_op jit(solution)/shard_map/all_to_all | solution.py:19
  331.8 7.3 %all-to-all-done.16 = bf16[16,2,512]{2,1,0:T(2,128)(2,1)S(1)} async-done(((bf16[16,2,512]{2,1,0:T(2,128)(2,1)}), bf16[16,2,512]{2,1,0:T(2,128)(2,1)S(1)}, u32[]{:S(2)}, u32[]{:S(2)}) %all-to-all-start.16) | async-done | bytes 32800 | tf_op jit(solution)/shard_map/all_to_all | solution.py:31
  339.9 7.2 %all_to_all.147 = f32[4,1,8192]{2,1,0:T(1,128)S(1)} all-to-all(f32[4,1,8192]{2,1,0:T(1,128)S(1)} %reshape.330), channel_id=1, replica_groups=mesh['gz'=8,'row'=4,'col'=16] {'row'}, dimensions={0} | all-to-all | bytes 262144 | tf_op jit(solution)/shard_map/all_to_all | solution.py:31
  348.9 13.1 %all_to_all.148 = f32[16,1,2048]{2,1,0:T(1,128)S(1)} all-to-all(f32[16,1,2048]{2,1,0:T(1,128)S(1)} %reshape.332), channel_id=1, replica_groups=mesh['gz'=8,'row'=4,'col'=16] {'col'}, dimensions={0} | all-to-all | bytes 262144 | tf_op jit(solution)/shard_map/all_to_all | solution.py:19
  367.5 7.0 %all-to-all-done.19 = bf16[16,2,1024]{2,1,0:T(2,128)(2,1)S(1)} async-done(((bf16[16,2,1024]{2,1,0:T(2,128)(2,1)}), bf16[16,2,1024]{2,1,0:T(2,128)(2,1)S(1)}, u32[]{:S(2)}, u32[]{:S(2)}) %all-to-all-start.19) | async-done | bytes 65568 | tf_op jit(solution)/shard_map/all_to_all | solution.py:31
  375.9 8.9 %all_to_all.149 = f32[4,1,16384]{2,1,0:T(1,128)S(1)} all-to-all(f32[4,1,16384]{2,1,0:T(1,128)S(1)} %reshape.336), channel_id=1, replica_groups=mesh['gz'=8,'row'=4,'col'=16] {'row'}, dimensions={0} | all-to-all | bytes 524288 | tf_op jit(solution)/shard_map/all_to_all | solution.py:31
  387.3 15.3 %all_to_all.150 = f32[16,1,4096]{2,1,0:T(1,128)S(1)} all-to-all(f32[16,1,4096]{2,1,0:T(1,128)S(1)} %reshape.338), channel_id=1, replica_groups=mesh['gz'=8,'row'=4,'col'=16] {'col'}, dimensions={0} | all-to-all | bytes 524288 | tf_op jit(solution)/shard_map/all_to_all | solution.py:19
  408.7 8.2 %all-to-all-done.22 = bf16[16,2,2048]{2,1,0:T(2,128)(2,1)S(1)} async-done(((bf16[16,2,2048]{2,1,0:T(2,128)(2,1)}), bf16[16,2,2048]{2,1,0:T(2,128)(2,1)S(1)}, u32[]{:S(2)}, u32[]{:S(2)}) %all-to-all-start.22) | async-done | bytes 131104 | tf_op jit(solution)/shard_map/all_to_all | solution.py:31
  422.1 4.4 all-to-all-done.23
  432.9 7.5 %all-to-all-done.24 = f32[16,1,1024]{2,1,0:T(1,128)S(1)} async-done(((f32[16,1,1024]{2,1,0:T(1,128)}), f32[16,1,1024]{2,1,0:T(1,128)S(1)}, u32[]{:S(2)}, u32[]{:S(2)}) %all-to-all-start.24) | async-done | bytes 65568 | tf_op jit(solution)/shard_map/all_to_all | solution.py:19
  445.8 7.3 %all-to-all-done.25 = bf16[16,2,512]{2,1,0:T(2,128)(2,1)S(1)} async-done(((bf16[16,2,512]{2,1,0:T(2,128)(2,1)}), bf16[16,2,512]{2,1,0:T(2,128)(2,1)S(1)}, u32[]{:S(2)}, u32[]{:S(2)}) %all-to-all-start.25) | async-done | bytes 32800 | tf_op jit(solution)/shard_map/all_to_all | solution.py:31
  453.8 7.2 %all_to_all.151 = f32[4,1,8192]{2,1,0:T(1,128)S(1)} all-to-all(f32[4,1,8192]{2,1,0:T(1,128)S(1)} %reshape.348), channel_id=1, replica_groups=mesh['gz'=8,'row'=4,'col'=16] {'row'}, dimensions={0} | all-to-all | bytes 262144 | tf_op jit(solution)/shard_map/all_to_all | solution.py:31
  463.4 4.8 %all-to-all-start.27 = ((f32[16,1,2048]{2,1,0:T(1,128)}), f32[16,1,2048]{2,1,0:T(1,128)S(1)}, u32[]{:S(2)}, u32[]{:S(2)}) async-start(f32[16,1,2048]{2,1,0:T(1,128)} %reshape.350), calls=%async_computation.27 | async-start | bytes 262144 | tf_op jit(solution)/shard_map/all_to_all | solution.py:19
  468.9 8.6 %all-to-all-done.27 = f32[16,1,2048]{2,1,0:T(1,128)S(1)} async-done(((f32[16,1,2048]{2,1,0:T(1,128)}), f32[16,1,2048]{2,1,0:T(1,128)S(1)}, u32[]{:S(2)}, u32[]{:S(2)}) %all-to-all-start.27) | async-done | bytes 131104 | tf_op jit(solution)/shard_map/all_to_all | solution.py:19
  (255 shorter events, 112.9 us)
Async XLA Ops:
  0.6 36.6 %copy-start.10 = (bf16[3,2,1]{0,1,2:T(2,128)(2,1)S(1)}, bf16[3,2,1]{0,1,2:T(2,128)(2,1)}, u32[]{:S(2)}) copy-start(bf16[3,2,1]{0,1,2:T(2,128)(2,1)} %constant.143) | copy-start | bytes 40
  0.6 53.6 %copy-start.7 = (s32[3]{0:T(128)S(1)}, s32[3]{0:T(128)}, u32[]{:S(2)}) copy-start(s32[3]{0:T(128)} %constant.63.clone) | copy-start | bytes 40
  0.7 36.1 %slice-start = ((bf16[14,64,256]{2,1,0:T(8,128)(2,1)}), bf16[8,64,256]{2,1,0:T(8,128)(2,1)S(1)}, s32[]{:S(2)}) async-start(bf16[14,64,256]{2,1,0:T(8,128)(2,1)} %param.17), calls=%async_computation.28 | async-start | bytes 524288 | tf_op jit(solution)/shard_map/slice | solution.py:115
  0.7 41.5 %copy-start.8 = (s32[8]{0:T(128)S(1)}, s32[8]{0:T(128)}, u32[]{:S(2)}) copy-start(s32[8]{0:T(128)} %param.21) | copy-start | bytes 100
  1.8 72.9 %copy-start = (bf16[14,64,256]{2,1,0:T(8,128)(2,1)S(1)}, bf16[14,64,256]{2,1,0:T(8,128)(2,1)}, u32[]{:S(2)}) copy-start(bf16[14,64,256]{2,1,0:T(8,128)(2,1)} %param.17) | copy-start | bytes 1376260
  2.7 20.7 %all-to-all-start = ((f32[16,1,2048]{2,1,0:T(1,128)}), f32[16,1,2048]{2,1,0:T(1,128)S(1)}, u32[]{:S(2)}, u32[]{:S(2)}) async-start(f32[16,1,2048]{2,1,0:T(1,128)} %reshape.296), calls=%async_computation | async-start | bytes 262144 | tf_op jit(solution)/shard_map/all_to_all | solution.py:19
  25.8 10.9 %all-to-all-start.1 = ((bf16[16,2,1024]{2,1,0:T(2,128)(2,1)}), bf16[16,2,1024]{2,1,0:T(2,128)(2,1)S(1)}, u32[]{:S(2)}, u32[]{:S(2)}) async-start(bf16[16,2,1024]{2,1,0:T(2,128)(2,1)} %reshape.298), calls=%async_computation.1 | async-start | bytes 131072 | tf_op jit(solution)/shard_map/all_to_all | solution.py:31
  38.2 8.5 %all-to-all-start.2 = ((f32[4,1,4096]{2,1,0:T(1,128)}), f32[4,1,4096]{2,1,0:T(1,128)S(1)}, u32[]{:S(2)}, u32[]{:S(2)}) async-start(f32[4,1,4096]{2,1,0:T(1,128)} %reshape.300), calls=%async_computation.2 | async-start | bytes 131072 | tf_op jit(solution)/shard_map/all_to_all | solution.py:31
  49.3 12.8 %all-to-all-start.3 = ((f32[16,1,1024]{2,1,0:T(1,128)}), f32[16,1,1024]{2,1,0:T(1,128)S(1)}, u32[]{:S(2)}, u32[]{:S(2)}) async-start(f32[16,1,1024]{2,1,0:T(1,128)} %reshape.302), calls=%async_computation.3 | async-start | bytes 131072 | tf_op jit(solution)/shard_map/all_to_all | solution.py:19
  63.7 10.9 %all-to-all-start.4 = ((bf16[16,2,512]{2,1,0:T(2,128)(2,1)}), bf16[16,2,512]{2,1,0:T(2,128)(2,1)S(1)}, u32[]{:S(2)}, u32[]{:S(2)}) async-start(bf16[16,2,512]{2,1,0:T(2,128)(2,1)} %reshape.304), calls=%async_computation.4 | async-start | bytes 65536 | tf_op jit(solution)/shard_map/all_to_all | solution.py:31
  199.0 4.0 copy-start.2
  199.0 4.0 copy-start.4
  203.3 31.6 %slice-start.2 = ((bf16[17,64,256]{2,1,0:T(8,128)(2,1)}), bf16[8,64,256]{2,1,0:T(8,128)(2,1)S(1)}, s32[]{:S(2)}) async-start(bf16[17,64,256]{2,1,0:T(8,128)(2,1)} %param.15), calls=%async_computation.30 | async-start | bytes 524288 | tf_op jit(solution)/shard_map/slice | solution.py:143
  203.5 31.8 %copy-start.5 = (bf16[7,8,1]{1,0,2:T(8,128)(2,1)S(1)}, bf16[7,8,1]{1,0,2:T(8,128)(2,1)}, u32[]{:S(2)}) copy-start(bf16[7,8,1]{1,0,2:T(8,128)(2,1)} %constant.142) | copy-start | bytes 340
  222.9 11.7 %all-to-all-start.7 = ((bf16[16,2,2048]{2,1,0:T(2,128)(2,1)}), bf16[16,2,2048]{2,1,0:T(2,128)(2,1)S(1)}, u32[]{:S(2)}, u32[]{:S(2)}) async-start(bf16[16,2,2048]{2,1,0:T(2,128)(2,1)} %reshape.310), calls=%async_computation.7 | async-start | bytes 262144 | tf_op jit(solution)/shard_map/all_to_all | solution.py:31
  234.9 35.8 %copy-start.6 = (bf16[7,2,1]{0,1,2:T(2,128)(2,1)S(1)}, bf16[7,2,1]{0,1,2:T(2,128)(2,1)}, u32[]{:S(2)}) copy-start(bf16[7,2,1]{0,1,2:T(2,128)(2,1)} %constant.144) | copy-start | bytes 88
  245.2 63.9 %copy-start.1 = (bf16[17,64,256]{2,1,0:T(8,128)(2,1)S(1)}, bf16[17,64,256]{2,1,0:T(8,128)(2,1)}, u32[]{:S(2)}) copy-start(bf16[17,64,256]{2,1,0:T(8,128)(2,1)} %param.16) | copy-start | bytes 1671172
  271.7 7.7 %all-to-all-start.11 = ((f32[4,1,4096]{2,1,0:T(1,128)}), f32[4,1,4096]{2,1,0:T(1,128)S(1)}, u32[]{:S(2)}, u32[]{:S(2)}) async-start(f32[4,1,4096]{2,1,0:T(1,128)} %reshape.318), calls=%async_computation.11 | async-start | bytes 131072 | tf_op jit(solution)/shard_map/all_to_all | solution.py:31
  293.8 10.9 %all-to-all-start.13 = ((bf16[16,2,512]{2,1,0:T(2,128)(2,1)}), bf16[16,2,512]{2,1,0:T(2,128)(2,1)S(1)}, u32[]{:S(2)}, u32[]{:S(2)}) async-start(bf16[16,2,512]{2,1,0:T(2,128)(2,1)} %reshape.322), calls=%async_computation.13 | async-start | bytes 65536 | tf_op jit(solution)/shard_map/all_to_all | solution.py:31
  305.9 7.7 %all-to-all-start.14 = ((f32[4,1,4096]{2,1,0:T(1,128)}), f32[4,1,4096]{2,1,0:T(1,128)S(1)}, u32[]{:S(2)}, u32[]{:S(2)}) async-start(f32[4,1,4096]{2,1,0:T(1,128)} %reshape.324), calls=%async_computation.14 | async-start | bytes 131072 | tf_op jit(solution)/shard_map/all_to_all | solution.py:31
  328.3 10.9 %all-to-all-start.16 = ((bf16[16,2,512]{2,1,0:T(2,128)(2,1)}), bf16[16,2,512]{2,1,0:T(2,128)(2,1)S(1)}, u32[]{:S(2)}, u32[]{:S(2)}) async-start(bf16[16,2,512]{2,1,0:T(2,128)(2,1)} %reshape.328), calls=%async_computation.16 | async-start | bytes 65536 | tf_op jit(solution)/shard_map/all_to_all | solution.py:31
  331.7 43.1 %copy-start.9 = (bf16[8,3,1]{0,1,2:T(4,128)(2,1)S(1)}, bf16[8,3,1]{0,1,2:T(4,128)(2,1)}, u32[]{:S(2)}) copy-start(bf16[8,3,1]{0,1,2:T(4,128)(2,1)} %constant.79) | copy-start | bytes 148
  339.7 35.5 %slice-start.1 = ((bf16[17,64,256]{2,1,0:T(8,128)(2,1)}), bf16[8,64,256]{2,1,0:T(8,128)(2,1)S(1)}, s32[]{:S(2)}) async-start(bf16[17,64,256]{2,1,0:T(8,128)(2,1)} %param.16), calls=%async_computation.29 | async-start | bytes 524288 | tf_op jit(solution)/shard_map/slice | solution.py:168
  363.9 10.6 %all-to-all-start.19 = ((bf16[16,2,1024]{2,1,0:T(2,128)(2,1)}), bf16[16,2,1024]{2,1,0:T(2,128)(2,1)S(1)}, u32[]{:S(2)}, u32[]{:S(2)}) async-start(bf16[16,2,1024]{2,1,0:T(2,128)(2,1)} %reshape.334), calls=%async_computation.19 | async-start | bytes 131072 | tf_op jit(solution)/shard_map/all_to_all | solution.py:31
  386.9 30.7 %copy-start.3 = (bf16[14,64,256]{2,1,0:T(8,128)(2,1)S(1)}, bf16[14,64,256]{2,1,0:T(8,128)(2,1)}, u32[]{:S(2)}) copy-start(bf16[14,64,256]{2,1,0:T(8,128)(2,1)} %param.18) | copy-start | bytes 1376260
  405.2 11.7 %all-to-all-start.22 = ((bf16[16,2,2048]{2,1,0:T(2,128)(2,1)}), bf16[16,2,2048]{2,1,0:T(2,128)(2,1)S(1)}, u32[]{:S(2)}, u32[]{:S(2)}) async-start(bf16[16,2,2048]{2,1,0:T(2,128)(2,1)} %reshape.340), calls=%async_computation.22 | async-start | bytes 262144 | tf_op jit(solution)/shard_map/all_to_all | solution.py:31
  418.7 7.8 %all-to-all-start.23 = ((f32[4,1,4096]{2,1,0:T(1,128)}), f32[4,1,4096]{2,1,0:T(1,128)S(1)}, u32[]{:S(2)}, u32[]{:S(2)}) async-start(f32[4,1,4096]{2,1,0:T(1,128)} %reshape.342), calls=%async_computation.23 | async-start | bytes 131072 | tf_op jit(solution)/shard_map/all_to_all | solution.py:31
  428.3 12.1 %all-to-all-start.24 = ((f32[16,1,1024]{2,1,0:T(1,128)}), f32[16,1,1024]{2,1,0:T(1,128)S(1)}, u32[]{:S(2)}, u32[]{:S(2)}) async-start(f32[16,1,1024]{2,1,0:T(1,128)} %reshape.344), calls=%async_computation.24 | async-start | bytes 131072 | tf_op jit(solution)/shard_map/all_to_all | solution.py:19
  442.1 10.9 %all-to-all-start.25 = ((bf16[16,2,512]{2,1,0:T(2,128)(2,1)}), bf16[16,2,512]{2,1,0:T(2,128)(2,1)S(1)}, u32[]{:S(2)}, u32[]{:S(2)}) async-start(bf16[16,2,512]{2,1,0:T(2,128)(2,1)} %reshape.346), calls=%async_computation.25 | async-start | bytes 65536 | tf_op jit(solution)/shard_map/all_to_all | solution.py:31
  463.4 14.0 %all-to-all-start.27 = ((f32[16,1,2048]{2,1,0:T(1,128)}), f32[16,1,2048]{2,1,0:T(1,128)S(1)}, u32[]{:S(2)}, u32[]{:S(2)}) async-start(f32[16,1,2048]{2,1,0:T(1,128)} %reshape.350), calls=%async_computation.27 | async-start | bytes 262144 | tf_op jit(solution)/shard_map/all_to_all | solution.py:19
where the time goes:
time: 482 us; the launch traced here: 479 us
  blocking collectives  215 us (45%)
  waiting for transfers between devices  107 us (22%)
  starting transfers between devices  67.3 us (14%)
  local copies, waits for them, and re-layouts  43.1 us (9%)
  other arithmetic  37.5 us (8%)
  matrix products  7.15 us (1%)
    all_to_all x6, blocking collectives, from_everyone(): return lax.all_to_all(copies, axis, split_axis=0, concat_axis=0, tiled=True)  134 us
    all_to_all x6, blocking collectives, sent_and_summed(): tiles = lax.all_to_all(cut_along(array, dim, size), axis, 0, 0, tiled=True)  81.1 us
    all_to_all x12, waiting for transfers between devices, from_everyone(): return lax.all_to_all(copies, axis, split_axis=0, concat_axis=0, tiled=True)  76.1 us
    all_to_all x12, starting transfers between devices, from_everyone(): return lax.all_to_all(copies, axis, split_axis=0, concat_axis=0, tiled=True)  41.4 us
    unnamed x83, local copies, waits for them, and re-layouts  33.9 us
    all_to_all x4, waiting for transfers between devices, sent_and_summed(): tiles = lax.all_to_all(cut_along(array, dim, size), axis, 0, 0, tiled=True)  30.8 us
    all_to_all x4, starting transfers between devices, sent_and_summed(): tiles = lax.all_to_all(cut_along(array, dim, size), axis, 0, 0, tiled=True)  25.9 us
    all_to_all x9, other arithmetic, from_everyone(): return lax.all_to_all(copies, axis, split_axis=0, concat_axis=0, tiled=True)  20.5 us
  transfers between devices with their start and end apart: 16, of which 16 were waited for; matrix products, arithmetic and copies ran while one was open for 1% of the time, Pallas kernels for 0%

commit v1 on v0

v1 whole, which is shorter than its diff:
```python
import jax
import jax.numpy as jnp
import numpy as np
from jax import lax
from jax.sharding import Mesh, PartitionSpec as P

SUB_LEVELS = 2
SUB_NODES = 3
F32 = jnp.float32
BF16 = jnp.bfloat16
CORES = 2


def level_span(depth):
    return 2**depth - 1, 2 ** (depth + 1) - 1


def depth_of(node):
    return (node + 1).bit_length() - 1


def above(node, level):
    return ((node + 1) >> (depth_of(node) - level)) - 1


def dot(spec, left, right):
    return jnp.einsum(spec, left, right, preferred_element_type=F32)


def swapped(array):
    return lax.ppermute(array, "core", [(0, 1), (1, 0)])


def summed(array, axis):
    copies = jnp.broadcast_to(array.astype(BF16), (lax.axis_size(axis), *array.shape))
    tiles = lax.all_to_all(copies, axis, 0, 0, tiled=True)
    return jnp.sum(tiles.astype(F32), axis=0)


def local(anc_lower, anc_upper, sub_lower, sub_upper, anc_rhs, sub_rhs, layer_subtree, sub_pattern):
    layers = lax.axis_size("gz")
    levels = layers.bit_length() - 1
    anc_count = layers - 1
    nrow, nz = lax.axis_size("row"), lax.axis_size("z")
    own, wide = sub_lower.shape[1:]
    size = wide * nrow
    pair_rows = own * CORES
    out_rows = wide // (nz * CORES)
    cols = sub_rhs.shape[2] // CORES
    per = cols // (layers * nrow)
    g, r, z, core = (lax.axis_index(name) for name in ("gz", "row", "z", "core"))

    sub_pairs = {}
    for m in range(SUB_NODES):
        for kind, count in ((0, levels), (1, depth_of(m))):
            for u in range(count):
                sub_pairs[m, kind, u] = len(sub_pairs)
    anc_pairs = {}
    for a in range(anc_count):
        for u in range(depth_of(a)):
            anc_pairs[a, u] = anc_count + len(anc_pairs)

    low_w = sub_pattern[:, 0].astype(BF16)
    up_w = sub_pattern[:, 1].astype(BF16)
    powers = jnp.asarray(2 ** (levels - np.arange(levels)), jnp.int32)
    heap_ids = (layer_subtree[:, None] + layers) // powers[None, :] - 1
    choose = heap_ids[:, :, None] == jnp.arange(anc_count, dtype=jnp.int32)
    choose = choose.astype(F32)
    choose_here = lax.dynamic_index_in_dim(choose, g, 0, keepdims=False)

    def halves(array, dim, base=0):
        first = lax.dynamic_slice_in_dim(array, base + core * own, own, dim)
        second = lax.dynamic_slice_in_dim(array, base + (1 - core) * own, own, dim)
        return jnp.concatenate([first, second], dim)

    def gathered(blocks):
        return lax.all_gather(blocks, "row", axis=2, tiled=True)

    low_two = (sub_lower, swapped(sub_lower))
    rhs_here = lax.dynamic_slice_in_dim(sub_rhs, core * cols, cols, 2)
    rhs_there = swapped(lax.dynamic_slice_in_dim(sub_rhs, (1 - core) * cols, cols, 2))
    rhs = jnp.concatenate([rhs_here, rhs_there], 1).transpose(0, 2, 1)
    mine = (g * nrow + r) * per
    anc_here = lax.dynamic_slice_in_dim(anc_rhs, core * cols + mine, per, 2)
    anc_there = swapped(lax.dynamic_slice_in_dim(anc_rhs, (1 - core) * cols + mine, per, 2))
    anc_given = jnp.concatenate([anc_here, anc_there], 1).transpose(0, 2, 1).astype(F32)
    up_two = (sub_upper, swapped(sub_upper))

    anc_low_row = gathered(anc_lower)
    anc_low = (anc_low_row, swapped(anc_low_row))
    anc_up_row = gathered(anc_upper)
    anc_up = (anc_up_row, swapped(anc_up_row))

    def transposed(two, index, v):
        return dot("rk,ki->ri", v[:, :own], two[0][index]) + dot("rk,ki->ri", v[:, own:], two[1][index])

    def applied(two, index, v):
        return jnp.concatenate([dot("rk,ik->ri", v, part[index]) for part in two], 1)

    def nodes_transposed(two, nodes, v):
        return jnp.stack([transposed(two, m, v[i]) for i, m in enumerate(nodes)])

    leaves = range(1, SUB_NODES)
    y_leaf = summed(nodes_transposed(low_two, leaves, rhs[1:]), "z").astype(BF16)
    y = {m: y_leaf[m - 1] for m in leaves}

    def low_part(m, kind, u):
        p = sub_pairs[m, kind, u]
        return applied(low_two, SUB_NODES + p, y[m] * low_w[p])

    update = sum(low_part(m, 1, 0) for m in leaves)
    residual = (rhs[0].astype(F32) - summed(update, "row")).astype(BF16)
    y[0] = summed(transposed(low_two, 0, residual), "z").astype(BF16)
    to_anc = jnp.stack([sum(low_part(m, 0, e) for m in range(SUB_NODES)) for e in range(levels)])
    to_anc = to_anc.reshape(levels, layers * nrow, per, pair_rows).transpose(1, 0, 2, 3)
    tiles = lax.all_to_all(to_anc.astype(BF16), ("gz", "row"), 0, 0, tiled=True)
    from_layers = jnp.sum(tiles.astype(F32).reshape(layers, nrow, levels, per, pair_rows), 1)
    reached = jnp.sum(choose[:, :, :, None, None] * from_layers[:, :, None], (0, 1))

    acc = [anc_given[a] - reached[a] for a in range(anc_count)]
    anc_y = {}
    for depth in reversed(range(levels)):
        nodes = range(*level_span(depth))
        given = jnp.stack([acc[a] for a in nodes]).astype(BF16)
        solved = summed(nodes_transposed(anc_low, nodes, given), "z").astype(BF16)
        for i, a in enumerate(nodes):
            anc_y[a] = solved[i]
            for u in range(depth):
                acc[above(a, u)] = acc[above(a, u)] - applied(anc_low, anc_pairs[a, u], solved[i])

    anc_z = {}
    anc_rows = {}
    for depth in range(levels):
        nodes = range(*level_span(depth))
        given = []
        for a in nodes:
            t = halves(anc_y[a], 1, z * pair_rows).astype(F32)
            for u in range(depth):
                t = t - applied(anc_up, anc_pairs[a, u], anc_z[above(a, u)])
            given.append(t.astype(BF16))
        solved = summed(nodes_transposed(anc_up, nodes, jnp.stack(given)), "z").astype(BF16)
        for i, a in enumerate(nodes):
            anc_z[a] = solved[i]
    every = jnp.stack([anc_z[a] for a in range(anc_count)])
    every = every.reshape(anc_count, per, nrow, wide).transpose(2, 0, 1, 3)
    every = jnp.broadcast_to(every, (layers, *every.shape)).reshape(-1, anc_count, per, wide)
    tiles = lax.all_to_all(every, ("gz", "row"), 0, 0, tiled=True)
    z_all = tiles.transpose(1, 0, 2, 3).reshape(anc_count, cols, wide)

    def out_slice(array, which):
        return lax.dynamic_slice_in_dim(array, (z * CORES + which) * out_rows, out_rows, 2)

    def joined(here, there):
        pair = jnp.where(core == 0, jnp.stack([here, there]), jnp.stack([there, here]))
        return jnp.concatenate([pair[0], pair[1]], -1)

    out_there = swapped(out_slice(z_all, 1 - core).transpose(0, 2, 1))
    out_here = out_slice(z_all, core).transpose(0, 2, 1)
    anc_out = joined(out_here, out_there).astype(F32)

    picked = dot("ea,ark->erk", choose_here.astype(BF16), z_all).astype(BF16)
    held = (r == z * nrow // nz).astype(F32)
    base = jnp.clip(z * pair_rows - r * wide, 0, wide - pair_rows)

    def up_part(m, kind, u, v):
        p = sub_pairs[m, kind, u]
        return applied(up_two, SUB_NODES + p, v * up_w[p])

    running = []
    for m in range(SUB_NODES):
        part = held * halves(y[m], 1, base).astype(F32)
        running.append(part - sum(up_part(m, 0, e, picked[e]) for e in range(levels)))

    def rows_first(m, v):
        return sum(
            dot("ki,rk->ir", up_two[i][m], v[:, i * own : (i + 1) * own]) for i in range(CORES)
        )

    t_root = summed(running[0], "row").astype(BF16)
    z_root = summed(transposed(up_two, 0, t_root), "z").astype(BF16)
    leaf = jnp.stack([running[m] - up_part(m, 1, 0, z_root) for m in leaves])
    t_leaf = summed(leaf, "row").astype(BF16)
    pieces = jnp.stack([rows_first(0, t_root)] + [rows_first(m, t_leaf[m - 1]) for m in leaves])
    pieces = pieces.astype(BF16).reshape(SUB_NODES, nz * CORES, out_rows, cols).transpose(1, 0, 2, 3)
    tiles = lax.all_to_all(pieces, ("z", "core"), 0, 0, tiled=True)
    owned = jnp.sum(tiles.astype(F32).reshape(nz, CORES, SUB_NODES, out_rows, cols), 0)
    sub_out = jnp.concatenate([owned[0], owned[1]], -1)
    return anc_out, sub_out


def solution(mesh):
    sizes = dict(mesh.shape)
    devices = mesh.devices.reshape(sizes["gz"], sizes["row"], sizes["col"] // CORES, CORES)
    split = Mesh(devices, ("gz", "row", "z", "core"))
    col = ("z", "core")
    in_specs = (
        P(None, col, "row"),
        P(None, col, "row"),
        P("gz", col, "row"),
        P("gz", col, "row"),
        P(None, col, None),
        P("gz", col, None),
        P(),
        P("gz", None),
    )
    out_specs = (P(None, ("row", "z", "core"), None), P("gz", ("row", "z", "core"), None))
    return jax.shard_map(local, mesh=split, in_specs=in_specs, out_specs=out_specs, check_vma=False)
```

time: 482 us -> 306 us (0.63)
  blocking collectives: 215 us -> 0 us
  matrix products: 7.15 us -> 81.3 us
  starting transfers between devices: 67.3 us -> 101 us
  waiting for transfers between devices: 107 us -> 78.1 us
  local copies, waits for them, and re-layouts: 43.1 us -> 16.1 us
  other arithmetic: 37.5 us -> 12.8 us
  between operations: 2.54 us -> 14.7 us
    all_to_all x12 -> x0, blocking collectives: 215 us -> none  [the longest x6 134 us: from_everyone(): return lax.all_to_all(copies, axis, split_axis=0, concat_axis=0, tiled=True)]
    dot_general x26 -> x125, matrix products: 7.15 us -> 81.3 us  [dot(): return jnp.einsum(spec, left, right, preferred_element_type=F32)]
    unnamed x83 -> x21, local copies, waits for them, and re-layouts: 33.9 us -> 2.68 us
    ppermute x0 -> x7, starting transfers between devices: none -> 30.7 us  [swapped(): return lax.ppermute(array, 'core', [(0, 1), (1, 0)])]
    all_to_all x19 -> x0, other arithmetic: 30 us -> none  [the longest x9 20.5 us: from_everyone(): return lax.all_to_all(copies, axis, split_axis=0, concat_axis=0, tiled=True)]
    all_to_all x16 -> x15, waiting for transfers between devices: 107 us -> 77.3 us  [the longest x12 52.5 us: summed(): tiles = lax.all_to_all(copies, axis, 0, 0, tiled=True)]
    mul x1, other arithmetic: 0.01 us -> 6.07 us  [up_part(): return applied(up_two, SUB_NODES + p, v * up_w[p])]
    all_to_all x16 -> x15, starting transfers between devices: 67.3 us -> 69.8 us  [the longest x12 50.8 us: summed(): tiles = lax.all_to_all(copies, axis, 0, 0, tiled=True)]
  transfers between devices with their start and end apart: 16 -> 24, of which waited for: 16 -> 12; matrix products, arithmetic and copies ran while one was open for 1% -> 34% of each run, Pallas kernels for 0% -> 0%
where the time goes in v1:
time: 306 us; the launch traced here: 304 us
  starting transfers between devices  101 us (33%)
  matrix products  81.3 us (27%)
  waiting for transfers between devices  78.1 us (26%)
  local copies, waits for them, and re-layouts  16.1 us (5%)
  between operations  14.7 us (5%)
  other arithmetic  12.8 us (4%)
    dot_general x125, matrix products, dot(): return jnp.einsum(spec, left, right, preferred_element_type=F32)  81.3 us
    all_to_all x12, waiting for transfers between devices, summed(): tiles = lax.all_to_all(copies, axis, 0, 0, tiled=True)  52.5 us
    all_to_all x12, starting transfers between devices, summed(): tiles = lax.all_to_all(copies, axis, 0, 0, tiled=True)  50.8 us
    ppermute x7, starting transfers between devices, swapped(): return lax.ppermute(array, 'core', [(0, 1), (1, 0)])  30.7 us
    all_to_all x1, starting transfers between devices, local(): tiles = lax.all_to_all(to_anc.astype(BF16), ('gz', 'row'), 0, 0, tiled=True)  9.99 us
    all_to_all x1, waiting for transfers between devices, local(): tiles = lax.all_to_all(every, ('gz', 'row'), 0, 0, tiled=True)  9.22 us
    all_to_all x1, waiting for transfers between devices, local(): tiles = lax.all_to_all(to_anc.astype(BF16), ('gz', 'row'), 0, 0, tiled=True)  8.77 us
    broadcast_in_dim x13, local copies, waits for them, and re-layouts, summed(): jnp.broadcast_to(array.astype(BF16), (lax.axis_size(axis), *array.shape))  7.07 us
  transfers between devices with their start and end apart: 24, of which 12 were waited for; matrix products, arithmetic and copies ran while one was open for 34% of the time, Pallas kernels for 0%

profile of v1, /device:TPU:1, one launch (start us, length us, event | category | flops | bytes accessed | tf_op | source)
XLA Modules:
  0.0 303.7 jit_solution(5136626686678730137)
XLA Ops:
  9.1 8.7 %collective-permute-start.1 = (bf16[3,64,32]{1,2,0:T(8,128)(2,1)S(1)}, bf16[3,64,32]{1,2,0:T(8,128)(2,1)S(1)}, u32[]{:S(2)}, u32[]{:S(2)}) collective-permute-start(bf16[3,64,32]{1,2,0:T(8,128)(2,1)S(1)} %copy.92), channel_id=1, source_target_pairs={{0,1},{1,0},{2,3},{3,2},{4,5},{5,4},{6,7},{7,6},{8,9},{9,8},{10,11... | collective-permute-start | bytes 36872 | tf_op jit(solution)/shard_map/ppermute | solution.py:31
  21.0 2.4 collective-permute-start
  26.4 4.7 %all-to-all-start = ((bf16[8,2,32,256]{3,2,1,0:T(8,128)(2,1)}), bf16[8,2,32,256]{3,2,1,0:T(8,128)(2,1)S(1)}, u32[]{:S(2)}, u32[]{:S(2)}) async-start(bf16[8,2,32,256]{3,2,1,0:T(8,128)(2,1)} %broadcast_in_dim.47), calls=%async_computation | async-start | bytes 524288 | tf_op jit(solution)/shard_map/all_to_all | solution.py:36
  33.0 10.4 %all-to-all-done = bf16[8,2,32,256]{3,2,1,0:T(8,128)(2,1)S(1)} async-done(((bf16[8,2,32,256]{3,2,1,0:T(8,128)(2,1)}), bf16[8,2,32,256]{3,2,1,0:T(8,128)(2,1)S(1)}, u32[]{:S(2)}, u32[]{:S(2)}) %all-to-all-start) | async-done | bytes 262176 | tf_op jit(solution)/shard_map/all_to_all | solution.py:36
  47.3 4.0 %all-to-all-start.1 = ((bf16[4,32,128]{2,1,0:T(8,128)(2,1)}), bf16[4,32,128]{2,1,0:T(8,128)(2,1)S(1)}, u32[]{:S(2)}, u32[]{:S(2)}) async-start(bf16[4,32,128]{2,1,0:T(8,128)(2,1)} %broadcast_in_dim.48), calls=%async_computation.1 | async-start | bytes 65536 | tf_op jit(solution)/shard_map/all_to_all | solution.py:36
  60.1 3.4 %all-to-all-start.2 = ((bf16[8,32,256]{2,1,0:T(8,128)(2,1)}), bf16[8,32,256]{2,1,0:T(8,128)(2,1)S(1)}, u32[]{:S(2)}, u32[]{:S(2)}) async-start(bf16[8,32,256]{2,1,0:T(8,128)(2,1)} %broadcast_in_dim.49), calls=%async_computation.2 | async-start | bytes 262144 | tf_op jit(solution)/shard_map/all_to_all | solution.py:36
  65.0 6.1 %all-to-all-done.2 = bf16[8,32,256]{2,1,0:T(8,128)(2,1)S(1)} async-done(((bf16[8,32,256]{2,1,0:T(8,128)(2,1)}), bf16[8,32,256]{2,1,0:T(8,128)(2,1)S(1)}, u32[]{:S(2)}, u32[]{:S(2)}) %all-to-all-start.2) | async-done | bytes 131104 | tf_op jit(solution)/shard_map/all_to_all | solution.py:36
  72.6 4.2 %collective-permute-start.3 = (bf16[17,64,1024]{2,1,0:T(8,128)(2,1)}, bf16[17,64,1024]{2,1,0:T(8,128)(2,1)}, u32[]{:S(2)}, u32[]{:S(2)}) collective-permute-start(bf16[17,64,1024]{2,1,0:T(8,128)(2,1)} %all-gather.3.cloned.1.call-done), channel_id=1, source_target_pairs={{0,1},{1,0},{2,3},{3,2},{4,5},{5,4},{6,7},{7,6},{8,9},{9,8},{10,11... | collective-permute-start | bytes 6684680 | tf_op jit(solution)/shard_map/ppermute | solution.py:31
  80.8 10.0 %all-to-all-start.3 = ((bf16[32,3,1,128]{3,1,2,0:T(4,128)(2,1)}), bf16[32,3,1,128]{3,1,2,0:T(4,128)(2,1)S(1)}, u32[]{:S(2)}, u32[]{:S(2)}) async-start(bf16[32,3,1,128]{3,1,2,0:T(4,128)(2,1)} %copy.60), calls=%async_computation.3 | async-start | bytes 65536 | tf_op jit(solution)/shard_map/all_to_all | solution.py:116
  90.9 8.8 %all-to-all-done.3 = bf16[32,3,1,128]{3,1,2,0:T(4,128)(2,1)S(1)} async-done(((bf16[32,3,1,128]{3,1,2,0:T(4,128)(2,1)}), bf16[32,3,1,128]{3,1,2,0:T(4,128)(2,1)S(1)}, u32[]{:S(2)}, u32[]{:S(2)}) %all-to-all-start.3) | async-done | bytes 24608 | tf_op jit(solution)/shard_map/all_to_all | solution.py:116
  109.1 3.3 %all-to-all-start.4 = ((bf16[8,4,1,1024]{3,1,2,0:T(4,128)(2,1)}), bf16[8,4,1,1024]{3,1,2,0:T(4,128)(2,1)S(1)}, u32[]{:S(2)}, u32[]{:S(2)}) async-start(bf16[8,4,1,1024]{3,1,2,0:T(4,128)(2,1)} %broadcast_in_dim.50), calls=%async_computation.4 | async-start | bytes 131072 | tf_op jit(solution)/shard_map/all_to_all | solution.py:36
  112.5 3.1 %collective-permute-start.6 = (bf16[14,64,256]{2,1,0:T(8,128)(2,1)S(1)}, bf16[14,64,256]{2,1,0:T(8,128)(2,1)S(1)}, u32[]{:S(2)}, u32[]{:S(2)}) collective-permute-start(bf16[14,64,256]{2,1,0:T(8,128)(2,1)S(1)} %copy-done.1), channel_id=1, source_target_pairs={{0,1},{1,0},{2,3},{3,2},{4,5},{5,4},{6,7},{7,6},{8,9},{9,8},{10,11... | collective-permute-start | bytes 1376264 | tf_op jit(solution)/shard_map/ppermute | solution.py:31
  133.3 4.9 %all-to-all-start.5 = ((bf16[8,2,1,1024]{3,1,2,0:T(2,128)(2,1)}), bf16[8,2,1,1024]{3,1,2,0:T(2,128)(2,1)S(1)}, u32[]{:S(2)}, u32[]{:S(2)}) async-start(bf16[8,2,1,1024]{3,1,2,0:T(2,128)(2,1)} %broadcast_in_dim.51), calls=%async_computation.5 | async-start | bytes 65536 | tf_op jit(solution)/shard_map/all_to_all | solution.py:36
  155.3 6.6 %all-to-all-start.6 = ((bf16[8,2,512]{2,1,0:T(2,128)(2,1)}), bf16[8,2,512]{2,1,0:T(2,128)(2,1)S(1)}, u32[]{:S(2)}, u32[]{:S(2)}) async-start(bf16[8,2,512]{2,1,0:T(2,128)(2,1)} %reshape.2267), calls=%async_computation.6 | async-start | bytes 32768 | tf_op jit(solution)/shard_map/all_to_all | solution.py:36
  162.1 6.6 %all-to-all-done.6 = bf16[8,2,512]{2,1,0:T(2,128)(2,1)S(1)} async-done(((bf16[8,2,512]{2,1,0:T(2,128)(2,1)}), bf16[8,2,512]{2,1,0:T(2,128)(2,1)S(1)}, u32[]{:S(2)}, u32[]{:S(2)}) %all-to-all-start.6) | async-done | bytes 16416 | tf_op jit(solution)/shard_map/all_to_all | solution.py:36
  171.4 3.3 %all-to-all-start.7 = ((bf16[8,2,512]{2,1,0:T(2,128)(2,1)}), bf16[8,2,512]{2,1,0:T(2,128)(2,1)S(1)}, u32[]{:S(2)}, u32[]{:S(2)}) async-start(bf16[8,2,512]{2,1,0:T(2,128)(2,1)} %reshape.2269), calls=%async_computation.7 | async-start | bytes 32768 | tf_op jit(solution)/shard_map/all_to_all | solution.py:36
  174.8 6.5 %all-to-all-done.7 = bf16[8,2,512]{2,1,0:T(2,128)(2,1)S(1)} async-done(((bf16[8,2,512]{2,1,0:T(2,128)(2,1)}), bf16[8,2,512]{2,1,0:T(2,128)(2,1)S(1)}, u32[]{:S(2)}, u32[]{:S(2)}) %all-to-all-start.7) | async-done | bytes 16416 | tf_op jit(solution)/shard_map/all_to_all | solution.py:36
  187.1 3.3 %all-to-all-start.8 = ((bf16[8,2,1,1024]{3,1,2,0:T(2,128)(2,1)}), bf16[8,2,1,1024]{3,1,2,0:T(2,128)(2,1)S(1)}, u32[]{:S(2)}, u32[]{:S(2)}) async-start(bf16[8,2,1,1024]{3,1,2,0:T(2,128)(2,1)} %broadcast_in_dim.54), calls=%async_computation.8 | async-start | bytes 65536 | tf_op jit(solution)/shard_map/all_to_all | solution.py:36
  195.2 2.0 all-to-all-done.8
  208.1 4.6 %all-to-all-start.9 = ((bf16[8,4,1,1024]{3,1,2,0:T(4,128)(2,1)}), bf16[8,4,1,1024]{3,1,2,0:T(4,128)(2,1)S(1)}, u32[]{:S(2)}, u32[]{:S(2)}) async-start(bf16[8,4,1,1024]{3,1,2,0:T(4,128)(2,1)} %broadcast_in_dim.55), calls=%async_computation.9 | async-start | bytes 131072 | tf_op jit(solution)/shard_map/all_to_all | solution.py:36
  212.7 7.2 %all-to-all-done.9 = bf16[8,4,1,1024]{3,1,2,0:T(4,128)(2,1)S(1)} async-done(((bf16[8,4,1,1024]{3,1,2,0:T(4,128)(2,1)}), bf16[8,4,1,1024]{3,1,2,0:T(4,128)(2,1)S(1)}, u32[]{:S(2)}, u32[]{:S(2)}) %all-to-all-start.9) | async-done | bytes 65568 | tf_op jit(solution)/shard_map/all_to_all | solution.py:36
  220.6 3.8 %all-to-all-start.10 = ((bf16[32,7,1,256]{3,1,2,0:T(8,128)(2,1)}), bf16[32,7,1,256]{3,1,2,0:T(8,128)(2,1)S(1)}, u32[]{:S(2)}, u32[]{:S(2)}) async-start(bf16[32,7,1,256]{3,1,2,0:T(8,128)(2,1)} %bitcast.309), calls=%async_computation.10 | async-start | bytes 262144 | tf_op jit(solution)/shard_map/all_to_all | solution.py:147
  224.7 9.2 %all-to-all-done.10 = bf16[32,7,1,256]{3,1,2,0:T(8,128)(2,1)S(1)} async-done(((bf16[32,7,1,256]{3,1,2,0:T(8,128)(2,1)}), bf16[32,7,1,256]{3,1,2,0:T(8,128)(2,1)S(1)}, u32[]{:S(2)}, u32[]{:S(2)}) %all-to-all-start.10) | async-done | bytes 114720 | tf_op jit(solution)/shard_map/all_to_all | solution.py:147
  234.1 6.1 %broadcast_multiply_fusion.3 = (bf16[1,32,256]{2,0,1:T(2,128)(2,1)S(1)}, bf16[1,32,256]{2,0,1:T(2,128)(2,1)S(1)}, bf16[1,32,256]{2,0,1:T(2,128)(2,1)S(1)}, bf16[...) fusion(bf16[]{:T(256)} %bitcast.351, ...), kind=kLoop, calls=%fused_computation.371 | loop fusion | flops 73728 | bytes 196626 | tf_op jit(solution)/shard_map/mul | solution.py:167
  241.7 3.3 %all-to-all-start.11 = ((bf16[4,32,128]{2,1,0:T(8,128)(2,1)}), bf16[4,32,128]{2,1,0:T(8,128)(2,1)S(1)}, u32[]{:S(2)}, u32[]{:S(2)}) async-start(bf16[4,32,128]{2,1,0:T(8,128)(2,1)} %broadcast_in_dim.58), calls=%async_computation.11 | async-start | bytes 65536 | tf_op jit(solution)/shard_map/all_to_all | solution.py:36
  245.9 8.4 %collective-permute-start.5 = (bf16[7,16,32]{1,0,2:T(8,128)(2,1)S(1)}, bf16[7,16,32]{1,0,2:T(8,128)(2,1)S(1)}, u32[]{:S(2)}, u32[]{:S(2)}) collective-permute-start(bf16[7,16,32]{1,0,2:T(8,128)(2,1)S(1)} %get-tuple-element.7), channel_id=1, source_target_pairs={{0,1},{1,0},{2,3},{3,2},{4,5},{5,4},{6,7},{7,6},{8,9},{9,8},{10,11... | collective-permute-start | bytes 21512 | tf_op jit(solution)/shard_map/ppermute | solution.py:31
  255.8 3.4 %all-to-all-start.12 = ((bf16[8,32,256]{2,1,0:T(8,128)(2,1)}), bf16[8,32,256]{2,1,0:T(8,128)(2,1)S(1)}, u32[]{:S(2)}, u32[]{:S(2)}) async-start(bf16[8,32,256]{2,1,0:T(8,128)(2,1)} %broadcast_in_dim.59), calls=%async_computation.12 | async-start | bytes 262144 | tf_op jit(solution)/shard_map/all_to_all | solution.py:36
  259.7 7.4 %all-to-all-done.12 = bf16[8,32,256]{2,1,0:T(8,128)(2,1)S(1)} async-done(((bf16[8,32,256]{2,1,0:T(8,128)(2,1)}), bf16[8,32,256]{2,1,0:T(8,128)(2,1)S(1)}, u32[]{:S(2)}, u32[]{:S(2)}) %all-to-all-start.12) | async-done | bytes 131104 | tf_op jit(solution)/shard_map/all_to_all | solution.py:36
  271.0 5.9 %all-to-all-start.13 = ((bf16[4,2,32,128]{3,2,1,0:T(8,128)(2,1)}), bf16[4,2,32,128]{3,2,1,0:T(8,128)(2,1)S(1)}, u32[]{:S(2)}, u32[]{:S(2)}) async-start(bf16[4,2,32,128]{3,2,1,0:T(8,128)(2,1)} %broadcast_in_dim.60), calls=%async_computation.13 | async-start | bytes 131072 | tf_op jit(solution)/shard_map/all_to_all | solution.py:36
  277.1 4.4 %all-to-all-done.13 = bf16[4,2,32,128]{3,2,1,0:T(8,128)(2,1)S(1)} async-done(((bf16[4,2,32,128]{3,2,1,0:T(8,128)(2,1)}), bf16[4,2,32,128]{3,2,1,0:T(8,128)(2,1)S(1)}, u32[]{:S(2)}, u32[]{:S(2)}) %all-to-all-start.13) | async-done | bytes 65568 | tf_op jit(solution)/shard_map/all_to_all | solution.py:36
  283.2 5.2 %all-to-all-start.14 = ((bf16[16,2,768]{2,1,0:T(2,128)(2,1)}), bf16[16,2,768]{2,1,0:T(2,128)(2,1)S(1)}, u32[]{:S(2)}, u32[]{:S(2)}) async-start(bf16[16,2,768]{2,1,0:T(2,128)(2,1)} %reshape.2271), calls=%async_computation.14 | async-start | bytes 98304 | tf_op jit(solution)/shard_map/all_to_all | solution.py:185
  289.2 6.8 %all-to-all-done.14 = bf16[16,2,768]{2,1,0:T(2,128)(2,1)S(1)} async-done(((bf16[16,2,768]{2,1,0:T(2,128)(2,1)}), bf16[16,2,768]{2,1,0:T(2,128)(2,1)S(1)}, u32[]{:S(2)}, u32[]{:S(2)}) %all-to-all-start.14) | async-done | bytes 49184 | tf_op jit(solution)/shard_map/all_to_all | solution.py:185
  (287 shorter events, 110.8 us)
Async XLA Ops:
  7.2 23.9 %copy-start.3 = (s32[3]{0:T(128)S(1)}, s32[3]{0:T(128)}, u32[]{:S(2)}) copy-start(s32[3]{0:T(128)} %constant.103.clone) | copy-start | bytes 40
  7.2 17.8 %copy-start = (bf16[14,64,256]{2,1,0:T(8,128)(2,1)S(1)}, bf16[14,64,256]{2,1,0:T(8,128)(2,1)}, u32[]{:S(2)}) copy-start(bf16[14,64,256]{2,1,0:T(8,128)(2,1)} %param.11) | copy-start | bytes 1376260
  7.2 24.1 %copy-start.4 = (s32[11,2]{0,1:T(2,128)S(1)}, s32[11,2]{0,1:T(2,128)}, u32[]{:S(2)}) copy-start(s32[11,2]{0,1:T(2,128)} %param.16) | copy-start | bytes 268
  7.2 65.4 %all-gather.3.cloned.1.call-start = ((), (), s32[]{:S(2)}) async-start(), calls=%async_computation.15 | async-start | bytes 2785280 | tf_op jit(solution)/shard_map/all_gather | solution.py:77
  7.9 107.8 %all-gather.5.cloned.1.call-start = ((), (), s32[]{:S(2)}) async-start(), calls=%async_computation.16 | async-start | bytes 2785280 | tf_op jit(solution)/shard_map/all_gather | solution.py:77
  9.1 15.8 %collective-permute-start.1 = (bf16[3,64,32]{1,2,0:T(8,128)(2,1)S(1)}, bf16[3,64,32]{1,2,0:T(8,128)(2,1)S(1)}, u32[]{:S(2)}, u32[]{:S(2)}) collective-permute-start(bf16[3,64,32]{1,2,0:T(8,128)(2,1)S(1)} %copy.92), channel_id=1, source_target_pairs={{0,1},{1,0},{2,3},{3,2},{4,5},{5,4},{6,7},{7,6},{8,9},{9,8},{10,11... | collective-permute-start | bytes 36872 | tf_op jit(solution)/shard_map/ppermute | solution.py:31
  17.8 7.4 %collective-permute-start.2 = (bf16[14,64,256]{2,1,0:T(8,128)(2,1)}, bf16[14,64,256]{2,1,0:T(8,128)(2,1)S(1)}, u32[]{:S(2)}, u32[]{:S(2)}) collective-permute-start(bf16[14,64,256]{2,1,0:T(8,128)(2,1)} %param.11), channel_id=1, source_target_pairs={{0,1},{1,0},{2,3},{3,2},{4,5},{5,4},{6,7},{7,6},{8,9},{9,8},{10,11... | collective-permute-start | bytes 1376264 | tf_op jit(solution)/shard_map/ppermute | solution.py:31
  21.0 69.8 %collective-permute-start = (bf16[7,64,1]{1,0,2:T(8,128)(2,1)S(1)}, bf16[7,64,1]{1,0,2:T(8,128)(2,1)S(1)}, u32[]{:S(2)}, u32[]{:S(2)}) collective-permute-start(bf16[7,64,1]{1,0,2:T(8,128)(2,1)S(1)} %copy.90), channel_id=1, source_target_pairs={{0,1},{1,0},{2,3},{3,2},{4,5},{5,4},{6,7},{7,6},{8,9},{9,8},{10,11... | collective-permute-start | bytes 2696 | tf_op jit(solution)/shard_map/ppermute | solution.py:31
  26.4 17.1 %all-to-all-start = ((bf16[8,2,32,256]{3,2,1,0:T(8,128)(2,1)}), bf16[8,2,32,256]{3,2,1,0:T(8,128)(2,1)S(1)}, u32[]{:S(2)}, u32[]{:S(2)}) async-start(bf16[8,2,32,256]{3,2,1,0:T(8,128)(2,1)} %broadcast_in_dim.47), calls=%async_computation | async-start | bytes 524288 | tf_op jit(solution)/shard_map/all_to_all | solution.py:36
  44.2 68.2 %copy-start.1 = (bf16[14,64,256]{2,1,0:T(8,128)(2,1)S(1)}, bf16[14,64,256]{2,1,0:T(8,128)(2,1)}, u32[]{:S(2)}) copy-start(bf16[14,64,256]{2,1,0:T(8,128)(2,1)} %param.12) | copy-start | bytes 1376260
  47.3 11.8 %all-to-all-start.1 = ((bf16[4,32,128]{2,1,0:T(8,128)(2,1)}), bf16[4,32,128]{2,1,0:T(8,128)(2,1)S(1)}, u32[]{:S(2)}, u32[]{:S(2)}) async-start(bf16[4,32,128]{2,1,0:T(8,128)(2,1)} %broadcast_in_dim.48), calls=%async_computation.1 | async-start | bytes 65536 | tf_op jit(solution)/shard_map/all_to_all | solution.py:36
  60.1 11.0 %all-to-all-start.2 = ((bf16[8,32,256]{2,1,0:T(8,128)(2,1)}), bf16[8,32,256]{2,1,0:T(8,128)(2,1)S(1)}, u32[]{:S(2)}, u32[]{:S(2)}) async-start(bf16[8,32,256]{2,1,0:T(8,128)(2,1)} %broadcast_in_dim.49), calls=%async_computation.2 | async-start | bytes 262144 | tf_op jit(solution)/shard_map/all_to_all | solution.py:36
  72.6 31.4 %collective-permute-start.3 = (bf16[17,64,1024]{2,1,0:T(8,128)(2,1)}, bf16[17,64,1024]{2,1,0:T(8,128)(2,1)}, u32[]{:S(2)}, u32[]{:S(2)}) collective-permute-start(bf16[17,64,1024]{2,1,0:T(8,128)(2,1)} %all-gather.3.cloned.1.call-done), channel_id=1, source_target_pairs={{0,1},{1,0},{2,3},{3,2},{4,5},{5,4},{6,7},{7,6},{8,9},{9,8},{10,11... | collective-permute-start | bytes 6684680 | tf_op jit(solution)/shard_map/ppermute | solution.py:31
  80.8 18.8 %all-to-all-start.3 = ((bf16[32,3,1,128]{3,1,2,0:T(4,128)(2,1)}), bf16[32,3,1,128]{3,1,2,0:T(4,128)(2,1)S(1)}, u32[]{:S(2)}, u32[]{:S(2)}) async-start(bf16[32,3,1,128]{3,1,2,0:T(4,128)(2,1)} %copy.60), calls=%async_computation.3 | async-start | bytes 65536 | tf_op jit(solution)/shard_map/all_to_all | solution.py:116
  109.1 10.5 %all-to-all-start.4 = ((bf16[8,4,1,1024]{3,1,2,0:T(4,128)(2,1)}), bf16[8,4,1,1024]{3,1,2,0:T(4,128)(2,1)S(1)}, u32[]{:S(2)}, u32[]{:S(2)}) async-start(bf16[8,4,1,1024]{3,1,2,0:T(4,128)(2,1)} %broadcast_in_dim.50), calls=%async_computation.4 | async-start | bytes 131072 | tf_op jit(solution)/shard_map/all_to_all | solution.py:36
  112.5 128.0 %collective-permute-start.6 = (bf16[14,64,256]{2,1,0:T(8,128)(2,1)S(1)}, bf16[14,64,256]{2,1,0:T(8,128)(2,1)S(1)}, u32[]{:S(2)}, u32[]{:S(2)}) collective-permute-start(bf16[14,64,256]{2,1,0:T(8,128)(2,1)S(1)} %copy-done.1), channel_id=1, source_target_pairs={{0,1},{1,0},{2,3},{3,2},{4,5},{5,4},{6,7},{7,6},{8,9},{9,8},{10,11... | collective-permute-start | bytes 1376264 | tf_op jit(solution)/shard_map/ppermute | solution.py:31
  115.7 53.2 %collective-permute-start.4 = (bf16[17,64,1024]{2,1,0:T(8,128)(2,1)}, bf16[17,64,1024]{2,1,0:T(8,128)(2,1)}, u32[]{:S(2)}, u32[]{:S(2)}) collective-permute-start(bf16[17,64,1024]{2,1,0:T(8,128)(2,1)} %all-gather.5.cloned.1.call-done), channel_id=1, source_target_pairs={{0,1},{1,0},{2,3},{3,2},{4,5},{5,4},{6,7},{7,6},{8,9},{9,8},{10,11... | collective-permute-start | bytes 6684680 | tf_op jit(solution)/shard_map/ppermute | solution.py:31
  119.7 49.0 %copy-start.2 = (bf16[17,64,1024]{2,1,0:T(8,128)(2,1)S(1)}, bf16[17,64,1024]{2,1,0:T(8,128)(2,1)}, u32[]{:S(2)}) copy-start(bf16[17,64,1024]{2,1,0:T(8,128)(2,1)} %all-gather.5.cloned.1.call-done) | copy-start | bytes 6684676
  133.3 13.6 %all-to-all-start.5 = ((bf16[8,2,1,1024]{3,1,2,0:T(2,128)(2,1)}), bf16[8,2,1,1024]{3,1,2,0:T(2,128)(2,1)S(1)}, u32[]{:S(2)}, u32[]{:S(2)}) async-start(bf16[8,2,1,1024]{3,1,2,0:T(2,128)(2,1)} %broadcast_in_dim.51), calls=%async_computation.5 | async-start | bytes 65536 | tf_op jit(solution)/shard_map/all_to_all | solution.py:36
  155.3 13.3 %all-to-all-start.6 = ((bf16[8,2,512]{2,1,0:T(2,128)(2,1)}), bf16[8,2,512]{2,1,0:T(2,128)(2,1)S(1)}, u32[]{:S(2)}, u32[]{:S(2)}) async-start(bf16[8,2,512]{2,1,0:T(2,128)(2,1)} %reshape.2267), calls=%async_computation.6 | async-start | bytes 32768 | tf_op jit(solution)/shard_map/all_to_all | solution.py:36
  171.4 9.9 %all-to-all-start.7 = ((bf16[8,2,512]{2,1,0:T(2,128)(2,1)}), bf16[8,2,512]{2,1,0:T(2,128)(2,1)S(1)}, u32[]{:S(2)}, u32[]{:S(2)}) async-start(bf16[8,2,512]{2,1,0:T(2,128)(2,1)} %reshape.2269), calls=%async_computation.7 | async-start | bytes 32768 | tf_op jit(solution)/shard_map/all_to_all | solution.py:36
  187.1 10.1 %all-to-all-start.8 = ((bf16[8,2,1,1024]{3,1,2,0:T(2,128)(2,1)}), bf16[8,2,1,1024]{3,1,2,0:T(2,128)(2,1)S(1)}, u32[]{:S(2)}, u32[]{:S(2)}) async-start(bf16[8,2,1,1024]{3,1,2,0:T(2,128)(2,1)} %broadcast_in_dim.54), calls=%async_computation.8 | async-start | bytes 65536 | tf_op jit(solution)/shard_map/all_to_all | solution.py:36
  208.1 11.8 %all-to-all-start.9 = ((bf16[8,4,1,1024]{3,1,2,0:T(4,128)(2,1)}), bf16[8,4,1,1024]{3,1,2,0:T(4,128)(2,1)S(1)}, u32[]{:S(2)}, u32[]{:S(2)}) async-start(bf16[8,4,1,1024]{3,1,2,0:T(4,128)(2,1)} %broadcast_in_dim.55), calls=%async_computation.9 | async-start | bytes 131072 | tf_op jit(solution)/shard_map/all_to_all | solution.py:36
  220.6 13.3 %all-to-all-start.10 = ((bf16[32,7,1,256]{3,1,2,0:T(8,128)(2,1)}), bf16[32,7,1,256]{3,1,2,0:T(8,128)(2,1)S(1)}, u32[]{:S(2)}, u32[]{:S(2)}) async-start(bf16[32,7,1,256]{3,1,2,0:T(8,128)(2,1)} %bitcast.309), calls=%async_computation.10 | async-start | bytes 262144 | tf_op jit(solution)/shard_map/all_to_all | solution.py:147
  241.7 13.1 %all-to-all-start.11 = ((bf16[4,32,128]{2,1,0:T(8,128)(2,1)}), bf16[4,32,128]{2,1,0:T(8,128)(2,1)S(1)}, u32[]{:S(2)}, u32[]{:S(2)}) async-start(bf16[4,32,128]{2,1,0:T(8,128)(2,1)} %broadcast_in_dim.58), calls=%async_computation.11 | async-start | bytes 65536 | tf_op jit(solution)/shard_map/all_to_all | solution.py:36
  245.9 13.7 %collective-permute-start.5 = (bf16[7,16,32]{1,0,2:T(8,128)(2,1)S(1)}, bf16[7,16,32]{1,0,2:T(8,128)(2,1)S(1)}, u32[]{:S(2)}, u32[]{:S(2)}) collective-permute-start(bf16[7,16,32]{1,0,2:T(8,128)(2,1)S(1)} %get-tuple-element.7), channel_id=1, source_target_pairs={{0,1},{1,0},{2,3},{3,2},{4,5},{5,4},{6,7},{7,6},{8,9},{9,8},{10,11... | collective-permute-start | bytes 21512 | tf_op jit(solution)/shard_map/ppermute | solution.py:31
  255.8 11.3 %all-to-all-start.12 = ((bf16[8,32,256]{2,1,0:T(8,128)(2,1)}), bf16[8,32,256]{2,1,0:T(8,128)(2,1)S(1)}, u32[]{:S(2)}, u32[]{:S(2)}) async-start(bf16[8,32,256]{2,1,0:T(8,128)(2,1)} %broadcast_in_dim.59), calls=%async_computation.12 | async-start | bytes 262144 | tf_op jit(solution)/shard_map/all_to_all | solution.py:36
  271.0 10.4 %all-to-all-start.13 = ((bf16[4,2,32,128]{3,2,1,0:T(8,128)(2,1)}), bf16[4,2,32,128]{3,2,1,0:T(8,128)(2,1)S(1)}, u32[]{:S(2)}, u32[]{:S(2)}) async-start(bf16[4,2,32,128]{3,2,1,0:T(8,128)(2,1)} %broadcast_in_dim.60), calls=%async_computation.13 | async-start | bytes 131072 | tf_op jit(solution)/shard_map/all_to_all | solution.py:36
  283.2 12.8 %all-to-all-start.14 = ((bf16[16,2,768]{2,1,0:T(2,128)(2,1)}), bf16[16,2,768]{2,1,0:T(2,128)(2,1)S(1)}, u32[]{:S(2)}, u32[]{:S(2)}) async-start(bf16[16,2,768]{2,1,0:T(2,128)(2,1)} %reshape.2271), calls=%async_computation.14 | async-start | bytes 98304 | tf_op jit(solution)/shard_map/all_to_all | solution.py:185
Sparse Core Ops, SparseCore 0:
  10.1 44.9 all-gather.2
  57.2 40.9 all-gather.4

commit v2 on v1

v2 whole, which is shorter than its diff:
```python
import functools

import jax
import jax.numpy as jnp
import numpy as np
from jax import lax
from jax.experimental import pallas as pl
from jax.experimental.pallas import tpu as pltpu
from jax.sharding import Mesh, PartitionSpec as P

SUB_LEVELS = 2
SUB_NODES = 3
LEAVES = (1, 2)
CORES = 2
ROWS8 = 8
F32 = jnp.float32
BF16 = jnp.bfloat16
VMEM_BYTES = 24 * 2**20


def level_span(depth):
    return 2**depth - 1, 2 ** (depth + 1) - 1


def depth_of(node):
    return (node + 1).bit_length() - 1


def above(node, level):
    return ((node + 1) >> (depth_of(node) - level)) - 1


def swapped(array):
    return lax.ppermute(array, "core", [(0, 1), (1, 0)])


def shape(dtype, *dims):
    return jax.ShapeDtypeStruct(dims, dtype)


def run(body, outs, smem, vmem, scratch=()):
    in_specs = [pl.BlockSpec(memory_space=pltpu.SMEM)] * len(smem)
    in_specs += [pl.BlockSpec(memory_space=pltpu.VMEM)] * len(vmem)
    single = not isinstance(outs, (list, tuple))
    spec = pl.BlockSpec(memory_space=pltpu.VMEM)
    return pl.pallas_call(
        body,
        out_shape=outs,
        in_specs=in_specs,
        out_specs=spec if single else [spec] * len(outs),
        scratch_shapes=list(scratch),
        compiler_params=pltpu.CompilerParams(vmem_limit_bytes=VMEM_BYTES),
    )(*smem, *vmem)


def total(tiles_ref):
    value = tiles_ref[0].astype(F32)
    for i in range(1, tiles_ref.shape[0]):
        value = value + tiles_ref[i].astype(F32)
    return value


def to_all(out_ref, value):
    value = value.astype(out_ref.dtype)
    for i in range(out_ref.shape[0]):
        out_ref[i] = value


def block(own_ref, other_ref, index):
    return jnp.concatenate([own_ref[index], other_ref[index]], 0)


def times(v, matrix):
    return lax.dot_general(v, matrix, (((1,), (0,)), ((), ())), preferred_element_type=F32)


def times_t(v, matrix):
    return lax.dot_general(v, matrix, (((1,), (1,)), ((), ())), preferred_element_type=F32)


def in_row(v, row):
    rows = lax.broadcasted_iota(jnp.int32, v.shape, 0)
    return jnp.where(rows == row, v, 0.0)


def own_first(v, core):
    return jnp.where(core == 1, pltpu.roll(v, v.shape[1] // 2, 1), v)


class Pairs:
    def __init__(self, levels, anc_count):
        self.sub = {}
        for m in range(SUB_NODES):
            for kind, count in ((0, levels), (1, depth_of(m))):
                for u in range(count):
                    self.sub[m, kind, u] = len(self.sub)
        self.anc = {}
        for a in range(anc_count):
            for u in range(depth_of(a)):
                self.anc[a, u] = anc_count + len(self.anc)


def sub_leaf_solve(rhs, own, other, out):
    for m in LEAVES:
        part = times(rhs[m], block(own, other, m)).astype(BF16)
        for i in range(out.shape[0]):
            out[i, m - 1] = part


def sub_low(y, w, pairs, own, other, m, kind, u):
    p = pairs.sub[m, kind, u]
    return w[p] * times_t(y, block(own, other, SUB_NODES + p))


def sub_leaf_update(pairs, w, tiles, own, other, y_out, out):
    y = total(tiles).astype(BF16)
    y_out[...] = y
    value = sum(sub_low(y[m - 1], w, pairs, own, other, m, 1, 0) for m in LEAVES)
    to_all(out, value)


def sub_leaf_anc(pairs, levels, w, y, own, other, out):
    for e in range(levels):
        out[e] = sum(sub_low(y[m - 1], w, pairs, own, other, m, 0, e) for m in LEAVES)


def sub_root_solve(tiles, rhs, own, other, out):
    given = (rhs[0].astype(F32) - total(tiles)).astype(BF16)
    to_all(out, times(given, block(own, other, 0)))


def sub_root_anc(pairs, levels, w, tiles, so_far, own, other, y_out, out):
    y = total(tiles).astype(BF16)
    y_out[...] = y
    out[...] = jnp.zeros_like(out)
    for e in range(levels):
        out[:, e, :] = so_far[e] + sub_low(y, w, pairs, own, other, 0, 0, e)


def solve_level(pairs, depth, v8, own, other, out, scratch):
    first, stop = level_span(depth)
    value = jnp.zeros_like(scratch)
    for i, a in enumerate(range(first, stop)):
        value = value + in_row(times(v8, block(own, other, i)), a)
    scratch[...] = value
    to_all(out, scratch[first : first + out.shape[1], :])


def anc_first(pairs, depth, tiles, choose, given, own, other, acc_out, out, scratch):
    acc = given[...]
    for e in range(choose.shape[0]):
        acc = acc - lax.dot_general(
            choose[e],
            tiles[:, e, :],
            (((1,), (0,)), ((), ())),
            precision=lax.Precision.HIGHEST,
            preferred_element_type=F32,
        )
    acc_out[...] = acc
    solve_level(pairs, depth, acc.astype(BF16), own, other, out, scratch)


def anc_forward(pairs, depth, tiles, y_in, acc_in, low, low_x, own, other, y_out, acc_out, out, scratch):
    first, stop = level_span(depth)
    y_out[...] = y_in[...]
    y_out[first:stop, :] = total(tiles)[: stop - first].astype(BF16).astype(F32)
    acc = acc_in[...]
    start = pairs.anc[first, 0]
    for d in range(first, stop):
        y = jnp.broadcast_to(y_out[d : d + 1, :], y_out.shape)
        for u in range(depth):
            v = in_row(y, above(d, u)).astype(BF16)
            acc = acc - times_t(v, block(low, low_x, pairs.anc[d, u] - start))
    acc_out[...] = acc
    solve_level(pairs, depth - 1, acc.astype(BF16), own, other, out, scratch)


def anc_turn(pairs, where, tiles, y_in, own, other, y_out, out, scratch):
    core, z = where[0], where[1]
    y_out[...] = y_in[...]
    y_out[0:1, :] = total(tiles)[:1].astype(BF16).astype(F32)
    pair_rows = own.shape[1] * CORES
    t = own_first(y_out[:, pl.ds(pl.multiple_of(z * pair_rows, pair_rows), pair_rows)], core)
    solve_level(pairs, 0, t.astype(BF16), own, other, out, scratch)


def anc_backward(pairs, depth, where, tiles, z_in, y_in, up, up_x, own, other, z_out, out, scratch):
    core, z = where[0], where[1]
    first, stop = level_span(depth - 1)
    z_out[...] = z_in[...]
    z_out[first:stop, :] = total(tiles)[: stop - first].astype(BF16).astype(F32)
    pair_rows = own.shape[1] * CORES
    acc = own_first(y_in[:, pl.ds(pl.multiple_of(z * pair_rows, pair_rows), pair_rows)], core)
    first, stop = level_span(depth)
    start = pairs.anc[first, 0]
    for a in range(first, stop):
        for u in range(depth):
            q = above(a, u)
            v = in_row(jnp.broadcast_to(z_out[q : q + 1, :], z_out.shape), a).astype(BF16)
            acc = acc - times_t(v, block(up, up_x, pairs.anc[a, u] - start))
    solve_level(pairs, depth, acc.astype(BF16), own, other, out, scratch)


def anc_spread(depth, nrow, tiles, z_in, out, scratch):
    first, stop = level_span(depth)
    scratch[...] = z_in[...]
    scratch[first:stop, :] = total(tiles)
    wide = out.shape[2]
    for i in range(out.shape[0]):
        r = i % nrow
        out[i] = scratch[:, r * wide : (r + 1) * wide].astype(BF16)


def sub_turn(pairs, levels, where, ids, w, tiles, y_root, y_leaf, own, other, kept, out, scratch):
    core, held, base = where[0], where[3], where[4]
    scratch[...] = tiles[...].astype(F32)
    picked = []
    for e in range(levels):
        value = 0.0
        for a in range(*level_span(e)):
            value = value + jnp.where(ids[e] == a, 1.0, 0.0) * scratch[:, a, :]
        picked.append(value.astype(BF16))
    pair_rows = own.shape[1] * CORES
    scale = held.astype(F32)
    for m in range(SUB_NODES):
        span = pl.ds(pl.multiple_of(base, pair_rows), pair_rows)
        y = y_root[:, span] if m == 0 else y_leaf[m - 1, :, span]
        value = scale * own_first(y.astype(F32), core)
        for e in range(levels):
            p = pairs.sub[m, 0, e]
            value = value - w[p] * times_t(picked[e], block(own, other, SUB_NODES + p))
        if m == 0:
            to_all(out, value)
        else:
            kept[m - 1] = value


def sub_root_back(tiles, own, other, kept, out):
    value = times(total(tiles).astype(BF16), block(own, other, 0))
    kept[...] = value
    to_all(out, value)


def sub_leaf_back(pairs, w, tiles, kept, own, other, out):
    z = total(tiles).astype(BF16)
    for m in LEAVES:
        p = pairs.sub[m, 1, 0]
        value = kept[m - 1] - w[p] * times_t(z, block(own, other, SUB_NODES + p))
        for i in range(out.shape[0]):
            out[i, m - 1] = value.astype(BF16)


def sub_finish(tiles, root, own, other, out):
    t = total(tiles).astype(BF16)
    parts = [root[...]] + [times(t[m - 1], block(own, other, m)) for m in LEAVES]
    fill = out.shape[2] - sum(part.shape[0] for part in parts)
    if fill:
        parts.append(jnp.zeros((fill, parts[0].shape[1]), F32))
    flipped = jnp.concatenate(parts, 0).T
    out[...] = flipped.reshape(out.shape).astype(BF16)


def local(anc_lower, anc_upper, sub_lower, sub_upper, anc_rhs, sub_rhs, layer_subtree, sub_pattern):
    layers = lax.axis_size("gz")
    levels = layers.bit_length() - 1
    anc_count = layers - 1
    nrow, nz = lax.axis_size("row"), lax.axis_size("z")
    own, wide = sub_lower.shape[1:]
    size = wide * nrow
    pair_rows = own * CORES
    out_rows = wide // (nz * CORES)
    cols = sub_rhs.shape[2] // CORES
    g, r, z, core = (lax.axis_index(name) for name in ("gz", "row", "z", "core"))
    pairs = Pairs(levels, anc_count)
    part = functools.partial
    scr8 = pltpu.VMEM((ROWS8, size), F32)

    low_w = sub_pattern[:, 0].astype(F32)
    up_w = sub_pattern[:, 1].astype(F32)
    powers = jnp.asarray(2 ** (levels - np.arange(levels)), jnp.int32)
    heap_ids = (layer_subtree[:, None] + layers) // powers[None, :] - 1
    nodes = jnp.arange(ROWS8, dtype=jnp.int32)
    choose = (heap_ids.T[:, None, :] == nodes[None, :, None]).astype(F32)
    choose = jnp.repeat(choose, nrow, axis=2)
    ids_here = lax.dynamic_index_in_dim(heap_ids, g, 0, keepdims=False)
    held = (r == z * nrow // nz).astype(jnp.int32)
    base = jnp.clip(z * pair_rows - r * wide, 0, wide - pair_rows)
    where = jnp.stack([core, z, jnp.int32(nz), held, base]).astype(jnp.int32)

    def gathered(blocks):
        return lax.all_gather(blocks, "row", axis=2, tiled=True)

    def exchange(array, axes):
        return lax.all_to_all(array, axes, 0, 0, tiled=True)

    low = (sub_lower, swapped(sub_lower))
    rhs_here = lax.dynamic_slice_in_dim(sub_rhs, core * cols, cols, 2)
    rhs_there = swapped(lax.dynamic_slice_in_dim(sub_rhs, (1 - core) * cols, cols, 2))
    rhs = jnp.concatenate([rhs_here, rhs_there], 1).transpose(0, 2, 1)
    mine = g * nrow + r
    anc_here = lax.dynamic_slice_in_dim(anc_rhs, core * cols + mine, 1, 2)
    anc_there = swapped(lax.dynamic_slice_in_dim(anc_rhs, (1 - core) * cols + mine, 1, 2))
    given8 = jnp.concatenate([anc_here, anc_there], 1)[:, :, 0].astype(F32)
    given8 = jnp.pad(given8, ((0, ROWS8 - anc_count), (0, 0)))
    up = (sub_upper, swapped(sub_upper))
    anc_low_row = gathered(anc_lower)
    anc_low = (anc_low_row, swapped(anc_low_row))
    anc_up_row = gathered(anc_upper)
    anc_up = (anc_up_row, swapped(anc_up_row))

    def diagonal(two, depth):
        first, stop = level_span(depth)
        return [array[first:stop] for array in two]

    def pair_blocks(two, depth):
        first, stop = level_span(depth)
        start = pairs.anc[first, 0]
        return [array[start : start + (stop - first) * depth] for array in two]

    def level_shape(depth):
        return shape(BF16, nz, max(2, 2**depth), size)

    tiles = run(sub_leaf_solve, shape(BF16, nz, 2, cols, wide), (), (rhs, *low))
    tiles = exchange(tiles, "z")
    y_leaf, tiles = run(
        part(sub_leaf_update, pairs),
        (shape(BF16, 2, cols, wide), shape(BF16, nrow, cols, pair_rows)),
        (low_w,),
        (tiles, *low),
    )
    tiles = exchange(tiles, "row")
    so_far = run(
        part(sub_leaf_anc, pairs, levels),
        shape(F32, levels, cols, pair_rows),
        (low_w,),
        (y_leaf, *low),
    )
    tiles = run(sub_root_solve, shape(BF16, nz, cols, wide), (), (tiles, rhs, *low))
    tiles = exchange(tiles, "z")
    y_root, tiles = run(
        part(sub_root_anc, pairs, levels),
        (shape(BF16, cols, wide), shape(F32, cols, ROWS8, pair_rows)),
        (low_w,),
        (tiles, so_far, *low),
    )
    tiles = exchange(tiles, ("gz", "row"))

    y8 = jnp.zeros((ROWS8, size), F32)
    acc, tiles = run(
        part(anc_first, pairs, levels - 1),
        (shape(F32, ROWS8, pair_rows), level_shape(levels - 1)),
        (),
        (tiles, choose, given8, *diagonal(anc_low, levels - 1)),
        (scr8,),
    )
    tiles = exchange(tiles, "z")
    for depth in range(levels - 1, 0, -1):
        y8, acc, tiles = run(
            part(anc_forward, pairs, depth),
            (shape(F32, ROWS8, size), shape(F32, ROWS8, pair_rows), level_shape(depth - 1)),
            (),
            (tiles, y8, acc, *pair_blocks(anc_low, depth), *diagonal(anc_low, depth - 1)),
            (scr8,),
        )
        tiles = exchange(tiles, "z")
    y8, tiles = run(
        part(anc_turn, pairs),
        (shape(F32, ROWS8, size), level_shape(0)),
        (where,),
        (tiles, y8, *diagonal(anc_up, 0)),
        (scr8,),
    )
    tiles = exchange(tiles, "z")
    z8 = jnp.zeros((ROWS8, size), F32)
    for depth in range(1, levels):
        z8, tiles = run(
            part(anc_backward, pairs, depth),
            (shape(F32, ROWS8, size), level_shape(depth)),
            (where,),
            (tiles, z8, y8, *pair_blocks(anc_up, depth), *diagonal(anc_up, depth)),
            (scr8,),
        )
        tiles = exchange(tiles, "z")
    tiles = run(
        part(anc_spread, levels - 1, nrow),
        shape(BF16, layers * nrow, ROWS8, wide),
        (),
        (tiles, z8),
        (scr8,),
    )
    z_all = exchange(tiles, ("gz", "row"))

    kept, tiles = run(
        part(sub_turn, pairs, levels),
        (shape(F32, 2, cols, pair_rows), shape(BF16, nrow, cols, pair_rows)),
        (where, ids_here, up_w),
        (z_all, y_root, y_leaf, *up),
        (pltpu.VMEM(z_all.shape, F32),),
    )
    tiles = exchange(tiles, "row")

    def out_slice(which):
        start = (z * CORES + which) * out_rows
        return lax.dynamic_slice_in_dim(z_all, start, out_rows, 2)[:, :anc_count].transpose(1, 2, 0)

    def joined(here, there):
        flipped = core == 1
        return jnp.concatenate([jnp.where(flipped, there, here), jnp.where(flipped, here, there)], -1)

    anc_out = joined(out_slice(core), swapped(out_slice(1 - core))).astype(F32)

    root, tiles = run(
        sub_root_back,
        (shape(F32, cols, wide), shape(BF16, nz, cols, wide)),
        (),
        (tiles, *up),
    )
    tiles = exchange(tiles, "z")
    tiles = run(
        part(sub_leaf_back, pairs),
        shape(BF16, nrow, 2, cols, pair_rows),
        (up_w,),
        (tiles, kept, *up),
    )
    tiles = exchange(tiles, "row")
    packed = -(-SUB_NODES * cols // 128) * 128
    tiles = run(
        sub_finish,
        shape(BF16, nz * CORES, out_rows, packed),
        (),
        (tiles, root, *up),
    )
    tiles = exchange(tiles, ("z", "core"))
    sums = jnp.sum(tiles.astype(F32).reshape(nz, CORES, out_rows, packed), 0)
    sums = sums[:, :, : SUB_NODES * cols].reshape(CORES, out_rows, SUB_NODES, cols)
    sub_out = sums.transpose(2, 1, 0, 3).reshape(SUB_NODES, out_rows, CORES * cols)
    return anc_out, sub_out


def solution(mesh):
    sizes = dict(mesh.shape)
    devices = mesh.devices.reshape(sizes["gz"], sizes["row"], sizes["col"] // CORES, CORES)
    split = Mesh(devices, ("gz", "row", "z", "core"))
    col = ("z", "core")
    in_specs = (
        P(None, col, "row"),
        P(None, col, "row"),
        P("gz", col, "row"),
        P("gz", col, "row"),
        P(None, col, None),
        P("gz", col, None),
        P(),
        P("gz", None),
    )
    out_specs = (P(None, ("row", "z", "core"), None), P("gz", ("row", "z", "core"), None))
    return jax.shard_map(local, mesh=split, in_specs=in_specs, out_specs=out_specs, check_vma=False)
```

time: 306 us -> 325 us (1.062)
  matrix products: 81.3 us -> 0 us
  waiting for transfers between devices: 78.1 us -> 155 us
  Pallas kernels: 0 us -> 18 us
  local copies, waits for them, and re-layouts: 16.1 us -> 30.1 us
  other arithmetic: 12.8 us -> 2.73 us
  blocking collectives: 0 us -> 6.65 us
  starting transfers between devices: 101 us -> 95.4 us
    dot_general x125 -> x0, matrix products: 81.3 us -> none  [dot(): return jnp.einsum(spec, left, right, preferred_element_type=F32)]
    all_gather x2, waiting for transfers between devices: 0.02 us -> 76.7 us  [gathered(): return lax.all_gather(blocks, 'row', axis=2, tiled=True)]
    pallas_call x0 -> x16, Pallas kernels: none -> 18 us  [run(): pl.pallas_call(body, out_shape=outs, in_specs=in_specs, out_specs=spec if...]
    slice x5 -> x16, local copies, waits for them, and re-layouts: 1.41 us -> 18.4 us  [the longest x10 10.9 us: diagonal(): return [array[first:stop] for array in two]]
    broadcast_in_dim x14 -> x1, local copies, waits for them, and re-layouts: 7.72 us -> 0.02 us  [local(): choose = jnp.repeat(choose, nrow, axis=2)]
    all_to_all x0 -> x1, blocking collectives: none -> 6.65 us  [exchange(): return lax.all_to_all(array, axes, 0, 0, tiled=True)]
    all_to_all x15 -> x14, starting transfers between devices: 69.8 us -> 63.5 us  [exchange(): return lax.all_to_all(array, axes, 0, 0, tiled=True)]
    mul x1 -> x0, other arithmetic: 6.07 us -> none  [up_part(): return applied(up_two, SUB_NODES + p, v * up_w[p])]
  transfers between devices with their start and end apart: 24 -> 23, of which waited for: 12 -> 14; matrix products, arithmetic and copies ran while one was open for 34% -> 7% of each run, Pallas kernels for 0% -> 4%
where the time goes in v2:
time: 325 us; the launch traced here: 322 us
  waiting for transfers between devices  155 us (48%)
  starting transfers between devices  95.4 us (29%)
  local copies, waits for them, and re-layouts  30.1 us (9%)
  Pallas kernels  18 us (6%)
  between operations  14.6 us (4%)
  blocking collectives  6.65 us (2%)
    all_to_all x14, waiting for transfers between devices, exchange(): return lax.all_to_all(array, axes, 0, 0, tiled=True)  76.9 us
    all_gather x2, waiting for transfers between devices, gathered(): return lax.all_gather(blocks, 'row', axis=2, tiled=True)  76.7 us
    all_to_all x14, starting transfers between devices, exchange(): return lax.all_to_all(array, axes, 0, 0, tiled=True)  63.5 us
    ppermute x7, starting transfers between devices, swapped(): return lax.ppermute(array, 'core', [(0, 1), (1, 0)])  31.9 us
    pallas_call x16, Pallas kernels, run(): pl.pallas_call(body, out_shape=outs, in_specs=in_specs, out_specs=spec if...  18 us
    slice x10, local copies, waits for them, and re-layouts, diagonal(): return [array[first:stop] for array in two]  10.9 us
    unnamed x48, local copies, waits for them, and re-layouts  8.3 us
    slice x6, local copies, waits for them, and re-layouts, pair_blocks(): return [array[start:start + (stop - first) * depth] for array in two]  7.44 us
  transfers between devices with their start and end apart: 23, of which 14 were waited for; matrix products, arithmetic and copies ran while one was open for 7% of the time, Pallas kernels for 4%

profile of v2, /device:TPU:1, one launch (start us, length us, event | category | flops | bytes accessed | tf_op | source)
XLA Modules:
  0.0 322.5 jit_solution(15465558834998394638)
XLA Ops:
  8.7 45.9 %all-gather.3.cloned.1.call-done = bf16[17,64,1024]{2,1,0:T(8,128)(2,1)} async-done(((bf16[17,64,256]{2,1,0:T(8,128)(2,1)}), bf16[17,64,1024]{2,1,0:T(8,128)(2,1)}) %all-gather.3.cloned.1.call-update) | async-done | bytes 2228240 | tf_op jit(solution)/shard_map/all_gather | solution.py:291
  54.6 3.9 %collective-permute-start.3 = (bf16[17,64,1024]{2,1,0:T(8,128)(2,1)}, bf16[17,64,1024]{2,1,0:T(8,128)(2,1)}, u32[]{:S(2)}, u32[]{:S(2)}) collective-permute-start(bf16[17,64,1024]{2,1,0:T(8,128)(2,1)} %all-gather.3.cloned.1.call-done), channel_id=1, source_target_pairs={{0,1},{1,0},{2,3},{3,2},{4,5},{5,4},{6,7},{7,6},{8,9},{9,8},{10,11... | collective-permute-start | bytes 6684680 | tf_op jit(solution)/shard_map/ppermute | solution.py:34
  67.2 30.8 %all-gather.5.cloned.1.call-done = bf16[17,64,1024]{2,1,0:T(8,128)(2,1)} async-done(((bf16[17,64,256]{2,1,0:T(8,128)(2,1)}), bf16[17,64,1024]{2,1,0:T(8,128)(2,1)}) %all-gather.5.cloned.1.call-update) | async-done | bytes 2228240 | tf_op jit(solution)/shard_map/all_gather | solution.py:291
  98.1 3.9 %collective-permute-start.4 = (bf16[17,64,1024]{2,1,0:T(8,128)(2,1)}, bf16[17,64,1024]{2,1,0:T(8,128)(2,1)}, u32[]{:S(2)}, u32[]{:S(2)}) collective-permute-start(bf16[17,64,1024]{2,1,0:T(8,128)(2,1)} %all-gather.5.cloned.1.call-done), channel_id=1, source_target_pairs={{0,1},{1,0},{2,3},{3,2},{4,5},{5,4},{6,7},{7,6},{8,9},{9,8},{10,11... | collective-permute-start | bytes 6684680 | tf_op jit(solution)/shard_map/ppermute | solution.py:34
  103.0 7.1 %all-to-all-start = ((bf16[8,2,32,256]{3,2,1,0:T(8,128)(2,1)}), bf16[8,2,32,256]{3,2,1,0:T(8,128)(2,1)S(1)}, u32[]{:S(2)}, u32[]{:S(2)}) async-start(bf16[8,2,32,256]{3,2,1,0:T(8,128)(2,1)} %shard_map.104), calls=%async_computation | async-start | bytes 524288 | tf_op jit(solution)/shard_map/all_to_all | solution.py:294
  110.7 11.7 %all-to-all-done.tiles = bf16[8,2,32,256]{3,2,1,0:T(8,128)(2,1)S(1)} async-done(((bf16[8,2,32,256]{3,2,1,0:T(8,128)(2,1)}), bf16[8,2,32,256]{3,2,1,0:T(8,128)(2,1)S(1)}, u32[]{:S(2)}, u32[]{:S(2)}) %all-to-all-start) | async-done | bytes 262176 | tf_op jit(solution)/shard_map/all_to_all | solution.py:294
  123.8 3.7 %all-to-all-start.1 = ((bf16[4,32,128]{2,1,0:T(8,128)(2,1)}), bf16[4,32,128]{2,1,0:T(8,128)(2,1)S(1)}, u32[]{:S(2)}, u32[]{:S(2)}) async-start(bf16[4,32,128]{2,1,0:T(8,128)(2,1)} %get-tuple-element.23), calls=%async_computation.1 | async-start | bytes 65536 | tf_op jit(solution)/shard_map/all_to_all | solution.py:294
  127.6 4.1 %all-to-all-done.1.tiles = bf16[4,32,128]{2,1,0:T(8,128)(2,1)S(1)} async-done(((bf16[4,32,128]{2,1,0:T(8,128)(2,1)}), bf16[4,32,128]{2,1,0:T(8,128)(2,1)S(1)}, u32[]{:S(2)}, u32[]{:S(2)}) %all-to-all-start.1) | async-done | bytes 32800 | tf_op jit(solution)/shard_map/all_to_all | solution.py:294
  132.5 3.4 %all-to-all-start.2 = ((bf16[8,32,256]{2,1,0:T(8,128)(2,1)}), bf16[8,32,256]{2,1,0:T(8,128)(2,1)S(1)}, u32[]{:S(2)}, u32[]{:S(2)}) async-start(bf16[8,32,256]{2,1,0:T(8,128)(2,1)} %shard_map.106), calls=%async_computation.2 | async-start | bytes 262144 | tf_op jit(solution)/shard_map/all_to_all | solution.py:294
  137.1 6.7 %all-to-all-done.2.tiles = bf16[8,32,256]{2,1,0:T(8,128)(2,1)S(1)} async-done(((bf16[8,32,256]{2,1,0:T(8,128)(2,1)}), bf16[8,32,256]{2,1,0:T(8,128)(2,1)S(1)}, u32[]{:S(2)}, u32[]{:S(2)}) %all-to-all-start.2) | async-done | bytes 131104 | tf_op jit(solution)/shard_map/all_to_all | solution.py:294
  145.2 7.6 %all-to-all-start.3 = ((f32[32,8,128]{2,1,0:T(8,128)}), f32[32,8,128]{2,1,0:T(8,128)S(1)}, u32[]{:S(2)}, u32[]{:S(2)}) async-start(f32[32,8,128]{2,1,0:T(8,128)} %get-tuple-element.25), calls=%async_computation.3 | async-start | bytes 262144 | tf_op jit(solution)/shard_map/all_to_all | solution.py:294
  157.4 4.8 %all-to-all-done.3.tiles = f32[32,8,128]{2,1,0:T(8,128)S(1)} async-done(((f32[32,8,128]{2,1,0:T(8,128)}), f32[32,8,128]{2,1,0:T(8,128)S(1)}, u32[]{:S(2)}, u32[]{:S(2)}) %all-to-all-start.3) | async-done | bytes 131104 | tf_op jit(solution)/shard_map/all_to_all | solution.py:294
  163.4 3.3 %all-to-all-start.4 = ((bf16[8,4,1024]{2,1,0:T(4,128)(2,1)}), bf16[8,4,1024]{2,1,0:T(4,128)(2,1)S(1)}, u32[]{:S(2)}, u32[]{:S(2)}) async-start(bf16[8,4,1024]{2,1,0:T(4,128)(2,1)} %get-tuple-element.26), calls=%async_computation.4 | async-start | bytes 131072 | tf_op jit(solution)/shard_map/all_to_all | solution.py:294
  169.2 4.7 %all-to-all-done.4.tiles = bf16[8,4,1024]{2,1,0:T(4,128)(2,1)S(1)} async-done(((bf16[8,4,1024]{2,1,0:T(4,128)(2,1)}), bf16[8,4,1024]{2,1,0:T(4,128)(2,1)S(1)}, u32[]{:S(2)}, u32[]{:S(2)}) %all-to-all-start.4) | async-done | bytes 65568 | tf_op jit(solution)/shard_map/all_to_all | solution.py:294
  175.4 3.3 %all-to-all-start.5 = ((bf16[8,2,1024]{2,1,0:T(2,128)(2,1)}), bf16[8,2,1024]{2,1,0:T(2,128)(2,1)S(1)}, u32[]{:S(2)}, u32[]{:S(2)}) async-start(bf16[8,2,1024]{2,1,0:T(2,128)(2,1)} %get-tuple-element.28), calls=%async_computation.5 | async-start | bytes 65536 | tf_op jit(solution)/shard_map/all_to_all | solution.py:294
  180.7 4.8 %all-to-all-done.5.tiles = bf16[8,2,1024]{2,1,0:T(2,128)(2,1)S(1)} async-done(((bf16[8,2,1024]{2,1,0:T(2,128)(2,1)}), bf16[8,2,1024]{2,1,0:T(2,128)(2,1)S(1)}, u32[]{:S(2)}, u32[]{:S(2)}) %all-to-all-start.5) | async-done | bytes 32800 | tf_op jit(solution)/shard_map/all_to_all | solution.py:294
  186.5 3.5 %all-to-all-start.6 = ((bf16[8,2,1024]{2,1,0:T(2,128)(2,1)}), bf16[8,2,1024]{2,1,0:T(2,128)(2,1)S(1)}, u32[]{:S(2)}, u32[]{:S(2)}) async-start(bf16[8,2,1024]{2,1,0:T(2,128)(2,1)} %get-tuple-element.31), calls=%async_computation.6 | async-start | bytes 65536 | tf_op jit(solution)/shard_map/all_to_all | solution.py:294
  192.9 3.9 %all-to-all-done.6.tiles = bf16[8,2,1024]{2,1,0:T(2,128)(2,1)S(1)} async-done(((bf16[8,2,1024]{2,1,0:T(2,128)(2,1)}), bf16[8,2,1024]{2,1,0:T(2,128)(2,1)S(1)}, u32[]{:S(2)}, u32[]{:S(2)}) %all-to-all-start.6) | async-done | bytes 32800 | tf_op jit(solution)/shard_map/all_to_all | solution.py:294
  198.2 3.3 %all-to-all-start.7 = ((bf16[8,2,1024]{2,1,0:T(2,128)(2,1)}), bf16[8,2,1024]{2,1,0:T(2,128)(2,1)S(1)}, u32[]{:S(2)}, u32[]{:S(2)}) async-start(bf16[8,2,1024]{2,1,0:T(2,128)(2,1)} %get-tuple-element.33), calls=%async_computation.7 | async-start | bytes 65536 | tf_op jit(solution)/shard_map/all_to_all | solution.py:294
  202.6 5.7 %all-to-all-done.7.tiles = bf16[8,2,1024]{2,1,0:T(2,128)(2,1)S(1)} async-done(((bf16[8,2,1024]{2,1,0:T(2,128)(2,1)}), bf16[8,2,1024]{2,1,0:T(2,128)(2,1)S(1)}, u32[]{:S(2)}, u32[]{:S(2)}) %all-to-all-start.7) | async-done | bytes 32800 | tf_op jit(solution)/shard_map/all_to_all | solution.py:294
  210.6 4.0 %all-to-all-start.8 = ((bf16[8,2,1024]{2,1,0:T(2,128)(2,1)}), bf16[8,2,1024]{2,1,0:T(2,128)(2,1)}, u32[]{:S(2)}, u32[]{:S(2)}) async-start(bf16[8,2,1024]{2,1,0:T(2,128)(2,1)} %get-tuple-element.35), calls=%async_computation.8 | async-start | bytes 65536 | tf_op jit(solution)/shard_map/all_to_all | solution.py:294
  214.6 10.8 %collective-permute-start.6 = (bf16[14,64,256]{2,1,0:T(8,128)(2,1)S(1)}, bf16[14,64,256]{2,1,0:T(8,128)(2,1)S(1)}, u32[]{:S(2)}, u32[]{:S(2)}) collective-permute-start(bf16[14,64,256]{2,1,0:T(8,128)(2,1)S(1)} %copy-done.1), channel_id=1, source_target_pairs={{0,1},{1,0},{2,3},{3,2},{4,5},{5,4},{6,7},{7,6},{8,9},{9,8},{10,11... | collective-permute-start | bytes 1376264 | tf_op jit(solution)/shard_map/ppermute | solution.py:34
  237.1 6.9 %all-to-all-start.9 = ((bf16[8,4,1024]{2,1,0:T(4,128)(2,1)}), bf16[8,4,1024]{2,1,0:T(4,128)(2,1)S(1)}, u32[]{:S(2)}, u32[]{:S(2)}) async-start(bf16[8,4,1024]{2,1,0:T(4,128)(2,1)} %copy-done.7), calls=%async_computation.9 | async-start | bytes 131072 | tf_op jit(solution)/shard_map/all_to_all | solution.py:294
  244.1 7.1 %all-to-all-done.9.tiles = bf16[8,4,1024]{2,1,0:T(4,128)(2,1)S(1)} async-done(((bf16[8,4,1024]{2,1,0:T(4,128)(2,1)}), bf16[8,4,1024]{2,1,0:T(4,128)(2,1)S(1)}, u32[]{:S(2)}, u32[]{:S(2)}) %all-to-all-start.9) | async-done | bytes 65568 | tf_op jit(solution)/shard_map/all_to_all | solution.py:294
  252.6 3.9 %all-to-all-start.10 = ((bf16[32,8,256]{2,1,0:T(8,128)(2,1)}), bf16[32,8,256]{2,1,0:T(8,128)(2,1)S(1)}, u32[]{:S(2)}, u32[]{:S(2)}) async-start(bf16[32,8,256]{2,1,0:T(8,128)(2,1)} %shard_map.115), calls=%async_computation.10 | async-start | bytes 262144 | tf_op jit(solution)/shard_map/all_to_all | solution.py:294
  257.4 8.5 %all-to-all-done.10.tiles = bf16[32,8,256]{2,1,0:T(8,128)(2,1)S(1)} async-done(((bf16[32,8,256]{2,1,0:T(8,128)(2,1)}), bf16[32,8,256]{2,1,0:T(8,128)(2,1)S(1)}, u32[]{:S(2)}, u32[]{:S(2)}) %all-to-all-start.10) | async-done | bytes 131104 | tf_op jit(solution)/shard_map/all_to_all | solution.py:294
  268.9 6.6 %all_to_all.75.tiles = bf16[4,32,128]{2,1,0:T(8,128)(2,1)S(1)} all-to-all(bf16[4,32,128]{2,1,0:T(8,128)(2,1)S(1)} %get-tuple-element.40), channel_id=1, replica_groups=mesh['gz'=8,'row'=4,'z'=8,'core'=2] {'row'}, dimensions={0} | all-to-all | bytes 65536 | tf_op jit(solution)/shard_map/all_to_all | solution.py:294
  276.3 3.4 %all-to-all-start.12 = ((bf16[8,32,256]{2,1,0:T(8,128)(2,1)}), bf16[8,32,256]{2,1,0:T(8,128)(2,1)S(1)}, u32[]{:S(2)}, u32[]{:S(2)}) async-start(bf16[8,32,256]{2,1,0:T(8,128)(2,1)} %get-tuple-element.41), calls=%async_computation.12 | async-start | bytes 262144 | tf_op jit(solution)/shard_map/all_to_all | solution.py:294
  279.7 7.8 %all-to-all-done.12.tiles = bf16[8,32,256]{2,1,0:T(8,128)(2,1)S(1)} async-done(((bf16[8,32,256]{2,1,0:T(8,128)(2,1)}), bf16[8,32,256]{2,1,0:T(8,128)(2,1)S(1)}, u32[]{:S(2)}, u32[]{:S(2)}) %all-to-all-start.12) | async-done | bytes 131104 | tf_op jit(solution)/shard_map/all_to_all | solution.py:294
  292.3 7.0 %collective-permute-start.5 = (bf16[7,16,32]{1,0,2:T(8,128)(2,1)S(1)}, bf16[7,16,32]{1,0,2:T(8,128)(2,1)S(1)}, u32[]{:S(2)}, u32[]{:S(2)}) collective-permute-start(bf16[7,16,32]{1,0,2:T(8,128)(2,1)S(1)} %dynamic-slice_bitcast_fusion.1), channel_id=1, source_target_pairs={{0,1},{1,0},{2,3},{3,2},{4,5},{5,4},{6,7},{7,6},{8,9},{9,8},{10,11... | collective-permute-start | bytes 21512 | tf_op jit(solution)/shard_map/ppermute | solution.py:34
  300.1 6.8 %all-to-all-start.14 = ((bf16[16,16,128]{2,1,0:T(8,128)(2,1)}), bf16[16,16,128]{2,1,0:T(8,128)(2,1)S(1)}, u32[]{:S(2)}, u32[]{:S(2)}) async-start(bf16[16,16,128]{2,1,0:T(8,128)(2,1)} %shard_map.119), calls=%async_computation.14 | async-start | bytes 131072 | tf_op jit(solution)/shard_map/all_to_all | solution.py:294
  308.0 6.8 %all-to-all-done.14 = bf16[16,16,128]{2,1,0:T(8,128)(2,1)S(1)} async-done(((bf16[16,16,128]{2,1,0:T(8,128)(2,1)}), bf16[16,16,128]{2,1,0:T(8,128)(2,1)S(1)}, u32[]{:S(2)}, u32[]{:S(2)}) %all-to-all-start.14) | async-done | bytes 65568 | tf_op jit(solution)/shard_map/all_to_all | solution.py:294
  (122 shorter events, 61.8 us)
Async XLA Ops:
  7.2 94.9 %copy-start = (bf16[14,64,256]{2,1,0:T(8,128)(2,1)S(1)}, bf16[14,64,256]{2,1,0:T(8,128)(2,1)}, u32[]{:S(2)}) copy-start(bf16[14,64,256]{2,1,0:T(8,128)(2,1)} %own.13) | copy-start | bytes 1376260
  7.2 102.9 %copy-start.21 = (s32[8]{0:T(128)S(1)}, s32[8]{0:T(128)}, u32[]{:S(2)}) copy-start(s32[8]{0:T(128)} %param.15) | copy-start | bytes 100
  7.2 103.0 %copy-start.20 = (s32[11,2]{0,1:T(2,128)S(1)}, s32[11,2]{0,1:T(2,128)}, u32[]{:S(2)}) copy-start(s32[11,2]{0,1:T(2,128)} %param.16) | copy-start | bytes 268
  7.2 47.4 %all-gather.3.cloned.1.call-start = ((), (), s32[]{:S(2)}) async-start(), calls=%async_computation.15 | async-start | bytes 2785280 | tf_op jit(solution)/shard_map/all_gather | solution.py:291
  7.9 119.5 %copy-start.17 = (s32[3]{0:T(128)S(1)}, s32[3]{0:T(128)}, u32[]{:S(2)}) copy-start(s32[3]{0:T(128)} %constant.73.clone) | copy-start | bytes 40
  7.9 90.1 %all-gather.5.cloned.1.call-start = ((), (), s32[]{:S(2)}) async-start(), calls=%async_computation.16 | async-start | bytes 2785280 | tf_op jit(solution)/shard_map/all_gather | solution.py:291
  54.6 101.8 %collective-permute-start.3 = (bf16[17,64,1024]{2,1,0:T(8,128)(2,1)}, bf16[17,64,1024]{2,1,0:T(8,128)(2,1)}, u32[]{:S(2)}, u32[]{:S(2)}) collective-permute-start(bf16[17,64,1024]{2,1,0:T(8,128)(2,1)} %all-gather.3.cloned.1.call-done), channel_id=1, source_target_pairs={{0,1},{1,0},{2,3},{3,2},{4,5},{5,4},{6,7},{7,6},{8,9},{9,8},{10,11... | collective-permute-start | bytes 6684680 | tf_op jit(solution)/shard_map/ppermute | solution.py:34
  58.5 43.6 %collective-permute-start.1 = (bf16[14,64,256]{2,1,0:T(8,128)(2,1)}, bf16[14,64,256]{2,1,0:T(8,128)(2,1)S(1)}, u32[]{:S(2)}, u32[]{:S(2)}) collective-permute-start(bf16[14,64,256]{2,1,0:T(8,128)(2,1)} %own.13), channel_id=1, source_target_pairs={{0,1},{1,0},{2,3},{3,2},{4,5},{5,4},{6,7},{7,6},{8,9},{9,8},{10,11... | collective-permute-start | bytes 1376264 | tf_op jit(solution)/shard_map/ppermute | solution.py:34
  61.5 40.5 %collective-permute-start = (bf16[3,64,32]{1,2,0:T(8,128)(2,1)S(1)}, bf16[3,64,32]{1,2,0:T(8,128)(2,1)S(1)}, u32[]{:S(2)}, u32[]{:S(2)}) collective-permute-start(bf16[3,64,32]{1,2,0:T(8,128)(2,1)S(1)} %copy.38), channel_id=1, source_target_pairs={{0,1},{1,0},{2,3},{3,2},{4,5},{5,4},{6,7},{7,6},{8,9},{9,8},{10,11... | collective-permute-start | bytes 36872 | tf_op jit(solution)/shard_map/ppermute | solution.py:34
  65.2 71.0 %collective-permute-start.2 = (bf16[7,64,1]{1,0,2:T(8,128)(2,1)S(1)}, bf16[7,64,1]{1,0,2:T(8,128)(2,1)S(1)}, u32[]{:S(2)}, u32[]{:S(2)}) collective-permute-start(bf16[7,64,1]{1,0,2:T(8,128)(2,1)S(1)} %copy.40), channel_id=1, source_target_pairs={{0,1},{1,0},{2,3},{3,2},{4,5},{5,4},{6,7},{7,6},{8,9},{9,8},{10,11... | collective-permute-start | bytes 2696 | tf_op jit(solution)/shard_map/ppermute | solution.py:34
  98.1 93.9 %collective-permute-start.4 = (bf16[17,64,1024]{2,1,0:T(8,128)(2,1)}, bf16[17,64,1024]{2,1,0:T(8,128)(2,1)}, u32[]{:S(2)}, u32[]{:S(2)}) collective-permute-start(bf16[17,64,1024]{2,1,0:T(8,128)(2,1)} %all-gather.5.cloned.1.call-done), channel_id=1, source_target_pairs={{0,1},{1,0},{2,3},{3,2},{4,5},{5,4},{6,7},{7,6},{8,9},{9,8},{10,11... | collective-permute-start | bytes 6684680 | tf_op jit(solution)/shard_map/ppermute | solution.py:34
  103.0 19.5 %all-to-all-start = ((bf16[8,2,32,256]{3,2,1,0:T(8,128)(2,1)}), bf16[8,2,32,256]{3,2,1,0:T(8,128)(2,1)S(1)}, u32[]{:S(2)}, u32[]{:S(2)}) async-start(bf16[8,2,32,256]{3,2,1,0:T(8,128)(2,1)} %shard_map.104), calls=%async_computation | async-start | bytes 524288 | tf_op jit(solution)/shard_map/all_to_all | solution.py:294
  110.1 35.1 %copy-start.18 = (s32[8]{0:T(128)}, s32[8]{0:T(128)S(1)}, u32[]{:S(2)}) copy-start(s32[8]{0:T(128)S(1)} %broadcast_add_fusion) | copy-start | bytes 100
  110.1 35.1 %copy-start.19 = (pred[8]{0:T(512)(128)(4,1)}, pred[8]{0:T(512)(128)(4,1)S(1)}, u32[]{:S(2)}) copy-start(pred[8]{0:T(512)(128)(4,1)S(1)} %sign_compare_fusion) | copy-start | bytes 28
  123.8 29.1 %copy-start.5 = (bf16[2,32,256]{2,1,0:T(8,128)(2,1)}, bf16[2,32,256]{2,1,0:T(8,128)(2,1)S(1)}, u32[]{:S(2)}) copy-start(bf16[2,32,256]{2,1,0:T(8,128)(2,1)S(1)} %get-tuple-element.24.y.y_leaf) | copy-start | bytes 98308
  123.8 8.0 %all-to-all-start.1 = ((bf16[4,32,128]{2,1,0:T(8,128)(2,1)}), bf16[4,32,128]{2,1,0:T(8,128)(2,1)S(1)}, u32[]{:S(2)}, u32[]{:S(2)}) async-start(bf16[4,32,128]{2,1,0:T(8,128)(2,1)} %get-tuple-element.23), calls=%async_computation.1 | async-start | bytes 65536 | tf_op jit(solution)/shard_map/all_to_all | solution.py:294
  132.5 11.3 %all-to-all-start.2 = ((bf16[8,32,256]{2,1,0:T(8,128)(2,1)}), bf16[8,32,256]{2,1,0:T(8,128)(2,1)S(1)}, u32[]{:S(2)}, u32[]{:S(2)}) async-start(bf16[8,32,256]{2,1,0:T(8,128)(2,1)} %shard_map.106), calls=%async_computation.2 | async-start | bytes 262144 | tf_op jit(solution)/shard_map/all_to_all | solution.py:294
  145.2 17.1 %all-to-all-start.3 = ((f32[32,8,128]{2,1,0:T(8,128)}), f32[32,8,128]{2,1,0:T(8,128)S(1)}, u32[]{:S(2)}, u32[]{:S(2)}) async-start(f32[32,8,128]{2,1,0:T(8,128)} %get-tuple-element.25), calls=%async_computation.3 | async-start | bytes 262144 | tf_op jit(solution)/shard_map/all_to_all | solution.py:294
  163.4 10.5 %all-to-all-start.4 = ((bf16[8,4,1024]{2,1,0:T(4,128)(2,1)}), bf16[8,4,1024]{2,1,0:T(4,128)(2,1)S(1)}, u32[]{:S(2)}, u32[]{:S(2)}) async-start(bf16[8,4,1024]{2,1,0:T(4,128)(2,1)} %get-tuple-element.26), calls=%async_computation.4 | async-start | bytes 131072 | tf_op jit(solution)/shard_map/all_to_all | solution.py:294
  175.4 10.1 %all-to-all-start.5 = ((bf16[8,2,1024]{2,1,0:T(2,128)(2,1)}), bf16[8,2,1024]{2,1,0:T(2,128)(2,1)S(1)}, u32[]{:S(2)}, u32[]{:S(2)}) async-start(bf16[8,2,1024]{2,1,0:T(2,128)(2,1)} %get-tuple-element.28), calls=%async_computation.5 | async-start | bytes 65536 | tf_op jit(solution)/shard_map/all_to_all | solution.py:294
  178.8 29.5 %copy-start.12 = (s32[5]{0:T(128)}, s32[5]{0:T(128)S(1)}, u32[]{:S(2)}) copy-start(s32[5]{0:T(128)S(1)} %stack.23.where) | copy-start | bytes 64
  186.5 10.3 %all-to-all-start.6 = ((bf16[8,2,1024]{2,1,0:T(2,128)(2,1)}), bf16[8,2,1024]{2,1,0:T(2,128)(2,1)S(1)}, u32[]{:S(2)}, u32[]{:S(2)}) async-start(bf16[8,2,1024]{2,1,0:T(2,128)(2,1)} %get-tuple-element.31), calls=%async_computation.6 | async-start | bytes 65536 | tf_op jit(solution)/shard_map/all_to_all | solution.py:294
  198.2 10.1 %all-to-all-start.7 = ((bf16[8,2,1024]{2,1,0:T(2,128)(2,1)}), bf16[8,2,1024]{2,1,0:T(2,128)(2,1)S(1)}, u32[]{:S(2)}, u32[]{:S(2)}) async-start(bf16[8,2,1024]{2,1,0:T(2,128)(2,1)} %get-tuple-element.33), calls=%async_computation.7 | async-start | bytes 65536 | tf_op jit(solution)/shard_map/all_to_all | solution.py:294
  210.6 20.4 %all-to-all-start.8 = ((bf16[8,2,1024]{2,1,0:T(2,128)(2,1)}), bf16[8,2,1024]{2,1,0:T(2,128)(2,1)}, u32[]{:S(2)}, u32[]{:S(2)}) async-start(bf16[8,2,1024]{2,1,0:T(2,128)(2,1)} %get-tuple-element.35), calls=%async_computation.8 | async-start | bytes 65536 | tf_op jit(solution)/shard_map/all_to_all | solution.py:294
  214.6 42.8 %collective-permute-start.6 = (bf16[14,64,256]{2,1,0:T(8,128)(2,1)S(1)}, bf16[14,64,256]{2,1,0:T(8,128)(2,1)S(1)}, u32[]{:S(2)}, u32[]{:S(2)}) collective-permute-start(bf16[14,64,256]{2,1,0:T(8,128)(2,1)S(1)} %copy-done.1), channel_id=1, source_target_pairs={{0,1},{1,0},{2,3},{3,2},{4,5},{5,4},{6,7},{7,6},{8,9},{9,8},{10,11... | collective-permute-start | bytes 1376264 | tf_op jit(solution)/shard_map/ppermute | solution.py:34
  237.1 50.4 %copy-start.16 = (f32[11]{0:T(128)S(1)}, f32[11]{0:T(128)}, u32[]{:S(2)}) copy-start(f32[11]{0:T(128)} %get-tuple-element.64.w) | copy-start | bytes 136
  237.1 14.1 %all-to-all-start.9 = ((bf16[8,4,1024]{2,1,0:T(4,128)(2,1)}), bf16[8,4,1024]{2,1,0:T(4,128)(2,1)S(1)}, u32[]{:S(2)}, u32[]{:S(2)}) async-start(bf16[8,4,1024]{2,1,0:T(4,128)(2,1)} %copy-done.7), calls=%async_computation.9 | async-start | bytes 131072 | tf_op jit(solution)/shard_map/all_to_all | solution.py:294
  252.6 13.3 %all-to-all-start.10 = ((bf16[32,8,256]{2,1,0:T(8,128)(2,1)}), bf16[32,8,256]{2,1,0:T(8,128)(2,1)S(1)}, u32[]{:S(2)}, u32[]{:S(2)}) async-start(bf16[32,8,256]{2,1,0:T(8,128)(2,1)} %shard_map.115), calls=%async_computation.10 | async-start | bytes 262144 | tf_op jit(solution)/shard_map/all_to_all | solution.py:294
  276.3 11.2 %all-to-all-start.12 = ((bf16[8,32,256]{2,1,0:T(8,128)(2,1)}), bf16[8,32,256]{2,1,0:T(8,128)(2,1)S(1)}, u32[]{:S(2)}, u32[]{:S(2)}) async-start(bf16[8,32,256]{2,1,0:T(8,128)(2,1)} %get-tuple-element.41), calls=%async_computation.12 | async-start | bytes 262144 | tf_op jit(solution)/shard_map/all_to_all | solution.py:294
  288.9 10.4 %all-to-all-start.13 = ((bf16[4,2,32,128]{3,2,1,0:T(8,128)(2,1)}), bf16[4,2,32,128]{3,2,1,0:T(8,128)(2,1)S(1)}, u32[]{:S(2)}, u32[]{:S(2)}) async-start(bf16[4,2,32,128]{3,2,1,0:T(8,128)(2,1)} %shard_map.118), calls=%async_computation.13 | async-start | bytes 131072 | tf_op jit(solution)/shard_map/all_to_all | solution.py:294
  292.3 14.7 %collective-permute-start.5 = (bf16[7,16,32]{1,0,2:T(8,128)(2,1)S(1)}, bf16[7,16,32]{1,0,2:T(8,128)(2,1)S(1)}, u32[]{:S(2)}, u32[]{:S(2)}) collective-permute-start(bf16[7,16,32]{1,0,2:T(8,128)(2,1)S(1)} %dynamic-slice_bitcast_fusion.1), channel_id=1, source_target_pairs={{0,1},{1,0},{2,3},{3,2},{4,5},{5,4},{6,7},{7,6},{8,9},{9,8},{10,11... | collective-permute-start | bytes 21512 | tf_op jit(solution)/shard_map/ppermute | solution.py:34
  300.1 14.7 %all-to-all-start.14 = ((bf16[16,16,128]{2,1,0:T(8,128)(2,1)}), bf16[16,16,128]{2,1,0:T(8,128)(2,1)S(1)}, u32[]{:S(2)}, u32[]{:S(2)}) async-start(bf16[16,16,128]{2,1,0:T(8,128)(2,1)} %shard_map.119), calls=%async_computation.14 | async-start | bytes 131072 | tf_op jit(solution)/shard_map/all_to_all | solution.py:294
  (13 other events, 52.2 us)
Sparse Core Ops, SparseCore 0:
  10.1 44.4 all-gather.2
  56.7 41.3 all-gather.4

commit v3 on v2

--- a/solution.py
+++ b/solution.py
@@ -15,7 +15,7 @@
 ROWS8 = 8
 F32 = jnp.float32
 BF16 = jnp.bfloat16
-VMEM_BYTES = 24 * 2**20
+VMEM_BYTES = 12 * 2**20
 
 
 def level_span(depth):
@@ -100,7 +100,12 @@
                 self.anc[a, u] = anc_count + len(self.anc)
 
 
-def sub_leaf_solve(rhs, own, other, out):
+def sub_leaf_solve(where, here, there, own, other, rhs, out):
+    core = where[0]
+    cols = rhs.shape[1]
+    for m in range(SUB_NODES):
+        flipped = jnp.concatenate([here[m], there[m]], 0).astype(F32).T
+        rhs[m] = jnp.where(core == 0, flipped[:cols], flipped[cols:]).astype(BF16)
     for m in LEAVES:
         part = times(rhs[m], block(own, other, m)).astype(BF16)
         for i in range(out.shape[0]):
@@ -144,6 +149,15 @@
         value = value + in_row(times(v8, block(own, other, i)), a)
     scratch[...] = value
     to_all(out, scratch[first : first + out.shape[1], :])
+
+
+def anc_prepare(where, here, there, out):
+    lanes = lax.broadcasted_iota(jnp.int32, (ROWS8, here.shape[2]), 1)
+    pick = jnp.where(lanes == where[5], 1.0, 0.0).astype(BF16)
+    value = jnp.zeros_like(out)
+    for a in range(here.shape[0]):
+        value = value + in_row(times_t(pick, block(here, there, a)), a)
+    out[...] = value
 
 
 def anc_first(pairs, depth, tiles, choose, given, own, other, acc_out, out, scratch):
@@ -212,7 +226,7 @@
 
 
 def sub_turn(pairs, levels, where, ids, w, tiles, y_root, y_leaf, own, other, kept, out, scratch):
-    core, held, base = where[0], where[3], where[4]
+    core, held, base = where[0], where[2], where[3]
     scratch[...] = tiles[...].astype(F32)
     picked = []
     for e in range(levels):
@@ -285,7 +299,7 @@
     ids_here = lax.dynamic_index_in_dim(heap_ids, g, 0, keepdims=False)
     held = (r == z * nrow // nz).astype(jnp.int32)
     base = jnp.clip(z * pair_rows - r * wide, 0, wide - pair_rows)
-    where = jnp.stack([core, z, jnp.int32(nz), held, base]).astype(jnp.int32)
+    where = jnp.stack([core, z, held, base, jnp.int32(0), core * cols + g * nrow + r]).astype(jnp.int32)
 
     def gathered(blocks):
         return lax.all_gather(blocks, "row", axis=2, tiled=True)
@@ -294,19 +308,11 @@
         return lax.all_to_all(array, axes, 0, 0, tiled=True)
 
     low = (sub_lower, swapped(sub_lower))
-    rhs_here = lax.dynamic_slice_in_dim(sub_rhs, core * cols, cols, 2)
-    rhs_there = swapped(lax.dynamic_slice_in_dim(sub_rhs, (1 - core) * cols, cols, 2))
-    rhs = jnp.concatenate([rhs_here, rhs_there], 1).transpose(0, 2, 1)
-    mine = g * nrow + r
-    anc_here = lax.dynamic_slice_in_dim(anc_rhs, core * cols + mine, 1, 2)
-    anc_there = swapped(lax.dynamic_slice_in_dim(anc_rhs, (1 - core) * cols + mine, 1, 2))
-    given8 = jnp.concatenate([anc_here, anc_there], 1)[:, :, 0].astype(F32)
-    given8 = jnp.pad(given8, ((0, ROWS8 - anc_count), (0, 0)))
+    rhs_there = swapped(sub_rhs)
+    anc_there = swapped(anc_rhs)
     up = (sub_upper, swapped(sub_upper))
     anc_low_row = gathered(anc_lower)
-    anc_low = (anc_low_row, swapped(anc_low_row))
     anc_up_row = gathered(anc_upper)
-    anc_up = (anc_up_row, swapped(anc_up_row))
 
     def diagonal(two, depth):
         first, stop = level_span(depth)
@@ -320,7 +326,12 @@
     def level_shape(depth):
         return shape(BF16, nz, max(2, 2**depth), size)
 
-    tiles = run(sub_leaf_solve, shape(BF16, nz, 2, cols, wide), (), (rhs, *low))
+    rhs, tiles = run(
+        sub_leaf_solve,
+        (shape(BF16, SUB_NODES, cols, pair_rows), shape(BF16, nz, 2, cols, wide)),
+        (where,),
+        (sub_rhs, rhs_there, *low),
+    )
     tiles = exchange(tiles, "z")
     y_leaf, tiles = run(
         part(sub_leaf_update, pairs),
@@ -337,6 +348,9 @@
     )
     tiles = run(sub_root_solve, shape(BF16, nz, cols, wide), (), (tiles, rhs, *low))
     tiles = exchange(tiles, "z")
+    anc_low_row, tiles = lax.optimization_barrier((anc_low_row, tiles))
+    anc_low = (anc_low_row, swapped(anc_low_row))
+    given8 = run(anc_prepare, shape(F32, ROWS8, pair_rows), (where,), (anc_rhs, anc_there))
     y_root, tiles = run(
         part(sub_root_anc, pairs, levels),
         (shape(BF16, cols, wide), shape(F32, cols, ROWS8, pair_rows)),
@@ -355,6 +369,9 @@
     )
     tiles = exchange(tiles, "z")
     for depth in range(levels - 1, 0, -1):
+        if depth == 1:
+            anc_up_row, tiles = lax.optimization_barrier((anc_up_row, tiles))
+            anc_up = (anc_up_row, swapped(anc_up_row))
         y8, acc, tiles = run(
             part(anc_forward, pairs, depth),
             (shape(F32, ROWS8, size), shape(F32, ROWS8, pair_rows), level_shape(depth - 1)),

time: 325 us -> 250 us (0.77)
  waiting for transfers between devices: 155 us -> 69.4 us
  blocking collectives: 6.65 us -> 25.6 us
  starting transfers between devices: 95.4 us -> 89.9 us
    all_gather x2, waiting for transfers between devices: 76.7 us -> 0.02 us  [gathered(): return lax.all_gather(blocks, 'row', axis=2, tiled=True)]
    all_to_all x1 -> x3, blocking collectives: 6.65 us -> 25.6 us  [exchange(): return lax.all_to_all(array, axes, 0, 0, tiled=True)]
    all_to_all x14 -> x12, waiting for transfers between devices: 76.9 us -> 67.3 us  [exchange(): return lax.all_to_all(array, axes, 0, 0, tiled=True)]
    all_to_all x14 -> x12, starting transfers between devices: 63.5 us -> 54.3 us  [exchange(): return lax.all_to_all(array, axes, 0, 0, tiled=True)]
    ppermute x7, starting transfers between devices: 31.9 us -> 35.6 us  [swapped(): return lax.ppermute(array, 'core', [(0, 1), (1, 0)])]
    unnamed x48 -> x42, local copies, waits for them, and re-layouts: 8.3 us -> 8.85 us
    pallas_call x16 -> x17, Pallas kernels: 18 us -> 18.1 us  [run(): pl.pallas_call(body, out_shape=outs, in_specs=in_specs, out_specs=spec if...]
  transfers between devices with their start and end apart: 23 -> 21, of which waited for: 14 -> 11; matrix products, arithmetic and copies ran while one was open for 7% -> 8% of each run, Pallas kernels for 4% -> 5%
where the time goes in v3:
time: 250 us; the launch traced here: 248 us
  starting transfers between devices  89.9 us (36%)
  waiting for transfers between devices  69.4 us (28%)
  local copies, waits for them, and re-layouts  28.6 us (11%)
  blocking collectives  25.6 us (10%)
  Pallas kernels  18.1 us (7%)
  between operations  14.6 us (6%)
    all_to_all x12, waiting for transfers between devices, exchange(): return lax.all_to_all(array, axes, 0, 0, tiled=True)  67.3 us
    all_to_all x12, starting transfers between devices, exchange(): return lax.all_to_all(array, axes, 0, 0, tiled=True)  54.3 us
    ppermute x7, starting transfers between devices, swapped(): return lax.ppermute(array, 'core', [(0, 1), (1, 0)])  35.6 us
    all_to_all x3, blocking collectives, exchange(): return lax.all_to_all(array, axes, 0, 0, tiled=True)  25.6 us
    pallas_call x17, Pallas kernels, run(): pl.pallas_call(body, out_shape=outs, in_specs=in_specs, out_specs=spec if...  18.1 us
    slice x10, local copies, waits for them, and re-layouts, diagonal(): return [array[first:stop] for array in two]  10.9 us
    unnamed x42, local copies, waits for them, and re-layouts  8.85 us
    slice x6, local copies, waits for them, and re-layouts, pair_blocks(): return [array[start:start + (stop - first) * depth] for array in two]  7.45 us
  transfers between devices with their start and end apart: 21, of which 11 were waited for; matrix products, arithmetic and copies ran while one was open for 8% of the time, Pallas kernels for 5%

profile of v3, /device:TPU:1, one launch (start us, length us, event | category | flops | bytes accessed | tf_op | source)
XLA Modules:
  0.0 248.1 jit_solution(2901606961822660407)
XLA Ops:
  8.0 8.7 %collective-permute-start.1 = (bf16[14,64,256]{2,1,0:T(8,128)(2,1)}, bf16[14,64,256]{2,1,0:T(8,128)(2,1)S(1)}, u32[]{:S(2)}, u32[]{:S(2)}) collective-permute-start(bf16[14,64,256]{2,1,0:T(8,128)(2,1)} %own.13), channel_id=1, source_target_pairs={{0,1},{1,0},{2,3},{3,2},{4,5},{5,4},{6,7},{7,6},{8,9},{9,8},{10,11... | collective-permute-start | bytes 1376264 | tf_op jit(solution)/shard_map/ppermute | solution.py:34
  16.8 2.1 collective-permute-start
  23.6 4.7 %all-to-all-start = ((bf16[8,2,32,256]{3,2,1,0:T(8,128)(2,1)}), bf16[8,2,32,256]{3,2,1,0:T(8,128)(2,1)S(1)}, u32[]{:S(2)}, u32[]{:S(2)}) async-start(bf16[8,2,32,256]{3,2,1,0:T(8,128)(2,1)} %get-tuple-element.29), calls=%async_computation | async-start | bytes 524288 | tf_op jit(solution)/shard_map/all_to_all | solution.py:308
  28.3 12.2 %all-to-all-done.tiles = bf16[8,2,32,256]{3,2,1,0:T(8,128)(2,1)S(1)} async-done(((bf16[8,2,32,256]{3,2,1,0:T(8,128)(2,1)}), bf16[8,2,32,256]{3,2,1,0:T(8,128)(2,1)S(1)}, u32[]{:S(2)}, u32[]{:S(2)}) %all-to-all-start) | async-done | bytes 262176 | tf_op jit(solution)/shard_map/all_to_all | solution.py:308
  41.2 8.6 %all_to_all.75.tiles = bf16[4,32,128]{2,1,0:T(8,128)(2,1)S(1)} all-to-all(bf16[4,32,128]{2,1,0:T(8,128)(2,1)S(1)} %get-tuple-element.30), channel_id=1, replica_groups=mesh['gz'=8,'row'=4,'z'=8,'core'=2] {'row'}, dimensions={0} | all-to-all | bytes 65536 | tf_op jit(solution)/shard_map/all_to_all | solution.py:308
  49.9 10.4 %all_to_all.76.tiles = bf16[8,32,256]{2,1,0:T(8,128)(2,1)S(1)} all-to-all(bf16[8,32,256]{2,1,0:T(8,128)(2,1)S(1)} %shard_map.106), channel_id=1, replica_groups=mesh['gz'=8,'row'=4,'z'=8,'core'=2] {'z'}, dimensions={0} | all-to-all | bytes 262144 | tf_op jit(solution)/shard_map/all_to_all | solution.py:308
  60.3 5.0 %collective-permute-start.3 = (bf16[17,64,1024]{2,1,0:T(8,128)(2,1)}, bf16[17,64,1024]{2,1,0:T(8,128)(2,1)}, u32[]{:S(2)}, u32[]{:S(2)}) collective-permute-start(bf16[17,64,1024]{2,1,0:T(8,128)(2,1)} %all-gather.5.cloned.1.call-done), channel_id=1, source_target_pairs={{0,1},{1,0},{2,3},{3,2},{4,5},{5,4},{6,7},{7,6},{8,9},{9,8},{10,11... | collective-permute-start | bytes 6684680 | tf_op jit(solution)/shard_map/ppermute | solution.py:34
  65.3 1.9 collective-permute-start.2
  70.1 7.4 %all-to-all-start.3 = ((f32[32,8,128]{2,1,0:T(8,128)}), f32[32,8,128]{2,1,0:T(8,128)S(1)}, u32[]{:S(2)}, u32[]{:S(2)}) async-start(f32[32,8,128]{2,1,0:T(8,128)} %get-tuple-element.34), calls=%async_computation.3 | async-start | bytes 262144 | tf_op jit(solution)/shard_map/all_to_all | solution.py:308
  83.1 3.8 %all-to-all-done.3.tiles = f32[32,8,128]{2,1,0:T(8,128)S(1)} async-done(((f32[32,8,128]{2,1,0:T(8,128)}), f32[32,8,128]{2,1,0:T(8,128)S(1)}, u32[]{:S(2)}, u32[]{:S(2)}) %all-to-all-start.3) | async-done | bytes 131104 | tf_op jit(solution)/shard_map/all_to_all | solution.py:308
  88.0 3.3 %all-to-all-start.4 = ((bf16[8,4,1024]{2,1,0:T(4,128)(2,1)}), bf16[8,4,1024]{2,1,0:T(4,128)(2,1)S(1)}, u32[]{:S(2)}, u32[]{:S(2)}) async-start(bf16[8,4,1024]{2,1,0:T(4,128)(2,1)} %get-tuple-element.36), calls=%async_computation.4 | async-start | bytes 131072 | tf_op jit(solution)/shard_map/all_to_all | solution.py:308
  93.7 4.7 %all-to-all-done.4.tiles = bf16[8,4,1024]{2,1,0:T(4,128)(2,1)S(1)} async-done(((bf16[8,4,1024]{2,1,0:T(4,128)(2,1)}), bf16[8,4,1024]{2,1,0:T(4,128)(2,1)S(1)}, u32[]{:S(2)}, u32[]{:S(2)}) %all-to-all-start.4) | async-done | bytes 65568 | tf_op jit(solution)/shard_map/all_to_all | solution.py:308
  99.9 3.3 %all-to-all-start.5 = ((bf16[8,2,1024]{2,1,0:T(2,128)(2,1)}), bf16[8,2,1024]{2,1,0:T(2,128)(2,1)S(1)}, u32[]{:S(2)}, u32[]{:S(2)}) async-start(bf16[8,2,1024]{2,1,0:T(2,128)(2,1)} %get-tuple-element.38), calls=%async_computation.5 | async-start | bytes 65536 | tf_op jit(solution)/shard_map/all_to_all | solution.py:308
  103.3 6.8 %all-to-all-done.5.tiles = bf16[8,2,1024]{2,1,0:T(2,128)(2,1)S(1)} async-done(((bf16[8,2,1024]{2,1,0:T(2,128)(2,1)}), bf16[8,2,1024]{2,1,0:T(2,128)(2,1)S(1)}, u32[]{:S(2)}, u32[]{:S(2)}) %all-to-all-start.5) | async-done | bytes 32800 | tf_op jit(solution)/shard_map/all_to_all | solution.py:308
  110.1 6.3 %collective-permute-start.4 = (bf16[17,64,1024]{2,1,0:T(8,128)(2,1)}, bf16[17,64,1024]{2,1,0:T(8,128)(2,1)}, u32[]{:S(2)}, u32[]{:S(2)}) collective-permute-start(bf16[17,64,1024]{2,1,0:T(8,128)(2,1)} %all-gather.3.cloned.1.call-done), channel_id=1, source_target_pairs={{0,1},{1,0},{2,3},{3,2},{4,5},{5,4},{6,7},{7,6},{8,9},{9,8},{10,11... | collective-permute-start | bytes 6684680 | tf_op jit(solution)/shard_map/ppermute | solution.py:34
  119.2 3.5 %all-to-all-start.6 = ((bf16[8,2,1024]{2,1,0:T(2,128)(2,1)}), bf16[8,2,1024]{2,1,0:T(2,128)(2,1)S(1)}, u32[]{:S(2)}, u32[]{:S(2)}) async-start(bf16[8,2,1024]{2,1,0:T(2,128)(2,1)} %get-tuple-element.42), calls=%async_computation.6 | async-start | bytes 65536 | tf_op jit(solution)/shard_map/all_to_all | solution.py:308
  125.6 3.9 %all-to-all-done.6.tiles = bf16[8,2,1024]{2,1,0:T(2,128)(2,1)S(1)} async-done(((bf16[8,2,1024]{2,1,0:T(2,128)(2,1)}), bf16[8,2,1024]{2,1,0:T(2,128)(2,1)S(1)}, u32[]{:S(2)}, u32[]{:S(2)}) %all-to-all-start.6) | async-done | bytes 32800 | tf_op jit(solution)/shard_map/all_to_all | solution.py:308
  130.9 3.3 %all-to-all-start.7 = ((bf16[8,2,1024]{2,1,0:T(2,128)(2,1)}), bf16[8,2,1024]{2,1,0:T(2,128)(2,1)S(1)}, u32[]{:S(2)}, u32[]{:S(2)}) async-start(bf16[8,2,1024]{2,1,0:T(2,128)(2,1)} %get-tuple-element.45), calls=%async_computation.7 | async-start | bytes 65536 | tf_op jit(solution)/shard_map/all_to_all | solution.py:308
  135.3 5.7 %all-to-all-done.7.tiles = bf16[8,2,1024]{2,1,0:T(2,128)(2,1)S(1)} async-done(((bf16[8,2,1024]{2,1,0:T(2,128)(2,1)}), bf16[8,2,1024]{2,1,0:T(2,128)(2,1)S(1)}, u32[]{:S(2)}, u32[]{:S(2)}) %all-to-all-start.7) | async-done | bytes 32800 | tf_op jit(solution)/shard_map/all_to_all | solution.py:308
  143.3 4.0 %all-to-all-start.8 = ((bf16[8,2,1024]{2,1,0:T(2,128)(2,1)}), bf16[8,2,1024]{2,1,0:T(2,128)(2,1)}, u32[]{:S(2)}, u32[]{:S(2)}) async-start(bf16[8,2,1024]{2,1,0:T(2,128)(2,1)} %get-tuple-element.47), calls=%async_computation.8 | async-start | bytes 65536 | tf_op jit(solution)/shard_map/all_to_all | solution.py:308
  147.2 4.2 %collective-permute-start.6 = (bf16[14,64,256]{2,1,0:T(8,128)(2,1)S(1)}, bf16[14,64,256]{2,1,0:T(8,128)(2,1)S(1)}, u32[]{:S(2)}, u32[]{:S(2)}) collective-permute-start(bf16[14,64,256]{2,1,0:T(8,128)(2,1)S(1)} %copy-done.2), channel_id=1, source_target_pairs={{0,1},{1,0},{2,3},{3,2},{4,5},{5,4},{6,7},{7,6},{8,9},{9,8},{10,11... | collective-permute-start | bytes 1376264 | tf_op jit(solution)/shard_map/ppermute | solution.py:34
  162.6 6.8 %all-to-all-start.9 = ((bf16[8,4,1024]{2,1,0:T(4,128)(2,1)}), bf16[8,4,1024]{2,1,0:T(4,128)(2,1)S(1)}, u32[]{:S(2)}, u32[]{:S(2)}) async-start(bf16[8,4,1024]{2,1,0:T(4,128)(2,1)} %copy-done.9), calls=%async_computation.9 | async-start | bytes 131072 | tf_op jit(solution)/shard_map/all_to_all | solution.py:308
  169.4 7.1 %all-to-all-done.9.tiles = bf16[8,4,1024]{2,1,0:T(4,128)(2,1)S(1)} async-done(((bf16[8,4,1024]{2,1,0:T(4,128)(2,1)}), bf16[8,4,1024]{2,1,0:T(4,128)(2,1)S(1)}, u32[]{:S(2)}, u32[]{:S(2)}) %all-to-all-start.9) | async-done | bytes 65568 | tf_op jit(solution)/shard_map/all_to_all | solution.py:308
  178.0 4.4 %all-to-all-start.10 = ((bf16[32,8,256]{2,1,0:T(8,128)(2,1)}), bf16[32,8,256]{2,1,0:T(8,128)(2,1)S(1)}, u32[]{:S(2)}, u32[]{:S(2)}) async-start(bf16[32,8,256]{2,1,0:T(8,128)(2,1)} %shard_map.116), calls=%async_computation.10 | async-start | bytes 262144 | tf_op jit(solution)/shard_map/all_to_all | solution.py:308
  183.3 8.5 %all-to-all-done.10.tiles = bf16[32,8,256]{2,1,0:T(8,128)(2,1)S(1)} async-done(((bf16[32,8,256]{2,1,0:T(8,128)(2,1)}), bf16[32,8,256]{2,1,0:T(8,128)(2,1)S(1)}, u32[]{:S(2)}, u32[]{:S(2)}) %all-to-all-start.10) | async-done | bytes 131104 | tf_op jit(solution)/shard_map/all_to_all | solution.py:308
  194.2 6.6 %all_to_all.77.tiles = bf16[4,32,128]{2,1,0:T(8,128)(2,1)S(1)} all-to-all(bf16[4,32,128]{2,1,0:T(8,128)(2,1)S(1)} %get-tuple-element.52), channel_id=1, replica_groups=mesh['gz'=8,'row'=4,'z'=8,'core'=2] {'row'}, dimensions={0} | all-to-all | bytes 65536 | tf_op jit(solution)/shard_map/all_to_all | solution.py:308
  201.6 3.4 %all-to-all-start.12 = ((bf16[8,32,256]{2,1,0:T(8,128)(2,1)}), bf16[8,32,256]{2,1,0:T(8,128)(2,1)S(1)}, u32[]{:S(2)}, u32[]{:S(2)}) async-start(bf16[8,32,256]{2,1,0:T(8,128)(2,1)} %get-tuple-element.53), calls=%async_computation.12 | async-start | bytes 262144 | tf_op jit(solution)/shard_map/all_to_all | solution.py:308
  205.0 7.8 %all-to-all-done.12.tiles = bf16[8,32,256]{2,1,0:T(8,128)(2,1)S(1)} async-done(((bf16[8,32,256]{2,1,0:T(8,128)(2,1)}), bf16[8,32,256]{2,1,0:T(8,128)(2,1)S(1)}, u32[]{:S(2)}, u32[]{:S(2)}) %all-to-all-start.12) | async-done | bytes 131104 | tf_op jit(solution)/shard_map/all_to_all | solution.py:308
  214.1 3.3 %all-to-all-start.13 = ((bf16[4,2,32,128]{3,2,1,0:T(8,128)(2,1)}), bf16[4,2,32,128]{3,2,1,0:T(8,128)(2,1)S(1)}, u32[]{:S(2)}, u32[]{:S(2)}) async-start(bf16[4,2,32,128]{3,2,1,0:T(8,128)(2,1)} %shard_map.119), calls=%async_computation.13 | async-start | bytes 131072 | tf_op jit(solution)/shard_map/all_to_all | solution.py:308
  217.5 7.3 %collective-permute-start.5 = (bf16[7,16,32]{1,0,2:T(8,128)(2,1)S(1)}, bf16[7,16,32]{1,0,2:T(8,128)(2,1)S(1)}, u32[]{:S(2)}, u32[]{:S(2)}) collective-permute-start(bf16[7,16,32]{1,0,2:T(8,128)(2,1)S(1)} %dynamic-slice_bitcast_fusion.1), channel_id=1, source_target_pairs={{0,1},{1,0},{2,3},{3,2},{4,5},{5,4},{6,7},{7,6},{8,9},{9,8},{10,11... | collective-permute-start | bytes 21512 | tf_op jit(solution)/shard_map/ppermute | solution.py:34
  225.7 6.8 %all-to-all-start.14 = ((bf16[16,16,128]{2,1,0:T(8,128)(2,1)}), bf16[16,16,128]{2,1,0:T(8,128)(2,1)S(1)}, u32[]{:S(2)}, u32[]{:S(2)}) async-start(bf16[16,16,128]{2,1,0:T(8,128)(2,1)} %shard_map.120), calls=%async_computation.14 | async-start | bytes 131072 | tf_op jit(solution)/shard_map/all_to_all | solution.py:308
  233.6 6.8 %all-to-all-done.14 = bf16[16,16,128]{2,1,0:T(8,128)(2,1)S(1)} async-done(((bf16[16,16,128]{2,1,0:T(8,128)(2,1)}), bf16[16,16,128]{2,1,0:T(8,128)(2,1)S(1)}, u32[]{:S(2)}, u32[]{:S(2)}) %all-to-all-start.14) | async-done | bytes 65568 | tf_op jit(solution)/shard_map/all_to_all | solution.py:308
  (110 shorter events, 50.8 us)
Async XLA Ops:
  7.2 33.3 %copy-start.1 = (bf16[14,64,256]{2,1,0:T(8,128)(2,1)S(1)}, bf16[14,64,256]{2,1,0:T(8,128)(2,1)}, u32[]{:S(2)}) copy-start(bf16[14,64,256]{2,1,0:T(8,128)(2,1)} %own.13) | copy-start | bytes 1376260
  7.2 21.1 %copy-start.19 = (s32[11,2]{0,1:T(2,128)S(1)}, s32[11,2]{0,1:T(2,128)}, u32[]{:S(2)}) copy-start(s32[11,2]{0,1:T(2,128)} %param.16) | copy-start | bytes 268
  7.2 53.2 %all-gather.5.cloned.1.call-start = ((), (), s32[]{:S(2)}) async-start(), calls=%async_computation.16 | async-start | bytes 2785280 | tf_op jit(solution)/shard_map/all_gather | solution.py:305
  7.9 95.4 %all-gather.3.cloned.1.call-start = ((), (), s32[]{:S(2)}) async-start(), calls=%async_computation.15 | async-start | bytes 2785280 | tf_op jit(solution)/shard_map/all_gather | solution.py:305
  8.0 12.3 %collective-permute-start.1 = (bf16[14,64,256]{2,1,0:T(8,128)(2,1)}, bf16[14,64,256]{2,1,0:T(8,128)(2,1)S(1)}, u32[]{:S(2)}, u32[]{:S(2)}) collective-permute-start(bf16[14,64,256]{2,1,0:T(8,128)(2,1)} %own.13), channel_id=1, source_target_pairs={{0,1},{1,0},{2,3},{3,2},{4,5},{5,4},{6,7},{7,6},{8,9},{9,8},{10,11... | collective-permute-start | bytes 1376264 | tf_op jit(solution)/shard_map/ppermute | solution.py:34
  16.7 48.6 %copy-start.8 = (bf16[7,64,64]{2,1,0:T(8,128)(2,1)S(1)}, bf16[7,64,64]{2,1,0:T(8,128)(2,1)}, u32[]{:S(2)}) copy-start(bf16[7,64,64]{2,1,0:T(8,128)(2,1)} %here.3) | copy-start | bytes 172036
  16.8 50.5 %copy-start.20 = (s32[8]{0:T(128)S(1)}, s32[8]{0:T(128)}, u32[]{:S(2)}) copy-start(s32[8]{0:T(128)} %param.15) | copy-start | bytes 100
  16.8 50.5 %copy-start.17 = (s32[3]{0:T(128)S(1)}, s32[3]{0:T(128)}, u32[]{:S(2)}) copy-start(s32[3]{0:T(128)} %constant.68.clone) | copy-start | bytes 40
  16.8 3.5 %collective-permute-start = (bf16[3,64,64]{2,1,0:T(8,128)(2,1)}, bf16[3,64,64]{2,1,0:T(8,128)(2,1)S(1)}, u32[]{:S(2)}, u32[]{:S(2)}) collective-permute-start(bf16[3,64,64]{2,1,0:T(8,128)(2,1)} %here.2), channel_id=1, source_target_pairs={{0,1},{1,0},{2,3},{3,2},{4,5},{5,4},{6,7},{7,6},{8,9},{9,8},{10,11... | collective-permute-start | bytes 73736 | tf_op jit(solution)/shard_map/ppermute | solution.py:34
  20.3 1.0 copy-start
  23.6 16.9 %all-to-all-start = ((bf16[8,2,32,256]{3,2,1,0:T(8,128)(2,1)}), bf16[8,2,32,256]{3,2,1,0:T(8,128)(2,1)S(1)}, u32[]{:S(2)}, u32[]{:S(2)}) async-start(bf16[8,2,32,256]{3,2,1,0:T(8,128)(2,1)} %get-tuple-element.29), calls=%async_computation | async-start | bytes 524288 | tf_op jit(solution)/shard_map/all_to_all | solution.py:308
  41.2 36.5 %copy-start.6 = (bf16[2,32,256]{2,1,0:T(8,128)(2,1)}, bf16[2,32,256]{2,1,0:T(8,128)(2,1)S(1)}, u32[]{:S(2)}) copy-start(bf16[2,32,256]{2,1,0:T(8,128)(2,1)S(1)} %get-tuple-element.33.y.y_leaf) | copy-start | bytes 98308
  60.3 21.6 %collective-permute-start.3 = (bf16[17,64,1024]{2,1,0:T(8,128)(2,1)}, bf16[17,64,1024]{2,1,0:T(8,128)(2,1)}, u32[]{:S(2)}, u32[]{:S(2)}) collective-permute-start(bf16[17,64,1024]{2,1,0:T(8,128)(2,1)} %all-gather.5.cloned.1.call-done), channel_id=1, source_target_pairs={{0,1},{1,0},{2,3},{3,2},{4,5},{5,4},{6,7},{7,6},{8,9},{9,8},{10,11... | collective-permute-start | bytes 6684680 | tf_op jit(solution)/shard_map/ppermute | solution.py:34
  65.3 12.3 %collective-permute-start.2 = (bf16[7,64,64]{2,1,0:T(8,128)(2,1)S(1)}, bf16[7,64,64]{2,1,0:T(8,128)(2,1)S(1)}, u32[]{:S(2)}, u32[]{:S(2)}) collective-permute-start(bf16[7,64,64]{2,1,0:T(8,128)(2,1)S(1)} %copy-done.8), channel_id=1, source_target_pairs={{0,1},{1,0},{2,3},{3,2},{4,5},{5,4},{6,7},{7,6},{8,9},{9,8},{10,11... | collective-permute-start | bytes 172040 | tf_op jit(solution)/shard_map/ppermute | solution.py:34
  70.1 7.6 %copy-start.15 = (bf16[32,256]{1,0:T(8,128)(2,1)}, bf16[32,256]{1,0:T(8,128)(2,1)S(1)}, u32[]{:S(2)}) copy-start(bf16[32,256]{1,0:T(8,128)(2,1)S(1)} %get-tuple-element.51.y_root) | copy-start | bytes 49156
  70.1 16.8 %all-to-all-start.3 = ((f32[32,8,128]{2,1,0:T(8,128)}), f32[32,8,128]{2,1,0:T(8,128)S(1)}, u32[]{:S(2)}, u32[]{:S(2)}) async-start(f32[32,8,128]{2,1,0:T(8,128)} %get-tuple-element.34), calls=%async_computation.3 | async-start | bytes 262144 | tf_op jit(solution)/shard_map/all_to_all | solution.py:308
  88.0 10.5 %all-to-all-start.4 = ((bf16[8,4,1024]{2,1,0:T(4,128)(2,1)}), bf16[8,4,1024]{2,1,0:T(4,128)(2,1)S(1)}, u32[]{:S(2)}, u32[]{:S(2)}) async-start(bf16[8,4,1024]{2,1,0:T(4,128)(2,1)} %get-tuple-element.36), calls=%async_computation.4 | async-start | bytes 131072 | tf_op jit(solution)/shard_map/all_to_all | solution.py:308
  99.9 10.1 %all-to-all-start.5 = ((bf16[8,2,1024]{2,1,0:T(2,128)(2,1)}), bf16[8,2,1024]{2,1,0:T(2,128)(2,1)S(1)}, u32[]{:S(2)}, u32[]{:S(2)}) async-start(bf16[8,2,1024]{2,1,0:T(2,128)(2,1)} %get-tuple-element.38), calls=%async_computation.5 | async-start | bytes 65536 | tf_op jit(solution)/shard_map/all_to_all | solution.py:308
  110.1 14.6 %collective-permute-start.4 = (bf16[17,64,1024]{2,1,0:T(8,128)(2,1)}, bf16[17,64,1024]{2,1,0:T(8,128)(2,1)}, u32[]{:S(2)}, u32[]{:S(2)}) collective-permute-start(bf16[17,64,1024]{2,1,0:T(8,128)(2,1)} %all-gather.3.cloned.1.call-done), channel_id=1, source_target_pairs={{0,1},{1,0},{2,3},{3,2},{4,5},{5,4},{6,7},{7,6},{8,9},{9,8},{10,11... | collective-permute-start | bytes 6684680 | tf_op jit(solution)/shard_map/ppermute | solution.py:34
  119.2 28.0 %copy-start.2 = (bf16[14,64,256]{2,1,0:T(8,128)(2,1)S(1)}, bf16[14,64,256]{2,1,0:T(8,128)(2,1)}, u32[]{:S(2)}) copy-start(bf16[14,64,256]{2,1,0:T(8,128)(2,1)} %own.17) | copy-start | bytes 1376260
  119.2 10.3 %all-to-all-start.6 = ((bf16[8,2,1024]{2,1,0:T(2,128)(2,1)}), bf16[8,2,1024]{2,1,0:T(2,128)(2,1)S(1)}, u32[]{:S(2)}, u32[]{:S(2)}) async-start(bf16[8,2,1024]{2,1,0:T(2,128)(2,1)} %get-tuple-element.42), calls=%async_computation.6 | async-start | bytes 65536 | tf_op jit(solution)/shard_map/all_to_all | solution.py:308
  130.9 20.6 %copy-start.4 = (f32[8,1024]{1,0:T(8,128)}, f32[8,1024]{1,0:T(8,128)S(1)}, u32[]{:S(2)}) copy-start(f32[8,1024]{1,0:T(8,128)S(1)} %get-tuple-element.46.y_in) | copy-start | bytes 98308
  130.9 10.1 %all-to-all-start.7 = ((bf16[8,2,1024]{2,1,0:T(2,128)(2,1)}), bf16[8,2,1024]{2,1,0:T(2,128)(2,1)S(1)}, u32[]{:S(2)}, u32[]{:S(2)}) async-start(bf16[8,2,1024]{2,1,0:T(2,128)(2,1)} %get-tuple-element.45), calls=%async_computation.7 | async-start | bytes 65536 | tf_op jit(solution)/shard_map/all_to_all | solution.py:308
  143.3 13.9 %all-to-all-start.8 = ((bf16[8,2,1024]{2,1,0:T(2,128)(2,1)}), bf16[8,2,1024]{2,1,0:T(2,128)(2,1)}, u32[]{:S(2)}, u32[]{:S(2)}) async-start(bf16[8,2,1024]{2,1,0:T(2,128)(2,1)} %get-tuple-element.47), calls=%async_computation.8 | async-start | bytes 65536 | tf_op jit(solution)/shard_map/all_to_all | solution.py:308
  147.2 36.0 %collective-permute-start.6 = (bf16[14,64,256]{2,1,0:T(8,128)(2,1)S(1)}, bf16[14,64,256]{2,1,0:T(8,128)(2,1)S(1)}, u32[]{:S(2)}, u32[]{:S(2)}) collective-permute-start(bf16[14,64,256]{2,1,0:T(8,128)(2,1)S(1)} %copy-done.2), channel_id=1, source_target_pairs={{0,1},{1,0},{2,3},{3,2},{4,5},{5,4},{6,7},{7,6},{8,9},{9,8},{10,11... | collective-permute-start | bytes 1376264 | tf_op jit(solution)/shard_map/ppermute | solution.py:34
  157.1 1.0 copy-start.3
  162.6 13.9 %all-to-all-start.9 = ((bf16[8,4,1024]{2,1,0:T(4,128)(2,1)}), bf16[8,4,1024]{2,1,0:T(4,128)(2,1)S(1)}, u32[]{:S(2)}, u32[]{:S(2)}) async-start(bf16[8,4,1024]{2,1,0:T(4,128)(2,1)} %copy-done.9), calls=%async_computation.9 | async-start | bytes 131072 | tf_op jit(solution)/shard_map/all_to_all | solution.py:308
  178.0 13.7 %all-to-all-start.10 = ((bf16[32,8,256]{2,1,0:T(8,128)(2,1)}), bf16[32,8,256]{2,1,0:T(8,128)(2,1)S(1)}, u32[]{:S(2)}, u32[]{:S(2)}) async-start(bf16[32,8,256]{2,1,0:T(8,128)(2,1)} %shard_map.116), calls=%async_computation.10 | async-start | bytes 262144 | tf_op jit(solution)/shard_map/all_to_all | solution.py:308
  201.6 11.2 %all-to-all-start.12 = ((bf16[8,32,256]{2,1,0:T(8,128)(2,1)}), bf16[8,32,256]{2,1,0:T(8,128)(2,1)S(1)}, u32[]{:S(2)}, u32[]{:S(2)}) async-start(bf16[8,32,256]{2,1,0:T(8,128)(2,1)} %get-tuple-element.53), calls=%async_computation.12 | async-start | bytes 262144 | tf_op jit(solution)/shard_map/all_to_all | solution.py:308
  214.1 10.7 %all-to-all-start.13 = ((bf16[4,2,32,128]{3,2,1,0:T(8,128)(2,1)}), bf16[4,2,32,128]{3,2,1,0:T(8,128)(2,1)S(1)}, u32[]{:S(2)}, u32[]{:S(2)}) async-start(bf16[4,2,32,128]{3,2,1,0:T(8,128)(2,1)} %shard_map.119), calls=%async_computation.13 | async-start | bytes 131072 | tf_op jit(solution)/shard_map/all_to_all | solution.py:308
  217.5 15.0 %collective-permute-start.5 = (bf16[7,16,32]{1,0,2:T(8,128)(2,1)S(1)}, bf16[7,16,32]{1,0,2:T(8,128)(2,1)S(1)}, u32[]{:S(2)}, u32[]{:S(2)}) collective-permute-start(bf16[7,16,32]{1,0,2:T(8,128)(2,1)S(1)} %dynamic-slice_bitcast_fusion.1), channel_id=1, source_target_pairs={{0,1},{1,0},{2,3},{3,2},{4,5},{5,4},{6,7},{7,6},{8,9},{9,8},{10,11... | collective-permute-start | bytes 21512 | tf_op jit(solution)/shard_map/ppermute | solution.py:34
  225.7 14.7 %all-to-all-start.14 = ((bf16[16,16,128]{2,1,0:T(8,128)(2,1)}), bf16[16,16,128]{2,1,0:T(8,128)(2,1)S(1)}, u32[]{:S(2)}, u32[]{:S(2)}) async-start(bf16[16,16,128]{2,1,0:T(8,128)(2,1)} %shard_map.120), calls=%async_computation.14 | async-start | bytes 131072 | tf_op jit(solution)/shard_map/all_to_all | solution.py:308
  (10 other events, 7.0 us)
Sparse Core Ops, SparseCore 0:
  10.1 44.4 all-gather.4
  56.7 42.1 all-gather.2

commit v4 on v3

--- a/solution.py
+++ b/solution.py
@@ -8,7 +8,7 @@
 from jax.experimental.pallas import tpu as pltpu
 from jax.sharding import Mesh, PartitionSpec as P
 
-SUB_LEVELS = 2
+
 SUB_NODES = 3
 LEAVES = (1, 2)
 CORES = 2
@@ -38,9 +38,11 @@
     return jax.ShapeDtypeStruct(dims, dtype)
 
 
-def run(body, outs, smem, vmem, scratch=()):
+def run(body, outs, smem, vmem, scratch=(), far=()):
     in_specs = [pl.BlockSpec(memory_space=pltpu.SMEM)] * len(smem)
     in_specs += [pl.BlockSpec(memory_space=pltpu.VMEM)] * len(vmem)
+    in_specs += [pl.BlockSpec(memory_space=pltpu.HBM)] * len(far)
+    far = [pltpu.with_memory_space_constraint(array, pltpu.HBM) for array in far]
     single = not isinstance(outs, (list, tuple))
     spec = pl.BlockSpec(memory_space=pltpu.VMEM)
     return pl.pallas_call(
@@ -50,7 +52,7 @@
         out_specs=spec if single else [spec] * len(outs),
         scratch_shapes=list(scratch),
         compiler_params=pltpu.CompilerParams(vmem_limit_bytes=VMEM_BYTES),
-    )(*smem, *vmem)
+    )(*smem, *vmem, *far)
 
 
 def total(tiles_ref):
@@ -134,19 +136,41 @@
     to_all(out, times(given, block(own, other, 0)))
 
 
-def sub_root_anc(pairs, levels, w, tiles, so_far, own, other, y_out, out):
+def sub_root_anc(pairs, levels, w, tiles, so_far, own, other, y_out, out, scratch):
     y = total(tiles).astype(BF16)
     y_out[...] = y
-    out[...] = jnp.zeros_like(out)
+    scratch[...] = jnp.zeros_like(scratch)
     for e in range(levels):
-        out[:, e, :] = so_far[e] + sub_low(y, w, pairs, own, other, 0, 0, e)
-
-
-def solve_level(pairs, depth, v8, own, other, out, scratch):
+        scratch[:, e, :] = so_far[e] + sub_low(y, w, pairs, own, other, 0, 0, e)
+    out[...] = scratch[...].astype(BF16)
+
+
+def fetch(blocks, near, near_x, sems, own, other):
+    copies = []
+    at = 0
+    while at < len(blocks):
+        count = 1
+        while at + count < len(blocks) and blocks[at + count] == blocks[at] + count:
+            count += 1
+        for j, (source, target) in enumerate(((own, near), (other, near_x))):
+            copies.append(
+                pltpu.make_async_copy(
+                    source.at[pl.ds(blocks[at], count)],
+                    target.at[pl.ds(at, count)],
+                    sems.at[at, j],
+                )
+            )
+        at += count
+    for copy in copies:
+        copy.start()
+    return copies
+
+
+def solve_level(depth, v8, offset, near, near_x, out, scratch):
     first, stop = level_span(depth)
     value = jnp.zeros_like(scratch)
     for i, a in enumerate(range(first, stop)):
-        value = value + in_row(times(v8, block(own, other, i)), a)
+        value = value + in_row(times(v8, block(near, near_x, offset + i)), a)
     scratch[...] = value
     to_all(out, scratch[first : first + out.shape[1], :])
 
@@ -160,59 +184,107 @@
     out[...] = value
 
 
-def anc_first(pairs, depth, tiles, choose, given, own, other, acc_out, out, scratch):
+def anc_first(
+    blocks, depth, tiles, choose, given, own, other, acc_out, out, scratch, near, near_x, sems, arrived
+):
+    copies = fetch(blocks, near, near_x, sems, own, other)
+    arrived[...] = tiles[...].astype(F32)
     acc = given[...]
     for e in range(choose.shape[0]):
         acc = acc - lax.dot_general(
             choose[e],
-            tiles[:, e, :],
+            arrived[:, e, :],
             (((1,), (0,)), ((), ())),
             precision=lax.Precision.HIGHEST,
             preferred_element_type=F32,
         )
     acc_out[...] = acc
-    solve_level(pairs, depth, acc.astype(BF16), own, other, out, scratch)
-
-
-def anc_forward(pairs, depth, tiles, y_in, acc_in, low, low_x, own, other, y_out, acc_out, out, scratch):
+    for copy in copies:
+        copy.wait()
+    solve_level(depth, acc.astype(BF16), 0, near, near_x, out, scratch)
+
+
+def pair_sum(depth, u, values, offset, blocks, down):
     first, stop = level_span(depth)
-    y_out[...] = y_in[...]
-    y_out[first:stop, :] = total(tiles)[: stop - first].astype(BF16).astype(F32)
+    result = 0.0
+    for i, d in enumerate(range(first, stop)):
+        source, target = (d, above(d, u)) if down else (above(d, u), d)
+        v = jnp.broadcast_to(values[source : source + 1, :], values.shape)
+        v = in_row(v, target).astype(BF16)
+        result = result + times_t(v, block(*blocks, offset + i))
+    return result
+
+
+def level_rows(depth, tiles, out):
+    first, stop = level_span(depth)
+    out[...] = jnp.zeros_like(out)
+    out[first:stop, :] = total(tiles)[: stop - first].astype(BF16).astype(F32)
+
+
+def anc_forward(
+    blocks, depth, tiles, acc_in, own, other, y_out, acc_out, out, scratch, near, near_x, sems
+):
+    copies = fetch(blocks, near, near_x, sems, own, other)
+    level_rows(depth, tiles, y_out)
+    for copy in copies:
+        copy.wait()
+    acc = acc_in[...] - pair_sum(depth, depth - 1, y_out, 0, (near, near_x), True)
+    acc_out[...] = acc
+    solve_level(depth - 1, acc.astype(BF16), 2**depth, near, near_x, out, scratch)
+
+
+def other_pairs(blocks, depth, down, values, acc_in, own, other, acc_out, near, near_x, sems):
+    copies = fetch(blocks, near, near_x, sems, own, other)
     acc = acc_in[...]
-    start = pairs.anc[first, 0]
-    for d in range(first, stop):
-        y = jnp.broadcast_to(y_out[d : d + 1, :], y_out.shape)
-        for u in range(depth):
-            v = in_row(y, above(d, u)).astype(BF16)
-            acc = acc - times_t(v, block(low, low_x, pairs.anc[d, u] - start))
+    for copy in copies:
+        copy.wait()
+    for u in range(depth - 1):
+        acc = acc - pair_sum(depth, u, values, u * 2**depth, (near, near_x), down)
     acc_out[...] = acc
-    solve_level(pairs, depth - 1, acc.astype(BF16), own, other, out, scratch)
-
-
-def anc_turn(pairs, where, tiles, y_in, own, other, y_out, out, scratch):
+
+
+def z_rows(where, values, rows):
     core, z = where[0], where[1]
-    y_out[...] = y_in[...]
-    y_out[0:1, :] = total(tiles)[:1].astype(BF16).astype(F32)
-    pair_rows = own.shape[1] * CORES
-    t = own_first(y_out[:, pl.ds(pl.multiple_of(z * pair_rows, pair_rows), pair_rows)], core)
-    solve_level(pairs, 0, t.astype(BF16), own, other, out, scratch)
-
-
-def anc_backward(pairs, depth, where, tiles, z_in, y_in, up, up_x, own, other, z_out, out, scratch):
-    core, z = where[0], where[1]
-    first, stop = level_span(depth - 1)
-    z_out[...] = z_in[...]
-    z_out[first:stop, :] = total(tiles)[: stop - first].astype(BF16).astype(F32)
-    pair_rows = own.shape[1] * CORES
-    acc = own_first(y_in[:, pl.ds(pl.multiple_of(z * pair_rows, pair_rows), pair_rows)], core)
-    first, stop = level_span(depth)
-    start = pairs.anc[first, 0]
-    for a in range(first, stop):
-        for u in range(depth):
-            q = above(a, u)
-            v = in_row(jnp.broadcast_to(z_out[q : q + 1, :], z_out.shape), a).astype(BF16)
-            acc = acc - times_t(v, block(up, up_x, pairs.anc[a, u] - start))
-    solve_level(pairs, depth, acc.astype(BF16), own, other, out, scratch)
+    return own_first(values[:, pl.ds(pl.multiple_of(z * rows, rows), rows)], core)
+
+
+def anc_turn(blocks, where, tiles, own, other, y_out, out, scratch, near, near_x, sems):
+    copies = fetch(blocks, near, near_x, sems, own, other)
+    level_rows(0, tiles, y_out)
+    t = z_rows(where, y_out, own.shape[1] * CORES)
+    for copy in copies:
+        copy.wait()
+    solve_level(0, t.astype(BF16), 0, near, near_x, out, scratch)
+
+
+def anc_start(where, *refs):
+    out = refs[-1]
+    out[...] = sum(z_rows(where, values, out.shape[1]) for values in refs[:-1])
+
+
+def added(*refs):
+    refs[-1][...] = sum(values[...] for values in refs[:-1])
+
+
+def anc_backward(
+    blocks, depth, tiles, acc_in, own, other, z_out, out, scratch, near, near_x, sems
+):
+    copies = fetch(blocks, near, near_x, sems, own, other)
+    level_rows(depth - 1, tiles, z_out)
+    for copy in copies:
+        copy.wait()
+    acc = acc_in[...] - pair_sum(depth, depth - 1, z_out, 0, (near, near_x), False)
+    solve_level(depth, acc.astype(BF16), 2**depth, near, near_x, out, scratch)
+
+
+def sub_pieces(where, y_root, y_leaf, out):
+    core, held, base = where[0], where[2], where[3]
+    rows = out.shape[2]
+    span = pl.ds(pl.multiple_of(base, rows), rows)
+    scale = held.astype(F32)
+    for m in range(SUB_NODES):
+        y = y_root[:, span] if m == 0 else y_leaf[m - 1, :, span]
+        out[m] = scale * own_first(y.astype(F32), core)
 
 
 def anc_spread(depth, nrow, tiles, z_in, out, scratch):
@@ -225,8 +297,7 @@
         out[i] = scratch[:, r * wide : (r + 1) * wide].astype(BF16)
 
 
-def sub_turn(pairs, levels, where, ids, w, tiles, y_root, y_leaf, own, other, kept, out, scratch):
-    core, held, base = where[0], where[2], where[3]
+def sub_turn(pairs, levels, ids, w, tiles, y_own, own, other, kept, out, scratch):
     scratch[...] = tiles[...].astype(F32)
     picked = []
     for e in range(levels):
@@ -234,12 +305,8 @@
         for a in range(*level_span(e)):
             value = value + jnp.where(ids[e] == a, 1.0, 0.0) * scratch[:, a, :]
         picked.append(value.astype(BF16))
-    pair_rows = own.shape[1] * CORES
-    scale = held.astype(F32)
     for m in range(SUB_NODES):
-        span = pl.ds(pl.multiple_of(base, pair_rows), pair_rows)
-        y = y_root[:, span] if m == 0 else y_leaf[m - 1, :, span]
-        value = scale * own_first(y.astype(F32), core)
+        value = y_own[m]
         for e in range(levels):
             p = pairs.sub[m, 0, e]
             value = value - w[p] * times_t(picked[e], block(own, other, SUB_NODES + p))
@@ -307,24 +374,38 @@
     def exchange(array, axes):
         return lax.all_to_all(array, axes, 0, 0, tiled=True)
 
+    def two_cores(array):
+        return array, swapped(array)
+
+    def tied(send, *others):
+        return lax.optimization_barrier((send, *others))
+
     low = (sub_lower, swapped(sub_lower))
     rhs_there = swapped(sub_rhs)
-    anc_there = swapped(anc_rhs)
-    up = (sub_upper, swapped(sub_upper))
     anc_low_row = gathered(anc_lower)
     anc_up_row = gathered(anc_upper)
 
-    def diagonal(two, depth):
-        first, stop = level_span(depth)
-        return [array[first:stop] for array in two]
-
-    def pair_blocks(two, depth):
-        first, stop = level_span(depth)
-        start = pairs.anc[first, 0]
-        return [array[start : start + (stop - first) * depth] for array in two]
+    def diagonal(depth):
+        return list(range(*level_span(depth)))
+
+    def pair_blocks(depth, u):
+        return [pairs.anc[a, u] for a in range(*level_span(depth))]
+
+    def anc_run(body, blocks, outs, smem, vmem, two, scratch, *fixed):
+        near = pltpu.VMEM((len(blocks), *two[0].shape[1:]), BF16)
+        sems = pltpu.SemaphoreType.DMA((len(blocks), CORES))
+        scratch = (*scratch[:1], near, near, sems, *scratch[1:])
+        return run(part(body, blocks, *fixed), outs, smem, vmem, scratch, two)
+
+    def others(depth, down, values, acc, two):
+        blocks = [index for u in range(depth - 1) for index in pair_blocks(depth, u)]
+        return anc_run(other_pairs, blocks, acc_shape, (), (values, acc), two, (), depth, down)
 
     def level_shape(depth):
         return shape(BF16, nz, max(2, 2**depth), size)
+
+    acc_shape = shape(F32, ROWS8, pair_rows)
+    row_shape = shape(F32, ROWS8, size)
 
     rhs, tiles = run(
         sub_leaf_solve,
@@ -332,7 +413,11 @@
         (where,),
         (sub_rhs, rhs_there, *low),
     )
+    tiles, anc_rhs = tied(tiles, anc_rhs)
+    anc_there = swapped(anc_rhs)
+    given8 = run(anc_prepare, acc_shape, (where,), (anc_rhs, anc_there))
     tiles = exchange(tiles, "z")
+    tiles, given8, choose, low_w, up_w = tied(tiles, given8, choose, low_w, up_w)
     y_leaf, tiles = run(
         part(sub_leaf_update, pairs),
         (shape(BF16, 2, cols, wide), shape(BF16, nrow, cols, pair_rows)),
@@ -346,58 +431,87 @@
         (low_w,),
         (y_leaf, *low),
     )
+    tiles, so_far = tied(tiles, so_far)
     tiles = run(sub_root_solve, shape(BF16, nz, cols, wide), (), (tiles, rhs, *low))
     tiles = exchange(tiles, "z")
-    anc_low_row, tiles = lax.optimization_barrier((anc_low_row, tiles))
-    anc_low = (anc_low_row, swapped(anc_low_row))
-    given8 = run(anc_prepare, shape(F32, ROWS8, pair_rows), (where,), (anc_rhs, anc_there))
+    tiles, anc_low_row = tied(tiles, anc_low_row)
+    anc_low = two_cores(anc_low_row)
+    c_scratch = pltpu.VMEM((layers * nrow, ROWS8, pair_rows), F32)
     y_root, tiles = run(
         part(sub_root_anc, pairs, levels),
-        (shape(BF16, cols, wide), shape(F32, cols, ROWS8, pair_rows)),
+        (shape(BF16, cols, wide), shape(BF16, layers * nrow, ROWS8, pair_rows)),
         (low_w,),
         (tiles, so_far, *low),
+        (c_scratch,),
     )
     tiles = exchange(tiles, ("gz", "row"))
 
-    y8 = jnp.zeros((ROWS8, size), F32)
-    acc, tiles = run(
-        part(anc_first, pairs, levels - 1),
-        (shape(F32, ROWS8, pair_rows), level_shape(levels - 1)),
+    acc, tiles = anc_run(
+        anc_first,
+        diagonal(levels - 1),
+        (acc_shape, level_shape(levels - 1)),
         (),
-        (tiles, choose, given8, *diagonal(anc_low, levels - 1)),
-        (scr8,),
+        (tiles, choose, given8),
+        anc_low,
+        (scr8, c_scratch),
+        levels - 1,
     )
     tiles = exchange(tiles, "z")
+    y_parts = []
     for depth in range(levels - 1, 0, -1):
         if depth == 1:
-            anc_up_row, tiles = lax.optimization_barrier((anc_up_row, tiles))
-            anc_up = (anc_up_row, swapped(anc_up_row))
-        y8, acc, tiles = run(
-            part(anc_forward, pairs, depth),
-            (shape(F32, ROWS8, size), shape(F32, ROWS8, pair_rows), level_shape(depth - 1)),
+            tiles, anc_up_row = tied(tiles, anc_up_row)
+            anc_up = two_cores(anc_up_row)
+        y8, acc, tiles = anc_run(
+            anc_forward,
+            pair_blocks(depth, depth - 1) + diagonal(depth - 1),
+            (row_shape, acc_shape, level_shape(depth - 1)),
             (),
-            (tiles, y8, acc, *pair_blocks(anc_low, depth), *diagonal(anc_low, depth - 1)),
+            (tiles, acc),
+            anc_low,
             (scr8,),
+            depth,
         )
+        y_parts.append(y8)
         tiles = exchange(tiles, "z")
-    y8, tiles = run(
-        part(anc_turn, pairs),
-        (shape(F32, ROWS8, size), level_shape(0)),
+        if depth > 1:
+            acc = others(depth, True, y8, acc, anc_low)
+            tiles, acc = tied(tiles, acc)
+    y8, tiles = anc_run(
+        anc_turn,
+        diagonal(0),
+        (row_shape, level_shape(0)),
         (where,),
-        (tiles, y8, *diagonal(anc_up, 0)),
+        (tiles,),
+        anc_up,
         (scr8,),
     )
+    y_parts.append(y8)
     tiles = exchange(tiles, "z")
-    z8 = jnp.zeros((ROWS8, size), F32)
+    start8 = run(anc_start, acc_shape, (where,), y_parts)
+    tiles, start8 = tied(tiles, start8)
+    z8 = None
     for depth in range(1, levels):
-        z8, tiles = run(
-            part(anc_backward, pairs, depth),
-            (shape(F32, ROWS8, size), level_shape(depth)),
-            (where,),
-            (tiles, z8, y8, *pair_blocks(anc_up, depth), *diagonal(anc_up, depth)),
+        acc = start8
+        if depth > 1:
+            acc = others(depth, False, z8, acc, anc_up)
+            tiles, acc = tied(tiles, acc)
+        z_now, tiles = anc_run(
+            anc_backward,
+            pair_blocks(depth, depth - 1) + diagonal(depth),
+            (row_shape, level_shape(depth)),
+            (),
+            (tiles, acc),
+            anc_up,
             (scr8,),
+            depth,
         )
+        if depth == levels - 1:
+            tiles, sub_upper = tied(tiles, sub_upper)
         tiles = exchange(tiles, "z")
+        z8 = z_now if z8 is None else run(added, row_shape, (), (z8, z_now))
+        tiles, z8 = tied(tiles, z8)
+    up = two_cores(sub_upper)
     tiles = run(
         part(anc_spread, levels - 1, nrow),
         shape(BF16, layers * nrow, ROWS8, wide),
@@ -406,12 +520,15 @@
         (scr8,),
     )
     z_all = exchange(tiles, ("gz", "row"))
+    y_own = run(sub_pieces, shape(F32, SUB_NODES, cols, pair_rows), (where,), (y_root, y_leaf))
+    z_all, y_own, ids_here, up_there = tied(z_all, y_own, ids_here, up[1])
+    up = (up[0], up_there)
 
     kept, tiles = run(
         part(sub_turn, pairs, levels),
         (shape(F32, 2, cols, pair_rows), shape(BF16, nrow, cols, pair_rows)),
-        (where, ids_here, up_w),
-        (z_all, y_root, y_leaf, *up),
+        (ids_here, up_w),
+        (z_all, y_own, *up),
         (pltpu.VMEM(z_all.shape, F32),),
     )
     tiles = exchange(tiles, "row")
@@ -470,4 +587,5 @@
         P("gz", None),
     )
     out_specs = (P(None, ("row", "z", "core"), None), P("gz", ("row", "z", "core"), None))
+
     return jax.shard_map(local, mesh=split, in_specs=in_specs, out_specs=out_specs, check_vma=False)

time: 250 us -> 242 us (0.968)
  local copies, waits for them, and re-layouts: 28.6 us -> 5.96 us
  blocking collectives: 25.6 us -> 45.1 us
  Pallas kernels: 18.1 us -> 29.1 us
  starting transfers between devices: 89.9 us -> 81 us
  waiting for transfers between devices: 69.4 us -> 62.3 us
    all_to_all x3 -> x5, blocking collectives: 25.6 us -> 45.1 us  [exchange(): return lax.all_to_all(array, axes, 0, 0, tiled=True)]
    slice x16 -> x0, local copies, waits for them, and re-layouts: 18.4 us -> none  [the longest x10 10.9 us: diagonal(): return [array[first:stop] for array in two]]
    pallas_call x17 -> x22, Pallas kernels: 18.1 us -> 29.1 us  [run(): pl.pallas_call(body, out_shape=outs, in_specs=in_specs, out_specs=spec if...]
    all_to_all x12 -> x10, starting transfers between devices: 54.3 us -> 43.6 us  [exchange(): return lax.all_to_all(array, axes, 0, 0, tiled=True)]
    all_to_all x12 -> x10, waiting for transfers between devices: 67.3 us -> 60.7 us  [exchange(): return lax.all_to_all(array, axes, 0, 0, tiled=True)]
    unnamed x42 -> x18, local copies, waits for them, and re-layouts: 8.85 us -> 4.64 us
  transfers between devices with their start and end apart: 21 -> 19, of which waited for: 11 -> 10; matrix products, arithmetic and copies ran while one was open for 8% -> 1% of each run, Pallas kernels for 5% -> 7%
where the time goes in v4:
time: 242 us; the launch traced here: 241 us
  starting transfers between devices  81 us (33%)
  waiting for transfers between devices  62.3 us (26%)
  blocking collectives  45.1 us (19%)
  Pallas kernels  29.1 us (12%)
  between operations  14.4 us (6%)
  local copies, waits for them, and re-layouts  5.96 us (2%)
  other arithmetic  2.61 us (1%)
    all_to_all x10, waiting for transfers between devices, exchange(): return lax.all_to_all(array, axes, 0, 0, tiled=True)  60.7 us
    all_to_all x5, blocking collectives, exchange(): return lax.all_to_all(array, axes, 0, 0, tiled=True)  45.1 us
    all_to_all x10, starting transfers between devices, exchange(): return lax.all_to_all(array, axes, 0, 0, tiled=True)  43.6 us
    ppermute x7, starting transfers between devices, swapped(): return lax.ppermute(array, 'core', [(0, 1), (1, 0)])  37.4 us
    pallas_call x22, Pallas kernels, run(): pl.pallas_call(body, out_shape=outs, in_specs=in_specs, out_specs=spec if...  29.1 us
  transfers between devices with their start and end apart: 19, of which 10 were waited for; matrix products, arithmetic and copies ran while one was open for 1% of the time, Pallas kernels for 7%

profile of v4, /device:TPU:1, one launch (start us, length us, event | category | flops | bytes accessed | tf_op | source)
XLA Modules:
  0.0 240.5 jit_solution(15563026914866609546)
XLA Ops:
  8.0 8.7 %collective-permute-start.1 = (bf16[14,64,256]{2,1,0:T(8,128)(2,1)}, bf16[14,64,256]{2,1,0:T(8,128)(2,1)S(1)}, u32[]{:S(2)}, u32[]{:S(2)}) collective-permute-start(bf16[14,64,256]{2,1,0:T(8,128)(2,1)} %own.9), channel_id=1, source_target_pairs={{0,1},{1,0},{2,3},{3,2},{4,5},{5,4},{6,7},{7,6},{8,9},{9,8},{10,11... | collective-permute-start | bytes 1376264 | tf_op jit(solution)/shard_map/ppermute | solution.py:34
  23.4 4.7 %all-to-all-start = ((bf16[8,2,32,256]{3,2,1,0:T(8,128)(2,1)}), bf16[8,2,32,256]{3,2,1,0:T(8,128)(2,1)S(1)}, u32[]{:S(2)}, u32[]{:S(2)}) async-start(bf16[8,2,32,256]{3,2,1,0:T(8,128)(2,1)} %get-tuple-element.55), calls=%async_computation | async-start | bytes 524288 | tf_op jit(solution)/shard_map/all_to_all | solution.py:375
  28.4 2.7 %collective-permute-start.2 = (bf16[7,64,64]{2,1,0:T(8,128)(2,1)S(1)}, bf16[7,64,64]{2,1,0:T(8,128)(2,1)S(1)}, u32[]{:S(2)}, u32[]{:S(2)}) collective-permute-start(bf16[7,64,64]{2,1,0:T(8,128)(2,1)S(1)} %copy-done.3), channel_id=1, source_target_pairs={{0,1},{1,0},{2,3},{3,2},{4,5},{5,4},{6,7},{7,6},{8,9},{9,8},{10,11... | collective-permute-start | bytes 172040 | tf_op jit(solution)/shard_map/ppermute | solution.py:34
  32.8 6.1 %all-to-all-done.tiles = bf16[8,2,32,256]{3,2,1,0:T(8,128)(2,1)S(1)} async-done(((bf16[8,2,32,256]{3,2,1,0:T(8,128)(2,1)}), bf16[8,2,32,256]{3,2,1,0:T(8,128)(2,1)S(1)}, u32[]{:S(2)}, u32[]{:S(2)}) %all-to-all-start) | async-done | bytes 262176 | tf_op jit(solution)/shard_map/all_to_all | solution.py:375
  40.2 4.0 %all-to-all-start.1 = ((bf16[4,32,128]{2,1,0:T(8,128)(2,1)}), bf16[4,32,128]{2,1,0:T(8,128)(2,1)S(1)}, u32[]{:S(2)}, u32[]{:S(2)}) async-start(bf16[4,32,128]{2,1,0:T(8,128)(2,1)} %get-tuple-element.59), calls=%async_computation.1 | async-start | bytes 65536 | tf_op jit(solution)/shard_map/all_to_all | solution.py:375
  45.0 4.0 %all-to-all-done.1.tiles = bf16[4,32,128]{2,1,0:T(8,128)(2,1)S(1)} async-done(((bf16[4,32,128]{2,1,0:T(8,128)(2,1)}), bf16[4,32,128]{2,1,0:T(8,128)(2,1)S(1)}, u32[]{:S(2)}, u32[]{:S(2)}) %all-to-all-start.1) | async-done | bytes 32800 | tf_op jit(solution)/shard_map/all_to_all | solution.py:375
  49.1 10.3 %all_to_all.75.tiles = bf16[8,32,256]{2,1,0:T(8,128)(2,1)S(1)} all-to-all(bf16[8,32,256]{2,1,0:T(8,128)(2,1)S(1)} %shard_map.108), channel_id=1, replica_groups=mesh['gz'=8,'row'=4,'z'=8,'core'=2] {'z'}, dimensions={0} | all-to-all | bytes 262144 | tf_op jit(solution)/shard_map/all_to_all | solution.py:375
  59.4 6.5 %collective-permute-start.3 = (bf16[17,64,1024]{2,1,0:T(8,128)(2,1)}, bf16[17,64,1024]{2,1,0:T(8,128)(2,1)S(1)}, u32[]{:S(2)}, u32[]{:S(2)}) collective-permute-start(bf16[17,64,1024]{2,1,0:T(8,128)(2,1)} %all-gather.3.cloned.1.call-done.own), channel_id=1, source_target_pairs={{0,1},{1,0},{2,3},{3,2},{4,5},{5,4},{6,7},{7,6},{8,9},{9,8},{10,11... | collective-permute-start | bytes 6684680 | tf_op jit(solution)/shard_map/ppermute | solution.py:34
  67.4 7.4 %all-to-all-start.3 = ((bf16[32,8,128]{2,1,0:T(8,128)(2,1)}), bf16[32,8,128]{2,1,0:T(8,128)(2,1)S(1)}, u32[]{:S(2)}, u32[]{:S(2)}) async-start(bf16[32,8,128]{2,1,0:T(8,128)(2,1)} %get-tuple-element.65), calls=%async_computation.3 | async-start | bytes 131072 | tf_op jit(solution)/shard_map/all_to_all | solution.py:375
  74.9 8.9 %all-to-all-done.3.tiles = bf16[32,8,128]{2,1,0:T(8,128)(2,1)S(1)} async-done(((bf16[32,8,128]{2,1,0:T(8,128)(2,1)}), bf16[32,8,128]{2,1,0:T(8,128)(2,1)S(1)}, u32[]{:S(2)}, u32[]{:S(2)}) %all-to-all-start.3) | async-done | bytes 65568 | tf_op jit(solution)/shard_map/all_to_all | solution.py:375
  86.8 9.6 %all_to_all.76.tiles = bf16[8,4,1024]{2,1,0:T(4,128)(2,1)S(1)} all-to-all(bf16[8,4,1024]{2,1,0:T(4,128)(2,1)S(1)} %get-tuple-element.69), channel_id=1, replica_groups=mesh['gz'=8,'row'=4,'z'=8,'core'=2] {'z'}, dimensions={0} | all-to-all | bytes 131072 | tf_op jit(solution)/shard_map/all_to_all | solution.py:375
  96.4 2.9 %shard_map.111 = (f32[8,1024]{1,0:T(8,128)S(1)}, f32[8,128]{1,0:T(8,128)S(1)}, bf16[8,2,1024]{2,1,0:T(2,128)(2,1)}) custom-call(bf16[8,4,1024]{2,1,0:T(4,128)(2,1)S(1)} %all_to_all.76.tiles, f32[8,128]{1,0:T(8,128)S(1)} %get-tuple-element.70.acc_in, bf16[17,64,1024]{2,1,0:T(8,128)(2,1)} %all-gather.3.cloned.1.call-done.own, bf16[17,64,1024]{2,1,0:T(8,128)(2,1)} %copy-done.5), custom_call_target="tpu_custom_call" | custom-call | tf_op jit(solution)/shard_map/pallas_call | solution.py:48
  99.3 3.4 %all-to-all-start.5 = ((bf16[8,2,1024]{2,1,0:T(2,128)(2,1)}), bf16[8,2,1024]{2,1,0:T(2,128)(2,1)S(1)}, u32[]{:S(2)}, u32[]{:S(2)}) async-start(bf16[8,2,1024]{2,1,0:T(2,128)(2,1)} %get-tuple-element.71), calls=%async_computation.5 | async-start | bytes 65536 | tf_op jit(solution)/shard_map/all_to_all | solution.py:375
  104.4 5.1 %all-to-all-done.5.tiles = bf16[8,2,1024]{2,1,0:T(2,128)(2,1)S(1)} async-done(((bf16[8,2,1024]{2,1,0:T(2,128)(2,1)}), bf16[8,2,1024]{2,1,0:T(2,128)(2,1)S(1)}, u32[]{:S(2)}, u32[]{:S(2)}) %all-to-all-start.5) | async-done | bytes 32800 | tf_op jit(solution)/shard_map/all_to_all | solution.py:375
  109.5 5.4 %collective-permute-start.4 = (bf16[17,64,1024]{2,1,0:T(8,128)(2,1)}, bf16[17,64,1024]{2,1,0:T(8,128)(2,1)S(1)}, u32[]{:S(2)}, u32[]{:S(2)}) collective-permute-start(bf16[17,64,1024]{2,1,0:T(8,128)(2,1)} %all-gather.5.cloned.1.call-done.own), channel_id=1, source_target_pairs={{0,1},{1,0},{2,3},{3,2},{4,5},{5,4},{6,7},{7,6},{8,9},{9,8},{10,11... | collective-permute-start | bytes 6684680 | tf_op jit(solution)/shard_map/ppermute | solution.py:34
  117.0 9.2 %all_to_all.77.tiles = bf16[8,2,1024]{2,1,0:T(2,128)(2,1)S(1)} all-to-all(bf16[8,2,1024]{2,1,0:T(2,128)(2,1)S(1)} %get-tuple-element.77), channel_id=1, replica_groups=mesh['gz'=8,'row'=4,'z'=8,'core'=2] {'z'}, dimensions={0} | all-to-all | bytes 65536 | tf_op jit(solution)/shard_map/all_to_all | solution.py:375
  129.9 3.4 %all-to-all-start.7 = ((bf16[8,2,1024]{2,1,0:T(2,128)(2,1)}), bf16[8,2,1024]{2,1,0:T(2,128)(2,1)S(1)}, u32[]{:S(2)}, u32[]{:S(2)}) async-start(bf16[8,2,1024]{2,1,0:T(2,128)(2,1)} %get-tuple-element.79), calls=%async_computation.7 | async-start | bytes 65536 | tf_op jit(solution)/shard_map/all_to_all | solution.py:375
  133.9 6.2 %all-to-all-done.7.tiles = bf16[8,2,1024]{2,1,0:T(2,128)(2,1)S(1)} async-done(((bf16[8,2,1024]{2,1,0:T(2,128)(2,1)}), bf16[8,2,1024]{2,1,0:T(2,128)(2,1)S(1)}, u32[]{:S(2)}, u32[]{:S(2)}) %all-to-all-start.7) | async-done | bytes 32800 | tf_op jit(solution)/shard_map/all_to_all | solution.py:375
  141.9 9.2 %all_to_all.78.tiles = bf16[8,2,1024]{2,1,0:T(2,128)(2,1)S(1)} all-to-all(bf16[8,2,1024]{2,1,0:T(2,128)(2,1)S(1)} %get-tuple-element.84), channel_id=1, replica_groups=mesh['gz'=8,'row'=4,'z'=8,'core'=2] {'z'}, dimensions={0} | all-to-all | bytes 65536 | tf_op jit(solution)/shard_map/all_to_all | solution.py:375
  152.9 3.3 %shard_map.118 = (f32[8,1024]{1,0:T(8,128)S(1)}, bf16[8,4,1024]{2,1,0:T(4,128)(2,1)}) custom-call(bf16[8,2,1024]{2,1,0:T(2,128)(2,1)S(1)} %all_to_all.78.tiles, f32[8,128]{1,0:T(8,128)S(1)} %shard_map.117.acc_in, bf16[17,64,1024]{2,1,0:T(8,128)(2,1)} %all-gather.5.cloned.1.call-done.own, bf16[17,64,1024]{2,1,0:T(8,128)(2,1)} %copy-done.6), custom_call_target="tpu_custom_call" | custom-call | tf_op jit(solution)/shard_map/pallas_call | solution.py:48
  156.3 5.4 %collective-permute-start.5 = (bf16[14,64,256]{2,1,0:T(8,128)(2,1)S(1)}, bf16[14,64,256]{2,1,0:T(8,128)(2,1)S(1)}, u32[]{:S(2)}, u32[]{:S(2)}) collective-permute-start(bf16[14,64,256]{2,1,0:T(8,128)(2,1)S(1)} %copy-done.2), channel_id=1, source_target_pairs={{0,1},{1,0},{2,3},{3,2},{4,5},{5,4},{6,7},{7,6},{8,9},{9,8},{10,11... | collective-permute-start | bytes 1376264 | tf_op jit(solution)/shard_map/ppermute | solution.py:34
  161.7 3.4 %all-to-all-start.9 = ((bf16[8,4,1024]{2,1,0:T(4,128)(2,1)}), bf16[8,4,1024]{2,1,0:T(4,128)(2,1)S(1)}, u32[]{:S(2)}, u32[]{:S(2)}) async-start(bf16[8,4,1024]{2,1,0:T(4,128)(2,1)} %get-tuple-element.91), calls=%async_computation.9 | async-start | bytes 131072 | tf_op jit(solution)/shard_map/all_to_all | solution.py:375
  165.1 7.3 %all-to-all-done.9.tiles = bf16[8,4,1024]{2,1,0:T(4,128)(2,1)S(1)} async-done(((bf16[8,4,1024]{2,1,0:T(4,128)(2,1)}), bf16[8,4,1024]{2,1,0:T(4,128)(2,1)S(1)}, u32[]{:S(2)}, u32[]{:S(2)}) %all-to-all-start.9) | async-done | bytes 65568 | tf_op jit(solution)/shard_map/all_to_all | solution.py:375
  173.0 3.9 %all-to-all-start.10 = ((bf16[32,8,256]{2,1,0:T(8,128)(2,1)}), bf16[32,8,256]{2,1,0:T(8,128)(2,1)S(1)}, u32[]{:S(2)}, u32[]{:S(2)}) async-start(bf16[32,8,256]{2,1,0:T(8,128)(2,1)} %shard_map.120), calls=%async_computation.10 | async-start | bytes 262144 | tf_op jit(solution)/shard_map/all_to_all | solution.py:375
  177.7 8.6 %all-to-all-done.10.tiles = bf16[32,8,256]{2,1,0:T(8,128)(2,1)S(1)} async-done(((bf16[32,8,256]{2,1,0:T(8,128)(2,1)}), bf16[32,8,256]{2,1,0:T(8,128)(2,1)S(1)}, u32[]{:S(2)}, u32[]{:S(2)}) %all-to-all-start.10) | async-done | bytes 131104 | tf_op jit(solution)/shard_map/all_to_all | solution.py:375
  187.2 6.7 %all_to_all.79.tiles = bf16[4,32,128]{2,1,0:T(8,128)(2,1)S(1)} all-to-all(bf16[4,32,128]{2,1,0:T(8,128)(2,1)S(1)} %get-tuple-element.102), channel_id=1, replica_groups=mesh['gz'=8,'row'=4,'z'=8,'core'=2] {'row'}, dimensions={0} | all-to-all | bytes 65536 | tf_op jit(solution)/shard_map/all_to_all | solution.py:375
  194.7 3.4 %all-to-all-start.12 = ((bf16[8,32,256]{2,1,0:T(8,128)(2,1)}), bf16[8,32,256]{2,1,0:T(8,128)(2,1)S(1)}, u32[]{:S(2)}, u32[]{:S(2)}) async-start(bf16[8,32,256]{2,1,0:T(8,128)(2,1)} %get-tuple-element.103), calls=%async_computation.12 | async-start | bytes 262144 | tf_op jit(solution)/shard_map/all_to_all | solution.py:375
  198.1 7.8 %all-to-all-done.12.tiles = bf16[8,32,256]{2,1,0:T(8,128)(2,1)S(1)} async-done(((bf16[8,32,256]{2,1,0:T(8,128)(2,1)}), bf16[8,32,256]{2,1,0:T(8,128)(2,1)S(1)}, u32[]{:S(2)}, u32[]{:S(2)}) %all-to-all-start.12) | async-done | bytes 131104 | tf_op jit(solution)/shard_map/all_to_all | solution.py:375
  207.2 3.3 %all-to-all-start.13 = ((bf16[4,2,32,128]{3,2,1,0:T(8,128)(2,1)}), bf16[4,2,32,128]{3,2,1,0:T(8,128)(2,1)S(1)}, u32[]{:S(2)}, u32[]{:S(2)}) async-start(bf16[4,2,32,128]{3,2,1,0:T(8,128)(2,1)} %shard_map.124), calls=%async_computation.13 | async-start | bytes 131072 | tf_op jit(solution)/shard_map/all_to_all | solution.py:375
  210.6 6.7 %collective-permute-start.6 = (bf16[7,16,32]{1,0,2:T(8,128)(2,1)S(1)}, bf16[7,16,32]{1,0,2:T(8,128)(2,1)S(1)}, u32[]{:S(2)}, u32[]{:S(2)}) collective-permute-start(bf16[7,16,32]{1,0,2:T(8,128)(2,1)S(1)} %dynamic-slice_bitcast_fusion.1), channel_id=1, source_target_pairs={{0,1},{1,0},{2,3},{3,2},{4,5},{5,4},{6,7},{7,6},{8,9},{9,8},{10,11... | collective-permute-start | bytes 21512 | tf_op jit(solution)/shard_map/ppermute | solution.py:34
  218.1 6.8 %all-to-all-start.14 = ((bf16[16,16,128]{2,1,0:T(8,128)(2,1)}), bf16[16,16,128]{2,1,0:T(8,128)(2,1)S(1)}, u32[]{:S(2)}, u32[]{:S(2)}) async-start(bf16[16,16,128]{2,1,0:T(8,128)(2,1)} %shard_map.125), calls=%async_computation.14 | async-start | bytes 131072 | tf_op jit(solution)/shard_map/all_to_all | solution.py:375
  226.0 6.8 %all-to-all-done.14 = bf16[16,16,128]{2,1,0:T(8,128)(2,1)S(1)} async-done(((bf16[16,16,128]{2,1,0:T(8,128)(2,1)}), bf16[16,16,128]{2,1,0:T(8,128)(2,1)S(1)}, u32[]{:S(2)}, u32[]{:S(2)}) %all-to-all-start.14) | async-done | bytes 65568 | tf_op jit(solution)/shard_map/all_to_all | solution.py:375
  (72 shorter events, 35.1 us)
Async XLA Ops:
  7.2 20.9 %copy-start.7 = (s32[3]{0:T(128)S(1)}, s32[3]{0:T(128)}, u32[]{:S(2)}) copy-start(s32[3]{0:T(128)} %constant.67.clone) | copy-start | bytes 40
  7.2 31.7 %copy-start.1 = (bf16[14,64,256]{2,1,0:T(8,128)(2,1)S(1)}, bf16[14,64,256]{2,1,0:T(8,128)(2,1)}, u32[]{:S(2)}) copy-start(bf16[14,64,256]{2,1,0:T(8,128)(2,1)} %own.9) | copy-start | bytes 1376260
  7.2 21.2 %copy-start.3 = (bf16[7,64,64]{2,1,0:T(8,128)(2,1)S(1)}, bf16[7,64,64]{2,1,0:T(8,128)(2,1)}, u32[]{:S(2)}) copy-start(bf16[7,64,64]{2,1,0:T(8,128)(2,1)} %here.2) | copy-start | bytes 172036
  7.2 23.9 %copy-start.8 = (s32[11,2]{0,1:T(2,128)S(1)}, s32[11,2]{0,1:T(2,128)}, u32[]{:S(2)}) copy-start(s32[11,2]{0,1:T(2,128)} %param.16) | copy-start | bytes 268
  7.2 52.2 %all-gather.3.cloned.1.call-start = ((), (), s32[]{:S(2)}) async-start(), calls=%async_computation.15 | async-start | bytes 2785280 | tf_op jit(solution)/shard_map/all_gather | solution.py:372
  7.9 101.6 %all-gather.5.cloned.1.call-start = ((), (), s32[]{:S(2)}) async-start(), calls=%async_computation.16 | async-start | bytes 2785280 | tf_op jit(solution)/shard_map/all_gather | solution.py:372
  8.0 12.1 %collective-permute-start.1 = (bf16[14,64,256]{2,1,0:T(8,128)(2,1)}, bf16[14,64,256]{2,1,0:T(8,128)(2,1)S(1)}, u32[]{:S(2)}, u32[]{:S(2)}) collective-permute-start(bf16[14,64,256]{2,1,0:T(8,128)(2,1)} %own.9), channel_id=1, source_target_pairs={{0,1},{1,0},{2,3},{3,2},{4,5},{5,4},{6,7},{7,6},{8,9},{9,8},{10,11... | collective-permute-start | bytes 1376264 | tf_op jit(solution)/shard_map/ppermute | solution.py:34
  16.7 3.4 %collective-permute-start = (bf16[3,64,64]{2,1,0:T(8,128)(2,1)}, bf16[3,64,64]{2,1,0:T(8,128)(2,1)S(1)}, u32[]{:S(2)}, u32[]{:S(2)}) collective-permute-start(bf16[3,64,64]{2,1,0:T(8,128)(2,1)} %here.1), channel_id=1, source_target_pairs={{0,1},{1,0},{2,3},{3,2},{4,5},{5,4},{6,7},{7,6},{8,9},{9,8},{10,11... | collective-permute-start | bytes 73736 | tf_op jit(solution)/shard_map/ppermute | solution.py:34
  20.1 1.0 copy-start
  21.1 0.8 copy-start.4
  23.4 15.4 %all-to-all-start = ((bf16[8,2,32,256]{3,2,1,0:T(8,128)(2,1)}), bf16[8,2,32,256]{3,2,1,0:T(8,128)(2,1)S(1)}, u32[]{:S(2)}, u32[]{:S(2)}) async-start(bf16[8,2,32,256]{3,2,1,0:T(8,128)(2,1)} %get-tuple-element.55), calls=%async_computation | async-start | bytes 524288 | tf_op jit(solution)/shard_map/all_to_all | solution.py:375
  28.4 3.6 %collective-permute-start.2 = (bf16[7,64,64]{2,1,0:T(8,128)(2,1)S(1)}, bf16[7,64,64]{2,1,0:T(8,128)(2,1)S(1)}, u32[]{:S(2)}, u32[]{:S(2)}) collective-permute-start(bf16[7,64,64]{2,1,0:T(8,128)(2,1)S(1)} %copy-done.3), channel_id=1, source_target_pairs={{0,1},{1,0},{2,3},{3,2},{4,5},{5,4},{6,7},{7,6},{8,9},{9,8},{10,11... | collective-permute-start | bytes 172040 | tf_op jit(solution)/shard_map/ppermute | solution.py:34
  40.2 8.8 %all-to-all-start.1 = ((bf16[4,32,128]{2,1,0:T(8,128)(2,1)}), bf16[4,32,128]{2,1,0:T(8,128)(2,1)S(1)}, u32[]{:S(2)}, u32[]{:S(2)}) async-start(bf16[4,32,128]{2,1,0:T(8,128)(2,1)} %get-tuple-element.59), calls=%async_computation.1 | async-start | bytes 65536 | tf_op jit(solution)/shard_map/all_to_all | solution.py:375
  59.4 24.4 %collective-permute-start.3 = (bf16[17,64,1024]{2,1,0:T(8,128)(2,1)}, bf16[17,64,1024]{2,1,0:T(8,128)(2,1)S(1)}, u32[]{:S(2)}, u32[]{:S(2)}) collective-permute-start(bf16[17,64,1024]{2,1,0:T(8,128)(2,1)} %all-gather.3.cloned.1.call-done.own), channel_id=1, source_target_pairs={{0,1},{1,0},{2,3},{3,2},{4,5},{5,4},{6,7},{7,6},{8,9},{9,8},{10,11... | collective-permute-start | bytes 6684680 | tf_op jit(solution)/shard_map/ppermute | solution.py:34
  67.4 16.4 %all-to-all-start.3 = ((bf16[32,8,128]{2,1,0:T(8,128)(2,1)}), bf16[32,8,128]{2,1,0:T(8,128)(2,1)S(1)}, u32[]{:S(2)}, u32[]{:S(2)}) async-start(bf16[32,8,128]{2,1,0:T(8,128)(2,1)} %get-tuple-element.65), calls=%async_computation.3 | async-start | bytes 131072 | tf_op jit(solution)/shard_map/all_to_all | solution.py:375
  83.8 1.4 copy-start.5
  99.3 10.2 %all-to-all-start.5 = ((bf16[8,2,1024]{2,1,0:T(2,128)(2,1)}), bf16[8,2,1024]{2,1,0:T(2,128)(2,1)S(1)}, u32[]{:S(2)}, u32[]{:S(2)}) async-start(bf16[8,2,1024]{2,1,0:T(2,128)(2,1)} %get-tuple-element.71), calls=%async_computation.5 | async-start | bytes 65536 | tf_op jit(solution)/shard_map/all_to_all | solution.py:375
  109.5 16.7 %collective-permute-start.4 = (bf16[17,64,1024]{2,1,0:T(8,128)(2,1)}, bf16[17,64,1024]{2,1,0:T(8,128)(2,1)S(1)}, u32[]{:S(2)}, u32[]{:S(2)}) collective-permute-start(bf16[17,64,1024]{2,1,0:T(8,128)(2,1)} %all-gather.5.cloned.1.call-done.own), channel_id=1, source_target_pairs={{0,1},{1,0},{2,3},{3,2},{4,5},{5,4},{6,7},{7,6},{8,9},{9,8},{10,11... | collective-permute-start | bytes 6684680 | tf_op jit(solution)/shard_map/ppermute | solution.py:34
  126.2 1.4 copy-start.6
  129.9 10.2 %all-to-all-start.7 = ((bf16[8,2,1024]{2,1,0:T(2,128)(2,1)}), bf16[8,2,1024]{2,1,0:T(2,128)(2,1)S(1)}, u32[]{:S(2)}, u32[]{:S(2)}) async-start(bf16[8,2,1024]{2,1,0:T(2,128)(2,1)} %get-tuple-element.79), calls=%async_computation.7 | async-start | bytes 65536 | tf_op jit(solution)/shard_map/all_to_all | solution.py:375
  152.9 3.4 %copy-start.2 = (bf16[14,64,256]{2,1,0:T(8,128)(2,1)S(1)}, bf16[14,64,256]{2,1,0:T(8,128)(2,1)}, u32[]{:S(2)}) copy-start(bf16[14,64,256]{2,1,0:T(8,128)(2,1)} %own.13) | copy-start | bytes 1376260
  156.3 30.0 %collective-permute-start.5 = (bf16[14,64,256]{2,1,0:T(8,128)(2,1)S(1)}, bf16[14,64,256]{2,1,0:T(8,128)(2,1)S(1)}, u32[]{:S(2)}, u32[]{:S(2)}) collective-permute-start(bf16[14,64,256]{2,1,0:T(8,128)(2,1)S(1)} %copy-done.2), channel_id=1, source_target_pairs={{0,1},{1,0},{2,3},{3,2},{4,5},{5,4},{6,7},{7,6},{8,9},{9,8},{10,11... | collective-permute-start | bytes 1376264 | tf_op jit(solution)/shard_map/ppermute | solution.py:34
  161.7 10.6 %all-to-all-start.9 = ((bf16[8,4,1024]{2,1,0:T(4,128)(2,1)}), bf16[8,4,1024]{2,1,0:T(4,128)(2,1)S(1)}, u32[]{:S(2)}, u32[]{:S(2)}) async-start(bf16[8,4,1024]{2,1,0:T(4,128)(2,1)} %get-tuple-element.91), calls=%async_computation.9 | async-start | bytes 131072 | tf_op jit(solution)/shard_map/all_to_all | solution.py:375
  173.0 13.3 %all-to-all-start.10 = ((bf16[32,8,256]{2,1,0:T(8,128)(2,1)}), bf16[32,8,256]{2,1,0:T(8,128)(2,1)S(1)}, u32[]{:S(2)}, u32[]{:S(2)}) async-start(bf16[32,8,256]{2,1,0:T(8,128)(2,1)} %shard_map.120), calls=%async_computation.10 | async-start | bytes 262144 | tf_op jit(solution)/shard_map/all_to_all | solution.py:375
  194.7 11.2 %all-to-all-start.12 = ((bf16[8,32,256]{2,1,0:T(8,128)(2,1)}), bf16[8,32,256]{2,1,0:T(8,128)(2,1)S(1)}, u32[]{:S(2)}, u32[]{:S(2)}) async-start(bf16[8,32,256]{2,1,0:T(8,128)(2,1)} %get-tuple-element.103), calls=%async_computation.12 | async-start | bytes 262144 | tf_op jit(solution)/shard_map/all_to_all | solution.py:375
  207.2 10.1 %all-to-all-start.13 = ((bf16[4,2,32,128]{3,2,1,0:T(8,128)(2,1)}), bf16[4,2,32,128]{3,2,1,0:T(8,128)(2,1)S(1)}, u32[]{:S(2)}, u32[]{:S(2)}) async-start(bf16[4,2,32,128]{3,2,1,0:T(8,128)(2,1)} %shard_map.124), calls=%async_computation.13 | async-start | bytes 131072 | tf_op jit(solution)/shard_map/all_to_all | solution.py:375
  210.6 14.4 %collective-permute-start.6 = (bf16[7,16,32]{1,0,2:T(8,128)(2,1)S(1)}, bf16[7,16,32]{1,0,2:T(8,128)(2,1)S(1)}, u32[]{:S(2)}, u32[]{:S(2)}) collective-permute-start(bf16[7,16,32]{1,0,2:T(8,128)(2,1)S(1)} %dynamic-slice_bitcast_fusion.1), channel_id=1, source_target_pairs={{0,1},{1,0},{2,3},{3,2},{4,5},{5,4},{6,7},{7,6},{8,9},{9,8},{10,11... | collective-permute-start | bytes 21512 | tf_op jit(solution)/shard_map/ppermute | solution.py:34
  218.1 14.7 %all-to-all-start.14 = ((bf16[16,16,128]{2,1,0:T(8,128)(2,1)}), bf16[16,16,128]{2,1,0:T(8,128)(2,1)S(1)}, u32[]{:S(2)}, u32[]{:S(2)}) async-start(bf16[16,16,128]{2,1,0:T(8,128)(2,1)} %shard_map.125), calls=%async_computation.14 | async-start | bytes 131072 | tf_op jit(solution)/shard_map/all_to_all | solution.py:375
Sparse Core Ops, SparseCore 0:
  10.1 44.4 all-gather.2
  56.7 42.5 all-gather.4

commit v5 on v4

--- a/solution.py
+++ b/solution.py
@@ -2,7 +2,6 @@
 
 import jax
 import jax.numpy as jnp
-import numpy as np
 from jax import lax
 from jax.experimental import pallas as pl
 from jax.experimental.pallas import tpu as pltpu
@@ -102,21 +101,31 @@
                 self.anc[a, u] = anc_count + len(self.anc)
 
 
-def sub_leaf_solve(where, here, there, own, other, rhs, out):
+def sub_leaf_solve(where, there, other, own, here, rhs, out, near, near_rhs, sems):
+    first, count = LEAVES[0], len(LEAVES)
+    copies = [
+        pltpu.make_async_copy(own.at[pl.ds(first, count)], near, sems.at[0]),
+        pltpu.make_async_copy(here, near_rhs, sems.at[1]),
+    ]
+    for copy in copies:
+        copy.start()
+    for copy in copies:
+        copy.wait()
     core = where[0]
     cols = rhs.shape[1]
     for m in range(SUB_NODES):
-        flipped = jnp.concatenate([here[m], there[m]], 0).astype(F32).T
+        flipped = jnp.concatenate([near_rhs[m], there[m]], 0).astype(F32).T
         rhs[m] = jnp.where(core == 0, flipped[:cols], flipped[cols:]).astype(BF16)
     for m in LEAVES:
-        part = times(rhs[m], block(own, other, m)).astype(BF16)
+        both = jnp.concatenate([near[m - first], other[m]], 0)
+        part = times(rhs[m], both).astype(BF16)
         for i in range(out.shape[0]):
             out[i, m - 1] = part
 
 
 def sub_low(y, w, pairs, own, other, m, kind, u):
     p = pairs.sub[m, kind, u]
-    return w[p] * times_t(y, block(own, other, SUB_NODES + p))
+    return w[p, 0].astype(F32) * times_t(y, block(own, other, SUB_NODES + p))
 
 
 def sub_leaf_update(pairs, w, tiles, own, other, y_out, out):
@@ -166,6 +175,11 @@
     return copies
 
 
+def load_blocks(blocks, own, other, near, near_x, sems):
+    for copy in fetch(blocks, near, near_x, sems, own, other):
+        copy.wait()
+
+
 def solve_level(depth, v8, offset, near, near_x, out, scratch):
     first, stop = level_span(depth)
     value = jnp.zeros_like(scratch)
@@ -175,7 +189,21 @@
     to_all(out, scratch[first : first + out.shape[1], :])
 
 
-def anc_prepare(where, here, there, out):
+def ancestor(subtree, g, layers, levels, e):
+    return lax.shift_right_logical(subtree[g] + layers, levels - e) - 1
+
+
+def anc_prepare(layers, nrow, where, subtree, here, there, choose, out):
+    levels = choose.shape[0]
+    rows = lax.broadcasted_iota(jnp.int32, choose.shape[1:], 0)
+    source = lax.broadcasted_iota(jnp.int32, choose.shape[1:], 1)
+    for e in range(levels):
+        value = jnp.zeros(choose.shape[1:], F32)
+        for g in range(layers):
+            ours = (source >= g * nrow) & (source < (g + 1) * nrow)
+            hit = ours & (rows == ancestor(subtree, g, layers, levels, e))
+            value = jnp.where(hit, 1.0, value)
+        choose[e] = value
     lanes = lax.broadcasted_iota(jnp.int32, (ROWS8, here.shape[2]), 1)
     pick = jnp.where(lanes == where[5], 1.0, 0.0).astype(BF16)
     value = jnp.zeros_like(out)
@@ -184,10 +212,7 @@
     out[...] = value
 
 
-def anc_first(
-    blocks, depth, tiles, choose, given, own, other, acc_out, out, scratch, near, near_x, sems, arrived
-):
-    copies = fetch(blocks, near, near_x, sems, own, other)
+def anc_first(depth, tiles, choose, given, near, near_x, acc_out, out, scratch, arrived):
     arrived[...] = tiles[...].astype(F32)
     acc = given[...]
     for e in range(choose.shape[0]):
@@ -199,8 +224,6 @@
             preferred_element_type=F32,
         )
     acc_out[...] = acc
-    for copy in copies:
-        copy.wait()
     solve_level(depth, acc.astype(BF16), 0, near, near_x, out, scratch)
 
 
@@ -221,13 +244,8 @@
     out[first:stop, :] = total(tiles)[: stop - first].astype(BF16).astype(F32)
 
 
-def anc_forward(
-    blocks, depth, tiles, acc_in, own, other, y_out, acc_out, out, scratch, near, near_x, sems
-):
-    copies = fetch(blocks, near, near_x, sems, own, other)
+def anc_forward(depth, tiles, acc_in, near, near_x, y_out, acc_out, out, scratch):
     level_rows(depth, tiles, y_out)
-    for copy in copies:
-        copy.wait()
     acc = acc_in[...] - pair_sum(depth, depth - 1, y_out, 0, (near, near_x), True)
     acc_out[...] = acc
     solve_level(depth - 1, acc.astype(BF16), 2**depth, near, near_x, out, scratch)
@@ -248,12 +266,9 @@
     return own_first(values[:, pl.ds(pl.multiple_of(z * rows, rows), rows)], core)
 
 
-def anc_turn(blocks, where, tiles, own, other, y_out, out, scratch, near, near_x, sems):
-    copies = fetch(blocks, near, near_x, sems, own, other)
+def anc_turn(where, tiles, near, near_x, y_out, out, scratch):
     level_rows(0, tiles, y_out)
-    t = z_rows(where, y_out, own.shape[1] * CORES)
-    for copy in copies:
-        copy.wait()
+    t = z_rows(where, y_out, near.shape[1] * CORES)
     solve_level(0, t.astype(BF16), 0, near, near_x, out, scratch)
 
 
@@ -266,13 +281,8 @@
     refs[-1][...] = sum(values[...] for values in refs[:-1])
 
 
-def anc_backward(
-    blocks, depth, tiles, acc_in, own, other, z_out, out, scratch, near, near_x, sems
-):
-    copies = fetch(blocks, near, near_x, sems, own, other)
+def anc_backward(depth, tiles, acc_in, near, near_x, z_out, out, scratch):
     level_rows(depth - 1, tiles, z_out)
-    for copy in copies:
-        copy.wait()
     acc = acc_in[...] - pair_sum(depth, depth - 1, z_out, 0, (near, near_x), False)
     solve_level(depth, acc.astype(BF16), 2**depth, near, near_x, out, scratch)
 
@@ -297,19 +307,20 @@
         out[i] = scratch[:, r * wide : (r + 1) * wide].astype(BF16)
 
 
-def sub_turn(pairs, levels, ids, w, tiles, y_own, own, other, kept, out, scratch):
+def sub_turn(pairs, layers, levels, where, subtree, w, tiles, y_own, own, other, kept, out, scratch):
     scratch[...] = tiles[...].astype(F32)
     picked = []
     for e in range(levels):
+        id_here = ancestor(subtree, where[4], layers, levels, e)
         value = 0.0
         for a in range(*level_span(e)):
-            value = value + jnp.where(ids[e] == a, 1.0, 0.0) * scratch[:, a, :]
+            value = value + jnp.where(id_here == a, 1.0, 0.0) * scratch[:, a, :]
         picked.append(value.astype(BF16))
     for m in range(SUB_NODES):
         value = y_own[m]
         for e in range(levels):
             p = pairs.sub[m, 0, e]
-            value = value - w[p] * times_t(picked[e], block(own, other, SUB_NODES + p))
+            value = value - w[p, 1].astype(F32) * times_t(picked[e], block(own, other, SUB_NODES + p))
         if m == 0:
             to_all(out, value)
         else:
@@ -326,7 +337,7 @@
     z = total(tiles).astype(BF16)
     for m in LEAVES:
         p = pairs.sub[m, 1, 0]
-        value = kept[m - 1] - w[p] * times_t(z, block(own, other, SUB_NODES + p))
+        value = kept[m - 1] - w[p, 1].astype(F32) * times_t(z, block(own, other, SUB_NODES + p))
         for i in range(out.shape[0]):
             out[i, m - 1] = value.astype(BF16)
 
@@ -356,17 +367,9 @@
     part = functools.partial
     scr8 = pltpu.VMEM((ROWS8, size), F32)
 
-    low_w = sub_pattern[:, 0].astype(F32)
-    up_w = sub_pattern[:, 1].astype(F32)
-    powers = jnp.asarray(2 ** (levels - np.arange(levels)), jnp.int32)
-    heap_ids = (layer_subtree[:, None] + layers) // powers[None, :] - 1
-    nodes = jnp.arange(ROWS8, dtype=jnp.int32)
-    choose = (heap_ids.T[:, None, :] == nodes[None, :, None]).astype(F32)
-    choose = jnp.repeat(choose, nrow, axis=2)
-    ids_here = lax.dynamic_index_in_dim(heap_ids, g, 0, keepdims=False)
     held = (r == z * nrow // nz).astype(jnp.int32)
     base = jnp.clip(z * pair_rows - r * wide, 0, wide - pair_rows)
-    where = jnp.stack([core, z, held, base, jnp.int32(0), core * cols + g * nrow + r]).astype(jnp.int32)
+    where = jnp.stack([core, z, held, base, g, core * cols + g * nrow + r]).astype(jnp.int32)
 
     def gathered(blocks):
         return lax.all_gather(blocks, "row", axis=2, tiled=True)
@@ -391,15 +394,17 @@
     def pair_blocks(depth, u):
         return [pairs.anc[a, u] for a in range(*level_span(depth))]
 
-    def anc_run(body, blocks, outs, smem, vmem, two, scratch, *fixed):
-        near = pltpu.VMEM((len(blocks), *two[0].shape[1:]), BF16)
+    def loaded(blocks, two):
+        near = shape(BF16, len(blocks), own, size)
         sems = pltpu.SemaphoreType.DMA((len(blocks), CORES))
-        scratch = (*scratch[:1], near, near, sems, *scratch[1:])
-        return run(part(body, blocks, *fixed), outs, smem, vmem, scratch, two)
+        return run(part(load_blocks, blocks), (near, near), (), (), (sems,), two)
 
     def others(depth, down, values, acc, two):
         blocks = [index for u in range(depth - 1) for index in pair_blocks(depth, u)]
-        return anc_run(other_pairs, blocks, acc_shape, (), (values, acc), two, (), depth, down)
+        near = pltpu.VMEM((len(blocks), own, size), BF16)
+        sems = pltpu.SemaphoreType.DMA((len(blocks), CORES))
+        body = part(other_pairs, blocks, depth, down)
+        return run(body, acc_shape, (), (values, acc), (near, near, sems), two)
 
     def level_shape(depth):
         return shape(BF16, nz, max(2, 2**depth), size)
@@ -411,24 +416,35 @@
         sub_leaf_solve,
         (shape(BF16, SUB_NODES, cols, pair_rows), shape(BF16, nz, 2, cols, wide)),
         (where,),
-        (sub_rhs, rhs_there, *low),
+        (rhs_there, low[1]),
+        (
+            pltpu.VMEM((len(LEAVES), own, wide), BF16),
+            pltpu.VMEM(sub_rhs.shape, BF16),
+            pltpu.SemaphoreType.DMA((2,)),
+        ),
+        (sub_lower, sub_rhs),
     )
     tiles, anc_rhs = tied(tiles, anc_rhs)
     anc_there = swapped(anc_rhs)
-    given8 = run(anc_prepare, acc_shape, (where,), (anc_rhs, anc_there))
+    choose, given8 = run(
+        part(anc_prepare, layers, nrow),
+        (shape(F32, levels, ROWS8, layers * nrow), acc_shape),
+        (where, layer_subtree),
+        (anc_rhs, anc_there),
+    )
     tiles = exchange(tiles, "z")
-    tiles, given8, choose, low_w, up_w = tied(tiles, given8, choose, low_w, up_w)
+    tiles, given8, choose = tied(tiles, given8, choose)
     y_leaf, tiles = run(
         part(sub_leaf_update, pairs),
         (shape(BF16, 2, cols, wide), shape(BF16, nrow, cols, pair_rows)),
-        (low_w,),
+        (sub_pattern,),
         (tiles, *low),
     )
     tiles = exchange(tiles, "row")
     so_far = run(
         part(sub_leaf_anc, pairs, levels),
         shape(F32, levels, cols, pair_rows),
-        (low_w,),
+        (sub_pattern,),
         (y_leaf, *low),
     )
     tiles, so_far = tied(tiles, so_far)
@@ -440,51 +456,46 @@
     y_root, tiles = run(
         part(sub_root_anc, pairs, levels),
         (shape(BF16, cols, wide), shape(BF16, layers * nrow, ROWS8, pair_rows)),
-        (low_w,),
+        (sub_pattern,),
         (tiles, so_far, *low),
         (c_scratch,),
     )
     tiles = exchange(tiles, ("gz", "row"))
-
-    acc, tiles = anc_run(
-        anc_first,
-        diagonal(levels - 1),
+    near = loaded(diagonal(levels - 1), anc_low)
+    tiles, *near = tied(tiles, *near)
+
+    acc, tiles = run(
+        part(anc_first, levels - 1),
         (acc_shape, level_shape(levels - 1)),
         (),
-        (tiles, choose, given8),
-        anc_low,
+        (tiles, choose, given8, *near),
         (scr8, c_scratch),
-        levels - 1,
     )
     tiles = exchange(tiles, "z")
     y_parts = []
     for depth in range(levels - 1, 0, -1):
+        blocks = pair_blocks(depth, depth - 1) + diagonal(depth - 1)
+        near = loaded(blocks, anc_low)
+        tiles, *near = tied(tiles, *near)
         if depth == 1:
             tiles, anc_up_row = tied(tiles, anc_up_row)
             anc_up = two_cores(anc_up_row)
-        y8, acc, tiles = anc_run(
-            anc_forward,
-            pair_blocks(depth, depth - 1) + diagonal(depth - 1),
+        y8, acc, tiles = run(
+            part(anc_forward, depth),
             (row_shape, acc_shape, level_shape(depth - 1)),
             (),
-            (tiles, acc),
-            anc_low,
+            (tiles, acc, *near),
             (scr8,),
-            depth,
         )
         y_parts.append(y8)
         tiles = exchange(tiles, "z")
         if depth > 1:
             acc = others(depth, True, y8, acc, anc_low)
             tiles, acc = tied(tiles, acc)
-    y8, tiles = anc_run(
-        anc_turn,
-        diagonal(0),
-        (row_shape, level_shape(0)),
-        (where,),
-        (tiles,),
-        anc_up,
-        (scr8,),
+    near = loaded(diagonal(0), anc_up)
+    tiles, *near = tied(tiles, *near)
+    y8, tiles = run(
+        anc_turn, (row_shape, level_shape(0)), (where,), (tiles, *near), (scr8,)
     )
     y_parts.append(y8)
     tiles = exchange(tiles, "z")
@@ -493,24 +504,27 @@
     z8 = None
     for depth in range(1, levels):
         acc = start8
+        blocks = pair_blocks(depth, depth - 1) + diagonal(depth)
+        near = loaded(blocks, anc_up)
+        tiles, *near = tied(tiles, *near)
         if depth > 1:
             acc = others(depth, False, z8, acc, anc_up)
             tiles, acc = tied(tiles, acc)
-        z_now, tiles = anc_run(
-            anc_backward,
-            pair_blocks(depth, depth - 1) + diagonal(depth),
+        z_now, tiles = run(
+            part(anc_backward, depth),
             (row_shape, level_shape(depth)),
             (),
-            (tiles, acc),
-            anc_up,
+            (tiles, acc, *near),
             (scr8,),
-            depth,
         )
         if depth == levels - 1:
             tiles, sub_upper = tied(tiles, sub_upper)
         tiles = exchange(tiles, "z")
-        z8 = z_now if z8 is None else run(added, row_shape, (), (z8, z_now))
-        tiles, z8 = tied(tiles, z8)
+        if z8 is None:
+            z8 = z_now
+        else:
+            z8 = run(added, row_shape, (), (z8, z_now))
+            tiles, z8 = tied(tiles, z8)
     up = two_cores(sub_upper)
     tiles = run(
         part(anc_spread, levels - 1, nrow),
@@ -521,13 +535,13 @@
     )
     z_all = exchange(tiles, ("gz", "row"))
     y_own = run(sub_pieces, shape(F32, SUB_NODES, cols, pair_rows), (where,), (y_root, y_leaf))
-    z_all, y_own, ids_here, up_there = tied(z_all, y_own, ids_here, up[1])
+    z_all, y_own, up_there = tied(z_all, y_own, up[1])
     up = (up[0], up_there)
 
     kept, tiles = run(
-        part(sub_turn, pairs, levels),
+        part(sub_turn, pairs, layers, levels),
         (shape(F32, 2, cols, pair_rows), shape(BF16, nrow, cols, pair_rows)),
-        (ids_here, up_w),
+        (where, layer_subtree, sub_pattern),
         (z_all, y_own, *up),
         (pltpu.VMEM(z_all.shape, F32),),
     )
@@ -553,7 +567,7 @@
     tiles = run(
         part(sub_leaf_back, pairs),
         shape(BF16, nrow, 2, cols, pair_rows),
-        (up_w,),
+        (sub_pattern,),
         (tiles, kept, *up),
     )
     tiles = exchange(tiles, "row")

time: 242 us -> 233 us (0.963)
  blocking collectives: 45.1 us -> 17.1 us
  waiting for transfers between devices: 62.3 us -> 76.6 us
  starting transfers between devices: 81 us -> 89.2 us
  local copies, waits for them, and re-layouts: 5.96 us -> 1.35 us
  Pallas kernels: 29.1 us -> 32.5 us
    all_to_all x5 -> x2, blocking collectives: 45.1 us -> 17.1 us  [exchange(): return lax.all_to_all(array, axes, 0, 0, tiled=True)]
    all_to_all x10 -> x13, waiting for transfers between devices: 60.7 us -> 73.7 us  [exchange(): return lax.all_to_all(array, axes, 0, 0, tiled=True)]
    all_to_all x10 -> x13, starting transfers between devices: 43.6 us -> 53.6 us  [exchange(): return lax.all_to_all(array, axes, 0, 0, tiled=True)]
    unnamed x18 -> x11, local copies, waits for them, and re-layouts: 4.64 us -> 0.12 us
    pallas_call x22 -> x28, Pallas kernels: 29.1 us -> 32.5 us  [run(): pl.pallas_call(body, out_shape=outs, in_specs=in_specs, out_specs=spec if...]
  transfers between devices with their start and end apart: 19 -> 22, of which waited for: 10 -> 14; matrix products, arithmetic and copies ran while one was open for 1% -> 1% of each run, Pallas kernels for 7% -> 11%
where the time goes in v5:
time: 233 us; the launch traced here: 232 us
  starting transfers between devices  89.2 us (38%)
  waiting for transfers between devices  76.6 us (33%)
  Pallas kernels  32.5 us (14%)
  blocking collectives  17.1 us (7%)
  between operations  14.4 us (6%)
    all_to_all x13, waiting for transfers between devices, exchange(): return lax.all_to_all(array, axes, 0, 0, tiled=True)  73.7 us
    all_to_all x13, starting transfers between devices, exchange(): return lax.all_to_all(array, axes, 0, 0, tiled=True)  53.6 us
    ppermute x7, starting transfers between devices, swapped(): return lax.ppermute(array, 'core', [(0, 1), (1, 0)])  35.5 us
    pallas_call x28, Pallas kernels, run(): pl.pallas_call(body, out_shape=outs, in_specs=in_specs, out_specs=spec if...  32.5 us
    all_to_all x2, blocking collectives, exchange(): return lax.all_to_all(array, axes, 0, 0, tiled=True)  17.1 us
  transfers between devices with their start and end apart: 22, of which 14 were waited for; matrix products, arithmetic and copies ran while one was open for 1% of the time, Pallas kernels for 11%

profile of v5, /device:TPU:1, one launch (start us, length us, event | category | flops | bytes accessed | tf_op | source)
XLA Modules:
  0.0 231.9 jit_solution(1474503531813984616)
XLA Ops:
  8.0 8.7 %collective-permute-start.1 = (bf16[14,64,256]{2,1,0:T(8,128)(2,1)}, bf16[14,64,256]{2,1,0:T(8,128)(2,1)S(1)}, u32[]{:S(2)}, u32[]{:S(2)}) collective-permute-start(bf16[14,64,256]{2,1,0:T(8,128)(2,1)} %own.9), channel_id=1, source_target_pairs={{0,1},{1,0},{2,3},{3,2},{4,5},{5,4},{6,7},{7,6},{8,9},{9,8},{10,11... | collective-permute-start | bytes 1376264 | tf_op jit(solution)/shard_map/ppermute | solution.py:33
  22.5 4.7 %all-to-all-start = ((bf16[8,2,32,256]{3,2,1,0:T(8,128)(2,1)}), bf16[8,2,32,256]{3,2,1,0:T(8,128)(2,1)S(1)}, u32[]{:S(2)}, u32[]{:S(2)}) async-start(bf16[8,2,32,256]{3,2,1,0:T(8,128)(2,1)} %get-tuple-element.82), calls=%async_computation | async-start | bytes 524288 | tf_op jit(solution)/shard_map/all_to_all | solution.py:378
  31.2 8.2 %all-to-all-done.tiles = bf16[8,2,32,256]{3,2,1,0:T(8,128)(2,1)S(1)} async-done(((bf16[8,2,32,256]{3,2,1,0:T(8,128)(2,1)}), bf16[8,2,32,256]{3,2,1,0:T(8,128)(2,1)S(1)}, u32[]{:S(2)}, u32[]{:S(2)}) %all-to-all-start) | async-done | bytes 262176 | tf_op jit(solution)/shard_map/all_to_all | solution.py:378
  40.9 4.0 %all-to-all-start.1 = ((bf16[4,32,128]{2,1,0:T(8,128)(2,1)}), bf16[4,32,128]{2,1,0:T(8,128)(2,1)S(1)}, u32[]{:S(2)}, u32[]{:S(2)}) async-start(bf16[4,32,128]{2,1,0:T(8,128)(2,1)} %get-tuple-element.87), calls=%async_computation.1 | async-start | bytes 65536 | tf_op jit(solution)/shard_map/all_to_all | solution.py:378
  45.8 3.9 %all-to-all-done.1.tiles = bf16[4,32,128]{2,1,0:T(8,128)(2,1)S(1)} async-done(((bf16[4,32,128]{2,1,0:T(8,128)(2,1)}), bf16[4,32,128]{2,1,0:T(8,128)(2,1)S(1)}, u32[]{:S(2)}, u32[]{:S(2)}) %all-to-all-start.1) | async-done | bytes 32800 | tf_op jit(solution)/shard_map/all_to_all | solution.py:378
  49.8 10.4 %all_to_all.75.tiles = bf16[8,32,256]{2,1,0:T(8,128)(2,1)S(1)} all-to-all(bf16[8,32,256]{2,1,0:T(8,128)(2,1)S(1)} %shard_map.99), channel_id=1, replica_groups=mesh['gz'=8,'row'=4,'z'=8,'core'=2] {'z'}, dimensions={0} | all-to-all | bytes 262144 | tf_op jit(solution)/shard_map/all_to_all | solution.py:378
  60.2 5.0 %collective-permute-start.3 = (bf16[17,64,1024]{2,1,0:T(8,128)(2,1)}, bf16[17,64,1024]{2,1,0:T(8,128)(2,1)}, u32[]{:S(2)}, u32[]{:S(2)}) collective-permute-start(bf16[17,64,1024]{2,1,0:T(8,128)(2,1)} %all-gather.3.cloned.1.call-done.own), channel_id=1, source_target_pairs={{0,1},{1,0},{2,3},{3,2},{4,5},{5,4},{6,7},{7,6},{8,9},{9,8},{10,11... | collective-permute-start | bytes 6684680 | tf_op jit(solution)/shard_map/ppermute | solution.py:33
  66.7 7.4 %all-to-all-start.3 = ((bf16[32,8,128]{2,1,0:T(8,128)(2,1)}), bf16[32,8,128]{2,1,0:T(8,128)(2,1)S(1)}, u32[]{:S(2)}, u32[]{:S(2)}) async-start(bf16[32,8,128]{2,1,0:T(8,128)(2,1)} %get-tuple-element.93), calls=%async_computation.3 | async-start | bytes 131072 | tf_op jit(solution)/shard_map/all_to_all | solution.py:378
  75.5 7.6 %all-to-all-done.3.tiles = bf16[32,8,128]{2,1,0:T(8,128)(2,1)S(1)} async-done(((bf16[32,8,128]{2,1,0:T(8,128)(2,1)}), bf16[32,8,128]{2,1,0:T(8,128)(2,1)S(1)}, u32[]{:S(2)}, u32[]{:S(2)}) %all-to-all-start.3) | async-done | bytes 65568 | tf_op jit(solution)/shard_map/all_to_all | solution.py:378
  84.2 3.4 %all-to-all-start.4 = ((bf16[8,4,1024]{2,1,0:T(4,128)(2,1)}), bf16[8,4,1024]{2,1,0:T(4,128)(2,1)S(1)}, u32[]{:S(2)}, u32[]{:S(2)}) async-start(bf16[8,4,1024]{2,1,0:T(4,128)(2,1)} %get-tuple-element.102), calls=%async_computation.4 | async-start | bytes 131072 | tf_op jit(solution)/shard_map/all_to_all | solution.py:378
  89.2 5.6 %all-to-all-done.4.tiles = bf16[8,4,1024]{2,1,0:T(4,128)(2,1)S(1)} async-done(((bf16[8,4,1024]{2,1,0:T(4,128)(2,1)}), bf16[8,4,1024]{2,1,0:T(4,128)(2,1)S(1)}, u32[]{:S(2)}, u32[]{:S(2)}) %all-to-all-start.4) | async-done | bytes 65568 | tf_op jit(solution)/shard_map/all_to_all | solution.py:378
  96.0 3.3 %all-to-all-start.5 = ((bf16[8,2,1024]{2,1,0:T(2,128)(2,1)}), bf16[8,2,1024]{2,1,0:T(2,128)(2,1)S(1)}, u32[]{:S(2)}, u32[]{:S(2)}) async-start(bf16[8,2,1024]{2,1,0:T(2,128)(2,1)} %get-tuple-element.109), calls=%async_computation.5 | async-start | bytes 65536 | tf_op jit(solution)/shard_map/all_to_all | solution.py:378
  102.3 4.0 %all-to-all-done.5.tiles = bf16[8,2,1024]{2,1,0:T(2,128)(2,1)S(1)} async-done(((bf16[8,2,1024]{2,1,0:T(2,128)(2,1)}), bf16[8,2,1024]{2,1,0:T(2,128)(2,1)S(1)}, u32[]{:S(2)}, u32[]{:S(2)}) %all-to-all-start.5) | async-done | bytes 32800 | tf_op jit(solution)/shard_map/all_to_all | solution.py:378
  106.3 5.4 %collective-permute-start.4 = (bf16[17,64,1024]{2,1,0:T(8,128)(2,1)}, bf16[17,64,1024]{2,1,0:T(8,128)(2,1)}, u32[]{:S(2)}, u32[]{:S(2)}) collective-permute-start(bf16[17,64,1024]{2,1,0:T(8,128)(2,1)} %all-gather.5.cloned.1.call-done.own), channel_id=1, source_target_pairs={{0,1},{1,0},{2,3},{3,2},{4,5},{5,4},{6,7},{7,6},{8,9},{9,8},{10,11... | collective-permute-start | bytes 6684680 | tf_op jit(solution)/shard_map/ppermute | solution.py:33
  112.8 3.3 %all-to-all-start.6 = ((bf16[8,2,1024]{2,1,0:T(2,128)(2,1)}), bf16[8,2,1024]{2,1,0:T(2,128)(2,1)S(1)}, u32[]{:S(2)}, u32[]{:S(2)}) async-start(bf16[8,2,1024]{2,1,0:T(2,128)(2,1)} %get-tuple-element.120), calls=%async_computation.6 | async-start | bytes 65536 | tf_op jit(solution)/shard_map/all_to_all | solution.py:378
  117.1 5.8 %all-to-all-done.6.tiles = bf16[8,2,1024]{2,1,0:T(2,128)(2,1)S(1)} async-done(((bf16[8,2,1024]{2,1,0:T(2,128)(2,1)}), bf16[8,2,1024]{2,1,0:T(2,128)(2,1)S(1)}, u32[]{:S(2)}, u32[]{:S(2)}) %all-to-all-start.6) | async-done | bytes 32800 | tf_op jit(solution)/shard_map/all_to_all | solution.py:378
  124.3 3.3 %all-to-all-start.7 = ((bf16[8,2,1024]{2,1,0:T(2,128)(2,1)}), bf16[8,2,1024]{2,1,0:T(2,128)(2,1)S(1)}, u32[]{:S(2)}, u32[]{:S(2)}) async-start(bf16[8,2,1024]{2,1,0:T(2,128)(2,1)} %get-tuple-element.127), calls=%async_computation.7 | async-start | bytes 65536 | tf_op jit(solution)/shard_map/all_to_all | solution.py:378
  129.6 4.9 %all-to-all-done.7.tiles = bf16[8,2,1024]{2,1,0:T(2,128)(2,1)S(1)} async-done(((bf16[8,2,1024]{2,1,0:T(2,128)(2,1)}), bf16[8,2,1024]{2,1,0:T(2,128)(2,1)S(1)}, u32[]{:S(2)}, u32[]{:S(2)}) %all-to-all-start.7) | async-done | bytes 32800 | tf_op jit(solution)/shard_map/all_to_all | solution.py:378
  135.7 3.3 %all-to-all-start.8 = ((bf16[8,2,1024]{2,1,0:T(2,128)(2,1)}), bf16[8,2,1024]{2,1,0:T(2,128)(2,1)S(1)}, u32[]{:S(2)}, u32[]{:S(2)}) async-start(bf16[8,2,1024]{2,1,0:T(2,128)(2,1)} %get-tuple-element.137), calls=%async_computation.8 | async-start | bytes 65536 | tf_op jit(solution)/shard_map/all_to_all | solution.py:378
  142.6 3.2 %all-to-all-done.8.tiles = bf16[8,2,1024]{2,1,0:T(2,128)(2,1)S(1)} async-done(((bf16[8,2,1024]{2,1,0:T(2,128)(2,1)}), bf16[8,2,1024]{2,1,0:T(2,128)(2,1)S(1)}, u32[]{:S(2)}, u32[]{:S(2)}) %all-to-all-start.8) | async-done | bytes 32800 | tf_op jit(solution)/shard_map/all_to_all | solution.py:378
  147.4 5.4 %collective-permute-start.5 = (bf16[14,64,256]{2,1,0:T(8,128)(2,1)S(1)}, bf16[14,64,256]{2,1,0:T(8,128)(2,1)S(1)}, u32[]{:S(2)}, u32[]{:S(2)}) collective-permute-start(bf16[14,64,256]{2,1,0:T(8,128)(2,1)S(1)} %copy-done.1), channel_id=1, source_target_pairs={{0,1},{1,0},{2,3},{3,2},{4,5},{5,4},{6,7},{7,6},{8,9},{9,8},{10,11... | collective-permute-start | bytes 1376264 | tf_op jit(solution)/shard_map/ppermute | solution.py:33
  152.7 3.4 %all-to-all-start.9 = ((bf16[8,4,1024]{2,1,0:T(4,128)(2,1)}), bf16[8,4,1024]{2,1,0:T(4,128)(2,1)S(1)}, u32[]{:S(2)}, u32[]{:S(2)}) async-start(bf16[8,4,1024]{2,1,0:T(4,128)(2,1)} %get-tuple-element.147), calls=%async_computation.9 | async-start | bytes 131072 | tf_op jit(solution)/shard_map/all_to_all | solution.py:378
  156.1 7.3 %all-to-all-done.9.tiles = bf16[8,4,1024]{2,1,0:T(4,128)(2,1)S(1)} async-done(((bf16[8,4,1024]{2,1,0:T(4,128)(2,1)}), bf16[8,4,1024]{2,1,0:T(4,128)(2,1)S(1)}, u32[]{:S(2)}, u32[]{:S(2)}) %all-to-all-start.9) | async-done | bytes 65568 | tf_op jit(solution)/shard_map/all_to_all | solution.py:378
  164.1 3.8 %all-to-all-start.10 = ((bf16[32,8,256]{2,1,0:T(8,128)(2,1)}), bf16[32,8,256]{2,1,0:T(8,128)(2,1)S(1)}, u32[]{:S(2)}, u32[]{:S(2)}) async-start(bf16[32,8,256]{2,1,0:T(8,128)(2,1)} %shard_map.117), calls=%async_computation.10 | async-start | bytes 262144 | tf_op jit(solution)/shard_map/all_to_all | solution.py:378
  168.5 8.8 %all-to-all-done.10.tiles = bf16[32,8,256]{2,1,0:T(8,128)(2,1)S(1)} async-done(((bf16[32,8,256]{2,1,0:T(8,128)(2,1)}), bf16[32,8,256]{2,1,0:T(8,128)(2,1)S(1)}, u32[]{:S(2)}, u32[]{:S(2)}) %all-to-all-start.10) | async-done | bytes 131104 | tf_op jit(solution)/shard_map/all_to_all | solution.py:378
  178.4 6.7 %all_to_all.76.tiles = bf16[4,32,128]{2,1,0:T(8,128)(2,1)S(1)} all-to-all(bf16[4,32,128]{2,1,0:T(8,128)(2,1)S(1)} %get-tuple-element.156), channel_id=1, replica_groups=mesh['gz'=8,'row'=4,'z'=8,'core'=2] {'row'}, dimensions={0} | all-to-all | bytes 65536 | tf_op jit(solution)/shard_map/all_to_all | solution.py:378
  185.9 3.4 %all-to-all-start.12 = ((bf16[8,32,256]{2,1,0:T(8,128)(2,1)}), bf16[8,32,256]{2,1,0:T(8,128)(2,1)S(1)}, u32[]{:S(2)}, u32[]{:S(2)}) async-start(bf16[8,32,256]{2,1,0:T(8,128)(2,1)} %get-tuple-element.157), calls=%async_computation.12 | async-start | bytes 262144 | tf_op jit(solution)/shard_map/all_to_all | solution.py:378
  189.2 7.8 %all-to-all-done.12.tiles = bf16[8,32,256]{2,1,0:T(8,128)(2,1)S(1)} async-done(((bf16[8,32,256]{2,1,0:T(8,128)(2,1)}), bf16[8,32,256]{2,1,0:T(8,128)(2,1)S(1)}, u32[]{:S(2)}, u32[]{:S(2)}) %all-to-all-start.12) | async-done | bytes 131104 | tf_op jit(solution)/shard_map/all_to_all | solution.py:378
  198.5 3.3 %all-to-all-start.13 = ((bf16[4,2,32,128]{3,2,1,0:T(8,128)(2,1)}), bf16[4,2,32,128]{3,2,1,0:T(8,128)(2,1)S(1)}, u32[]{:S(2)}, u32[]{:S(2)}) async-start(bf16[4,2,32,128]{3,2,1,0:T(8,128)(2,1)} %shard_map.121), calls=%async_computation.13 | async-start | bytes 131072 | tf_op jit(solution)/shard_map/all_to_all | solution.py:378
  201.9 6.7 %collective-permute-start.6 = (bf16[7,16,32]{1,0,2:T(8,128)(2,1)S(1)}, bf16[7,16,32]{1,0,2:T(8,128)(2,1)S(1)}, u32[]{:S(2)}, u32[]{:S(2)}) collective-permute-start(bf16[7,16,32]{1,0,2:T(8,128)(2,1)S(1)} %dynamic-slice_bitcast_fusion.1), channel_id=1, source_target_pairs={{0,1},{1,0},{2,3},{3,2},{4,5},{5,4},{6,7},{7,6},{8,9},{9,8},{10,11... | collective-permute-start | bytes 21512 | tf_op jit(solution)/shard_map/ppermute | solution.py:33
  209.5 6.8 %all-to-all-start.14 = ((bf16[16,16,128]{2,1,0:T(8,128)(2,1)}), bf16[16,16,128]{2,1,0:T(8,128)(2,1)S(1)}, u32[]{:S(2)}, u32[]{:S(2)}) async-start(bf16[16,16,128]{2,1,0:T(8,128)(2,1)} %shard_map.122), calls=%async_computation.14 | async-start | bytes 131072 | tf_op jit(solution)/shard_map/all_to_all | solution.py:378
  217.4 6.8 %all-to-all-done.14 = bf16[16,16,128]{2,1,0:T(8,128)(2,1)S(1)} async-done(((bf16[16,16,128]{2,1,0:T(8,128)(2,1)}), bf16[16,16,128]{2,1,0:T(8,128)(2,1)S(1)}, u32[]{:S(2)}, u32[]{:S(2)}) %all-to-all-start.14) | async-done | bytes 65568 | tf_op jit(solution)/shard_map/all_to_all | solution.py:378
  (65 shorter events, 41.8 us)
Async XLA Ops:
  7.2 32.2 %copy-start = (bf16[14,64,256]{2,1,0:T(8,128)(2,1)S(1)}, bf16[14,64,256]{2,1,0:T(8,128)(2,1)}, u32[]{:S(2)}) copy-start(bf16[14,64,256]{2,1,0:T(8,128)(2,1)} %own.9) | copy-start | bytes 1376260
  7.2 20.0 %copy-start.2 = (bf16[7,64,64]{2,1,0:T(8,128)(2,1)S(1)}, bf16[7,64,64]{2,1,0:T(8,128)(2,1)}, u32[]{:S(2)}) copy-start(bf16[7,64,64]{2,1,0:T(8,128)(2,1)} %here.2) | copy-start | bytes 172036
  7.2 22.3 %copy-start.4 = (s32[11,2]{0,1:T(2,128)S(1)}, s32[11,2]{0,1:T(2,128)}, u32[]{:S(2)}) copy-start(s32[11,2]{0,1:T(2,128)} %param.15) | copy-start | bytes 268
  7.2 23.3 %copy-start.3 = (s32[8]{0:T(128)S(1)}, s32[8]{0:T(128)}, u32[]{:S(2)}) copy-start(s32[8]{0:T(128)} %subtree.3) | copy-start | bytes 100
  7.2 53.0 %all-gather.3.cloned.1.call-start = ((), (), s32[]{:S(2)}) async-start(), calls=%async_computation.15 | async-start | bytes 2785280 | tf_op jit(solution)/shard_map/all_gather | solution.py:375
  7.9 98.3 %all-gather.5.cloned.1.call-start = ((), (), s32[]{:S(2)}) async-start(), calls=%async_computation.16 | async-start | bytes 2785280 | tf_op jit(solution)/shard_map/all_gather | solution.py:375
  8.0 12.1 %collective-permute-start.1 = (bf16[14,64,256]{2,1,0:T(8,128)(2,1)}, bf16[14,64,256]{2,1,0:T(8,128)(2,1)S(1)}, u32[]{:S(2)}, u32[]{:S(2)}) collective-permute-start(bf16[14,64,256]{2,1,0:T(8,128)(2,1)} %own.9), channel_id=1, source_target_pairs={{0,1},{1,0},{2,3},{3,2},{4,5},{5,4},{6,7},{7,6},{8,9},{9,8},{10,11... | collective-permute-start | bytes 1376264 | tf_op jit(solution)/shard_map/ppermute | solution.py:33
  16.8 3.3 %collective-permute-start = (bf16[3,64,64]{2,1,0:T(8,128)(2,1)}, bf16[3,64,64]{2,1,0:T(8,128)(2,1)S(1)}, u32[]{:S(2)}, u32[]{:S(2)}) collective-permute-start(bf16[3,64,64]{2,1,0:T(8,128)(2,1)} %here.1), channel_id=1, source_target_pairs={{0,1},{1,0},{2,3},{3,2},{4,5},{5,4},{6,7},{7,6},{8,9},{9,8},{10,11... | collective-permute-start | bytes 73736 | tf_op jit(solution)/shard_map/ppermute | solution.py:33
  22.5 16.9 %all-to-all-start = ((bf16[8,2,32,256]{3,2,1,0:T(8,128)(2,1)}), bf16[8,2,32,256]{3,2,1,0:T(8,128)(2,1)S(1)}, u32[]{:S(2)}, u32[]{:S(2)}) async-start(bf16[8,2,32,256]{3,2,1,0:T(8,128)(2,1)} %get-tuple-element.82), calls=%async_computation | async-start | bytes 524288 | tf_op jit(solution)/shard_map/all_to_all | solution.py:378
  27.2 3.3 %collective-permute-start.2 = (bf16[7,64,64]{2,1,0:T(8,128)(2,1)S(1)}, bf16[7,64,64]{2,1,0:T(8,128)(2,1)S(1)}, u32[]{:S(2)}, u32[]{:S(2)}) collective-permute-start(bf16[7,64,64]{2,1,0:T(8,128)(2,1)S(1)} %copy-done.2), channel_id=1, source_target_pairs={{0,1},{1,0},{2,3},{3,2},{4,5},{5,4},{6,7},{7,6},{8,9},{9,8},{10,11... | collective-permute-start | bytes 172040 | tf_op jit(solution)/shard_map/ppermute | solution.py:33
  40.9 8.8 %all-to-all-start.1 = ((bf16[4,32,128]{2,1,0:T(8,128)(2,1)}), bf16[4,32,128]{2,1,0:T(8,128)(2,1)S(1)}, u32[]{:S(2)}, u32[]{:S(2)}) async-start(bf16[4,32,128]{2,1,0:T(8,128)(2,1)} %get-tuple-element.87), calls=%async_computation.1 | async-start | bytes 65536 | tf_op jit(solution)/shard_map/all_to_all | solution.py:378
  60.2 13.9 %collective-permute-start.3 = (bf16[17,64,1024]{2,1,0:T(8,128)(2,1)}, bf16[17,64,1024]{2,1,0:T(8,128)(2,1)}, u32[]{:S(2)}, u32[]{:S(2)}) collective-permute-start(bf16[17,64,1024]{2,1,0:T(8,128)(2,1)} %all-gather.3.cloned.1.call-done.own), channel_id=1, source_target_pairs={{0,1},{1,0},{2,3},{3,2},{4,5},{5,4},{6,7},{7,6},{8,9},{9,8},{10,11... | collective-permute-start | bytes 6684680 | tf_op jit(solution)/shard_map/ppermute | solution.py:33
  66.7 16.4 %all-to-all-start.3 = ((bf16[32,8,128]{2,1,0:T(8,128)(2,1)}), bf16[32,8,128]{2,1,0:T(8,128)(2,1)S(1)}, u32[]{:S(2)}, u32[]{:S(2)}) async-start(bf16[32,8,128]{2,1,0:T(8,128)(2,1)} %get-tuple-element.93), calls=%async_computation.3 | async-start | bytes 131072 | tf_op jit(solution)/shard_map/all_to_all | solution.py:378
  84.2 10.5 %all-to-all-start.4 = ((bf16[8,4,1024]{2,1,0:T(4,128)(2,1)}), bf16[8,4,1024]{2,1,0:T(4,128)(2,1)S(1)}, u32[]{:S(2)}, u32[]{:S(2)}) async-start(bf16[8,4,1024]{2,1,0:T(4,128)(2,1)} %get-tuple-element.102), calls=%async_computation.4 | async-start | bytes 131072 | tf_op jit(solution)/shard_map/all_to_all | solution.py:378
  96.0 10.2 %all-to-all-start.5 = ((bf16[8,2,1024]{2,1,0:T(2,128)(2,1)}), bf16[8,2,1024]{2,1,0:T(2,128)(2,1)S(1)}, u32[]{:S(2)}, u32[]{:S(2)}) async-start(bf16[8,2,1024]{2,1,0:T(2,128)(2,1)} %get-tuple-element.109), calls=%async_computation.5 | async-start | bytes 65536 | tf_op jit(solution)/shard_map/all_to_all | solution.py:378
  106.3 9.9 %collective-permute-start.4 = (bf16[17,64,1024]{2,1,0:T(8,128)(2,1)}, bf16[17,64,1024]{2,1,0:T(8,128)(2,1)}, u32[]{:S(2)}, u32[]{:S(2)}) collective-permute-start(bf16[17,64,1024]{2,1,0:T(8,128)(2,1)} %all-gather.5.cloned.1.call-done.own), channel_id=1, source_target_pairs={{0,1},{1,0},{2,3},{3,2},{4,5},{5,4},{6,7},{7,6},{8,9},{9,8},{10,11... | collective-permute-start | bytes 6684680 | tf_op jit(solution)/shard_map/ppermute | solution.py:33
  112.8 10.1 %all-to-all-start.6 = ((bf16[8,2,1024]{2,1,0:T(2,128)(2,1)}), bf16[8,2,1024]{2,1,0:T(2,128)(2,1)S(1)}, u32[]{:S(2)}, u32[]{:S(2)}) async-start(bf16[8,2,1024]{2,1,0:T(2,128)(2,1)} %get-tuple-element.120), calls=%async_computation.6 | async-start | bytes 65536 | tf_op jit(solution)/shard_map/all_to_all | solution.py:378
  124.3 10.1 %all-to-all-start.7 = ((bf16[8,2,1024]{2,1,0:T(2,128)(2,1)}), bf16[8,2,1024]{2,1,0:T(2,128)(2,1)S(1)}, u32[]{:S(2)}, u32[]{:S(2)}) async-start(bf16[8,2,1024]{2,1,0:T(2,128)(2,1)} %get-tuple-element.127), calls=%async_computation.7 | async-start | bytes 65536 | tf_op jit(solution)/shard_map/all_to_all | solution.py:378
  135.7 10.1 %all-to-all-start.8 = ((bf16[8,2,1024]{2,1,0:T(2,128)(2,1)}), bf16[8,2,1024]{2,1,0:T(2,128)(2,1)S(1)}, u32[]{:S(2)}, u32[]{:S(2)}) async-start(bf16[8,2,1024]{2,1,0:T(2,128)(2,1)} %get-tuple-element.137), calls=%async_computation.8 | async-start | bytes 65536 | tf_op jit(solution)/shard_map/all_to_all | solution.py:378
  140.8 6.6 %copy-start.1 = (bf16[14,64,256]{2,1,0:T(8,128)(2,1)S(1)}, bf16[14,64,256]{2,1,0:T(8,128)(2,1)}, u32[]{:S(2)}) copy-start(bf16[14,64,256]{2,1,0:T(8,128)(2,1)} %own.13) | copy-start | bytes 1376260
  147.4 30.0 %collective-permute-start.5 = (bf16[14,64,256]{2,1,0:T(8,128)(2,1)S(1)}, bf16[14,64,256]{2,1,0:T(8,128)(2,1)S(1)}, u32[]{:S(2)}, u32[]{:S(2)}) collective-permute-start(bf16[14,64,256]{2,1,0:T(8,128)(2,1)S(1)} %copy-done.1), channel_id=1, source_target_pairs={{0,1},{1,0},{2,3},{3,2},{4,5},{5,4},{6,7},{7,6},{8,9},{9,8},{10,11... | collective-permute-start | bytes 1376264 | tf_op jit(solution)/shard_map/ppermute | solution.py:33
  152.7 10.6 %all-to-all-start.9 = ((bf16[8,4,1024]{2,1,0:T(4,128)(2,1)}), bf16[8,4,1024]{2,1,0:T(4,128)(2,1)S(1)}, u32[]{:S(2)}, u32[]{:S(2)}) async-start(bf16[8,4,1024]{2,1,0:T(4,128)(2,1)} %get-tuple-element.147), calls=%async_computation.9 | async-start | bytes 131072 | tf_op jit(solution)/shard_map/all_to_all | solution.py:378
  164.1 13.3 %all-to-all-start.10 = ((bf16[32,8,256]{2,1,0:T(8,128)(2,1)}), bf16[32,8,256]{2,1,0:T(8,128)(2,1)S(1)}, u32[]{:S(2)}, u32[]{:S(2)}) async-start(bf16[32,8,256]{2,1,0:T(8,128)(2,1)} %shard_map.117), calls=%async_computation.10 | async-start | bytes 262144 | tf_op jit(solution)/shard_map/all_to_all | solution.py:378
  185.9 11.2 %all-to-all-start.12 = ((bf16[8,32,256]{2,1,0:T(8,128)(2,1)}), bf16[8,32,256]{2,1,0:T(8,128)(2,1)S(1)}, u32[]{:S(2)}, u32[]{:S(2)}) async-start(bf16[8,32,256]{2,1,0:T(8,128)(2,1)} %get-tuple-element.157), calls=%async_computation.12 | async-start | bytes 262144 | tf_op jit(solution)/shard_map/all_to_all | solution.py:378
  198.5 10.2 %all-to-all-start.13 = ((bf16[4,2,32,128]{3,2,1,0:T(8,128)(2,1)}), bf16[4,2,32,128]{3,2,1,0:T(8,128)(2,1)S(1)}, u32[]{:S(2)}, u32[]{:S(2)}) async-start(bf16[4,2,32,128]{3,2,1,0:T(8,128)(2,1)} %shard_map.121), calls=%async_computation.13 | async-start | bytes 131072 | tf_op jit(solution)/shard_map/all_to_all | solution.py:378
  201.9 14.5 %collective-permute-start.6 = (bf16[7,16,32]{1,0,2:T(8,128)(2,1)S(1)}, bf16[7,16,32]{1,0,2:T(8,128)(2,1)S(1)}, u32[]{:S(2)}, u32[]{:S(2)}) collective-permute-start(bf16[7,16,32]{1,0,2:T(8,128)(2,1)S(1)} %dynamic-slice_bitcast_fusion.1), channel_id=1, source_target_pairs={{0,1},{1,0},{2,3},{3,2},{4,5},{5,4},{6,7},{7,6},{8,9},{9,8},{10,11... | collective-permute-start | bytes 21512 | tf_op jit(solution)/shard_map/ppermute | solution.py:33
  209.5 14.7 %all-to-all-start.14 = ((bf16[16,16,128]{2,1,0:T(8,128)(2,1)}), bf16[16,16,128]{2,1,0:T(8,128)(2,1)S(1)}, u32[]{:S(2)}, u32[]{:S(2)}) async-start(bf16[16,16,128]{2,1,0:T(8,128)(2,1)} %shard_map.122), calls=%async_computation.14 | async-start | bytes 131072 | tf_op jit(solution)/shard_map/all_to_all | solution.py:378
Sparse Core Ops, SparseCore 0:
  10.1 44.4 all-gather.2
  56.7 42.3 all-gather.4

commit v6 on v5

--- a/solution.py
+++ b/solution.py
@@ -154,29 +154,31 @@
     out[...] = scratch[...].astype(BF16)
 
 
-def fetch(blocks, near, near_x, sems, own, other):
+def fetch(blocks, core, gathered, near, near_x, sems):
+    wide = gathered.shape[3]
     copies = []
     at = 0
     while at < len(blocks):
         count = 1
         while at + count < len(blocks) and blocks[at + count] == blocks[at] + count:
             count += 1
-        for j, (source, target) in enumerate(((own, near), (other, near_x))):
-            copies.append(
-                pltpu.make_async_copy(
-                    source.at[pl.ds(blocks[at], count)],
-                    target.at[pl.ds(at, count)],
-                    sems.at[at, j],
+        for r in range(gathered.shape[0] // CORES):
+            for which, target in ((core, near), (1 - core, near_x)):
+                copies.append(
+                    pltpu.make_async_copy(
+                        gathered.at[r * CORES + which, pl.ds(blocks[at], count)],
+                        target.at[pl.ds(at, count), :, pl.ds(r * wide, wide)],
+                        sems.at[len(copies)],
+                    )
                 )
-            )
         at += count
     for copy in copies:
         copy.start()
     return copies
 
 
-def load_blocks(blocks, own, other, near, near_x, sems):
-    for copy in fetch(blocks, near, near_x, sems, own, other):
+def load_blocks(blocks, where, gathered, near, near_x, sems):
+    for copy in fetch(blocks, where[0], gathered, near, near_x, sems):
         copy.wait()
 
 
@@ -251,8 +253,8 @@
     solve_level(depth - 1, acc.astype(BF16), 2**depth, near, near_x, out, scratch)
 
 
-def other_pairs(blocks, depth, down, values, acc_in, own, other, acc_out, near, near_x, sems):
-    copies = fetch(blocks, near, near_x, sems, own, other)
+def other_pairs(blocks, depth, down, where, values, acc_in, gathered, acc_out, near, near_x, sems):
+    copies = fetch(blocks, where[0], gathered, near, near_x, sems)
     acc = acc_in[...]
     for copy in copies:
         copy.wait()
@@ -372,7 +374,7 @@
     where = jnp.stack([core, z, held, base, g, core * cols + g * nrow + r]).astype(jnp.int32)
 
     def gathered(blocks):
-        return lax.all_gather(blocks, "row", axis=2, tiled=True)
+        return lax.all_gather(blocks, ("row", "core"), axis=0, tiled=False)
 
     def exchange(array, axes):
         return lax.all_to_all(array, axes, 0, 0, tiled=True)
@@ -385,8 +387,8 @@
 
     low = (sub_lower, swapped(sub_lower))
     rhs_there = swapped(sub_rhs)
-    anc_low_row = gathered(anc_lower)
-    anc_up_row = gathered(anc_upper)
+    anc_low = gathered(anc_lower)
+    anc_up = gathered(anc_upper)
 
     def diagonal(depth):
         return list(range(*level_span(depth)))
@@ -394,17 +396,17 @@
     def pair_blocks(depth, u):
         return [pairs.anc[a, u] for a in range(*level_span(depth))]
 
-    def loaded(blocks, two):
+    def loaded(blocks, stack):
         near = shape(BF16, len(blocks), own, size)
-        sems = pltpu.SemaphoreType.DMA((len(blocks), CORES))
-        return run(part(load_blocks, blocks), (near, near), (), (), (sems,), two)
-
-    def others(depth, down, values, acc, two):
+        sems = pltpu.SemaphoreType.DMA((len(blocks) * nrow * CORES,))
+        return run(part(load_blocks, blocks), (near, near), (where,), (), (sems,), (stack,))
+
+    def others(depth, down, values, acc, stack):
         blocks = [index for u in range(depth - 1) for index in pair_blocks(depth, u)]
         near = pltpu.VMEM((len(blocks), own, size), BF16)
-        sems = pltpu.SemaphoreType.DMA((len(blocks), CORES))
+        sems = pltpu.SemaphoreType.DMA((len(blocks) * nrow * CORES,))
         body = part(other_pairs, blocks, depth, down)
-        return run(body, acc_shape, (), (values, acc), (near, near, sems), two)
+        return run(body, acc_shape, (where,), (values, acc), (near, near, sems), (stack,))
 
     def level_shape(depth):
         return shape(BF16, nz, max(2, 2**depth), size)
@@ -450,8 +452,6 @@
     tiles, so_far = tied(tiles, so_far)
     tiles = run(sub_root_solve, shape(BF16, nz, cols, wide), (), (tiles, rhs, *low))
     tiles = exchange(tiles, "z")
-    tiles, anc_low_row = tied(tiles, anc_low_row)
-    anc_low = two_cores(anc_low_row)
     c_scratch = pltpu.VMEM((layers * nrow, ROWS8, pair_rows), F32)
     y_root, tiles = run(
         part(sub_root_anc, pairs, levels),
@@ -477,9 +477,6 @@
         blocks = pair_blocks(depth, depth - 1) + diagonal(depth - 1)
         near = loaded(blocks, anc_low)
         tiles, *near = tied(tiles, *near)
-        if depth == 1:
-            tiles, anc_up_row = tied(tiles, anc_up_row)
-            anc_up = two_cores(anc_up_row)
         y8, acc, tiles = run(
             part(anc_forward, depth),
             (row_shape, acc_shape, level_shape(depth - 1)),

time: 233 us -> 233 us (level)
  waiting for transfers between devices: 76.6 us -> 68.9 us
  Pallas kernels: 32.5 us -> 38.3 us
  local copies, waits for them, and re-layouts: 1.35 us -> 4.65 us
    all_to_all x13, waiting for transfers between devices: 73.7 us -> 65.8 us  [exchange(): return lax.all_to_all(array, axes, 0, 0, tiled=True)]
    pallas_call x28, Pallas kernels: 32.5 us -> 38.3 us  [run(): pl.pallas_call(body, out_shape=outs, in_specs=in_specs, out_specs=spec if...]
    ppermute x7 -> x5, starting transfers between devices: 35.5 us -> 31.5 us  [swapped(): return lax.ppermute(array, 'core', [(0, 1), (1, 0)])]
    unnamed x11 -> x13, local copies, waits for them, and re-layouts: 0.12 us -> 3.42 us
  transfers between devices with their start and end apart: 22 -> 20, of which waited for: 14 -> 14; matrix products, arithmetic and copies ran while one was open for 1% -> 1% of each run, Pallas kernels for 11% -> 13%
where the time goes in v6:
time: 233 us; the launch traced here: 231 us
  starting transfers between devices  86.9 us (37%)
  waiting for transfers between devices  68.9 us (30%)
  Pallas kernels  38.3 us (16%)
  blocking collectives  17.1 us (7%)
  between operations  14.4 us (6%)
  local copies, waits for them, and re-layouts  4.65 us (2%)
    all_to_all x13, waiting for transfers between devices, exchange(): return lax.all_to_all(array, axes, 0, 0, tiled=True)  65.8 us
    all_to_all x13, starting transfers between devices, exchange(): return lax.all_to_all(array, axes, 0, 0, tiled=True)  55.3 us
    pallas_call x28, Pallas kernels, run(): pl.pallas_call(body, out_shape=outs, in_specs=in_specs, out_specs=spec if...  38.3 us
    ppermute x5, starting transfers between devices, swapped(): return lax.ppermute(array, 'core', [(0, 1), (1, 0)])  31.5 us
    all_to_all x2, blocking collectives, exchange(): return lax.all_to_all(array, axes, 0, 0, tiled=True)  17.1 us
  transfers between devices with their start and end apart: 20, of which 14 were waited for; matrix products, arithmetic and copies ran while one was open for 1% of the time, Pallas kernels for 13%

profile of v6, /device:TPU:1, one launch (start us, length us, event | category | flops | bytes accessed | tf_op | source)
XLA Modules:
  0.0 231.1 jit_solution(10454127304189801171)
XLA Ops:
  8.7 8.7 %collective-permute-start.1 = (bf16[14,64,256]{2,1,0:T(8,128)(2,1)}, bf16[14,64,256]{2,1,0:T(8,128)(2,1)S(1)}, u32[]{:S(2)}, u32[]{:S(2)}) collective-permute-start(bf16[14,64,256]{2,1,0:T(8,128)(2,1)} %own.9), channel_id=1, source_target_pairs={{0,1},{1,0},{2,3},{3,2},{4,5},{5,4},{6,7},{7,6},{8,9},{9,8},{10,11... | collective-permute-start | bytes 1376264 | tf_op jit(solution)/shard_map/ppermute | solution.py:33
  23.1 4.7 %all-to-all-start = ((bf16[8,2,32,256]{3,2,1,0:T(8,128)(2,1)}), bf16[8,2,32,256]{3,2,1,0:T(8,128)(2,1)S(1)}, u32[]{:S(2)}, u32[]{:S(2)}) async-start(bf16[8,2,32,256]{3,2,1,0:T(8,128)(2,1)} %get-tuple-element.78), calls=%async_computation | async-start | bytes 524288 | tf_op jit(solution)/shard_map/all_to_all | solution.py:380
  33.7 6.4 %all-to-all-done.tiles = bf16[8,2,32,256]{3,2,1,0:T(8,128)(2,1)S(1)} async-done(((bf16[8,2,32,256]{3,2,1,0:T(8,128)(2,1)}), bf16[8,2,32,256]{3,2,1,0:T(8,128)(2,1)S(1)}, u32[]{:S(2)}, u32[]{:S(2)}) %all-to-all-start) | async-done | bytes 262176 | tf_op jit(solution)/shard_map/all_to_all | solution.py:380
  42.5 4.0 %all-to-all-start.1 = ((bf16[4,32,128]{2,1,0:T(8,128)(2,1)}), bf16[4,32,128]{2,1,0:T(8,128)(2,1)S(1)}, u32[]{:S(2)}, u32[]{:S(2)}) async-start(bf16[4,32,128]{2,1,0:T(8,128)(2,1)} %get-tuple-element.83), calls=%async_computation.1 | async-start | bytes 65536 | tf_op jit(solution)/shard_map/all_to_all | solution.py:380
  47.4 3.9 %all-to-all-done.1.tiles = bf16[4,32,128]{2,1,0:T(8,128)(2,1)S(1)} async-done(((bf16[4,32,128]{2,1,0:T(8,128)(2,1)}), bf16[4,32,128]{2,1,0:T(8,128)(2,1)S(1)}, u32[]{:S(2)}, u32[]{:S(2)}) %all-to-all-start.1) | async-done | bytes 32800 | tf_op jit(solution)/shard_map/all_to_all | solution.py:380
  51.5 10.4 %all_to_all.75.tiles = bf16[8,32,256]{2,1,0:T(8,128)(2,1)S(1)} all-to-all(bf16[8,32,256]{2,1,0:T(8,128)(2,1)S(1)} %shard_map.99), channel_id=1, replica_groups=mesh['gz'=8,'row'=4,'z'=8,'core'=2] {'z'}, dimensions={0} | all-to-all | bytes 262144 | tf_op jit(solution)/shard_map/all_to_all | solution.py:380
  63.4 7.8 %all-to-all-start.3 = ((bf16[32,8,128]{2,1,0:T(8,128)(2,1)}), bf16[32,8,128]{2,1,0:T(8,128)(2,1)S(1)}, u32[]{:S(2)}, u32[]{:S(2)}) async-start(bf16[32,8,128]{2,1,0:T(8,128)(2,1)} %get-tuple-element.88), calls=%async_computation.3 | async-start | bytes 131072 | tf_op jit(solution)/shard_map/all_to_all | solution.py:380
  73.4 6.6 %all-to-all-done.3.tiles = bf16[32,8,128]{2,1,0:T(8,128)(2,1)S(1)} async-done(((bf16[32,8,128]{2,1,0:T(8,128)(2,1)}), bf16[32,8,128]{2,1,0:T(8,128)(2,1)S(1)}, u32[]{:S(2)}, u32[]{:S(2)}) %all-to-all-start.3) | async-done | bytes 65568 | tf_op jit(solution)/shard_map/all_to_all | solution.py:380
  81.2 3.3 %all-to-all-start.4 = ((bf16[8,4,1024]{2,1,0:T(4,128)(2,1)}), bf16[8,4,1024]{2,1,0:T(4,128)(2,1)S(1)}, u32[]{:S(2)}, u32[]{:S(2)}) async-start(bf16[8,4,1024]{2,1,0:T(4,128)(2,1)} %get-tuple-element.96), calls=%async_computation.4 | async-start | bytes 131072 | tf_op jit(solution)/shard_map/all_to_all | solution.py:380
  84.5 2.4 %shard_map.103 = (bf16[6,64,1024]{2,1,0:T(8,128)(2,1)S(1)}, bf16[6,64,1024]{2,1,0:T(8,128)(2,1)S(1)}) custom-call(s32[6]{0:T(128)S(1)} %stack.31.where, bf16[8,17,64,256]{3,2,1,0:T(8,128)(2,1)} %bitcast.25), custom_call_target="tpu_custom_call" | custom-call | tf_op jit(solution)/shard_map/pallas_call | solution.py:47
  87.0 4.7 %all-to-all-done.4.tiles = bf16[8,4,1024]{2,1,0:T(4,128)(2,1)S(1)} async-done(((bf16[8,4,1024]{2,1,0:T(4,128)(2,1)}), bf16[8,4,1024]{2,1,0:T(4,128)(2,1)S(1)}, u32[]{:S(2)}, u32[]{:S(2)}) %all-to-all-start.4) | async-done | bytes 65568 | tf_op jit(solution)/shard_map/all_to_all | solution.py:380
  93.0 3.3 %all-to-all-start.5 = ((bf16[8,2,1024]{2,1,0:T(2,128)(2,1)}), bf16[8,2,1024]{2,1,0:T(2,128)(2,1)S(1)}, u32[]{:S(2)}, u32[]{:S(2)}) async-start(bf16[8,2,1024]{2,1,0:T(2,128)(2,1)} %get-tuple-element.103), calls=%async_computation.5 | async-start | bytes 65536 | tf_op jit(solution)/shard_map/all_to_all | solution.py:380
  98.2 2.4 %shard_map.105.acc_in = f32[8,128]{1,0:T(8,128)S(1)} custom-call(s32[6]{0:T(128)S(1)} %stack.31.where, f32[8,1024]{1,0:T(8,128)S(1)} %get-tuple-element.104.values.refs_0_, f32[8,128]{1,0:T(8,128)S(1)} %get-tuple-element.105.acc_in, bf16[8,17,64,256]{3,2,1,0:T(8,128)(2,1)} %bitcast.27), custom_call_target="tpu_custom_call" | custom-call | tf_op jit(solution)/shard_map/pallas_call | solution.py:47
  100.6 2.6 %all-to-all-done.5.tiles = bf16[8,2,1024]{2,1,0:T(2,128)(2,1)S(1)} async-done(((bf16[8,2,1024]{2,1,0:T(2,128)(2,1)}), bf16[8,2,1024]{2,1,0:T(2,128)(2,1)S(1)}, u32[]{:S(2)}, u32[]{:S(2)}) %all-to-all-start.5) | async-done | bytes 32800 | tf_op jit(solution)/shard_map/all_to_all | solution.py:380
  104.2 4.0 %all-to-all-start.6 = ((bf16[8,2,1024]{2,1,0:T(2,128)(2,1)}), bf16[8,2,1024]{2,1,0:T(2,128)(2,1)S(1)}, u32[]{:S(2)}, u32[]{:S(2)}) async-start(bf16[8,2,1024]{2,1,0:T(2,128)(2,1)} %get-tuple-element.113), calls=%async_computation.6 | async-start | bytes 65536 | tf_op jit(solution)/shard_map/all_to_all | solution.py:380
  109.7 5.4 %all-to-all-done.6.tiles = bf16[8,2,1024]{2,1,0:T(2,128)(2,1)S(1)} async-done(((bf16[8,2,1024]{2,1,0:T(2,128)(2,1)}), bf16[8,2,1024]{2,1,0:T(2,128)(2,1)S(1)}, u32[]{:S(2)}, u32[]{:S(2)}) %all-to-all-start.6) | async-done | bytes 32800 | tf_op jit(solution)/shard_map/all_to_all | solution.py:380
  116.5 3.3 %all-to-all-start.7 = ((bf16[8,2,1024]{2,1,0:T(2,128)(2,1)}), bf16[8,2,1024]{2,1,0:T(2,128)(2,1)S(1)}, u32[]{:S(2)}, u32[]{:S(2)}) async-start(bf16[8,2,1024]{2,1,0:T(2,128)(2,1)} %get-tuple-element.119), calls=%async_computation.7 | async-start | bytes 65536 | tf_op jit(solution)/shard_map/all_to_all | solution.py:380
  122.5 4.1 %all-to-all-done.7.tiles = bf16[8,2,1024]{2,1,0:T(2,128)(2,1)S(1)} async-done(((bf16[8,2,1024]{2,1,0:T(2,128)(2,1)}), bf16[8,2,1024]{2,1,0:T(2,128)(2,1)S(1)}, u32[]{:S(2)}, u32[]{:S(2)}) %all-to-all-start.7) | async-done | bytes 32800 | tf_op jit(solution)/shard_map/all_to_all | solution.py:380
  127.8 3.3 %all-to-all-start.8 = ((bf16[8,2,1024]{2,1,0:T(2,128)(2,1)}), bf16[8,2,1024]{2,1,0:T(2,128)(2,1)S(1)}, u32[]{:S(2)}, u32[]{:S(2)}) async-start(bf16[8,2,1024]{2,1,0:T(2,128)(2,1)} %get-tuple-element.129), calls=%async_computation.8 | async-start | bytes 65536 | tf_op jit(solution)/shard_map/all_to_all | solution.py:380
  131.2 2.7 %shard_map.113 = (bf16[8,64,1024]{2,1,0:T(8,128)(2,1)S(1)}, bf16[8,64,1024]{2,1,0:T(8,128)(2,1)S(1)}) custom-call(s32[6]{0:T(128)S(1)} %stack.31.where, bf16[8,17,64,256]{3,2,1,0:T(8,128)(2,1)} %bitcast.22), custom_call_target="tpu_custom_call" | custom-call | tf_op jit(solution)/shard_map/pallas_call | solution.py:47
  139.5 11.6 %collective-permute-start.3 = (bf16[14,64,256]{2,1,0:T(8,128)(2,1)S(1)}, bf16[14,64,256]{2,1,0:T(8,128)(2,1)S(1)}, u32[]{:S(2)}, u32[]{:S(2)}) collective-permute-start(bf16[14,64,256]{2,1,0:T(8,128)(2,1)S(1)} %copy-done.2), channel_id=1, source_target_pairs={{0,1},{1,0},{2,3},{3,2},{4,5},{5,4},{6,7},{7,6},{8,9},{9,8},{10,11... | collective-permute-start | bytes 1376264 | tf_op jit(solution)/shard_map/ppermute | solution.py:33
  151.1 4.1 %all-to-all-start.9 = ((bf16[8,4,1024]{2,1,0:T(4,128)(2,1)}), bf16[8,4,1024]{2,1,0:T(4,128)(2,1)S(1)}, u32[]{:S(2)}, u32[]{:S(2)}) async-start(bf16[8,4,1024]{2,1,0:T(4,128)(2,1)} %get-tuple-element.139), calls=%async_computation.9 | async-start | bytes 131072 | tf_op jit(solution)/shard_map/all_to_all | solution.py:380
  155.2 7.1 %all-to-all-done.9.tiles = bf16[8,4,1024]{2,1,0:T(4,128)(2,1)S(1)} async-done(((bf16[8,4,1024]{2,1,0:T(4,128)(2,1)}), bf16[8,4,1024]{2,1,0:T(4,128)(2,1)S(1)}, u32[]{:S(2)}, u32[]{:S(2)}) %all-to-all-start.9) | async-done | bytes 65568 | tf_op jit(solution)/shard_map/all_to_all | solution.py:380
  163.0 3.8 %all-to-all-start.10 = ((bf16[32,8,256]{2,1,0:T(8,128)(2,1)}), bf16[32,8,256]{2,1,0:T(8,128)(2,1)S(1)}, u32[]{:S(2)}, u32[]{:S(2)}) async-start(bf16[32,8,256]{2,1,0:T(8,128)(2,1)} %shard_map.117), calls=%async_computation.10 | async-start | bytes 262144 | tf_op jit(solution)/shard_map/all_to_all | solution.py:380
  167.5 8.8 %all-to-all-done.10.tiles = bf16[32,8,256]{2,1,0:T(8,128)(2,1)S(1)} async-done(((bf16[32,8,256]{2,1,0:T(8,128)(2,1)}), bf16[32,8,256]{2,1,0:T(8,128)(2,1)S(1)}, u32[]{:S(2)}, u32[]{:S(2)}) %all-to-all-start.10) | async-done | bytes 131104 | tf_op jit(solution)/shard_map/all_to_all | solution.py:380
  177.3 6.7 %all_to_all.76.tiles = bf16[4,32,128]{2,1,0:T(8,128)(2,1)S(1)} all-to-all(bf16[4,32,128]{2,1,0:T(8,128)(2,1)S(1)} %get-tuple-element.148), channel_id=1, replica_groups=mesh['gz'=8,'row'=4,'z'=8,'core'=2] {'row'}, dimensions={0} | all-to-all | bytes 65536 | tf_op jit(solution)/shard_map/all_to_all | solution.py:380
  184.8 3.4 %all-to-all-start.12 = ((bf16[8,32,256]{2,1,0:T(8,128)(2,1)}), bf16[8,32,256]{2,1,0:T(8,128)(2,1)S(1)}, u32[]{:S(2)}, u32[]{:S(2)}) async-start(bf16[8,32,256]{2,1,0:T(8,128)(2,1)} %get-tuple-element.149), calls=%async_computation.12 | async-start | bytes 262144 | tf_op jit(solution)/shard_map/all_to_all | solution.py:380
  188.2 7.8 %all-to-all-done.12.tiles = bf16[8,32,256]{2,1,0:T(8,128)(2,1)S(1)} async-done(((bf16[8,32,256]{2,1,0:T(8,128)(2,1)}), bf16[8,32,256]{2,1,0:T(8,128)(2,1)S(1)}, u32[]{:S(2)}, u32[]{:S(2)}) %all-to-all-start.12) | async-done | bytes 131104 | tf_op jit(solution)/shard_map/all_to_all | solution.py:380
  197.5 3.3 %all-to-all-start.13 = ((bf16[4,2,32,128]{3,2,1,0:T(8,128)(2,1)}), bf16[4,2,32,128]{3,2,1,0:T(8,128)(2,1)S(1)}, u32[]{:S(2)}, u32[]{:S(2)}) async-start(bf16[4,2,32,128]{3,2,1,0:T(8,128)(2,1)} %shard_map.121), calls=%async_computation.13 | async-start | bytes 131072 | tf_op jit(solution)/shard_map/all_to_all | solution.py:380
  200.9 7.0 %collective-permute-start.4 = (bf16[7,16,32]{1,0,2:T(8,128)(2,1)S(1)}, bf16[7,16,32]{1,0,2:T(8,128)(2,1)S(1)}, u32[]{:S(2)}, u32[]{:S(2)}) collective-permute-start(bf16[7,16,32]{1,0,2:T(8,128)(2,1)S(1)} %dynamic-slice_bitcast_fusion.1), channel_id=1, source_target_pairs={{0,1},{1,0},{2,3},{3,2},{4,5},{5,4},{6,7},{7,6},{8,9},{9,8},{10,11... | collective-permute-start | bytes 21512 | tf_op jit(solution)/shard_map/ppermute | solution.py:33
  208.7 6.8 %all-to-all-start.14 = ((bf16[16,16,128]{2,1,0:T(8,128)(2,1)}), bf16[16,16,128]{2,1,0:T(8,128)(2,1)S(1)}, u32[]{:S(2)}, u32[]{:S(2)}) async-start(bf16[16,16,128]{2,1,0:T(8,128)(2,1)} %shard_map.122), calls=%async_computation.14 | async-start | bytes 131072 | tf_op jit(solution)/shard_map/all_to_all | solution.py:380
  216.6 6.8 %all-to-all-done.14 = bf16[16,16,128]{2,1,0:T(8,128)(2,1)S(1)} async-done(((bf16[16,16,128]{2,1,0:T(8,128)(2,1)}), bf16[16,16,128]{2,1,0:T(8,128)(2,1)S(1)}, u32[]{:S(2)}, u32[]{:S(2)}) %all-to-all-start.14) | async-done | bytes 65568 | tf_op jit(solution)/shard_map/all_to_all | solution.py:380
  (63 shorter events, 45.3 us)
Async XLA Ops:
  7.2 39.4 %copy-start.1 = (bf16[14,64,256]{2,1,0:T(8,128)(2,1)S(1)}, bf16[14,64,256]{2,1,0:T(8,128)(2,1)}, u32[]{:S(2)}) copy-start(bf16[14,64,256]{2,1,0:T(8,128)(2,1)} %own.9) | copy-start | bytes 1376260
  7.2 64.1 %all-gather.5.cloned.1.call-start = ((), (), s32[]{:S(2)}) async-start(), calls=%async_computation.15 | async-start | bytes 5013504 | tf_op jit(solution)/shard_map/all_gather | solution.py:377
  7.9 100.3 %all-gather.7.cloned.1.call-start = ((), (), s32[]{:S(2)}) async-start(), calls=%async_computation.16 | async-start | bytes 5013504 | tf_op jit(solution)/shard_map/all_gather | solution.py:377
  8.7 12.1 %collective-permute-start.1 = (bf16[14,64,256]{2,1,0:T(8,128)(2,1)}, bf16[14,64,256]{2,1,0:T(8,128)(2,1)S(1)}, u32[]{:S(2)}, u32[]{:S(2)}) collective-permute-start(bf16[14,64,256]{2,1,0:T(8,128)(2,1)} %own.9), channel_id=1, source_target_pairs={{0,1},{1,0},{2,3},{3,2},{4,5},{5,4},{6,7},{7,6},{8,9},{9,8},{10,11... | collective-permute-start | bytes 1376264 | tf_op jit(solution)/shard_map/ppermute | solution.py:33
  17.4 3.3 %collective-permute-start = (bf16[3,64,64]{2,1,0:T(8,128)(2,1)}, bf16[3,64,64]{2,1,0:T(8,128)(2,1)S(1)}, u32[]{:S(2)}, u32[]{:S(2)}) collective-permute-start(bf16[3,64,64]{2,1,0:T(8,128)(2,1)} %here.1), channel_id=1, source_target_pairs={{0,1},{1,0},{2,3},{3,2},{4,5},{5,4},{6,7},{7,6},{8,9},{9,8},{10,11... | collective-permute-start | bytes 73736 | tf_op jit(solution)/shard_map/ppermute | solution.py:33
  23.1 16.9 %all-to-all-start = ((bf16[8,2,32,256]{3,2,1,0:T(8,128)(2,1)}), bf16[8,2,32,256]{3,2,1,0:T(8,128)(2,1)S(1)}, u32[]{:S(2)}, u32[]{:S(2)}) async-start(bf16[8,2,32,256]{3,2,1,0:T(8,128)(2,1)} %get-tuple-element.78), calls=%async_computation | async-start | bytes 524288 | tf_op jit(solution)/shard_map/all_to_all | solution.py:380
  27.8 3.5 %collective-permute-start.2 = (bf16[7,64,64]{2,1,0:T(8,128)(2,1)}, bf16[7,64,64]{2,1,0:T(8,128)(2,1)S(1)}, u32[]{:S(2)}, u32[]{:S(2)}) collective-permute-start(bf16[7,64,64]{2,1,0:T(8,128)(2,1)} %here.2), channel_id=1, source_target_pairs={{0,1},{1,0},{2,3},{3,2},{4,5},{5,4},{6,7},{7,6},{8,9},{9,8},{10,11... | collective-permute-start | bytes 172040 | tf_op jit(solution)/shard_map/ppermute | solution.py:33
  31.3 1.0 copy-start.3
  32.3 0.7 copy-start.4
  40.0 1.0 copy-start
  42.5 8.9 %all-to-all-start.1 = ((bf16[4,32,128]{2,1,0:T(8,128)(2,1)}), bf16[4,32,128]{2,1,0:T(8,128)(2,1)S(1)}, u32[]{:S(2)}, u32[]{:S(2)}) async-start(bf16[4,32,128]{2,1,0:T(8,128)(2,1)} %get-tuple-element.83), calls=%async_computation.1 | async-start | bytes 65536 | tf_op jit(solution)/shard_map/all_to_all | solution.py:380
  63.4 16.6 %all-to-all-start.3 = ((bf16[32,8,128]{2,1,0:T(8,128)(2,1)}), bf16[32,8,128]{2,1,0:T(8,128)(2,1)S(1)}, u32[]{:S(2)}, u32[]{:S(2)}) async-start(bf16[32,8,128]{2,1,0:T(8,128)(2,1)} %get-tuple-element.88), calls=%async_computation.3 | async-start | bytes 131072 | tf_op jit(solution)/shard_map/all_to_all | solution.py:380
  81.2 10.5 %all-to-all-start.4 = ((bf16[8,4,1024]{2,1,0:T(4,128)(2,1)}), bf16[8,4,1024]{2,1,0:T(4,128)(2,1)S(1)}, u32[]{:S(2)}, u32[]{:S(2)}) async-start(bf16[8,4,1024]{2,1,0:T(4,128)(2,1)} %get-tuple-element.96), calls=%async_computation.4 | async-start | bytes 131072 | tf_op jit(solution)/shard_map/all_to_all | solution.py:380
  93.0 10.1 %all-to-all-start.5 = ((bf16[8,2,1024]{2,1,0:T(2,128)(2,1)}), bf16[8,2,1024]{2,1,0:T(2,128)(2,1)S(1)}, u32[]{:S(2)}, u32[]{:S(2)}) async-start(bf16[8,2,1024]{2,1,0:T(2,128)(2,1)} %get-tuple-element.103), calls=%async_computation.5 | async-start | bytes 65536 | tf_op jit(solution)/shard_map/all_to_all | solution.py:380
  104.2 10.9 %all-to-all-start.6 = ((bf16[8,2,1024]{2,1,0:T(2,128)(2,1)}), bf16[8,2,1024]{2,1,0:T(2,128)(2,1)S(1)}, u32[]{:S(2)}, u32[]{:S(2)}) async-start(bf16[8,2,1024]{2,1,0:T(2,128)(2,1)} %get-tuple-element.113), calls=%async_computation.6 | async-start | bytes 65536 | tf_op jit(solution)/shard_map/all_to_all | solution.py:380
  116.5 10.1 %all-to-all-start.7 = ((bf16[8,2,1024]{2,1,0:T(2,128)(2,1)}), bf16[8,2,1024]{2,1,0:T(2,128)(2,1)S(1)}, u32[]{:S(2)}, u32[]{:S(2)}) async-start(bf16[8,2,1024]{2,1,0:T(2,128)(2,1)} %get-tuple-element.119), calls=%async_computation.7 | async-start | bytes 65536 | tf_op jit(solution)/shard_map/all_to_all | solution.py:380
  127.8 10.1 %all-to-all-start.8 = ((bf16[8,2,1024]{2,1,0:T(2,128)(2,1)}), bf16[8,2,1024]{2,1,0:T(2,128)(2,1)S(1)}, u32[]{:S(2)}, u32[]{:S(2)}) async-start(bf16[8,2,1024]{2,1,0:T(2,128)(2,1)} %get-tuple-element.129), calls=%async_computation.8 | async-start | bytes 65536 | tf_op jit(solution)/shard_map/all_to_all | solution.py:380
  131.2 8.3 %copy-start.2 = (bf16[14,64,256]{2,1,0:T(8,128)(2,1)S(1)}, bf16[14,64,256]{2,1,0:T(8,128)(2,1)}, u32[]{:S(2)}) copy-start(bf16[14,64,256]{2,1,0:T(8,128)(2,1)} %own.13) | copy-start | bytes 1376260
  133.9 42.3 %copy-start.5 = (s32[8]{0:T(128)S(1)}, s32[8]{0:T(128)}, u32[]{:S(2)}) copy-start(s32[8]{0:T(128)} %subtree.3) | copy-start | bytes 100
  139.5 36.7 %collective-permute-start.3 = (bf16[14,64,256]{2,1,0:T(8,128)(2,1)S(1)}, bf16[14,64,256]{2,1,0:T(8,128)(2,1)S(1)}, u32[]{:S(2)}, u32[]{:S(2)}) collective-permute-start(bf16[14,64,256]{2,1,0:T(8,128)(2,1)S(1)} %copy-done.2), channel_id=1, source_target_pairs={{0,1},{1,0},{2,3},{3,2},{4,5},{5,4},{6,7},{7,6},{8,9},{9,8},{10,11... | collective-permute-start | bytes 1376264 | tf_op jit(solution)/shard_map/ppermute | solution.py:33
  151.1 11.2 %all-to-all-start.9 = ((bf16[8,4,1024]{2,1,0:T(4,128)(2,1)}), bf16[8,4,1024]{2,1,0:T(4,128)(2,1)S(1)}, u32[]{:S(2)}, u32[]{:S(2)}) async-start(bf16[8,4,1024]{2,1,0:T(4,128)(2,1)} %get-tuple-element.139), calls=%async_computation.9 | async-start | bytes 131072 | tf_op jit(solution)/shard_map/all_to_all | solution.py:380
  163.0 13.3 %all-to-all-start.10 = ((bf16[32,8,256]{2,1,0:T(8,128)(2,1)}), bf16[32,8,256]{2,1,0:T(8,128)(2,1)S(1)}, u32[]{:S(2)}, u32[]{:S(2)}) async-start(bf16[32,8,256]{2,1,0:T(8,128)(2,1)} %shard_map.117), calls=%async_computation.10 | async-start | bytes 262144 | tf_op jit(solution)/shard_map/all_to_all | solution.py:380
  184.8 11.2 %all-to-all-start.12 = ((bf16[8,32,256]{2,1,0:T(8,128)(2,1)}), bf16[8,32,256]{2,1,0:T(8,128)(2,1)S(1)}, u32[]{:S(2)}, u32[]{:S(2)}) async-start(bf16[8,32,256]{2,1,0:T(8,128)(2,1)} %get-tuple-element.149), calls=%async_computation.12 | async-start | bytes 262144 | tf_op jit(solution)/shard_map/all_to_all | solution.py:380
  197.5 10.4 %all-to-all-start.13 = ((bf16[4,2,32,128]{3,2,1,0:T(8,128)(2,1)}), bf16[4,2,32,128]{3,2,1,0:T(8,128)(2,1)S(1)}, u32[]{:S(2)}, u32[]{:S(2)}) async-start(bf16[4,2,32,128]{3,2,1,0:T(8,128)(2,1)} %shard_map.121), calls=%async_computation.13 | async-start | bytes 131072 | tf_op jit(solution)/shard_map/all_to_all | solution.py:380
  200.9 14.7 %collective-permute-start.4 = (bf16[7,16,32]{1,0,2:T(8,128)(2,1)S(1)}, bf16[7,16,32]{1,0,2:T(8,128)(2,1)S(1)}, u32[]{:S(2)}, u32[]{:S(2)}) collective-permute-start(bf16[7,16,32]{1,0,2:T(8,128)(2,1)S(1)} %dynamic-slice_bitcast_fusion.1), channel_id=1, source_target_pairs={{0,1},{1,0},{2,3},{3,2},{4,5},{5,4},{6,7},{7,6},{8,9},{9,8},{10,11... | collective-permute-start | bytes 21512 | tf_op jit(solution)/shard_map/ppermute | solution.py:33
  208.7 14.7 %all-to-all-start.14 = ((bf16[16,16,128]{2,1,0:T(8,128)(2,1)}), bf16[16,16,128]{2,1,0:T(8,128)(2,1)S(1)}, u32[]{:S(2)}, u32[]{:S(2)}) async-start(bf16[16,16,128]{2,1,0:T(8,128)(2,1)} %shard_map.122), calls=%async_computation.14 | async-start | bytes 131072 | tf_op jit(solution)/shard_map/all_to_all | solution.py:380
Sparse Core Ops, SparseCore 0:
  10.1 44.6 all-gather.4
  57.0 39.1 all-gather.6

commit v7 on v6

--- a/solution.py
+++ b/solution.py
@@ -154,32 +154,52 @@
     out[...] = scratch[...].astype(BF16)
 
 
-def fetch(blocks, core, gathered, near, near_x, sems):
-    wide = gathered.shape[3]
+def fetch(groups, core, near, near_x, sems):
     copies = []
-    at = 0
-    while at < len(blocks):
-        count = 1
-        while at + count < len(blocks) and blocks[at + count] == blocks[at] + count:
-            count += 1
-        for r in range(gathered.shape[0] // CORES):
-            for which, target in ((core, near), (1 - core, near_x)):
-                copies.append(
-                    pltpu.make_async_copy(
-                        gathered.at[r * CORES + which, pl.ds(blocks[at], count)],
-                        target.at[pl.ds(at, count), :, pl.ds(r * wide, wide)],
-                        sems.at[len(copies)],
+    base = 0
+    for blocks, gathered in groups:
+        wide = gathered.shape[3]
+        at = 0
+        while at < len(blocks):
+            count = 1
+            while at + count < len(blocks) and blocks[at + count] == blocks[at] + count:
+                count += 1
+            for r in range(gathered.shape[0] // CORES):
+                for which, target in ((core, near), (1 - core, near_x)):
+                    copies.append(
+                        pltpu.make_async_copy(
+                            gathered.at[r * CORES + which, pl.ds(blocks[at], count)],
+                            target.at[pl.ds(base + at, count), :, pl.ds(r * wide, wide)],
+                            sems.at[len(copies)],
+                        )
                     )
-                )
-        at += count
+            at += count
+        base += len(blocks)
     for copy in copies:
         copy.start()
     return copies
 
 
-def load_blocks(blocks, where, gathered, near, near_x, sems):
-    for copy in fetch(blocks, where[0], gathered, near, near_x, sems):
+def load_blocks(lists, where, *refs):
+    *stacks, near, near_x, sems = refs
+    for copy in fetch(list(zip(lists, stacks)), where[0], near, near_x, sems):
         copy.wait()
+
+
+def make_root(where, low, upper, root, root_x, near, near_x, near_up, sems, up_sem):
+    copy = pltpu.make_async_copy(upper, near_up, up_sem.at[0])
+    copy.start()
+    for other in fetch([([0], low)], where[0], near, near_x, sems):
+        other.wait()
+    copy.wait()
+    left = block(near, near_x, 0)
+    own, wide = upper.shape[1:]
+    span = left.shape[1] // own
+    for r in range(upper.shape[0] // span):
+        right = near_up[r * span : (r + 1) * span].reshape(span * own, wide)
+        value = times(left, right).astype(BF16)
+        root[0, :, r * wide : (r + 1) * wide] = value[:own]
+        root_x[0, :, r * wide : (r + 1) * wide] = value[own:]
 
 
 def solve_level(depth, v8, offset, near, near_x, out, scratch):
@@ -254,7 +274,7 @@
 
 
 def other_pairs(blocks, depth, down, where, values, acc_in, gathered, acc_out, near, near_x, sems):
-    copies = fetch(blocks, where[0], gathered, near, near_x, sems)
+    copies = fetch([(blocks, gathered)], where[0], near, near_x, sems)
     acc = acc_in[...]
     for copy in copies:
         copy.wait()
@@ -268,10 +288,10 @@
     return own_first(values[:, pl.ds(pl.multiple_of(z * rows, rows), rows)], core)
 
 
-def anc_turn(where, tiles, near, near_x, y_out, out, scratch):
-    level_rows(0, tiles, y_out)
-    t = z_rows(where, y_out, near.shape[1] * CORES)
-    solve_level(0, t.astype(BF16), 0, near, near_x, out, scratch)
+def anc_turn(tiles, acc_in, near, near_x, root, root_x, y_out, out, scratch):
+    level_rows(1, tiles, y_out)
+    acc = acc_in[...] - pair_sum(1, 0, y_out, 0, (near, near_x), True)
+    solve_level(0, acc.astype(BF16), 0, root, root_x, out, scratch)
 
 
 def anc_start(where, *refs):
@@ -285,8 +305,8 @@
 
 def anc_backward(depth, tiles, acc_in, near, near_x, z_out, out, scratch):
     level_rows(depth - 1, tiles, z_out)
-    acc = acc_in[...] - pair_sum(depth, depth - 1, z_out, 0, (near, near_x), False)
-    solve_level(depth, acc.astype(BF16), 2**depth, near, near_x, out, scratch)
+    acc = acc_in[...] - pair_sum(depth, depth - 1, z_out, 2**depth, (near, near_x), False)
+    solve_level(depth, acc.astype(BF16), 0, near, near_x, out, scratch)
 
 
 def sub_pieces(where, y_root, y_leaf, out):
@@ -373,8 +393,8 @@
     base = jnp.clip(z * pair_rows - r * wide, 0, wide - pair_rows)
     where = jnp.stack([core, z, held, base, g, core * cols + g * nrow + r]).astype(jnp.int32)
 
-    def gathered(blocks):
-        return lax.all_gather(blocks, ("row", "core"), axis=0, tiled=False)
+    def gathered(blocks, axes):
+        return lax.all_gather(blocks, axes, axis=0, tiled=False)
 
     def exchange(array, axes):
         return lax.all_to_all(array, axes, 0, 0, tiled=True)
@@ -387,26 +407,38 @@
 
     low = (sub_lower, swapped(sub_lower))
     rhs_there = swapped(sub_rhs)
-    anc_low = gathered(anc_lower)
-    anc_up = gathered(anc_upper)
+    anc_low = gathered(anc_lower, ("row", "core"))
 
     def diagonal(depth):
         return list(range(*level_span(depth)))
 
+    up_split = pairs.anc[level_span(levels - 1)[0], 0]
+
+    def from_up(blocks):
+        first = [index - 1 for index in blocks if index < up_split]
+        return (first, up_a), ([index - up_split for index in blocks if index >= up_split], up_b)
+
     def pair_blocks(depth, u):
         return [pairs.anc[a, u] for a in range(*level_span(depth))]
 
-    def loaded(blocks, stack):
-        near = shape(BF16, len(blocks), own, size)
-        sems = pltpu.SemaphoreType.DMA((len(blocks) * nrow * CORES,))
-        return run(part(load_blocks, blocks), (near, near), (where,), (), (sems,), (stack,))
-
-    def others(depth, down, values, acc, stack):
-        blocks = [index for u in range(depth - 1) for index in pair_blocks(depth, u)]
+    def loaded(groups):
+        groups = [group for group in groups if group[0]]
+        lists = [blocks for blocks, stack in groups]
+        count = sum(len(blocks) for blocks in lists)
+        near = shape(BF16, count, own, size)
+        sems = pltpu.SemaphoreType.DMA((count * nrow * CORES,))
+        stacks = [stack for blocks, stack in groups]
+        return run(part(load_blocks, lists), (near, near), (where,), (), (sems,), stacks)
+
+    def others(depth, down, values, acc, group):
+        blocks, stack = group
         near = pltpu.VMEM((len(blocks), own, size), BF16)
         sems = pltpu.SemaphoreType.DMA((len(blocks) * nrow * CORES,))
         body = part(other_pairs, blocks, depth, down)
         return run(body, acc_shape, (where,), (values, acc), (near, near, sems), (stack,))
+
+    def older_pairs(depth):
+        return [index for u in range(depth - 1) for index in pair_blocks(depth, u)]
 
     def level_shape(depth):
         return shape(BF16, nz, max(2, 2**depth), size)
@@ -434,6 +466,10 @@
         (where, layer_subtree),
         (anc_rhs, anc_there),
     )
+    given8, anc_upper = tied(given8, anc_upper)
+    root_up = gathered(anc_upper[0], ("row", "z", "core"))
+    up_a = gathered(anc_upper[1:up_split], ("row", "core"))
+    up_b = gathered(anc_upper[up_split:], ("row", "core"))
     tiles = exchange(tiles, "z")
     tiles, given8, choose = tied(tiles, given8, choose)
     y_leaf, tiles = run(
@@ -461,7 +497,7 @@
         (c_scratch,),
     )
     tiles = exchange(tiles, ("gz", "row"))
-    near = loaded(diagonal(levels - 1), anc_low)
+    near = loaded([(diagonal(levels - 1), anc_low)])
     tiles, *near = tied(tiles, *near)
 
     acc, tiles = run(
@@ -472,10 +508,26 @@
         (scr8, c_scratch),
     )
     tiles = exchange(tiles, "z")
+    near_root = pltpu.VMEM((1, own, size), BF16)
+    root = run(
+        make_root,
+        (shape(BF16, 1, own, size), shape(BF16, 1, own, size)),
+        (where,),
+        (),
+        (
+            near_root,
+            near_root,
+            pltpu.VMEM(root_up.shape, BF16),
+            pltpu.SemaphoreType.DMA((nrow * CORES,)),
+            pltpu.SemaphoreType.DMA((1,)),
+        ),
+        (anc_low, root_up),
+    )
+    tiles, *root = tied(tiles, *root)
     y_parts = []
-    for depth in range(levels - 1, 0, -1):
+    for depth in range(levels - 1, 1, -1):
         blocks = pair_blocks(depth, depth - 1) + diagonal(depth - 1)
-        near = loaded(blocks, anc_low)
+        near = loaded([(blocks, anc_low)])
         tiles, *near = tied(tiles, *near)
         y8, acc, tiles = run(
             part(anc_forward, depth),
@@ -486,13 +538,16 @@
         )
         y_parts.append(y8)
         tiles = exchange(tiles, "z")
-        if depth > 1:
-            acc = others(depth, True, y8, acc, anc_low)
-            tiles, acc = tied(tiles, acc)
-    near = loaded(diagonal(0), anc_up)
+        acc = others(depth, True, y8, acc, (older_pairs(depth), anc_low))
+        tiles, acc = tied(tiles, acc)
+    near = loaded([(pair_blocks(1, 0), anc_low)])
     tiles, *near = tied(tiles, *near)
     y8, tiles = run(
-        anc_turn, (row_shape, level_shape(0)), (where,), (tiles, *near), (scr8,)
+        anc_turn,
+        (row_shape, level_shape(0)),
+        (),
+        (tiles, acc, *near, *root),
+        (scr8,),
     )
     y_parts.append(y8)
     tiles = exchange(tiles, "z")
@@ -501,11 +556,12 @@
     z8 = None
     for depth in range(1, levels):
         acc = start8
-        blocks = pair_blocks(depth, depth - 1) + diagonal(depth)
-        near = loaded(blocks, anc_up)
+        blocks = diagonal(depth) + pair_blocks(depth, depth - 1)
+        near = loaded(from_up(blocks))
         tiles, *near = tied(tiles, *near)
         if depth > 1:
-            acc = others(depth, False, z8, acc, anc_up)
+            group = [index - up_split for index in older_pairs(depth)], up_b
+            acc = others(depth, False, z8, acc, group)
             tiles, acc = tied(tiles, acc)
         z_now, tiles = run(
             part(anc_backward, depth),

time: 233 us -> 303 us (1.30)
  waiting for transfers between devices: 68.9 us -> 140 us
    all_gather x2 -> x4, waiting for transfers between devices: 0.03 us -> 80.3 us  [gathered(): return lax.all_gather(blocks, axes, axis=0, tiled=False)]
    all_to_all x13 -> x12, waiting for transfers between devices: 65.8 us -> 55.6 us  [exchange(): return lax.all_to_all(array, axes, 0, 0, tiled=True)]
    ppermute x5, starting transfers between devices: 31.5 us -> 22.3 us  [swapped(): return lax.ppermute(array, 'core', [(0, 1), (1, 0)])]
    all_to_all x13 -> x12, starting transfers between devices: 55.3 us -> 63.9 us  [exchange(): return lax.all_to_all(array, axes, 0, 0, tiled=True)]
    pallas_call x28 -> x27, Pallas kernels: 38.3 us -> 37.9 us  [run(): pl.pallas_call(body, out_shape=outs, in_specs=in_specs, out_specs=spec if...]
  transfers between devices with their start and end apart: 20 -> 21, of which waited for: 14 -> 13; matrix products, arithmetic and copies ran while one was open for 1% -> 1% of each run, Pallas kernels for 13% -> 11%
where the time goes in v7:
time: 303 us; the launch traced here: 301 us
  waiting for transfers between devices  140 us (46%)
  starting transfers between devices  86.4 us (29%)
  Pallas kernels  37.9 us (13%)
  blocking collectives  17.1 us (6%)
  between operations  14.1 us (5%)
  local copies, waits for them, and re-layouts  5.18 us (2%)
    all_gather x4, waiting for transfers between devices, gathered(): return lax.all_gather(blocks, axes, axis=0, tiled=False)  80.3 us
    all_to_all x12, starting transfers between devices, exchange(): return lax.all_to_all(array, axes, 0, 0, tiled=True)  63.9 us
    all_to_all x12, waiting for transfers between devices, exchange(): return lax.all_to_all(array, axes, 0, 0, tiled=True)  55.6 us
    pallas_call x27, Pallas kernels, run(): pl.pallas_call(body, out_shape=outs, in_specs=in_specs, out_specs=spec if...  37.9 us
    ppermute x5, starting transfers between devices, swapped(): return lax.ppermute(array, 'core', [(0, 1), (1, 0)])  22.3 us
    all_to_all x2, blocking collectives, exchange(): return lax.all_to_all(array, axes, 0, 0, tiled=True)  17.1 us
  transfers between devices with their start and end apart: 21, of which 13 were waited for; matrix products, arithmetic and copies ran while one was open for 1% of the time, Pallas kernels for 11%

profile of v7, /device:TPU:1, one launch (start us, length us, event | category | flops | bytes accessed | tf_op | source)
XLA Modules:
  0.0 301.2 jit_solution(14206265468889826698)
XLA Ops:
  8.0 8.7 %collective-permute-start.1 = (bf16[14,64,256]{2,1,0:T(8,128)(2,1)}, bf16[14,64,256]{2,1,0:T(8,128)(2,1)S(1)}, u32[]{:S(2)}, u32[]{:S(2)}) collective-permute-start(bf16[14,64,256]{2,1,0:T(8,128)(2,1)} %own.9), channel_id=1, source_target_pairs={{0,1},{1,0},{2,3},{3,2},{4,5},{5,4},{6,7},{7,6},{8,9},{9,8},{10,11... | collective-permute-start | bytes 1376264 | tf_op jit(solution)/shard_map/ppermute | solution.py:33
  31.1 4.7 %all-to-all-start = ((bf16[8,2,32,256]{3,2,1,0:T(8,128)(2,1)}), bf16[8,2,32,256]{3,2,1,0:T(8,128)(2,1)S(1)}, u32[]{:S(2)}, u32[]{:S(2)}) async-start(bf16[8,2,32,256]{3,2,1,0:T(8,128)(2,1)} %get-tuple-element.78), calls=%async_computation | async-start | bytes 524288 | tf_op jit(solution)/shard_map/all_to_all | solution.py:400
  35.9 12.1 %all-to-all-done.tiles = bf16[8,2,32,256]{3,2,1,0:T(8,128)(2,1)S(1)} async-done(((bf16[8,2,32,256]{3,2,1,0:T(8,128)(2,1)}), bf16[8,2,32,256]{3,2,1,0:T(8,128)(2,1)S(1)}, u32[]{:S(2)}, u32[]{:S(2)}) %all-to-all-start) | async-done | bytes 262176 | tf_op jit(solution)/shard_map/all_to_all | solution.py:400
  49.5 4.0 %all-to-all-start.1 = ((bf16[4,32,128]{2,1,0:T(8,128)(2,1)}), bf16[4,32,128]{2,1,0:T(8,128)(2,1)S(1)}, u32[]{:S(2)}, u32[]{:S(2)}) async-start(bf16[4,32,128]{2,1,0:T(8,128)(2,1)} %get-tuple-element.84), calls=%async_computation.1 | async-start | bytes 65536 | tf_op jit(solution)/shard_map/all_to_all | solution.py:400
  54.4 3.4 %all-to-all-done.1.tiles = bf16[4,32,128]{2,1,0:T(8,128)(2,1)S(1)} async-done(((bf16[4,32,128]{2,1,0:T(8,128)(2,1)}), bf16[4,32,128]{2,1,0:T(8,128)(2,1)S(1)}, u32[]{:S(2)}, u32[]{:S(2)}) %all-to-all-start.1) | async-done | bytes 32800 | tf_op jit(solution)/shard_map/all_to_all | solution.py:400
  58.0 10.4 %all_to_all.70.tiles = bf16[8,32,256]{2,1,0:T(8,128)(2,1)S(1)} all-to-all(bf16[8,32,256]{2,1,0:T(8,128)(2,1)S(1)} %shard_map.99), channel_id=1, replica_groups=mesh['gz'=8,'row'=4,'z'=8,'core'=2] {'z'}, dimensions={0} | all-to-all | bytes 262144 | tf_op jit(solution)/shard_map/all_to_all | solution.py:400
  69.9 7.9 %all-to-all-start.3 = ((bf16[32,8,128]{2,1,0:T(8,128)(2,1)}), bf16[32,8,128]{2,1,0:T(8,128)(2,1)S(1)}, u32[]{:S(2)}, u32[]{:S(2)}) async-start(bf16[32,8,128]{2,1,0:T(8,128)(2,1)} %get-tuple-element.89), calls=%async_computation.3 | async-start | bytes 131072 | tf_op jit(solution)/shard_map/all_to_all | solution.py:400
  80.0 6.7 %all-to-all-done.3.tiles = bf16[32,8,128]{2,1,0:T(8,128)(2,1)S(1)} async-done(((bf16[32,8,128]{2,1,0:T(8,128)(2,1)}), bf16[32,8,128]{2,1,0:T(8,128)(2,1)S(1)}, u32[]{:S(2)}, u32[]{:S(2)}) %all-to-all-start.3) | async-done | bytes 65568 | tf_op jit(solution)/shard_map/all_to_all | solution.py:400
  87.8 3.3 %all-to-all-start.4 = ((bf16[8,4,1024]{2,1,0:T(4,128)(2,1)}), bf16[8,4,1024]{2,1,0:T(4,128)(2,1)S(1)}, u32[]{:S(2)}, u32[]{:S(2)}) async-start(bf16[8,4,1024]{2,1,0:T(4,128)(2,1)} %get-tuple-element.97), calls=%async_computation.4 | async-start | bytes 131072 | tf_op jit(solution)/shard_map/all_to_all | solution.py:400
  91.2 2.4 shard_map.104
  93.6 48.2 %all-gather.8.cloned.1.call-done.upper = bf16[64,64,256]{2,1,0:T(8,128)(2,1)} async-done(((bf16[1,64,256]{2,1,0:T(8,128)(2,1)}), bf16[64,64,256]{2,1,0:T(8,128)(2,1)}) %all-gather.8.cloned.1.call-update) | async-done | bytes 2097168 | tf_op jit(solution)/shard_map/all_gather | solution.py:397
  141.8 2.8 shard_map.103
  146.0 3.9 %all-to-all-start.5 = ((bf16[8,2,1024]{2,1,0:T(2,128)(2,1)}), bf16[8,2,1024]{2,1,0:T(2,128)(2,1)S(1)}, u32[]{:S(2)}, u32[]{:S(2)}) async-start(bf16[8,2,1024]{2,1,0:T(2,128)(2,1)} %get-tuple-element.108), calls=%async_computation.5 | async-start | bytes 65536 | tf_op jit(solution)/shard_map/all_to_all | solution.py:400
  151.6 2.4 shard_map.106.acc_in
  154.0 2.8 all-to-all-done.5.tiles
  157.8 3.9 %all-to-all-start.6 = ((bf16[8,2,1024]{2,1,0:T(2,128)(2,1)}), bf16[8,2,1024]{2,1,0:T(2,128)(2,1)S(1)}, u32[]{:S(2)}, u32[]{:S(2)}) async-start(bf16[8,2,1024]{2,1,0:T(2,128)(2,1)} %get-tuple-element.120), calls=%async_computation.6 | async-start | bytes 65536 | tf_op jit(solution)/shard_map/all_to_all | solution.py:400
  161.7 9.9 %all-gather.12.cloned.1.call-done = bf16[64,64,256]{2,1,0:T(8,128)(2,1)} async-done(((bf16[8,64,256]{2,1,0:T(8,128)(2,1)}), bf16[64,64,256]{2,1,0:T(8,128)(2,1)}) %all-gather.12.cloned.1.call-update) | async-done | bytes 2097168 | tf_op jit(solution)/shard_map/all_gather | solution.py:397
  175.5 7.1 %all-to-all-start.7 = ((bf16[8,2,1024]{2,1,0:T(2,128)(2,1)}), bf16[8,2,1024]{2,1,0:T(2,128)(2,1)S(1)}, u32[]{:S(2)}, u32[]{:S(2)}) async-start(bf16[8,2,1024]{2,1,0:T(2,128)(2,1)} %get-tuple-element.129), calls=%async_computation.7 | async-start | bytes 65536 | tf_op jit(solution)/shard_map/all_to_all | solution.py:400
  182.6 22.1 %all-gather.14.cloned.1.call-done = bf16[64,64,256]{2,1,0:T(8,128)(2,1)} async-done(((bf16[8,64,256]{2,1,0:T(8,128)(2,1)}), bf16[64,64,256]{2,1,0:T(8,128)(2,1)}) %all-gather.14.cloned.1.call-update) | async-done | bytes 2097168 | tf_op jit(solution)/shard_map/all_gather | solution.py:397
  204.7 2.6 shard_map.112
  207.3 2.4 shard_map.113.acc_in
  213.5 7.1 %all-to-all-start.8 = ((bf16[8,4,1024]{2,1,0:T(4,128)(2,1)}), bf16[8,4,1024]{2,1,0:T(4,128)(2,1)S(1)}, u32[]{:S(2)}, u32[]{:S(2)}) async-start(bf16[8,4,1024]{2,1,0:T(4,128)(2,1)} %get-tuple-element.139), calls=%async_computation.8 | async-start | bytes 131072 | tf_op jit(solution)/shard_map/all_to_all | solution.py:400
  220.6 7.2 %all-to-all-done.8.tiles = bf16[8,4,1024]{2,1,0:T(4,128)(2,1)S(1)} async-done(((bf16[8,4,1024]{2,1,0:T(4,128)(2,1)}), bf16[8,4,1024]{2,1,0:T(4,128)(2,1)S(1)}, u32[]{:S(2)}, u32[]{:S(2)}) %all-to-all-start.8) | async-done | bytes 65568 | tf_op jit(solution)/shard_map/all_to_all | solution.py:400
  228.5 8.4 %all-to-all-start.9 = ((bf16[32,8,256]{2,1,0:T(8,128)(2,1)}), bf16[32,8,256]{2,1,0:T(8,128)(2,1)S(1)}, u32[]{:S(2)}, u32[]{:S(2)}) async-start(bf16[32,8,256]{2,1,0:T(8,128)(2,1)} %shard_map.116), calls=%async_computation.9 | async-start | bytes 262144 | tf_op jit(solution)/shard_map/all_to_all | solution.py:400
  237.5 8.8 %all-to-all-done.9.tiles = bf16[32,8,256]{2,1,0:T(8,128)(2,1)S(1)} async-done(((bf16[32,8,256]{2,1,0:T(8,128)(2,1)}), bf16[32,8,256]{2,1,0:T(8,128)(2,1)S(1)}, u32[]{:S(2)}, u32[]{:S(2)}) %all-to-all-start.9) | async-done | bytes 131104 | tf_op jit(solution)/shard_map/all_to_all | solution.py:400
  247.3 6.7 %all_to_all.71.tiles = bf16[4,32,128]{2,1,0:T(8,128)(2,1)S(1)} all-to-all(bf16[4,32,128]{2,1,0:T(8,128)(2,1)S(1)} %get-tuple-element.148), channel_id=1, replica_groups=mesh['gz'=8,'row'=4,'z'=8,'core'=2] {'row'}, dimensions={0} | all-to-all | bytes 65536 | tf_op jit(solution)/shard_map/all_to_all | solution.py:400
  254.8 3.4 %all-to-all-start.11 = ((bf16[8,32,256]{2,1,0:T(8,128)(2,1)}), bf16[8,32,256]{2,1,0:T(8,128)(2,1)S(1)}, u32[]{:S(2)}, u32[]{:S(2)}) async-start(bf16[8,32,256]{2,1,0:T(8,128)(2,1)} %get-tuple-element.149), calls=%async_computation.11 | async-start | bytes 262144 | tf_op jit(solution)/shard_map/all_to_all | solution.py:400
  258.2 7.8 %all-to-all-done.11.tiles = bf16[8,32,256]{2,1,0:T(8,128)(2,1)S(1)} async-done(((bf16[8,32,256]{2,1,0:T(8,128)(2,1)}), bf16[8,32,256]{2,1,0:T(8,128)(2,1)S(1)}, u32[]{:S(2)}, u32[]{:S(2)}) %all-to-all-start.11) | async-done | bytes 131104 | tf_op jit(solution)/shard_map/all_to_all | solution.py:400
  267.4 3.3 %all-to-all-start.12 = ((bf16[4,2,32,128]{3,2,1,0:T(8,128)(2,1)}), bf16[4,2,32,128]{3,2,1,0:T(8,128)(2,1)S(1)}, u32[]{:S(2)}, u32[]{:S(2)}) async-start(bf16[4,2,32,128]{3,2,1,0:T(8,128)(2,1)} %shard_map.120), calls=%async_computation.12 | async-start | bytes 131072 | tf_op jit(solution)/shard_map/all_to_all | solution.py:400
  270.8 7.4 %collective-permute-start.4 = (bf16[7,16,32]{1,0,2:T(8,128)(2,1)S(1)}, bf16[7,16,32]{1,0,2:T(8,128)(2,1)S(1)}, u32[]{:S(2)}, u32[]{:S(2)}) collective-permute-start(bf16[7,16,32]{1,0,2:T(8,128)(2,1)S(1)} %dynamic-slice_bitcast_fusion.1), channel_id=1, source_target_pairs={{0,1},{1,0},{2,3},{3,2},{4,5},{5,4},{6,7},{7,6},{8,9},{9,8},{10,11... | collective-permute-start | bytes 21512 | tf_op jit(solution)/shard_map/ppermute | solution.py:33
  279.1 6.8 %all-to-all-start.13 = ((bf16[16,16,128]{2,1,0:T(8,128)(2,1)}), bf16[16,16,128]{2,1,0:T(8,128)(2,1)S(1)}, u32[]{:S(2)}, u32[]{:S(2)}) async-start(bf16[16,16,128]{2,1,0:T(8,128)(2,1)} %shard_map.121), calls=%async_computation.13 | async-start | bytes 131072 | tf_op jit(solution)/shard_map/all_to_all | solution.py:400
  287.0 6.8 %all-to-all-done.13 = bf16[16,16,128]{2,1,0:T(8,128)(2,1)S(1)} async-done(((bf16[16,16,128]{2,1,0:T(8,128)(2,1)}), bf16[16,16,128]{2,1,0:T(8,128)(2,1)S(1)}, u32[]{:S(2)}, u32[]{:S(2)}) %all-to-all-start.13) | async-done | bytes 65568 | tf_op jit(solution)/shard_map/all_to_all | solution.py:400
  (70 shorter events, 41.6 us)
Async XLA Ops:
  7.2 40.9 %copy-start = (bf16[14,64,256]{2,1,0:T(8,128)(2,1)S(1)}, bf16[14,64,256]{2,1,0:T(8,128)(2,1)}, u32[]{:S(2)}) copy-start(bf16[14,64,256]{2,1,0:T(8,128)(2,1)} %own.9) | copy-start | bytes 1376260
  7.2 22.5 %copy-start.5 = (bf16[17,64,256]{2,1,0:T(8,128)(2,1)S(1)}, bf16[17,64,256]{2,1,0:T(8,128)(2,1)}, u32[]{:S(2)}) copy-start(bf16[17,64,256]{2,1,0:T(8,128)(2,1)} %param.9) | copy-start | bytes 1671172
  7.2 28.6 %copy-start.6 = (s32[11,2]{0,1:T(2,128)S(1)}, s32[11,2]{0,1:T(2,128)}, u32[]{:S(2)}) copy-start(s32[11,2]{0,1:T(2,128)} %param.15) | copy-start | bytes 268
  7.2 70.7 %all-gather.10.cloned.1.call-start = ((), (), s32[]{:S(2)}) async-start(), calls=%async_computation.15 | async-start | bytes 5013504 | tf_op jit(solution)/shard_map/all_gather | solution.py:397
  7.9 133.9 %all-gather.8.cloned.1.call-start = ((), (), s32[]{:S(2)}) async-start(), calls=%async_computation.14 | async-start | bytes 2129920 | tf_op jit(solution)/shard_map/all_gather | solution.py:397
  8.0 12.1 %collective-permute-start.1 = (bf16[14,64,256]{2,1,0:T(8,128)(2,1)}, bf16[14,64,256]{2,1,0:T(8,128)(2,1)S(1)}, u32[]{:S(2)}, u32[]{:S(2)}) collective-permute-start(bf16[14,64,256]{2,1,0:T(8,128)(2,1)} %own.9), channel_id=1, source_target_pairs={{0,1},{1,0},{2,3},{3,2},{4,5},{5,4},{6,7},{7,6},{8,9},{9,8},{10,11... | collective-permute-start | bytes 1376264 | tf_op jit(solution)/shard_map/ppermute | solution.py:33
  16.7 3.3 %collective-permute-start = (bf16[3,64,64]{2,1,0:T(8,128)(2,1)}, bf16[3,64,64]{2,1,0:T(8,128)(2,1)S(1)}, u32[]{:S(2)}, u32[]{:S(2)}) collective-permute-start(bf16[3,64,64]{2,1,0:T(8,128)(2,1)} %here.1), channel_id=1, source_target_pairs={{0,1},{1,0},{2,3},{3,2},{4,5},{5,4},{6,7},{7,6},{8,9},{9,8},{10,11... | collective-permute-start | bytes 73736 | tf_op jit(solution)/shard_map/ppermute | solution.py:33
  22.4 3.4 %collective-permute-start.2 = (bf16[7,64,64]{2,1,0:T(8,128)(2,1)}, bf16[7,64,64]{2,1,0:T(8,128)(2,1)S(1)}, u32[]{:S(2)}, u32[]{:S(2)}) collective-permute-start(bf16[7,64,64]{2,1,0:T(8,128)(2,1)} %here.2), channel_id=1, source_target_pairs={{0,1},{1,0},{2,3},{3,2},{4,5},{5,4},{6,7},{7,6},{8,9},{9,8},{10,11... | collective-permute-start | bytes 172040 | tf_op jit(solution)/shard_map/ppermute | solution.py:33
  25.9 0.9 copy-start.2
  26.8 0.7 copy-start.3
  29.6 142.0 %all-gather.12.cloned.1.call-start = ((), (), s32[]{:S(2)}) async-start(), calls=%async_computation.16 | async-start | bytes 2359296 | tf_op jit(solution)/shard_map/all_gather | solution.py:397
  30.6 174.2 %all-gather.14.cloned.1.call-start = ((), (), s32[]{:S(2)}) async-start(), calls=%async_computation.17 | async-start | bytes 2359296 | tf_op jit(solution)/shard_map/all_gather | solution.py:397
  31.1 16.9 %all-to-all-start = ((bf16[8,2,32,256]{3,2,1,0:T(8,128)(2,1)}), bf16[8,2,32,256]{3,2,1,0:T(8,128)(2,1)S(1)}, u32[]{:S(2)}, u32[]{:S(2)}) async-start(bf16[8,2,32,256]{3,2,1,0:T(8,128)(2,1)} %get-tuple-element.78), calls=%async_computation | async-start | bytes 524288 | tf_op jit(solution)/shard_map/all_to_all | solution.py:400
  49.5 8.3 %all-to-all-start.1 = ((bf16[4,32,128]{2,1,0:T(8,128)(2,1)}), bf16[4,32,128]{2,1,0:T(8,128)(2,1)S(1)}, u32[]{:S(2)}, u32[]{:S(2)}) async-start(bf16[4,32,128]{2,1,0:T(8,128)(2,1)} %get-tuple-element.84), calls=%async_computation.1 | async-start | bytes 65536 | tf_op jit(solution)/shard_map/all_to_all | solution.py:400
  69.9 16.8 %all-to-all-start.3 = ((bf16[32,8,128]{2,1,0:T(8,128)(2,1)}), bf16[32,8,128]{2,1,0:T(8,128)(2,1)S(1)}, u32[]{:S(2)}, u32[]{:S(2)}) async-start(bf16[32,8,128]{2,1,0:T(8,128)(2,1)} %get-tuple-element.89), calls=%async_computation.3 | async-start | bytes 131072 | tf_op jit(solution)/shard_map/all_to_all | solution.py:400
  87.8 56.8 %all-to-all-start.4 = ((bf16[8,4,1024]{2,1,0:T(4,128)(2,1)}), bf16[8,4,1024]{2,1,0:T(4,128)(2,1)S(1)}, u32[]{:S(2)}, u32[]{:S(2)}) async-start(bf16[8,4,1024]{2,1,0:T(4,128)(2,1)} %get-tuple-element.97), calls=%async_computation.4 | async-start | bytes 131072 | tf_op jit(solution)/shard_map/all_to_all | solution.py:400
  146.0 10.8 %all-to-all-start.5 = ((bf16[8,2,1024]{2,1,0:T(2,128)(2,1)}), bf16[8,2,1024]{2,1,0:T(2,128)(2,1)S(1)}, u32[]{:S(2)}, u32[]{:S(2)}) async-start(bf16[8,2,1024]{2,1,0:T(2,128)(2,1)} %get-tuple-element.108), calls=%async_computation.5 | async-start | bytes 65536 | tf_op jit(solution)/shard_map/all_to_all | solution.py:400
  157.8 16.5 %all-to-all-start.6 = ((bf16[8,2,1024]{2,1,0:T(2,128)(2,1)}), bf16[8,2,1024]{2,1,0:T(2,128)(2,1)S(1)}, u32[]{:S(2)}, u32[]{:S(2)}) async-start(bf16[8,2,1024]{2,1,0:T(2,128)(2,1)} %get-tuple-element.120), calls=%async_computation.6 | async-start | bytes 65536 | tf_op jit(solution)/shard_map/all_to_all | solution.py:400
  175.5 34.2 %all-to-all-start.7 = ((bf16[8,2,1024]{2,1,0:T(2,128)(2,1)}), bf16[8,2,1024]{2,1,0:T(2,128)(2,1)S(1)}, u32[]{:S(2)}, u32[]{:S(2)}) async-start(bf16[8,2,1024]{2,1,0:T(2,128)(2,1)} %get-tuple-element.129), calls=%async_computation.7 | async-start | bytes 65536 | tf_op jit(solution)/shard_map/all_to_all | solution.py:400
  207.3 4.0 %copy-start.1 = (bf16[14,64,256]{2,1,0:T(8,128)(2,1)S(1)}, bf16[14,64,256]{2,1,0:T(8,128)(2,1)}, u32[]{:S(2)}) copy-start(bf16[14,64,256]{2,1,0:T(8,128)(2,1)} %own.13) | copy-start | bytes 1376260
  207.3 38.9 %copy-start.4 = (s32[8]{0:T(128)S(1)}, s32[8]{0:T(128)}, u32[]{:S(2)}) copy-start(s32[8]{0:T(128)} %subtree.3) | copy-start | bytes 100
  211.3 35.0 %collective-permute-start.3 = (bf16[14,64,256]{2,1,0:T(8,128)(2,1)S(1)}, bf16[14,64,256]{2,1,0:T(8,128)(2,1)S(1)}, u32[]{:S(2)}, u32[]{:S(2)}) collective-permute-start(bf16[14,64,256]{2,1,0:T(8,128)(2,1)S(1)} %copy-done.1), channel_id=1, source_target_pairs={{0,1},{1,0},{2,3},{3,2},{4,5},{5,4},{6,7},{7,6},{8,9},{9,8},{10,11... | collective-permute-start | bytes 1376264 | tf_op jit(solution)/shard_map/ppermute | solution.py:33
  213.5 14.3 %all-to-all-start.8 = ((bf16[8,4,1024]{2,1,0:T(4,128)(2,1)}), bf16[8,4,1024]{2,1,0:T(4,128)(2,1)S(1)}, u32[]{:S(2)}, u32[]{:S(2)}) async-start(bf16[8,4,1024]{2,1,0:T(4,128)(2,1)} %get-tuple-element.139), calls=%async_computation.8 | async-start | bytes 131072 | tf_op jit(solution)/shard_map/all_to_all | solution.py:400
  228.5 17.8 %all-to-all-start.9 = ((bf16[32,8,256]{2,1,0:T(8,128)(2,1)}), bf16[32,8,256]{2,1,0:T(8,128)(2,1)S(1)}, u32[]{:S(2)}, u32[]{:S(2)}) async-start(bf16[32,8,256]{2,1,0:T(8,128)(2,1)} %shard_map.116), calls=%async_computation.9 | async-start | bytes 262144 | tf_op jit(solution)/shard_map/all_to_all | solution.py:400
  254.8 11.2 %all-to-all-start.11 = ((bf16[8,32,256]{2,1,0:T(8,128)(2,1)}), bf16[8,32,256]{2,1,0:T(8,128)(2,1)S(1)}, u32[]{:S(2)}, u32[]{:S(2)}) async-start(bf16[8,32,256]{2,1,0:T(8,128)(2,1)} %get-tuple-element.149), calls=%async_computation.11 | async-start | bytes 262144 | tf_op jit(solution)/shard_map/all_to_all | solution.py:400
  267.4 10.8 %all-to-all-start.12 = ((bf16[4,2,32,128]{3,2,1,0:T(8,128)(2,1)}), bf16[4,2,32,128]{3,2,1,0:T(8,128)(2,1)S(1)}, u32[]{:S(2)}, u32[]{:S(2)}) async-start(bf16[4,2,32,128]{3,2,1,0:T(8,128)(2,1)} %shard_map.120), calls=%async_computation.12 | async-start | bytes 131072 | tf_op jit(solution)/shard_map/all_to_all | solution.py:400
  270.8 15.1 %collective-permute-start.4 = (bf16[7,16,32]{1,0,2:T(8,128)(2,1)S(1)}, bf16[7,16,32]{1,0,2:T(8,128)(2,1)S(1)}, u32[]{:S(2)}, u32[]{:S(2)}) collective-permute-start(bf16[7,16,32]{1,0,2:T(8,128)(2,1)S(1)} %dynamic-slice_bitcast_fusion.1), channel_id=1, source_target_pairs={{0,1},{1,0},{2,3},{3,2},{4,5},{5,4},{6,7},{7,6},{8,9},{9,8},{10,11... | collective-permute-start | bytes 21512 | tf_op jit(solution)/shard_map/ppermute | solution.py:33
  279.1 14.7 %all-to-all-start.13 = ((bf16[16,16,128]{2,1,0:T(8,128)(2,1)}), bf16[16,16,128]{2,1,0:T(8,128)(2,1)S(1)}, u32[]{:S(2)}, u32[]{:S(2)}) async-start(bf16[16,16,128]{2,1,0:T(8,128)(2,1)} %shard_map.121), calls=%async_computation.13 | async-start | bytes 131072 | tf_op jit(solution)/shard_map/all_to_all | solution.py:400
Sparse Core Ops, SparseCore 0:
  10.1 44.3 all-gather.9
  57.9 83.8 all-gather.7
  144.0 27.6 all-gather.11
  173.6 31.0 all-gather.13

commit v8 on v6

--- a/solution.py
+++ b/solution.py
@@ -88,6 +88,10 @@
     return jnp.where(core == 1, pltpu.roll(v, v.shape[1] // 2, 1), v)
 
 
+def position():
+    return lax.axis_index("core"), lax.axis_index("z")
+
+
 class Pairs:
     def __init__(self, levels, anc_count):
         self.sub = {}
@@ -101,7 +105,7 @@
                 self.anc[a, u] = anc_count + len(self.anc)
 
 
-def sub_leaf_solve(where, there, other, own, here, rhs, out, near, near_rhs, sems):
+def sub_leaf_solve(there, other, own, here, rhs, out, near, near_rhs, sems):
     first, count = LEAVES[0], len(LEAVES)
     copies = [
         pltpu.make_async_copy(own.at[pl.ds(first, count)], near, sems.at[0]),
@@ -111,7 +115,7 @@
         copy.start()
     for copy in copies:
         copy.wait()
-    core = where[0]
+    core = lax.axis_index("core")
     cols = rhs.shape[1]
     for m in range(SUB_NODES):
         flipped = jnp.concatenate([near_rhs[m], there[m]], 0).astype(F32).T
@@ -125,13 +129,17 @@
 
 def sub_low(y, w, pairs, own, other, m, kind, u):
     p = pairs.sub[m, kind, u]
-    return w[p, 0].astype(F32) * times_t(y, block(own, other, SUB_NODES + p))
-
-
-def sub_leaf_update(pairs, w, tiles, own, other, y_out, out):
+    return w[p : p + 1, :] * times_t(y, block(own, other, SUB_NODES + p))
+
+
+def sub_leaf_update(pairs, w, tiles, local_low, other, y_out, out):
     y = total(tiles).astype(BF16)
     y_out[...] = y
-    value = sum(sub_low(y[m - 1], w, pairs, own, other, m, 1, 0) for m in LEAVES)
+    value = 0.0
+    for i, m in enumerate(LEAVES):
+        p = pairs.sub[m, 1, 0]
+        both = jnp.concatenate([local_low[i], other[SUB_NODES + p]], 0)
+        value = value + w[p : p + 1, :] * times_t(y[i], both)
     to_all(out, value)
 
 
@@ -195,8 +203,25 @@
     return lax.shift_right_logical(subtree[g] + layers, levels - e) - 1
 
 
-def anc_prepare(layers, nrow, where, subtree, here, there, choose, out):
+def anc_prepare(pairs, layers, nrow, where, subtree, pattern, here, there, blocks, *outs):
+    choose, out, low_w, up_w, pick, local_low, sems = outs
+    copies = [
+        pltpu.make_async_copy(
+            blocks.at[SUB_NODES + pairs.sub[m, 1, 0]], local_low.at[i], sems.at[i]
+        )
+        for i, m in enumerate(LEAVES)
+    ]
+    for copy in copies:
+        copy.start()
     levels = choose.shape[0]
+    for target, column in ((low_w, 0), (up_w, 1)):
+        for p in range(pattern.shape[0]):
+            weight = pattern[p, column].astype(F32)
+            target[p : p + 1, :] = jnp.full((1, target.shape[1]), weight, F32)
+    nodes = lax.broadcasted_iota(jnp.int32, pick.shape[1:], 0)
+    for e in range(levels):
+        ours = nodes == ancestor(subtree, where[4], layers, levels, e)
+        pick[e] = jnp.where(ours, 1.0, 0.0)
     rows = lax.broadcasted_iota(jnp.int32, choose.shape[1:], 0)
     source = lax.broadcasted_iota(jnp.int32, choose.shape[1:], 1)
     for e in range(levels):
@@ -212,6 +237,8 @@
     for a in range(here.shape[0]):
         value = value + in_row(times_t(pick, block(here, there, a)), a)
     out[...] = value
+    for copy in copies:
+        copy.wait()
 
 
 def anc_first(depth, tiles, choose, given, near, near_x, acc_out, out, scratch, arrived):
@@ -263,20 +290,20 @@
     acc_out[...] = acc
 
 
-def z_rows(where, values, rows):
-    core, z = where[0], where[1]
+def z_rows(values, rows):
+    core, z = position()
     return own_first(values[:, pl.ds(pl.multiple_of(z * rows, rows), rows)], core)
 
 
-def anc_turn(where, tiles, near, near_x, y_out, out, scratch):
+def anc_turn(tiles, near, near_x, y_out, out, scratch):
     level_rows(0, tiles, y_out)
-    t = z_rows(where, y_out, near.shape[1] * CORES)
+    t = z_rows(y_out, near.shape[1] * CORES)
     solve_level(0, t.astype(BF16), 0, near, near_x, out, scratch)
 
 
-def anc_start(where, *refs):
+def anc_start(*refs):
     out = refs[-1]
-    out[...] = sum(z_rows(where, values, out.shape[1]) for values in refs[:-1])
+    out[...] = sum(z_rows(values, out.shape[1]) for values in refs[:-1])
 
 
 def added(*refs):
@@ -309,20 +336,19 @@
         out[i] = scratch[:, r * wide : (r + 1) * wide].astype(BF16)
 
 
-def sub_turn(pairs, layers, levels, where, subtree, w, tiles, y_own, own, other, kept, out, scratch):
+def sub_turn(pairs, levels, w, pick, tiles, y_own, own, other, kept, out, scratch):
     scratch[...] = tiles[...].astype(F32)
     picked = []
     for e in range(levels):
-        id_here = ancestor(subtree, where[4], layers, levels, e)
         value = 0.0
         for a in range(*level_span(e)):
-            value = value + jnp.where(id_here == a, 1.0, 0.0) * scratch[:, a, :]
+            value = value + pick[e, a : a + 1, :] * scratch[:, a, :]
         picked.append(value.astype(BF16))
     for m in range(SUB_NODES):
         value = y_own[m]
         for e in range(levels):
             p = pairs.sub[m, 0, e]
-            value = value - w[p, 1].astype(F32) * times_t(picked[e], block(own, other, SUB_NODES + p))
+            value = value - w[p : p + 1, :] * times_t(picked[e], block(own, other, SUB_NODES + p))
         if m == 0:
             to_all(out, value)
         else:
@@ -339,7 +365,7 @@
     z = total(tiles).astype(BF16)
     for m in LEAVES:
         p = pairs.sub[m, 1, 0]
-        value = kept[m - 1] - w[p, 1].astype(F32) * times_t(z, block(own, other, SUB_NODES + p))
+        value = kept[m - 1] - w[p : p + 1, :] * times_t(z, block(own, other, SUB_NODES + p))
         for i in range(out.shape[0]):
             out[i, m - 1] = value.astype(BF16)
 
@@ -388,7 +414,6 @@
     low = (sub_lower, swapped(sub_lower))
     rhs_there = swapped(sub_rhs)
     anc_low = gathered(anc_lower)
-    anc_up = gathered(anc_upper)
 
     def diagonal(depth):
         return list(range(*level_span(depth)))
@@ -417,7 +442,7 @@
     rhs, tiles = run(
         sub_leaf_solve,
         (shape(BF16, SUB_NODES, cols, pair_rows), shape(BF16, nz, 2, cols, wide)),
-        (where,),
+        (),
         (rhs_there, low[1]),
         (
             pltpu.VMEM((len(LEAVES), own, wide), BF16),
@@ -428,26 +453,38 @@
     )
     tiles, anc_rhs = tied(tiles, anc_rhs)
     anc_there = swapped(anc_rhs)
-    choose, given8 = run(
-        part(anc_prepare, layers, nrow),
-        (shape(F32, levels, ROWS8, layers * nrow), acc_shape),
-        (where, layer_subtree),
+    weights = shape(F32, sub_pattern.shape[0], pair_rows)
+    choose, given8, low_w, up_w, pick, local_low = run(
+        part(anc_prepare, pairs, layers, nrow),
+        (
+            shape(F32, levels, ROWS8, layers * nrow),
+            acc_shape,
+            weights,
+            weights,
+            shape(F32, levels, ROWS8, wide),
+            shape(BF16, len(LEAVES), own, wide),
+        ),
+        (where, layer_subtree, sub_pattern),
         (anc_rhs, anc_there),
-    )
+        (pltpu.SemaphoreType.DMA((len(LEAVES),)),),
+        (sub_lower,),
+    )
+    given8, anc_upper = tied(given8, anc_upper)
+    anc_up = gathered(anc_upper)
     tiles = exchange(tiles, "z")
-    tiles, given8, choose = tied(tiles, given8, choose)
+    tiles, given8, choose, low_w, local_low = tied(tiles, given8, choose, low_w, local_low)
     y_leaf, tiles = run(
         part(sub_leaf_update, pairs),
         (shape(BF16, 2, cols, wide), shape(BF16, nrow, cols, pair_rows)),
-        (sub_pattern,),
-        (tiles, *low),
+        (),
+        (low_w, tiles, local_low, low[1]),
     )
     tiles = exchange(tiles, "row")
     so_far = run(
         part(sub_leaf_anc, pairs, levels),
         shape(F32, levels, cols, pair_rows),
-        (sub_pattern,),
-        (y_leaf, *low),
+        (),
+        (low_w, y_leaf, *low),
     )
     tiles, so_far = tied(tiles, so_far)
     tiles = run(sub_root_solve, shape(BF16, nz, cols, wide), (), (tiles, rhs, *low))
@@ -456,8 +493,8 @@
     y_root, tiles = run(
         part(sub_root_anc, pairs, levels),
         (shape(BF16, cols, wide), shape(BF16, layers * nrow, ROWS8, pair_rows)),
-        (sub_pattern,),
-        (tiles, so_far, *low),
+        (),
+        (low_w, tiles, so_far, *low),
         (c_scratch,),
     )
     tiles = exchange(tiles, ("gz", "row"))
@@ -492,11 +529,11 @@
     near = loaded(diagonal(0), anc_up)
     tiles, *near = tied(tiles, *near)
     y8, tiles = run(
-        anc_turn, (row_shape, level_shape(0)), (where,), (tiles, *near), (scr8,)
+        anc_turn, (row_shape, level_shape(0)), (), (tiles, *near), (scr8,)
     )
     y_parts.append(y8)
     tiles = exchange(tiles, "z")
-    start8 = run(anc_start, acc_shape, (where,), y_parts)
+    start8 = run(anc_start, acc_shape, (), y_parts)
     tiles, start8 = tied(tiles, start8)
     z8 = None
     for depth in range(1, levels):
@@ -532,14 +569,14 @@
     )
     z_all = exchange(tiles, ("gz", "row"))
     y_own = run(sub_pieces, shape(F32, SUB_NODES, cols, pair_rows), (where,), (y_root, y_leaf))
-    z_all, y_own, up_there = tied(z_all, y_own, up[1])
+    z_all, y_own, up_there, up_w, pick = tied(z_all, y_own, up[1], up_w, pick)
     up = (up[0], up_there)
 
     kept, tiles = run(
-        part(sub_turn, pairs, layers, levels),
+        part(sub_turn, pairs, levels),
         (shape(F32, 2, cols, pair_rows), shape(BF16, nrow, cols, pair_rows)),
-        (where, layer_subtree, sub_pattern),
-        (z_all, y_own, *up),
+        (),
+        (up_w, pick, z_all, y_own, *up),
         (pltpu.VMEM(z_all.shape, F32),),
     )
     tiles = exchange(tiles, "row")
@@ -564,8 +601,8 @@
     tiles = run(
         part(sub_leaf_back, pairs),
         shape(BF16, nrow, 2, cols, pair_rows),
-        (sub_pattern,),
-        (tiles, kept, *up),
+        (),
+        (up_w, tiles, kept, *up),
     )
     tiles = exchange(tiles, "row")
     packed = -(-SUB_NODES * cols // 128) * 128

time: 233 us -> 232 us (level)
  blocking collectives: 17.1 us -> 33.8 us
  waiting for transfers between devices: 68.9 us -> 62.8 us
  Pallas kernels: 38.3 us -> 33.3 us
  starting transfers between devices: 86.9 us -> 82 us
    all_to_all x2 -> x3, blocking collectives: 17.1 us -> 33.8 us  [exchange(): return lax.all_to_all(array, axes, 0, 0, tiled=True)]
    all_to_all x13 -> x12, waiting for transfers between devices: 65.8 us -> 60.2 us  [exchange(): return lax.all_to_all(array, axes, 0, 0, tiled=True)]
    pallas_call x28, Pallas kernels: 38.3 us -> 33.3 us  [run(): pl.pallas_call(body, out_shape=outs, in_specs=in_specs, out_specs=spec if...]
    all_to_all x13 -> x12, starting transfers between devices: 55.3 us -> 50.7 us  [exchange(): return lax.all_to_all(array, axes, 0, 0, tiled=True)]
  transfers between devices with their start and end apart: 20 -> 19, of which waited for: 14 -> 13; matrix products, arithmetic and copies ran while one was open for 1% -> 1% of each run, Pallas kernels for 13% -> 12%
where the time goes in v8:
time: 232 us; the launch traced here: 231 us
  starting transfers between devices  82 us (35%)
  waiting for transfers between devices  62.8 us (27%)
  blocking collectives  33.8 us (15%)
  Pallas kernels  33.3 us (14%)
  between operations  14.4 us (6%)
  local copies, waits for them, and re-layouts  3.57 us (2%)
    all_to_all x12, waiting for transfers between devices, exchange(): return lax.all_to_all(array, axes, 0, 0, tiled=True)  60.2 us
    all_to_all x12, starting transfers between devices, exchange(): return lax.all_to_all(array, axes, 0, 0, tiled=True)  50.7 us
    all_to_all x3, blocking collectives, exchange(): return lax.all_to_all(array, axes, 0, 0, tiled=True)  33.8 us
    pallas_call x28, Pallas kernels, run(): pl.pallas_call(body, out_shape=outs, in_specs=in_specs, out_specs=spec if...  33.3 us
    ppermute x5, starting transfers between devices, swapped(): return lax.ppermute(array, 'core', [(0, 1), (1, 0)])  31.2 us
  transfers between devices with their start and end apart: 19, of which 13 were waited for; matrix products, arithmetic and copies ran while one was open for 1% of the time, Pallas kernels for 12%

profile of v8, /device:TPU:1, one launch (start us, length us, event | category | flops | bytes accessed | tf_op | source)
XLA Modules:
  0.0 230.5 jit_solution(2320109532491883965)
XLA Ops:
  8.0 8.7 %collective-permute-start.1 = (bf16[14,64,256]{2,1,0:T(8,128)(2,1)}, bf16[14,64,256]{2,1,0:T(8,128)(2,1)S(1)}, u32[]{:S(2)}, u32[]{:S(2)}) collective-permute-start(bf16[14,64,256]{2,1,0:T(8,128)(2,1)} %own.7), channel_id=1, source_target_pairs={{0,1},{1,0},{2,3},{3,2},{4,5},{5,4},{6,7},{7,6},{8,9},{9,8},{10,11... | collective-permute-start | bytes 1376264 | tf_op jit(solution)/shard_map/ppermute | solution.py:33
  27.7 16.7 %all_to_all.75.tiles = bf16[8,2,32,256]{3,2,1,0:T(8,128)(2,1)S(1)} all-to-all(bf16[8,2,32,256]{3,2,1,0:T(8,128)(2,1)S(1)} %get-tuple-element.88), channel_id=1, replica_groups=mesh['gz'=8,'row'=4,'z'=8,'core'=2] {'z'}, dimensions={0} | all-to-all | bytes 524288 | tf_op jit(solution)/shard_map/all_to_all | solution.py:406
  45.2 4.0 %all-to-all-start.1 = ((bf16[4,32,128]{2,1,0:T(8,128)(2,1)}), bf16[4,32,128]{2,1,0:T(8,128)(2,1)S(1)}, u32[]{:S(2)}, u32[]{:S(2)}) async-start(bf16[4,32,128]{2,1,0:T(8,128)(2,1)} %get-tuple-element.98), calls=%async_computation.1 | async-start | bytes 65536 | tf_op jit(solution)/shard_map/all_to_all | solution.py:406
  49.4 4.1 %all-to-all-done.1.tiles = bf16[4,32,128]{2,1,0:T(8,128)(2,1)S(1)} async-done(((bf16[4,32,128]{2,1,0:T(8,128)(2,1)}), bf16[4,32,128]{2,1,0:T(8,128)(2,1)S(1)}, u32[]{:S(2)}, u32[]{:S(2)}) %all-to-all-start.1) | async-done | bytes 32800 | tf_op jit(solution)/shard_map/all_to_all | solution.py:406
  53.6 10.4 %all_to_all.76.tiles = bf16[8,32,256]{2,1,0:T(8,128)(2,1)S(1)} all-to-all(bf16[8,32,256]{2,1,0:T(8,128)(2,1)S(1)} %shard_map.99), channel_id=1, replica_groups=mesh['gz'=8,'row'=4,'z'=8,'core'=2] {'z'}, dimensions={0} | all-to-all | bytes 262144 | tf_op jit(solution)/shard_map/all_to_all | solution.py:406
  64.9 7.9 %all-to-all-start.3 = ((bf16[32,8,128]{2,1,0:T(8,128)(2,1)}), bf16[32,8,128]{2,1,0:T(8,128)(2,1)S(1)}, u32[]{:S(2)}, u32[]{:S(2)}) async-start(bf16[32,8,128]{2,1,0:T(8,128)(2,1)} %get-tuple-element.103), calls=%async_computation.3 | async-start | bytes 131072 | tf_op jit(solution)/shard_map/all_to_all | solution.py:406
  75.0 6.7 %all-to-all-done.3.tiles = bf16[32,8,128]{2,1,0:T(8,128)(2,1)S(1)} async-done(((bf16[32,8,128]{2,1,0:T(8,128)(2,1)}), bf16[32,8,128]{2,1,0:T(8,128)(2,1)S(1)}, u32[]{:S(2)}, u32[]{:S(2)}) %all-to-all-start.3) | async-done | bytes 65568 | tf_op jit(solution)/shard_map/all_to_all | solution.py:406
  82.7 3.3 %all-to-all-start.4 = ((bf16[8,4,1024]{2,1,0:T(4,128)(2,1)}), bf16[8,4,1024]{2,1,0:T(4,128)(2,1)S(1)}, u32[]{:S(2)}, u32[]{:S(2)}) async-start(bf16[8,4,1024]{2,1,0:T(4,128)(2,1)} %get-tuple-element.111), calls=%async_computation.4 | async-start | bytes 131072 | tf_op jit(solution)/shard_map/all_to_all | solution.py:406
  86.1 2.4 %shard_map.103 = (bf16[6,64,1024]{2,1,0:T(8,128)(2,1)S(1)}, bf16[6,64,1024]{2,1,0:T(8,128)(2,1)S(1)}) custom-call(s32[6]{0:T(128)S(1)} %stack.31.where, bf16[8,17,64,256]{3,2,1,0:T(8,128)(2,1)} %bitcast.21), custom_call_target="tpu_custom_call" | custom-call | tf_op jit(solution)/shard_map/pallas_call | solution.py:47
  88.6 4.7 %all-to-all-done.4.tiles = bf16[8,4,1024]{2,1,0:T(4,128)(2,1)S(1)} async-done(((bf16[8,4,1024]{2,1,0:T(4,128)(2,1)}), bf16[8,4,1024]{2,1,0:T(4,128)(2,1)S(1)}, u32[]{:S(2)}, u32[]{:S(2)}) %all-to-all-start.4) | async-done | bytes 65568 | tf_op jit(solution)/shard_map/all_to_all | solution.py:406
  94.6 3.3 %all-to-all-start.5 = ((bf16[8,2,1024]{2,1,0:T(2,128)(2,1)}), bf16[8,2,1024]{2,1,0:T(2,128)(2,1)S(1)}, u32[]{:S(2)}, u32[]{:S(2)}) async-start(bf16[8,2,1024]{2,1,0:T(2,128)(2,1)} %get-tuple-element.118), calls=%async_computation.5 | async-start | bytes 65536 | tf_op jit(solution)/shard_map/all_to_all | solution.py:406
  99.8 2.4 %shard_map.105.acc_in = f32[8,128]{1,0:T(8,128)S(1)} custom-call(s32[6]{0:T(128)S(1)} %stack.31.where, f32[8,1024]{1,0:T(8,128)S(1)} %get-tuple-element.119.values.refs_0_, f32[8,128]{1,0:T(8,128)S(1)} %get-tuple-element.120.acc_in, bf16[8,17,64,256]{3,2,1,0:T(8,128)(2,1)} %bitcast.23), custom_call_target="tpu_custom_call" | custom-call | tf_op jit(solution)/shard_map/pallas_call | solution.py:47
  102.1 2.6 %all-to-all-done.5.tiles = bf16[8,2,1024]{2,1,0:T(2,128)(2,1)S(1)} async-done(((bf16[8,2,1024]{2,1,0:T(2,128)(2,1)}), bf16[8,2,1024]{2,1,0:T(2,128)(2,1)S(1)}, u32[]{:S(2)}, u32[]{:S(2)}) %all-to-all-start.5) | async-done | bytes 32800 | tf_op jit(solution)/shard_map/all_to_all | solution.py:406
  105.8 4.0 %all-to-all-start.6 = ((bf16[8,2,1024]{2,1,0:T(2,128)(2,1)}), bf16[8,2,1024]{2,1,0:T(2,128)(2,1)S(1)}, u32[]{:S(2)}, u32[]{:S(2)}) async-start(bf16[8,2,1024]{2,1,0:T(2,128)(2,1)} %get-tuple-element.128), calls=%async_computation.6 | async-start | bytes 65536 | tf_op jit(solution)/shard_map/all_to_all | solution.py:406
  111.3 5.4 %all-to-all-done.6.tiles = bf16[8,2,1024]{2,1,0:T(2,128)(2,1)S(1)} async-done(((bf16[8,2,1024]{2,1,0:T(2,128)(2,1)}), bf16[8,2,1024]{2,1,0:T(2,128)(2,1)S(1)}, u32[]{:S(2)}, u32[]{:S(2)}) %all-to-all-start.6) | async-done | bytes 32800 | tf_op jit(solution)/shard_map/all_to_all | solution.py:406
  117.5 3.3 %all-to-all-start.7 = ((bf16[8,2,1024]{2,1,0:T(2,128)(2,1)}), bf16[8,2,1024]{2,1,0:T(2,128)(2,1)S(1)}, u32[]{:S(2)}, u32[]{:S(2)}) async-start(bf16[8,2,1024]{2,1,0:T(2,128)(2,1)} %get-tuple-element.135), calls=%async_computation.7 | async-start | bytes 65536 | tf_op jit(solution)/shard_map/all_to_all | solution.py:406
  123.0 4.6 %all-to-all-done.7.tiles = bf16[8,2,1024]{2,1,0:T(2,128)(2,1)S(1)} async-done(((bf16[8,2,1024]{2,1,0:T(2,128)(2,1)}), bf16[8,2,1024]{2,1,0:T(2,128)(2,1)S(1)}, u32[]{:S(2)}, u32[]{:S(2)}) %all-to-all-start.7) | async-done | bytes 32800 | tf_op jit(solution)/shard_map/all_to_all | solution.py:406
  128.9 3.3 %all-to-all-start.8 = ((bf16[8,2,1024]{2,1,0:T(2,128)(2,1)}), bf16[8,2,1024]{2,1,0:T(2,128)(2,1)S(1)}, u32[]{:S(2)}, u32[]{:S(2)}) async-start(bf16[8,2,1024]{2,1,0:T(2,128)(2,1)} %get-tuple-element.145), calls=%async_computation.8 | async-start | bytes 65536 | tf_op jit(solution)/shard_map/all_to_all | solution.py:406
  132.2 2.7 %shard_map.113 = (bf16[8,64,1024]{2,1,0:T(8,128)(2,1)S(1)}, bf16[8,64,1024]{2,1,0:T(8,128)(2,1)S(1)}) custom-call(s32[6]{0:T(128)S(1)} %stack.31.where, bf16[8,17,64,256]{3,2,1,0:T(8,128)(2,1)} %bitcast.26), custom_call_target="tpu_custom_call" | custom-call | tf_op jit(solution)/shard_map/pallas_call | solution.py:47
  135.0 2.4 %shard_map.114.acc_in = f32[8,128]{1,0:T(8,128)S(1)} custom-call(s32[6]{0:T(128)S(1)} %stack.31.where, f32[8,1024]{1,0:T(8,128)S(1)} %get-tuple-element.149.values.refs_0_, f32[8,128]{1,0:T(8,128)S(1)} %shard_map.110.acc_in, bf16[8,17,64,256]{3,2,1,0:T(8,128)(2,1)} %bitcast.27), custom_call_target="tpu_custom_call" | custom-call | tf_op jit(solution)/shard_map/pallas_call | solution.py:47
  140.6 11.5 %collective-permute-start.3 = (bf16[14,64,256]{2,1,0:T(8,128)(2,1)S(1)}, bf16[14,64,256]{2,1,0:T(8,128)(2,1)S(1)}, u32[]{:S(2)}, u32[]{:S(2)}) collective-permute-start(bf16[14,64,256]{2,1,0:T(8,128)(2,1)S(1)} %copy-done.1), channel_id=1, source_target_pairs={{0,1},{1,0},{2,3},{3,2},{4,5},{5,4},{6,7},{7,6},{8,9},{9,8},{10,11... | collective-permute-start | bytes 1376264 | tf_op jit(solution)/shard_map/ppermute | solution.py:33
  152.0 4.1 %all-to-all-start.9 = ((bf16[8,4,1024]{2,1,0:T(4,128)(2,1)}), bf16[8,4,1024]{2,1,0:T(4,128)(2,1)S(1)}, u32[]{:S(2)}, u32[]{:S(2)}) async-start(bf16[8,4,1024]{2,1,0:T(4,128)(2,1)} %get-tuple-element.155), calls=%async_computation.9 | async-start | bytes 131072 | tf_op jit(solution)/shard_map/all_to_all | solution.py:406
  156.1 7.1 %all-to-all-done.9.tiles = bf16[8,4,1024]{2,1,0:T(4,128)(2,1)S(1)} async-done(((bf16[8,4,1024]{2,1,0:T(4,128)(2,1)}), bf16[8,4,1024]{2,1,0:T(4,128)(2,1)S(1)}, u32[]{:S(2)}, u32[]{:S(2)}) %all-to-all-start.9) | async-done | bytes 65568 | tf_op jit(solution)/shard_map/all_to_all | solution.py:406
  163.9 3.8 %all-to-all-start.10 = ((bf16[32,8,256]{2,1,0:T(8,128)(2,1)}), bf16[32,8,256]{2,1,0:T(8,128)(2,1)S(1)}, u32[]{:S(2)}, u32[]{:S(2)}) async-start(bf16[32,8,256]{2,1,0:T(8,128)(2,1)} %shard_map.117), calls=%async_computation.10 | async-start | bytes 262144 | tf_op jit(solution)/shard_map/all_to_all | solution.py:406
  168.4 8.8 %all-to-all-done.10.tiles = bf16[32,8,256]{2,1,0:T(8,128)(2,1)S(1)} async-done(((bf16[32,8,256]{2,1,0:T(8,128)(2,1)}), bf16[32,8,256]{2,1,0:T(8,128)(2,1)S(1)}, u32[]{:S(2)}, u32[]{:S(2)}) %all-to-all-start.10) | async-done | bytes 131104 | tf_op jit(solution)/shard_map/all_to_all | solution.py:406
  177.5 6.6 %all_to_all.77.tiles = bf16[4,32,128]{2,1,0:T(8,128)(2,1)S(1)} all-to-all(bf16[4,32,128]{2,1,0:T(8,128)(2,1)S(1)} %get-tuple-element.168), channel_id=1, replica_groups=mesh['gz'=8,'row'=4,'z'=8,'core'=2] {'row'}, dimensions={0} | all-to-all | bytes 65536 | tf_op jit(solution)/shard_map/all_to_all | solution.py:406
  185.0 3.4 %all-to-all-start.12 = ((bf16[8,32,256]{2,1,0:T(8,128)(2,1)}), bf16[8,32,256]{2,1,0:T(8,128)(2,1)S(1)}, u32[]{:S(2)}, u32[]{:S(2)}) async-start(bf16[8,32,256]{2,1,0:T(8,128)(2,1)} %get-tuple-element.169), calls=%async_computation.12 | async-start | bytes 262144 | tf_op jit(solution)/shard_map/all_to_all | solution.py:406
  188.4 7.8 %all-to-all-done.12.tiles = bf16[8,32,256]{2,1,0:T(8,128)(2,1)S(1)} async-done(((bf16[8,32,256]{2,1,0:T(8,128)(2,1)}), bf16[8,32,256]{2,1,0:T(8,128)(2,1)S(1)}, u32[]{:S(2)}, u32[]{:S(2)}) %all-to-all-start.12) | async-done | bytes 131104 | tf_op jit(solution)/shard_map/all_to_all | solution.py:406
  197.0 3.3 %all-to-all-start.13 = ((bf16[4,2,32,128]{3,2,1,0:T(8,128)(2,1)}), bf16[4,2,32,128]{3,2,1,0:T(8,128)(2,1)S(1)}, u32[]{:S(2)}, u32[]{:S(2)}) async-start(bf16[4,2,32,128]{3,2,1,0:T(8,128)(2,1)} %shard_map.121), calls=%async_computation.13 | async-start | bytes 131072 | tf_op jit(solution)/shard_map/all_to_all | solution.py:406
  200.4 7.0 %collective-permute-start.4 = (bf16[7,16,32]{1,0,2:T(8,128)(2,1)S(1)}, bf16[7,16,32]{1,0,2:T(8,128)(2,1)S(1)}, u32[]{:S(2)}, u32[]{:S(2)}) collective-permute-start(bf16[7,16,32]{1,0,2:T(8,128)(2,1)S(1)} %dynamic-slice_bitcast_fusion.1), channel_id=1, source_target_pairs={{0,1},{1,0},{2,3},{3,2},{4,5},{5,4},{6,7},{7,6},{8,9},{9,8},{10,11... | collective-permute-start | bytes 21512 | tf_op jit(solution)/shard_map/ppermute | solution.py:33
  208.2 6.8 %all-to-all-start.14 = ((bf16[16,16,128]{2,1,0:T(8,128)(2,1)}), bf16[16,16,128]{2,1,0:T(8,128)(2,1)S(1)}, u32[]{:S(2)}, u32[]{:S(2)}) async-start(bf16[16,16,128]{2,1,0:T(8,128)(2,1)} %shard_map.122), calls=%async_computation.14 | async-start | bytes 131072 | tf_op jit(solution)/shard_map/all_to_all | solution.py:406
  216.1 6.8 %all-to-all-done.14 = bf16[16,16,128]{2,1,0:T(8,128)(2,1)S(1)} async-done(((bf16[16,16,128]{2,1,0:T(8,128)(2,1)}), bf16[16,16,128]{2,1,0:T(8,128)(2,1)S(1)}, u32[]{:S(2)}, u32[]{:S(2)}) %all-to-all-start.14) | async-done | bytes 65568 | tf_op jit(solution)/shard_map/all_to_all | solution.py:406
  (58 shorter events, 36.0 us)
Async XLA Ops:
  7.2 42.0 %copy-start = (bf16[14,64,256]{2,1,0:T(8,128)(2,1)S(1)}, bf16[14,64,256]{2,1,0:T(8,128)(2,1)}, u32[]{:S(2)}) copy-start(bf16[14,64,256]{2,1,0:T(8,128)(2,1)} %own.7) | copy-start | bytes 1376260
  7.2 65.7 %all-gather.5.cloned.1.call-start = ((), (), s32[]{:S(2)}) async-start(), calls=%async_computation.15 | async-start | bytes 5013504 | tf_op jit(solution)/shard_map/all_gather | solution.py:403
  7.9 101.9 %all-gather.7.cloned.1.call-start = ((), (), s32[]{:S(2)}) async-start(), calls=%async_computation.16 | async-start | bytes 5013504 | tf_op jit(solution)/shard_map/all_gather | solution.py:403
  8.0 12.1 %collective-permute-start.1 = (bf16[14,64,256]{2,1,0:T(8,128)(2,1)}, bf16[14,64,256]{2,1,0:T(8,128)(2,1)S(1)}, u32[]{:S(2)}, u32[]{:S(2)}) collective-permute-start(bf16[14,64,256]{2,1,0:T(8,128)(2,1)} %own.7), channel_id=1, source_target_pairs={{0,1},{1,0},{2,3},{3,2},{4,5},{5,4},{6,7},{7,6},{8,9},{9,8},{10,11... | collective-permute-start | bytes 1376264 | tf_op jit(solution)/shard_map/ppermute | solution.py:33
  16.7 3.3 %collective-permute-start = (bf16[3,64,64]{2,1,0:T(8,128)(2,1)}, bf16[3,64,64]{2,1,0:T(8,128)(2,1)S(1)}, u32[]{:S(2)}, u32[]{:S(2)}) collective-permute-start(bf16[3,64,64]{2,1,0:T(8,128)(2,1)} %here.1), channel_id=1, source_target_pairs={{0,1},{1,0},{2,3},{3,2},{4,5},{5,4},{6,7},{7,6},{8,9},{9,8},{10,11... | collective-permute-start | bytes 73736 | tf_op jit(solution)/shard_map/ppermute | solution.py:33
  21.1 3.4 %collective-permute-start.2 = (bf16[7,64,64]{2,1,0:T(8,128)(2,1)}, bf16[7,64,64]{2,1,0:T(8,128)(2,1)S(1)}, u32[]{:S(2)}, u32[]{:S(2)}) collective-permute-start(bf16[7,64,64]{2,1,0:T(8,128)(2,1)} %here.2), channel_id=1, source_target_pairs={{0,1},{1,0},{2,3},{3,2},{4,5},{5,4},{6,7},{7,6},{8,9},{9,8},{10,11... | collective-permute-start | bytes 172040 | tf_op jit(solution)/shard_map/ppermute | solution.py:33
  24.6 0.9 copy-start.2
  25.5 0.7 copy-start.3
  45.2 8.3 %all-to-all-start.1 = ((bf16[4,32,128]{2,1,0:T(8,128)(2,1)}), bf16[4,32,128]{2,1,0:T(8,128)(2,1)S(1)}, u32[]{:S(2)}, u32[]{:S(2)}) async-start(bf16[4,32,128]{2,1,0:T(8,128)(2,1)} %get-tuple-element.98), calls=%async_computation.1 | async-start | bytes 65536 | tf_op jit(solution)/shard_map/all_to_all | solution.py:406
  64.9 16.8 %all-to-all-start.3 = ((bf16[32,8,128]{2,1,0:T(8,128)(2,1)}), bf16[32,8,128]{2,1,0:T(8,128)(2,1)S(1)}, u32[]{:S(2)}, u32[]{:S(2)}) async-start(bf16[32,8,128]{2,1,0:T(8,128)(2,1)} %get-tuple-element.103), calls=%async_computation.3 | async-start | bytes 131072 | tf_op jit(solution)/shard_map/all_to_all | solution.py:406
  82.7 10.5 %all-to-all-start.4 = ((bf16[8,4,1024]{2,1,0:T(4,128)(2,1)}), bf16[8,4,1024]{2,1,0:T(4,128)(2,1)S(1)}, u32[]{:S(2)}, u32[]{:S(2)}) async-start(bf16[8,4,1024]{2,1,0:T(4,128)(2,1)} %get-tuple-element.111), calls=%async_computation.4 | async-start | bytes 131072 | tf_op jit(solution)/shard_map/all_to_all | solution.py:406
  94.6 10.1 %all-to-all-start.5 = ((bf16[8,2,1024]{2,1,0:T(2,128)(2,1)}), bf16[8,2,1024]{2,1,0:T(2,128)(2,1)S(1)}, u32[]{:S(2)}, u32[]{:S(2)}) async-start(bf16[8,2,1024]{2,1,0:T(2,128)(2,1)} %get-tuple-element.118), calls=%async_computation.5 | async-start | bytes 65536 | tf_op jit(solution)/shard_map/all_to_all | solution.py:406
  105.8 10.9 %all-to-all-start.6 = ((bf16[8,2,1024]{2,1,0:T(2,128)(2,1)}), bf16[8,2,1024]{2,1,0:T(2,128)(2,1)S(1)}, u32[]{:S(2)}, u32[]{:S(2)}) async-start(bf16[8,2,1024]{2,1,0:T(2,128)(2,1)} %get-tuple-element.128), calls=%async_computation.6 | async-start | bytes 65536 | tf_op jit(solution)/shard_map/all_to_all | solution.py:406
  117.5 10.1 %all-to-all-start.7 = ((bf16[8,2,1024]{2,1,0:T(2,128)(2,1)}), bf16[8,2,1024]{2,1,0:T(2,128)(2,1)S(1)}, u32[]{:S(2)}, u32[]{:S(2)}) async-start(bf16[8,2,1024]{2,1,0:T(2,128)(2,1)} %get-tuple-element.135), calls=%async_computation.7 | async-start | bytes 65536 | tf_op jit(solution)/shard_map/all_to_all | solution.py:406
  128.9 10.1 %all-to-all-start.8 = ((bf16[8,2,1024]{2,1,0:T(2,128)(2,1)}), bf16[8,2,1024]{2,1,0:T(2,128)(2,1)S(1)}, u32[]{:S(2)}, u32[]{:S(2)}) async-start(bf16[8,2,1024]{2,1,0:T(2,128)(2,1)} %get-tuple-element.145), calls=%async_computation.8 | async-start | bytes 65536 | tf_op jit(solution)/shard_map/all_to_all | solution.py:406
  132.2 8.3 %copy-start.1 = (bf16[14,64,256]{2,1,0:T(8,128)(2,1)S(1)}, bf16[14,64,256]{2,1,0:T(8,128)(2,1)}, u32[]{:S(2)}) copy-start(bf16[14,64,256]{2,1,0:T(8,128)(2,1)} %own.11) | copy-start | bytes 1376260
  140.6 36.6 %collective-permute-start.3 = (bf16[14,64,256]{2,1,0:T(8,128)(2,1)S(1)}, bf16[14,64,256]{2,1,0:T(8,128)(2,1)S(1)}, u32[]{:S(2)}, u32[]{:S(2)}) collective-permute-start(bf16[14,64,256]{2,1,0:T(8,128)(2,1)S(1)} %copy-done.1), channel_id=1, source_target_pairs={{0,1},{1,0},{2,3},{3,2},{4,5},{5,4},{6,7},{7,6},{8,9},{9,8},{10,11... | collective-permute-start | bytes 1376264 | tf_op jit(solution)/shard_map/ppermute | solution.py:33
  152.0 11.2 %all-to-all-start.9 = ((bf16[8,4,1024]{2,1,0:T(4,128)(2,1)}), bf16[8,4,1024]{2,1,0:T(4,128)(2,1)S(1)}, u32[]{:S(2)}, u32[]{:S(2)}) async-start(bf16[8,4,1024]{2,1,0:T(4,128)(2,1)} %get-tuple-element.155), calls=%async_computation.9 | async-start | bytes 131072 | tf_op jit(solution)/shard_map/all_to_all | solution.py:406
  163.9 13.3 %all-to-all-start.10 = ((bf16[32,8,256]{2,1,0:T(8,128)(2,1)}), bf16[32,8,256]{2,1,0:T(8,128)(2,1)S(1)}, u32[]{:S(2)}, u32[]{:S(2)}) async-start(bf16[32,8,256]{2,1,0:T(8,128)(2,1)} %shard_map.117), calls=%async_computation.10 | async-start | bytes 262144 | tf_op jit(solution)/shard_map/all_to_all | solution.py:406
  185.0 11.2 %all-to-all-start.12 = ((bf16[8,32,256]{2,1,0:T(8,128)(2,1)}), bf16[8,32,256]{2,1,0:T(8,128)(2,1)S(1)}, u32[]{:S(2)}, u32[]{:S(2)}) async-start(bf16[8,32,256]{2,1,0:T(8,128)(2,1)} %get-tuple-element.169), calls=%async_computation.12 | async-start | bytes 262144 | tf_op jit(solution)/shard_map/all_to_all | solution.py:406
  197.0 10.4 %all-to-all-start.13 = ((bf16[4,2,32,128]{3,2,1,0:T(8,128)(2,1)}), bf16[4,2,32,128]{3,2,1,0:T(8,128)(2,1)S(1)}, u32[]{:S(2)}, u32[]{:S(2)}) async-start(bf16[4,2,32,128]{3,2,1,0:T(8,128)(2,1)} %shard_map.121), calls=%async_computation.13 | async-start | bytes 131072 | tf_op jit(solution)/shard_map/all_to_all | solution.py:406
  200.4 14.7 %collective-permute-start.4 = (bf16[7,16,32]{1,0,2:T(8,128)(2,1)S(1)}, bf16[7,16,32]{1,0,2:T(8,128)(2,1)S(1)}, u32[]{:S(2)}, u32[]{:S(2)}) collective-permute-start(bf16[7,16,32]{1,0,2:T(8,128)(2,1)S(1)} %dynamic-slice_bitcast_fusion.1), channel_id=1, source_target_pairs={{0,1},{1,0},{2,3},{3,2},{4,5},{5,4},{6,7},{7,6},{8,9},{9,8},{10,11... | collective-permute-start | bytes 21512 | tf_op jit(solution)/shard_map/ppermute | solution.py:33
  208.2 14.7 %all-to-all-start.14 = ((bf16[16,16,128]{2,1,0:T(8,128)(2,1)}), bf16[16,16,128]{2,1,0:T(8,128)(2,1)S(1)}, u32[]{:S(2)}, u32[]{:S(2)}) async-start(bf16[16,16,128]{2,1,0:T(8,128)(2,1)} %shard_map.122), calls=%async_computation.14 | async-start | bytes 131072 | tf_op jit(solution)/shard_map/all_to_all | solution.py:406
Sparse Core Ops, SparseCore 0:
  10.1 44.3 all-gather.4
  56.6 39.5 all-gather.6

commit v9 on v8

--- a/solution.py
+++ b/solution.py
@@ -143,22 +143,20 @@
     to_all(out, value)
 
 
-def sub_leaf_anc(pairs, levels, w, y, own, other, out):
-    for e in range(levels):
-        out[e] = sum(sub_low(y[m - 1], w, pairs, own, other, m, 0, e) for m in LEAVES)
-
-
 def sub_root_solve(tiles, rhs, own, other, out):
     given = (rhs[0].astype(F32) - total(tiles)).astype(BF16)
     to_all(out, times(given, block(own, other, 0)))
 
 
-def sub_root_anc(pairs, levels, w, tiles, so_far, own, other, y_out, out, scratch):
+def sub_root_anc(pairs, levels, w, tiles, y_leaf, own, other, y_out, out, scratch):
     y = total(tiles).astype(BF16)
     y_out[...] = y
     scratch[...] = jnp.zeros_like(scratch)
     for e in range(levels):
-        scratch[:, e, :] = so_far[e] + sub_low(y, w, pairs, own, other, 0, 0, e)
+        value = sub_low(y, w, pairs, own, other, 0, 0, e)
+        for m in LEAVES:
+            value = value + sub_low(y_leaf[m - 1], w, pairs, own, other, m, 0, e)
+        scratch[:, e, :] = value
     out[...] = scratch[...].astype(BF16)
 
 
@@ -355,6 +353,18 @@
             kept[m - 1] = value
 
 
+def anc_pieces(tiles, here, there, scratch):
+    core, z = position()
+    scratch[...] = tiles[...].astype(F32)
+    rows = here.shape[1]
+    line = lax.broadcasted_iota(jnp.int32, (rows, tiles.shape[2]), 0)
+    lane = lax.broadcasted_iota(jnp.int32, (rows, tiles.shape[2]), 1)
+    for out, which in ((here, core), (there, 1 - core)):
+        pick = jnp.where(lane == (z * CORES + which) * rows + line, 1.0, 0.0).astype(BF16)
+        for a in range(here.shape[0]):
+            out[a] = times_t(pick, scratch[:, a, :].astype(BF16)).astype(BF16)
+
+
 def sub_root_back(tiles, own, other, kept, out):
     value = times(total(tiles).astype(BF16), block(own, other, 0))
     kept[...] = value
@@ -480,13 +490,6 @@
         (low_w, tiles, local_low, low[1]),
     )
     tiles = exchange(tiles, "row")
-    so_far = run(
-        part(sub_leaf_anc, pairs, levels),
-        shape(F32, levels, cols, pair_rows),
-        (),
-        (low_w, y_leaf, *low),
-    )
-    tiles, so_far = tied(tiles, so_far)
     tiles = run(sub_root_solve, shape(BF16, nz, cols, wide), (), (tiles, rhs, *low))
     tiles = exchange(tiles, "z")
     c_scratch = pltpu.VMEM((layers * nrow, ROWS8, pair_rows), F32)
@@ -494,7 +497,7 @@
         part(sub_root_anc, pairs, levels),
         (shape(BF16, cols, wide), shape(BF16, layers * nrow, ROWS8, pair_rows)),
         (),
-        (low_w, tiles, so_far, *low),
+        (low_w, tiles, y_leaf, *low),
         (c_scratch,),
     )
     tiles = exchange(tiles, ("gz", "row"))
@@ -581,15 +584,9 @@
     )
     tiles = exchange(tiles, "row")
 
-    def out_slice(which):
-        start = (z * CORES + which) * out_rows
-        return lax.dynamic_slice_in_dim(z_all, start, out_rows, 2)[:, :anc_count].transpose(1, 2, 0)
-
     def joined(here, there):
         flipped = core == 1
         return jnp.concatenate([jnp.where(flipped, there, here), jnp.where(flipped, here, there)], -1)
-
-    anc_out = joined(out_slice(core), swapped(out_slice(1 - core))).astype(F32)
 
     root, tiles = run(
         sub_root_back,
@@ -613,6 +610,12 @@
         (tiles, root, *up),
     )
     tiles = exchange(tiles, ("z", "core"))
+    piece = shape(BF16, anc_count, out_rows, cols)
+    out_here, out_there = run(
+        anc_pieces, (piece, piece), (), (z_all,), (pltpu.VMEM(z_all.shape, F32),)
+    )
+    out_there = swapped(out_there)
+    anc_out = joined(out_here, out_there).astype(F32)
     sums = jnp.sum(tiles.astype(F32).reshape(nz, CORES, out_rows, packed), 0)
     sums = sums[:, :, : SUB_NODES * cols].reshape(CORES, out_rows, SUB_NODES, cols)
     sub_out = sums.transpose(2, 1, 0, 3).reshape(SUB_NODES, out_rows, CORES * cols)

time: 232 us -> 230 us (level)
  blocking collectives: 33.8 us -> 52.4 us
  waiting for transfers between devices: 62.8 us -> 51.3 us
  starting transfers between devices: 82 us -> 73.9 us
    all_to_all x3 -> x5, blocking collectives: 33.8 us -> 52.4 us  [exchange(): return lax.all_to_all(array, axes, 0, 0, tiled=True)]
    all_to_all x12 -> x10, waiting for transfers between devices: 60.2 us -> 48.7 us  [exchange(): return lax.all_to_all(array, axes, 0, 0, tiled=True)]
    all_to_all x12 -> x10, starting transfers between devices: 50.7 us -> 43 us  [exchange(): return lax.all_to_all(array, axes, 0, 0, tiled=True)]
  transfers between devices with their start and end apart: 19 -> 17, of which waited for: 13 -> 11; matrix products, arithmetic and copies ran while one was open for 1% -> 1% of each run, Pallas kernels for 12% -> 12%
where the time goes in v9:
time: 230 us; the launch traced here: 228 us
  starting transfers between devices  73.9 us (32%)
  blocking collectives  52.4 us (23%)
  waiting for transfers between devices  51.3 us (22%)
  Pallas kernels  32.4 us (14%)
  between operations  14.4 us (6%)
  local copies, waits for them, and re-layouts  3.25 us (1%)
    all_to_all x5, blocking collectives, exchange(): return lax.all_to_all(array, axes, 0, 0, tiled=True)  52.4 us
    all_to_all x10, waiting for transfers between devices, exchange(): return lax.all_to_all(array, axes, 0, 0, tiled=True)  48.7 us
    all_to_all x10, starting transfers between devices, exchange(): return lax.all_to_all(array, axes, 0, 0, tiled=True)  43 us
    pallas_call x28, Pallas kernels, run(): pl.pallas_call(body, out_shape=outs, in_specs=in_specs, out_specs=spec if...  32.4 us
    ppermute x5, starting transfers between devices, swapped(): return lax.ppermute(array, 'core', [(0, 1), (1, 0)])  30.8 us
  transfers between devices with their start and end apart: 17, of which 11 were waited for; matrix products, arithmetic and copies ran while one was open for 1% of the time, Pallas kernels for 12%

profile of v9, /device:TPU:1, one launch (start us, length us, event | category | flops | bytes accessed | tf_op | source)
XLA Modules:
  0.0 228.3 jit_solution(11582868222603423366)
XLA Ops:
  8.0 8.7 %collective-permute-start.1 = (bf16[14,64,256]{2,1,0:T(8,128)(2,1)}, bf16[14,64,256]{2,1,0:T(8,128)(2,1)S(1)}, u32[]{:S(2)}, u32[]{:S(2)}) collective-permute-start(bf16[14,64,256]{2,1,0:T(8,128)(2,1)} %own.5), channel_id=1, source_target_pairs={{0,1},{1,0},{2,3},{3,2},{4,5},{5,4},{6,7},{7,6},{8,9},{9,8},{10,11... | collective-permute-start | bytes 1376264 | tf_op jit(solution)/shard_map/ppermute | solution.py:33
  21.1 2.1 collective-permute-start.2
  27.7 16.7 %all_to_all.75.tiles = bf16[8,2,32,256]{3,2,1,0:T(8,128)(2,1)S(1)} all-to-all(bf16[8,2,32,256]{3,2,1,0:T(8,128)(2,1)S(1)} %get-tuple-element.88), channel_id=1, replica_groups=mesh['gz'=8,'row'=4,'z'=8,'core'=2] {'z'}, dimensions={0} | all-to-all | bytes 524288 | tf_op jit(solution)/shard_map/all_to_all | solution.py:416
  44.6 8.4 %all_to_all.76.tiles = bf16[4,32,128]{2,1,0:T(8,128)(2,1)S(1)} all-to-all(bf16[4,32,128]{2,1,0:T(8,128)(2,1)S(1)} %get-tuple-element.98), channel_id=1, replica_groups=mesh['gz'=8,'row'=4,'z'=8,'core'=2] {'row'}, dimensions={0} | all-to-all | bytes 65536 | tf_op jit(solution)/shard_map/all_to_all | solution.py:416
  53.1 10.3 %all_to_all.77.tiles = bf16[8,32,256]{2,1,0:T(8,128)(2,1)S(1)} all-to-all(bf16[8,32,256]{2,1,0:T(8,128)(2,1)S(1)} %shard_map.98), channel_id=1, replica_groups=mesh['gz'=8,'row'=4,'z'=8,'core'=2] {'z'}, dimensions={0} | all-to-all | bytes 262144 | tf_op jit(solution)/shard_map/all_to_all | solution.py:416
  64.4 8.1 %all-to-all-start.3 = ((bf16[32,8,128]{2,1,0:T(8,128)(2,1)}), bf16[32,8,128]{2,1,0:T(8,128)(2,1)S(1)}, u32[]{:S(2)}, u32[]{:S(2)}) async-start(bf16[32,8,128]{2,1,0:T(8,128)(2,1)} %get-tuple-element.101), calls=%async_computation.3 | async-start | bytes 131072 | tf_op jit(solution)/shard_map/all_to_all | solution.py:416
  72.5 2.1 shard_map.100
  74.6 6.7 %all-to-all-done.3.tiles = bf16[32,8,128]{2,1,0:T(8,128)(2,1)S(1)} async-done(((bf16[32,8,128]{2,1,0:T(8,128)(2,1)}), bf16[32,8,128]{2,1,0:T(8,128)(2,1)S(1)}, u32[]{:S(2)}, u32[]{:S(2)}) %all-to-all-start.3) | async-done | bytes 65568 | tf_op jit(solution)/shard_map/all_to_all | solution.py:416
  82.4 3.4 %all-to-all-start.4 = ((bf16[8,4,1024]{2,1,0:T(4,128)(2,1)}), bf16[8,4,1024]{2,1,0:T(4,128)(2,1)S(1)}, u32[]{:S(2)}, u32[]{:S(2)}) async-start(bf16[8,4,1024]{2,1,0:T(4,128)(2,1)} %get-tuple-element.109), calls=%async_computation.4 | async-start | bytes 131072 | tf_op jit(solution)/shard_map/all_to_all | solution.py:416
  85.8 2.4 %shard_map.102 = (bf16[6,64,1024]{2,1,0:T(8,128)(2,1)S(1)}, bf16[6,64,1024]{2,1,0:T(8,128)(2,1)S(1)}) custom-call(s32[6]{0:T(128)S(1)} %stack.31.where, bf16[8,17,64,256]{3,2,1,0:T(8,128)(2,1)} %bitcast.13), custom_call_target="tpu_custom_call" | custom-call | tf_op jit(solution)/shard_map/pallas_call | solution.py:47
  88.2 4.8 %all-to-all-done.4.tiles = bf16[8,4,1024]{2,1,0:T(4,128)(2,1)S(1)} async-done(((bf16[8,4,1024]{2,1,0:T(4,128)(2,1)}), bf16[8,4,1024]{2,1,0:T(4,128)(2,1)S(1)}, u32[]{:S(2)}, u32[]{:S(2)}) %all-to-all-start.4) | async-done | bytes 65568 | tf_op jit(solution)/shard_map/all_to_all | solution.py:416
  94.3 3.3 %all-to-all-start.5 = ((bf16[8,2,1024]{2,1,0:T(2,128)(2,1)}), bf16[8,2,1024]{2,1,0:T(2,128)(2,1)S(1)}, u32[]{:S(2)}, u32[]{:S(2)}) async-start(bf16[8,2,1024]{2,1,0:T(2,128)(2,1)} %get-tuple-element.116), calls=%async_computation.5 | async-start | bytes 65536 | tf_op jit(solution)/shard_map/all_to_all | solution.py:416
  99.4 2.4 %shard_map.104.acc_in = f32[8,128]{1,0:T(8,128)S(1)} custom-call(s32[6]{0:T(128)S(1)} %stack.31.where, f32[8,1024]{1,0:T(8,128)S(1)} %get-tuple-element.117.values.refs_0_, f32[8,128]{1,0:T(8,128)S(1)} %get-tuple-element.118.acc_in, bf16[8,17,64,256]{3,2,1,0:T(8,128)(2,1)} %bitcast.15), custom_call_target="tpu_custom_call" | custom-call | tf_op jit(solution)/shard_map/pallas_call | solution.py:47
  101.8 2.6 %all-to-all-done.5.tiles = bf16[8,2,1024]{2,1,0:T(2,128)(2,1)S(1)} async-done(((bf16[8,2,1024]{2,1,0:T(2,128)(2,1)}), bf16[8,2,1024]{2,1,0:T(2,128)(2,1)S(1)}, u32[]{:S(2)}, u32[]{:S(2)}) %all-to-all-start.5) | async-done | bytes 32800 | tf_op jit(solution)/shard_map/all_to_all | solution.py:416
  105.5 4.0 %all-to-all-start.6 = ((bf16[8,2,1024]{2,1,0:T(2,128)(2,1)}), bf16[8,2,1024]{2,1,0:T(2,128)(2,1)S(1)}, u32[]{:S(2)}, u32[]{:S(2)}) async-start(bf16[8,2,1024]{2,1,0:T(2,128)(2,1)} %get-tuple-element.126), calls=%async_computation.6 | async-start | bytes 65536 | tf_op jit(solution)/shard_map/all_to_all | solution.py:416
  111.0 5.4 %all-to-all-done.6.tiles = bf16[8,2,1024]{2,1,0:T(2,128)(2,1)S(1)} async-done(((bf16[8,2,1024]{2,1,0:T(2,128)(2,1)}), bf16[8,2,1024]{2,1,0:T(2,128)(2,1)S(1)}, u32[]{:S(2)}, u32[]{:S(2)}) %all-to-all-start.6) | async-done | bytes 32800 | tf_op jit(solution)/shard_map/all_to_all | solution.py:416
  117.2 3.3 %all-to-all-start.7 = ((bf16[8,2,1024]{2,1,0:T(2,128)(2,1)}), bf16[8,2,1024]{2,1,0:T(2,128)(2,1)S(1)}, u32[]{:S(2)}, u32[]{:S(2)}) async-start(bf16[8,2,1024]{2,1,0:T(2,128)(2,1)} %get-tuple-element.133), calls=%async_computation.7 | async-start | bytes 65536 | tf_op jit(solution)/shard_map/all_to_all | solution.py:416
  122.7 4.6 %all-to-all-done.7.tiles = bf16[8,2,1024]{2,1,0:T(2,128)(2,1)S(1)} async-done(((bf16[8,2,1024]{2,1,0:T(2,128)(2,1)}), bf16[8,2,1024]{2,1,0:T(2,128)(2,1)S(1)}, u32[]{:S(2)}, u32[]{:S(2)}) %all-to-all-start.7) | async-done | bytes 32800 | tf_op jit(solution)/shard_map/all_to_all | solution.py:416
  128.6 3.3 %all-to-all-start.8 = ((bf16[8,2,1024]{2,1,0:T(2,128)(2,1)}), bf16[8,2,1024]{2,1,0:T(2,128)(2,1)S(1)}, u32[]{:S(2)}, u32[]{:S(2)}) async-start(bf16[8,2,1024]{2,1,0:T(2,128)(2,1)} %get-tuple-element.143), calls=%async_computation.8 | async-start | bytes 65536 | tf_op jit(solution)/shard_map/all_to_all | solution.py:416
  131.9 2.7 %shard_map.112 = (bf16[8,64,1024]{2,1,0:T(8,128)(2,1)S(1)}, bf16[8,64,1024]{2,1,0:T(8,128)(2,1)S(1)}) custom-call(s32[6]{0:T(128)S(1)} %stack.31.where, bf16[8,17,64,256]{3,2,1,0:T(8,128)(2,1)} %bitcast.18), custom_call_target="tpu_custom_call" | custom-call | tf_op jit(solution)/shard_map/pallas_call | solution.py:47
  134.7 2.4 %shard_map.113.acc_in = f32[8,128]{1,0:T(8,128)S(1)} custom-call(s32[6]{0:T(128)S(1)} %stack.31.where, f32[8,1024]{1,0:T(8,128)S(1)} %get-tuple-element.147.values.refs_0_, f32[8,128]{1,0:T(8,128)S(1)} %shard_map.109.acc_in, bf16[8,17,64,256]{3,2,1,0:T(8,128)(2,1)} %bitcast.19), custom_call_target="tpu_custom_call" | custom-call | tf_op jit(solution)/shard_map/pallas_call | solution.py:47
  140.3 11.1 %collective-permute-start.3 = (bf16[14,64,256]{2,1,0:T(8,128)(2,1)S(1)}, bf16[14,64,256]{2,1,0:T(8,128)(2,1)S(1)}, u32[]{:S(2)}, u32[]{:S(2)}) collective-permute-start(bf16[14,64,256]{2,1,0:T(8,128)(2,1)S(1)} %copy-done), channel_id=1, source_target_pairs={{0,1},{1,0},{2,3},{3,2},{4,5},{5,4},{6,7},{7,6},{8,9},{9,8},{10,11... | collective-permute-start | bytes 1376264 | tf_op jit(solution)/shard_map/ppermute | solution.py:33
  151.3 4.0 %all-to-all-start.9 = ((bf16[8,4,1024]{2,1,0:T(4,128)(2,1)}), bf16[8,4,1024]{2,1,0:T(4,128)(2,1)S(1)}, u32[]{:S(2)}, u32[]{:S(2)}) async-start(bf16[8,4,1024]{2,1,0:T(4,128)(2,1)} %get-tuple-element.153), calls=%async_computation.9 | async-start | bytes 131072 | tf_op jit(solution)/shard_map/all_to_all | solution.py:416
  155.4 7.1 %all-to-all-done.9.tiles = bf16[8,4,1024]{2,1,0:T(4,128)(2,1)S(1)} async-done(((bf16[8,4,1024]{2,1,0:T(4,128)(2,1)}), bf16[8,4,1024]{2,1,0:T(4,128)(2,1)S(1)}, u32[]{:S(2)}, u32[]{:S(2)}) %all-to-all-start.9) | async-done | bytes 65568 | tf_op jit(solution)/shard_map/all_to_all | solution.py:416
  163.2 3.9 %all-to-all-start.10 = ((bf16[32,8,256]{2,1,0:T(8,128)(2,1)}), bf16[32,8,256]{2,1,0:T(8,128)(2,1)S(1)}, u32[]{:S(2)}, u32[]{:S(2)}) async-start(bf16[32,8,256]{2,1,0:T(8,128)(2,1)} %shard_map.116), calls=%async_computation.10 | async-start | bytes 262144 | tf_op jit(solution)/shard_map/all_to_all | solution.py:416
  167.7 8.8 %all-to-all-done.10.tiles = bf16[32,8,256]{2,1,0:T(8,128)(2,1)S(1)} async-done(((bf16[32,8,256]{2,1,0:T(8,128)(2,1)}), bf16[32,8,256]{2,1,0:T(8,128)(2,1)S(1)}, u32[]{:S(2)}, u32[]{:S(2)}) %all-to-all-start.10) | async-done | bytes 131104 | tf_op jit(solution)/shard_map/all_to_all | solution.py:416
  176.8 6.6 %all_to_all.78.tiles = bf16[4,32,128]{2,1,0:T(8,128)(2,1)S(1)} all-to-all(bf16[4,32,128]{2,1,0:T(8,128)(2,1)S(1)} %get-tuple-element.168), channel_id=1, replica_groups=mesh['gz'=8,'row'=4,'z'=8,'core'=2] {'row'}, dimensions={0} | all-to-all | bytes 65536 | tf_op jit(solution)/shard_map/all_to_all | solution.py:416
  183.6 10.3 %all_to_all.79.tiles = bf16[8,32,256]{2,1,0:T(8,128)(2,1)S(1)} all-to-all(bf16[8,32,256]{2,1,0:T(8,128)(2,1)S(1)} %get-tuple-element.169), channel_id=1, replica_groups=mesh['gz'=8,'row'=4,'z'=8,'core'=2] {'z'}, dimensions={0} | all-to-all | bytes 262144 | tf_op jit(solution)/shard_map/all_to_all | solution.py:416
  194.7 3.3 %all-to-all-start.13 = ((bf16[4,2,32,128]{3,2,1,0:T(8,128)(2,1)}), bf16[4,2,32,128]{3,2,1,0:T(8,128)(2,1)S(1)}, u32[]{:S(2)}, u32[]{:S(2)}) async-start(bf16[4,2,32,128]{3,2,1,0:T(8,128)(2,1)} %shard_map.121), calls=%async_computation.13 | async-start | bytes 131072 | tf_op jit(solution)/shard_map/all_to_all | solution.py:416
  198.6 6.9 %collective-permute-start.4 = (bf16[7,16,32]{2,1,0:T(8,128)(2,1)S(1)}, bf16[7,16,32]{2,1,0:T(8,128)(2,1)S(1)}, u32[]{:S(2)}, u32[]{:S(2)}) collective-permute-start(bf16[7,16,32]{2,1,0:T(8,128)(2,1)S(1)} %get-tuple-element.162), channel_id=1, source_target_pairs={{0,1},{1,0},{2,3},{3,2},{4,5},{5,4},{6,7},{7,6},{8,9},{9,8},{10,11... | collective-permute-start | bytes 21512 | tf_op jit(solution)/shard_map/ppermute | solution.py:33
  206.4 6.4 %all-to-all-start.14 = ((bf16[16,16,128]{2,1,0:T(8,128)(2,1)}), bf16[16,16,128]{2,1,0:T(8,128)(2,1)S(1)}, u32[]{:S(2)}, u32[]{:S(2)}) async-start(bf16[16,16,128]{2,1,0:T(8,128)(2,1)} %shard_map.122), calls=%async_computation.14 | async-start | bytes 131072 | tf_op jit(solution)/shard_map/all_to_all | solution.py:416
  213.5 7.1 %all-to-all-done.14 = bf16[16,16,128]{2,1,0:T(8,128)(2,1)S(1)} async-done(((bf16[16,16,128]{2,1,0:T(8,128)(2,1)}), bf16[16,16,128]{2,1,0:T(8,128)(2,1)S(1)}, u32[]{:S(2)}, u32[]{:S(2)}) %all-to-all-start.14) | async-done | bytes 65568 | tf_op jit(solution)/shard_map/all_to_all | solution.py:416
  (53 shorter events, 30.7 us)
Async XLA Ops:
  7.2 45.8 %copy-start.1 = (bf16[14,64,256]{2,1,0:T(8,128)(2,1)S(1)}, bf16[14,64,256]{2,1,0:T(8,128)(2,1)}, u32[]{:S(2)}) copy-start(bf16[14,64,256]{2,1,0:T(8,128)(2,1)} %own.5) | copy-start | bytes 1376260
  7.2 65.3 %all-gather.5.cloned.1.call-start = ((), (), s32[]{:S(2)}) async-start(), calls=%async_computation.15 | async-start | bytes 5013504 | tf_op jit(solution)/shard_map/all_gather | solution.py:413
  7.9 101.6 %all-gather.7.cloned.1.call-start = ((), (), s32[]{:S(2)}) async-start(), calls=%async_computation.16 | async-start | bytes 5013504 | tf_op jit(solution)/shard_map/all_gather | solution.py:413
  8.0 12.1 %collective-permute-start.1 = (bf16[14,64,256]{2,1,0:T(8,128)(2,1)}, bf16[14,64,256]{2,1,0:T(8,128)(2,1)S(1)}, u32[]{:S(2)}, u32[]{:S(2)}) collective-permute-start(bf16[14,64,256]{2,1,0:T(8,128)(2,1)} %own.5), channel_id=1, source_target_pairs={{0,1},{1,0},{2,3},{3,2},{4,5},{5,4},{6,7},{7,6},{8,9},{9,8},{10,11... | collective-permute-start | bytes 1376264 | tf_op jit(solution)/shard_map/ppermute | solution.py:33
  16.7 3.3 %collective-permute-start = (bf16[3,64,64]{2,1,0:T(8,128)(2,1)}, bf16[3,64,64]{2,1,0:T(8,128)(2,1)S(1)}, u32[]{:S(2)}, u32[]{:S(2)}) collective-permute-start(bf16[3,64,64]{2,1,0:T(8,128)(2,1)} %here.1), channel_id=1, source_target_pairs={{0,1},{1,0},{2,3},{3,2},{4,5},{5,4},{6,7},{7,6},{8,9},{9,8},{10,11... | collective-permute-start | bytes 73736 | tf_op jit(solution)/shard_map/ppermute | solution.py:33
  21.1 3.4 %collective-permute-start.2 = (bf16[7,64,64]{2,1,0:T(8,128)(2,1)}, bf16[7,64,64]{2,1,0:T(8,128)(2,1)S(1)}, u32[]{:S(2)}, u32[]{:S(2)}) collective-permute-start(bf16[7,64,64]{2,1,0:T(8,128)(2,1)} %here.2), channel_id=1, source_target_pairs={{0,1},{1,0},{2,3},{3,2},{4,5},{5,4},{6,7},{7,6},{8,9},{9,8},{10,11... | collective-permute-start | bytes 172040 | tf_op jit(solution)/shard_map/ppermute | solution.py:33
  24.6 0.9 copy-start.2
  25.5 0.7 copy-start.3
  64.4 16.9 %all-to-all-start.3 = ((bf16[32,8,128]{2,1,0:T(8,128)(2,1)}), bf16[32,8,128]{2,1,0:T(8,128)(2,1)S(1)}, u32[]{:S(2)}, u32[]{:S(2)}) async-start(bf16[32,8,128]{2,1,0:T(8,128)(2,1)} %get-tuple-element.101), calls=%async_computation.3 | async-start | bytes 131072 | tf_op jit(solution)/shard_map/all_to_all | solution.py:416
  82.4 10.5 %all-to-all-start.4 = ((bf16[8,4,1024]{2,1,0:T(4,128)(2,1)}), bf16[8,4,1024]{2,1,0:T(4,128)(2,1)S(1)}, u32[]{:S(2)}, u32[]{:S(2)}) async-start(bf16[8,4,1024]{2,1,0:T(4,128)(2,1)} %get-tuple-element.109), calls=%async_computation.4 | async-start | bytes 131072 | tf_op jit(solution)/shard_map/all_to_all | solution.py:416
  94.3 10.1 %all-to-all-start.5 = ((bf16[8,2,1024]{2,1,0:T(2,128)(2,1)}), bf16[8,2,1024]{2,1,0:T(2,128)(2,1)S(1)}, u32[]{:S(2)}, u32[]{:S(2)}) async-start(bf16[8,2,1024]{2,1,0:T(2,128)(2,1)} %get-tuple-element.116), calls=%async_computation.5 | async-start | bytes 65536 | tf_op jit(solution)/shard_map/all_to_all | solution.py:416
  105.5 10.9 %all-to-all-start.6 = ((bf16[8,2,1024]{2,1,0:T(2,128)(2,1)}), bf16[8,2,1024]{2,1,0:T(2,128)(2,1)S(1)}, u32[]{:S(2)}, u32[]{:S(2)}) async-start(bf16[8,2,1024]{2,1,0:T(2,128)(2,1)} %get-tuple-element.126), calls=%async_computation.6 | async-start | bytes 65536 | tf_op jit(solution)/shard_map/all_to_all | solution.py:416
  117.2 10.1 %all-to-all-start.7 = ((bf16[8,2,1024]{2,1,0:T(2,128)(2,1)}), bf16[8,2,1024]{2,1,0:T(2,128)(2,1)S(1)}, u32[]{:S(2)}, u32[]{:S(2)}) async-start(bf16[8,2,1024]{2,1,0:T(2,128)(2,1)} %get-tuple-element.133), calls=%async_computation.7 | async-start | bytes 65536 | tf_op jit(solution)/shard_map/all_to_all | solution.py:416
  128.6 10.1 %all-to-all-start.8 = ((bf16[8,2,1024]{2,1,0:T(2,128)(2,1)}), bf16[8,2,1024]{2,1,0:T(2,128)(2,1)S(1)}, u32[]{:S(2)}, u32[]{:S(2)}) async-start(bf16[8,2,1024]{2,1,0:T(2,128)(2,1)} %get-tuple-element.143), calls=%async_computation.8 | async-start | bytes 65536 | tf_op jit(solution)/shard_map/all_to_all | solution.py:416
  131.9 8.3 %copy-start = (bf16[14,64,256]{2,1,0:T(8,128)(2,1)S(1)}, bf16[14,64,256]{2,1,0:T(8,128)(2,1)}, u32[]{:S(2)}) copy-start(bf16[14,64,256]{2,1,0:T(8,128)(2,1)} %own.9) | copy-start | bytes 1376260
  140.3 36.2 %collective-permute-start.3 = (bf16[14,64,256]{2,1,0:T(8,128)(2,1)S(1)}, bf16[14,64,256]{2,1,0:T(8,128)(2,1)S(1)}, u32[]{:S(2)}, u32[]{:S(2)}) collective-permute-start(bf16[14,64,256]{2,1,0:T(8,128)(2,1)S(1)} %copy-done), channel_id=1, source_target_pairs={{0,1},{1,0},{2,3},{3,2},{4,5},{5,4},{6,7},{7,6},{8,9},{9,8},{10,11... | collective-permute-start | bytes 1376264 | tf_op jit(solution)/shard_map/ppermute | solution.py:33
  151.3 11.2 %all-to-all-start.9 = ((bf16[8,4,1024]{2,1,0:T(4,128)(2,1)}), bf16[8,4,1024]{2,1,0:T(4,128)(2,1)S(1)}, u32[]{:S(2)}, u32[]{:S(2)}) async-start(bf16[8,4,1024]{2,1,0:T(4,128)(2,1)} %get-tuple-element.153), calls=%async_computation.9 | async-start | bytes 131072 | tf_op jit(solution)/shard_map/all_to_all | solution.py:416
  163.2 13.3 %all-to-all-start.10 = ((bf16[32,8,256]{2,1,0:T(8,128)(2,1)}), bf16[32,8,256]{2,1,0:T(8,128)(2,1)S(1)}, u32[]{:S(2)}, u32[]{:S(2)}) async-start(bf16[32,8,256]{2,1,0:T(8,128)(2,1)} %shard_map.116), calls=%async_computation.10 | async-start | bytes 262144 | tf_op jit(solution)/shard_map/all_to_all | solution.py:416
  194.7 10.8 %all-to-all-start.13 = ((bf16[4,2,32,128]{3,2,1,0:T(8,128)(2,1)}), bf16[4,2,32,128]{3,2,1,0:T(8,128)(2,1)S(1)}, u32[]{:S(2)}, u32[]{:S(2)}) async-start(bf16[4,2,32,128]{3,2,1,0:T(8,128)(2,1)} %shard_map.121), calls=%async_computation.13 | async-start | bytes 131072 | tf_op jit(solution)/shard_map/all_to_all | solution.py:416
  198.6 14.2 %collective-permute-start.4 = (bf16[7,16,32]{2,1,0:T(8,128)(2,1)S(1)}, bf16[7,16,32]{2,1,0:T(8,128)(2,1)S(1)}, u32[]{:S(2)}, u32[]{:S(2)}) collective-permute-start(bf16[7,16,32]{2,1,0:T(8,128)(2,1)S(1)} %get-tuple-element.162), channel_id=1, source_target_pairs={{0,1},{1,0},{2,3},{3,2},{4,5},{5,4},{6,7},{7,6},{8,9},{9,8},{10,11... | collective-permute-start | bytes 21512 | tf_op jit(solution)/shard_map/ppermute | solution.py:33
  206.4 14.2 %all-to-all-start.14 = ((bf16[16,16,128]{2,1,0:T(8,128)(2,1)}), bf16[16,16,128]{2,1,0:T(8,128)(2,1)S(1)}, u32[]{:S(2)}, u32[]{:S(2)}) async-start(bf16[16,16,128]{2,1,0:T(8,128)(2,1)} %shard_map.122), calls=%async_computation.14 | async-start | bytes 131072 | tf_op jit(solution)/shard_map/all_to_all | solution.py:416
Sparse Core Ops, SparseCore 0:
  10.1 44.4 all-gather.4
  56.7 39.4 all-gather.6

commit v10 on v9

--- a/solution.py
+++ b/solution.py
@@ -304,10 +304,6 @@
     out[...] = sum(z_rows(values, out.shape[1]) for values in refs[:-1])
 
 
-def added(*refs):
-    refs[-1][...] = sum(values[...] for values in refs[:-1])
-
-
 def anc_backward(depth, tiles, acc_in, near, near_x, z_out, out, scratch):
     level_rows(depth - 1, tiles, z_out)
     acc = acc_in[...] - pair_sum(depth, depth - 1, z_out, 0, (near, near_x), False)
@@ -324,9 +320,10 @@
         out[m] = scale * own_first(y.astype(F32), core)
 
 
-def anc_spread(depth, nrow, tiles, z_in, out, scratch):
+def anc_spread(depth, nrow, tiles, *refs):
+    *z_parts, out, scratch = refs
     first, stop = level_span(depth)
-    scratch[...] = z_in[...]
+    scratch[...] = sum(values[...] for values in z_parts)
     scratch[first:stop, :] = total(tiles)
     wide = out.shape[2]
     for i in range(out.shape[0]):
@@ -501,8 +498,14 @@
         (c_scratch,),
     )
     tiles = exchange(tiles, ("gz", "row"))
+
+    def step_blocks(depth):
+        return pair_blocks(depth, depth - 1) + diagonal(depth - 1)
+
     near = loaded(diagonal(levels - 1), anc_low)
-    tiles, *near = tied(tiles, *near)
+    ready = loaded(step_blocks(levels - 1), anc_low)
+    tiles, *both = tied(tiles, *near, *ready)
+    near, ready = both[:2], both[2:]
 
     acc, tiles = run(
         part(anc_first, levels - 1),
@@ -514,9 +517,13 @@
     tiles = exchange(tiles, "z")
     y_parts = []
     for depth in range(levels - 1, 0, -1):
-        blocks = pair_blocks(depth, depth - 1) + diagonal(depth - 1)
-        near = loaded(blocks, anc_low)
-        tiles, *near = tied(tiles, *near)
+        near = ready
+        if depth < levels - 1:
+            near = loaded(step_blocks(depth), anc_low)
+            tiles, *near = tied(tiles, *near)
+        if depth == 1:
+            near_root = loaded(diagonal(0), anc_up)
+            tiles, *near_root = tied(tiles, *near_root)
         y8, acc, tiles = run(
             part(anc_forward, depth),
             (row_shape, acc_shape, level_shape(depth - 1)),
@@ -529,16 +536,13 @@
         if depth > 1:
             acc = others(depth, True, y8, acc, anc_low)
             tiles, acc = tied(tiles, acc)
-    near = loaded(diagonal(0), anc_up)
-    tiles, *near = tied(tiles, *near)
-    y8, tiles = run(
-        anc_turn, (row_shape, level_shape(0)), (), (tiles, *near), (scr8,)
-    )
+    y8, tiles = run(anc_turn, (row_shape, level_shape(0)), (), (tiles, *near_root), (scr8,))
     y_parts.append(y8)
     tiles = exchange(tiles, "z")
     start8 = run(anc_start, acc_shape, (), y_parts)
     tiles, start8 = tied(tiles, start8)
     z8 = None
+    z_parts = []
     for depth in range(1, levels):
         acc = start8
         blocks = pair_blocks(depth, depth - 1) + diagonal(depth)
@@ -554,22 +558,18 @@
             (tiles, acc, *near),
             (scr8,),
         )
-        if depth == levels - 1:
-            tiles, sub_upper = tied(tiles, sub_upper)
         tiles = exchange(tiles, "z")
-        if z8 is None:
-            z8 = z_now
-        else:
-            z8 = run(added, row_shape, (), (z8, z_now))
-            tiles, z8 = tied(tiles, z8)
-    up = two_cores(sub_upper)
+        z_parts.append(z_now)
+        z8 = z_now
     tiles = run(
         part(anc_spread, levels - 1, nrow),
         shape(BF16, layers * nrow, ROWS8, wide),
         (),
-        (tiles, z8),
+        (tiles, *z_parts),
         (scr8,),
     )
+    tiles, sub_upper = tied(tiles, sub_upper)
+    up = two_cores(sub_upper)
     z_all = exchange(tiles, ("gz", "row"))
     y_own = run(sub_pieces, shape(F32, SUB_NODES, cols, pair_rows), (where,), (y_root, y_leaf))
     z_all, y_own, up_there, up_w, pick = tied(z_all, y_own, up[1], up_w, pick)

time: 230 us -> 230 us (level)
  blocking collectives: 52.4 us -> 84.6 us
  waiting for transfers between devices: 51.3 us -> 32.1 us
  starting transfers between devices: 73.9 us -> 62.2 us
    all_to_all x5 -> x8, blocking collectives: 52.4 us -> 84.6 us  [exchange(): return lax.all_to_all(array, axes, 0, 0, tiled=True)]
    all_to_all x10 -> x7, waiting for transfers between devices: 48.7 us -> 29.5 us  [exchange(): return lax.all_to_all(array, axes, 0, 0, tiled=True)]
    all_to_all x10 -> x7, starting transfers between devices: 43 us -> 31.9 us  [exchange(): return lax.all_to_all(array, axes, 0, 0, tiled=True)]
    pallas_call x28 -> x27, Pallas kernels: 32.4 us -> 31 us  [run(): pl.pallas_call(body, out_shape=outs, in_specs=in_specs, out_specs=spec if...]
  transfers between devices with their start and end apart: 17 -> 14, of which waited for: 11 -> 8; matrix products, arithmetic and copies ran while one was open for 1% -> 1% of each run, Pallas kernels for 12% -> 10%
where the time goes in v10:
time: 230 us; the launch traced here: 228 us
  blocking collectives  84.6 us (37%)
  starting transfers between devices  62.2 us (27%)
  waiting for transfers between devices  32.1 us (14%)
  Pallas kernels  31 us (13%)
  between operations  14.3 us (6%)
  local copies, waits for them, and re-layouts  3.25 us (1%)
    all_to_all x8, blocking collectives, exchange(): return lax.all_to_all(array, axes, 0, 0, tiled=True)  84.6 us
    all_to_all x7, starting transfers between devices, exchange(): return lax.all_to_all(array, axes, 0, 0, tiled=True)  31.9 us
    pallas_call x27, Pallas kernels, run(): pl.pallas_call(body, out_shape=outs, in_specs=in_specs, out_specs=spec if...  31 us
    ppermute x5, starting transfers between devices, swapped(): return lax.ppermute(array, 'core', [(0, 1), (1, 0)])  30.2 us
    all_to_all x7, waiting for transfers between devices, exchange(): return lax.all_to_all(array, axes, 0, 0, tiled=True)  29.5 us
  transfers between devices with their start and end apart: 14, of which 8 were waited for; matrix products, arithmetic and copies ran while one was open for 1% of the time, Pallas kernels for 10%

profile of v10, /device:TPU:1, one launch (start us, length us, event | category | flops | bytes accessed | tf_op | source)
XLA Modules:
  0.0 228.2 jit_solution(7302417738803612893)
XLA Ops:
  8.0 8.7 %collective-permute-start.1 = (bf16[14,64,256]{2,1,0:T(8,128)(2,1)}, bf16[14,64,256]{2,1,0:T(8,128)(2,1)S(1)}, u32[]{:S(2)}, u32[]{:S(2)}) collective-permute-start(bf16[14,64,256]{2,1,0:T(8,128)(2,1)} %own.5), channel_id=1, source_target_pairs={{0,1},{1,0},{2,3},{3,2},{4,5},{5,4},{6,7},{7,6},{8,9},{9,8},{10,11... | collective-permute-start | bytes 1376264 | tf_op jit(solution)/shard_map/ppermute | solution.py:33
  16.7 1.9 collective-permute-start
  21.1 2.1 collective-permute-start.2
  27.7 16.7 %all_to_all.75.tiles = bf16[8,2,32,256]{3,2,1,0:T(8,128)(2,1)S(1)} all-to-all(bf16[8,2,32,256]{3,2,1,0:T(8,128)(2,1)S(1)} %get-tuple-element.85), channel_id=1, replica_groups=mesh['gz'=8,'row'=4,'z'=8,'core'=2] {'z'}, dimensions={0} | all-to-all | bytes 524288 | tf_op jit(solution)/shard_map/all_to_all | solution.py:413
  44.6 8.4 %all_to_all.76.tiles = bf16[4,32,128]{2,1,0:T(8,128)(2,1)S(1)} all-to-all(bf16[4,32,128]{2,1,0:T(8,128)(2,1)S(1)} %get-tuple-element.95), channel_id=1, replica_groups=mesh['gz'=8,'row'=4,'z'=8,'core'=2] {'row'}, dimensions={0} | all-to-all | bytes 65536 | tf_op jit(solution)/shard_map/all_to_all | solution.py:413
  53.1 10.3 %all_to_all.77.tiles = bf16[8,32,256]{2,1,0:T(8,128)(2,1)S(1)} all-to-all(bf16[8,32,256]{2,1,0:T(8,128)(2,1)S(1)} %shard_map.98), channel_id=1, replica_groups=mesh['gz'=8,'row'=4,'z'=8,'core'=2] {'z'}, dimensions={0} | all-to-all | bytes 262144 | tf_op jit(solution)/shard_map/all_to_all | solution.py:413
  64.4 8.1 %all-to-all-start.3 = ((bf16[32,8,128]{2,1,0:T(8,128)(2,1)}), bf16[32,8,128]{2,1,0:T(8,128)(2,1)S(1)}, u32[]{:S(2)}, u32[]{:S(2)}) async-start(bf16[32,8,128]{2,1,0:T(8,128)(2,1)} %get-tuple-element.98), calls=%async_computation.3 | async-start | bytes 131072 | tf_op jit(solution)/shard_map/all_to_all | solution.py:413
  72.5 2.4 %shard_map.101 = (bf16[6,64,1024]{2,1,0:T(8,128)(2,1)S(1)}, bf16[6,64,1024]{2,1,0:T(8,128)(2,1)S(1)}) custom-call(s32[6]{0:T(128)S(1)} %stack.31.where, bf16[8,17,64,256]{3,2,1,0:T(8,128)(2,1)} %bitcast.12), custom_call_target="tpu_custom_call" | custom-call | tf_op jit(solution)/shard_map/pallas_call | solution.py:47
  74.9 2.1 shard_map.100
  77.0 4.3 %all-to-all-done.3.tiles = bf16[32,8,128]{2,1,0:T(8,128)(2,1)S(1)} async-done(((bf16[32,8,128]{2,1,0:T(8,128)(2,1)}), bf16[32,8,128]{2,1,0:T(8,128)(2,1)S(1)}, u32[]{:S(2)}, u32[]{:S(2)}) %all-to-all-start.3) | async-done | bytes 65568 | tf_op jit(solution)/shard_map/all_to_all | solution.py:413
  81.8 9.6 %all_to_all.78.tiles = bf16[8,4,1024]{2,1,0:T(4,128)(2,1)S(1)} all-to-all(bf16[8,4,1024]{2,1,0:T(4,128)(2,1)S(1)} %get-tuple-element.108), channel_id=1, replica_groups=mesh['gz'=8,'row'=4,'z'=8,'core'=2] {'z'}, dimensions={0} | all-to-all | bytes 131072 | tf_op jit(solution)/shard_map/all_to_all | solution.py:413
  92.7 3.3 %all-to-all-start.5 = ((bf16[8,2,1024]{2,1,0:T(2,128)(2,1)}), bf16[8,2,1024]{2,1,0:T(2,128)(2,1)S(1)}, u32[]{:S(2)}, u32[]{:S(2)}) async-start(bf16[8,2,1024]{2,1,0:T(2,128)(2,1)} %get-tuple-element.112), calls=%async_computation.5 | async-start | bytes 65536 | tf_op jit(solution)/shard_map/all_to_all | solution.py:413
  96.1 1.8 shard_map.105
  97.9 2.4 %shard_map.104.acc_in = f32[8,128]{1,0:T(8,128)S(1)} custom-call(s32[6]{0:T(128)S(1)} %stack.31.where, f32[8,1024]{1,0:T(8,128)S(1)} %get-tuple-element.113.values.refs_0_, f32[8,128]{1,0:T(8,128)S(1)} %get-tuple-element.114.acc_in, bf16[8,17,64,256]{3,2,1,0:T(8,128)(2,1)} %bitcast.15), custom_call_target="tpu_custom_call" | custom-call | tf_op jit(solution)/shard_map/pallas_call | solution.py:47
  100.3 2.6 %all-to-all-done.5.tiles = bf16[8,2,1024]{2,1,0:T(2,128)(2,1)S(1)} async-done(((bf16[8,2,1024]{2,1,0:T(2,128)(2,1)}), bf16[8,2,1024]{2,1,0:T(2,128)(2,1)S(1)}, u32[]{:S(2)}, u32[]{:S(2)}) %all-to-all-start.5) | async-done | bytes 32800 | tf_op jit(solution)/shard_map/all_to_all | solution.py:413
  105.3 10.7 %all_to_all.79.tiles = bf16[8,2,1024]{2,1,0:T(2,128)(2,1)S(1)} all-to-all(bf16[8,2,1024]{2,1,0:T(2,128)(2,1)S(1)} %get-tuple-element.126), channel_id=1, replica_groups=mesh['gz'=8,'row'=4,'z'=8,'core'=2] {'z'}, dimensions={0} | all-to-all | bytes 65536 | tf_op jit(solution)/shard_map/all_to_all | solution.py:413
  116.8 3.3 %all-to-all-start.7 = ((bf16[8,2,1024]{2,1,0:T(2,128)(2,1)}), bf16[8,2,1024]{2,1,0:T(2,128)(2,1)S(1)}, u32[]{:S(2)}, u32[]{:S(2)}) async-start(bf16[8,2,1024]{2,1,0:T(2,128)(2,1)} %get-tuple-element.129), calls=%async_computation.7 | async-start | bytes 65536 | tf_op jit(solution)/shard_map/all_to_all | solution.py:413
  120.2 2.1 shard_map.110
  122.3 4.6 %all-to-all-done.7.tiles = bf16[8,2,1024]{2,1,0:T(2,128)(2,1)S(1)} async-done(((bf16[8,2,1024]{2,1,0:T(2,128)(2,1)}), bf16[8,2,1024]{2,1,0:T(2,128)(2,1)S(1)}, u32[]{:S(2)}, u32[]{:S(2)}) %all-to-all-start.7) | async-done | bytes 32800 | tf_op jit(solution)/shard_map/all_to_all | solution.py:413
  128.2 3.3 %all-to-all-start.8 = ((bf16[8,2,1024]{2,1,0:T(2,128)(2,1)}), bf16[8,2,1024]{2,1,0:T(2,128)(2,1)S(1)}, u32[]{:S(2)}, u32[]{:S(2)}) async-start(bf16[8,2,1024]{2,1,0:T(2,128)(2,1)} %get-tuple-element.139), calls=%async_computation.8 | async-start | bytes 65536 | tf_op jit(solution)/shard_map/all_to_all | solution.py:413
  131.5 2.7 %shard_map.112 = (bf16[8,64,1024]{2,1,0:T(8,128)(2,1)S(1)}, bf16[8,64,1024]{2,1,0:T(8,128)(2,1)S(1)}) custom-call(s32[6]{0:T(128)S(1)} %stack.31.where, bf16[8,17,64,256]{3,2,1,0:T(8,128)(2,1)} %bitcast.18), custom_call_target="tpu_custom_call" | custom-call | tf_op jit(solution)/shard_map/pallas_call | solution.py:47
  134.3 2.4 %shard_map.113.acc_in = f32[8,128]{1,0:T(8,128)S(1)} custom-call(s32[6]{0:T(128)S(1)} %stack.31.where, f32[8,1024]{1,0:T(8,128)S(1)} %get-tuple-element.143.values.refs_0_, f32[8,128]{1,0:T(8,128)S(1)} %shard_map.109.acc_in, bf16[8,17,64,256]{3,2,1,0:T(8,128)(2,1)} %bitcast.19), custom_call_target="tpu_custom_call" | custom-call | tf_op jit(solution)/shard_map/pallas_call | solution.py:47
  139.2 11.9 %all_to_all.80.tiles = bf16[8,4,1024]{2,1,0:T(4,128)(2,1)S(1)} all-to-all(bf16[8,4,1024]{2,1,0:T(4,128)(2,1)S(1)} %get-tuple-element.148), channel_id=1, replica_groups=mesh['gz'=8,'row'=4,'z'=8,'core'=2] {'z'}, dimensions={0} | all-to-all | bytes 131072 | tf_op jit(solution)/shard_map/all_to_all | solution.py:413
  151.8 11.6 %collective-permute-start.3 = (bf16[14,64,256]{2,1,0:T(8,128)(2,1)S(1)}, bf16[14,64,256]{2,1,0:T(8,128)(2,1)S(1)}, u32[]{:S(2)}, u32[]{:S(2)}) collective-permute-start(bf16[14,64,256]{2,1,0:T(8,128)(2,1)S(1)} %copy-done), channel_id=1, source_target_pairs={{0,1},{1,0},{2,3},{3,2},{4,5},{5,4},{6,7},{7,6},{8,9},{9,8},{10,11... | collective-permute-start | bytes 1376264 | tf_op jit(solution)/shard_map/ppermute | solution.py:33
  163.5 4.2 %all-to-all-start.10 = ((bf16[32,8,256]{2,1,0:T(8,128)(2,1)}), bf16[32,8,256]{2,1,0:T(8,128)(2,1)S(1)}, u32[]{:S(2)}, u32[]{:S(2)}) async-start(bf16[32,8,256]{2,1,0:T(8,128)(2,1)} %shard_map.115), calls=%async_computation.10 | async-start | bytes 262144 | tf_op jit(solution)/shard_map/all_to_all | solution.py:413
  168.3 9.3 %all-to-all-done.10.tiles = bf16[32,8,256]{2,1,0:T(8,128)(2,1)S(1)} async-done(((bf16[32,8,256]{2,1,0:T(8,128)(2,1)}), bf16[32,8,256]{2,1,0:T(8,128)(2,1)S(1)}, u32[]{:S(2)}, u32[]{:S(2)}) %all-to-all-start.10) | async-done | bytes 131104 | tf_op jit(solution)/shard_map/all_to_all | solution.py:413
  177.9 6.6 %all_to_all.81.tiles = bf16[4,32,128]{2,1,0:T(8,128)(2,1)S(1)} all-to-all(bf16[4,32,128]{2,1,0:T(8,128)(2,1)S(1)} %get-tuple-element.162), channel_id=1, replica_groups=mesh['gz'=8,'row'=4,'z'=8,'core'=2] {'row'}, dimensions={0} | all-to-all | bytes 65536 | tf_op jit(solution)/shard_map/all_to_all | solution.py:413
  184.7 10.3 %all_to_all.82.tiles = bf16[8,32,256]{2,1,0:T(8,128)(2,1)S(1)} all-to-all(bf16[8,32,256]{2,1,0:T(8,128)(2,1)S(1)} %get-tuple-element.163), channel_id=1, replica_groups=mesh['gz'=8,'row'=4,'z'=8,'core'=2] {'z'}, dimensions={0} | all-to-all | bytes 262144 | tf_op jit(solution)/shard_map/all_to_all | solution.py:413
  195.8 3.3 %all-to-all-start.13 = ((bf16[4,2,32,128]{3,2,1,0:T(8,128)(2,1)}), bf16[4,2,32,128]{3,2,1,0:T(8,128)(2,1)S(1)}, u32[]{:S(2)}, u32[]{:S(2)}) async-start(bf16[4,2,32,128]{3,2,1,0:T(8,128)(2,1)} %shard_map.120), calls=%async_computation.13 | async-start | bytes 131072 | tf_op jit(solution)/shard_map/all_to_all | solution.py:413
  199.7 5.8 %collective-permute-start.4 = (bf16[7,16,32]{2,1,0:T(8,128)(2,1)S(1)}, bf16[7,16,32]{2,1,0:T(8,128)(2,1)S(1)}, u32[]{:S(2)}, u32[]{:S(2)}) collective-permute-start(bf16[7,16,32]{2,1,0:T(8,128)(2,1)S(1)} %get-tuple-element.156), channel_id=1, source_target_pairs={{0,1},{1,0},{2,3},{3,2},{4,5},{5,4},{6,7},{7,6},{8,9},{9,8},{10,11... | collective-permute-start | bytes 21512 | tf_op jit(solution)/shard_map/ppermute | solution.py:33
  206.3 6.4 %all-to-all-start.14 = ((bf16[16,16,128]{2,1,0:T(8,128)(2,1)}), bf16[16,16,128]{2,1,0:T(8,128)(2,1)S(1)}, u32[]{:S(2)}, u32[]{:S(2)}) async-start(bf16[16,16,128]{2,1,0:T(8,128)(2,1)} %shard_map.121), calls=%async_computation.14 | async-start | bytes 131072 | tf_op jit(solution)/shard_map/all_to_all | solution.py:413
  213.4 7.1 %all-to-all-done.14 = bf16[16,16,128]{2,1,0:T(8,128)(2,1)S(1)} async-done(((bf16[16,16,128]{2,1,0:T(8,128)(2,1)}), bf16[16,16,128]{2,1,0:T(8,128)(2,1)S(1)}, u32[]{:S(2)}, u32[]{:S(2)}) %all-to-all-start.14) | async-done | bytes 65568 | tf_op jit(solution)/shard_map/all_to_all | solution.py:413
  (49 shorter events, 23.4 us)
Async XLA Ops:
  7.2 45.8 %copy-start.1 = (bf16[14,64,256]{2,1,0:T(8,128)(2,1)S(1)}, bf16[14,64,256]{2,1,0:T(8,128)(2,1)}, u32[]{:S(2)}) copy-start(bf16[14,64,256]{2,1,0:T(8,128)(2,1)} %own.5) | copy-start | bytes 1376260
  7.2 65.3 %all-gather.5.cloned.1.call-start = ((), (), s32[]{:S(2)}) async-start(), calls=%async_computation.15 | async-start | bytes 5013504 | tf_op jit(solution)/shard_map/all_gather | solution.py:410
  7.9 95.0 %all-gather.7.cloned.1.call-start = ((), (), s32[]{:S(2)}) async-start(), calls=%async_computation.16 | async-start | bytes 5013504 | tf_op jit(solution)/shard_map/all_gather | solution.py:410
  8.0 12.1 %collective-permute-start.1 = (bf16[14,64,256]{2,1,0:T(8,128)(2,1)}, bf16[14,64,256]{2,1,0:T(8,128)(2,1)S(1)}, u32[]{:S(2)}, u32[]{:S(2)}) collective-permute-start(bf16[14,64,256]{2,1,0:T(8,128)(2,1)} %own.5), channel_id=1, source_target_pairs={{0,1},{1,0},{2,3},{3,2},{4,5},{5,4},{6,7},{7,6},{8,9},{9,8},{10,11... | collective-permute-start | bytes 1376264 | tf_op jit(solution)/shard_map/ppermute | solution.py:33
  16.7 3.3 %collective-permute-start = (bf16[3,64,64]{2,1,0:T(8,128)(2,1)}, bf16[3,64,64]{2,1,0:T(8,128)(2,1)S(1)}, u32[]{:S(2)}, u32[]{:S(2)}) collective-permute-start(bf16[3,64,64]{2,1,0:T(8,128)(2,1)} %here.1), channel_id=1, source_target_pairs={{0,1},{1,0},{2,3},{3,2},{4,5},{5,4},{6,7},{7,6},{8,9},{9,8},{10,11... | collective-permute-start | bytes 73736 | tf_op jit(solution)/shard_map/ppermute | solution.py:33
  21.1 3.4 %collective-permute-start.2 = (bf16[7,64,64]{2,1,0:T(8,128)(2,1)}, bf16[7,64,64]{2,1,0:T(8,128)(2,1)S(1)}, u32[]{:S(2)}, u32[]{:S(2)}) collective-permute-start(bf16[7,64,64]{2,1,0:T(8,128)(2,1)} %here.2), channel_id=1, source_target_pairs={{0,1},{1,0},{2,3},{3,2},{4,5},{5,4},{6,7},{7,6},{8,9},{9,8},{10,11... | collective-permute-start | bytes 172040 | tf_op jit(solution)/shard_map/ppermute | solution.py:33
  24.6 0.9 copy-start.2
  25.5 0.7 copy-start.3
  64.4 16.9 %all-to-all-start.3 = ((bf16[32,8,128]{2,1,0:T(8,128)(2,1)}), bf16[32,8,128]{2,1,0:T(8,128)(2,1)S(1)}, u32[]{:S(2)}, u32[]{:S(2)}) async-start(bf16[32,8,128]{2,1,0:T(8,128)(2,1)} %get-tuple-element.98), calls=%async_computation.3 | async-start | bytes 131072 | tf_op jit(solution)/shard_map/all_to_all | solution.py:413
  92.7 10.1 %all-to-all-start.5 = ((bf16[8,2,1024]{2,1,0:T(2,128)(2,1)}), bf16[8,2,1024]{2,1,0:T(2,128)(2,1)S(1)}, u32[]{:S(2)}, u32[]{:S(2)}) async-start(bf16[8,2,1024]{2,1,0:T(2,128)(2,1)} %get-tuple-element.112), calls=%async_computation.5 | async-start | bytes 65536 | tf_op jit(solution)/shard_map/all_to_all | solution.py:413
  116.8 10.1 %all-to-all-start.7 = ((bf16[8,2,1024]{2,1,0:T(2,128)(2,1)}), bf16[8,2,1024]{2,1,0:T(2,128)(2,1)S(1)}, u32[]{:S(2)}, u32[]{:S(2)}) async-start(bf16[8,2,1024]{2,1,0:T(2,128)(2,1)} %get-tuple-element.129), calls=%async_computation.7 | async-start | bytes 65536 | tf_op jit(solution)/shard_map/all_to_all | solution.py:413
  128.2 10.1 %all-to-all-start.8 = ((bf16[8,2,1024]{2,1,0:T(2,128)(2,1)}), bf16[8,2,1024]{2,1,0:T(2,128)(2,1)S(1)}, u32[]{:S(2)}, u32[]{:S(2)}) async-start(bf16[8,2,1024]{2,1,0:T(2,128)(2,1)} %get-tuple-element.139), calls=%async_computation.8 | async-start | bytes 65536 | tf_op jit(solution)/shard_map/all_to_all | solution.py:413
  134.2 17.6 %copy-start = (bf16[14,64,256]{2,1,0:T(8,128)(2,1)S(1)}, bf16[14,64,256]{2,1,0:T(8,128)(2,1)}, u32[]{:S(2)}) copy-start(bf16[14,64,256]{2,1,0:T(8,128)(2,1)} %own.9) | copy-start | bytes 1376260
  151.8 25.7 %collective-permute-start.3 = (bf16[14,64,256]{2,1,0:T(8,128)(2,1)S(1)}, bf16[14,64,256]{2,1,0:T(8,128)(2,1)S(1)}, u32[]{:S(2)}, u32[]{:S(2)}) collective-permute-start(bf16[14,64,256]{2,1,0:T(8,128)(2,1)S(1)} %copy-done), channel_id=1, source_target_pairs={{0,1},{1,0},{2,3},{3,2},{4,5},{5,4},{6,7},{7,6},{8,9},{9,8},{10,11... | collective-permute-start | bytes 1376264 | tf_op jit(solution)/shard_map/ppermute | solution.py:33
  163.5 14.1 %all-to-all-start.10 = ((bf16[32,8,256]{2,1,0:T(8,128)(2,1)}), bf16[32,8,256]{2,1,0:T(8,128)(2,1)S(1)}, u32[]{:S(2)}, u32[]{:S(2)}) async-start(bf16[32,8,256]{2,1,0:T(8,128)(2,1)} %shard_map.115), calls=%async_computation.10 | async-start | bytes 262144 | tf_op jit(solution)/shard_map/all_to_all | solution.py:413
  195.8 9.7 %all-to-all-start.13 = ((bf16[4,2,32,128]{3,2,1,0:T(8,128)(2,1)}), bf16[4,2,32,128]{3,2,1,0:T(8,128)(2,1)S(1)}, u32[]{:S(2)}, u32[]{:S(2)}) async-start(bf16[4,2,32,128]{3,2,1,0:T(8,128)(2,1)} %shard_map.120), calls=%async_computation.13 | async-start | bytes 131072 | tf_op jit(solution)/shard_map/all_to_all | solution.py:413
  199.7 13.0 %collective-permute-start.4 = (bf16[7,16,32]{2,1,0:T(8,128)(2,1)S(1)}, bf16[7,16,32]{2,1,0:T(8,128)(2,1)S(1)}, u32[]{:S(2)}, u32[]{:S(2)}) collective-permute-start(bf16[7,16,32]{2,1,0:T(8,128)(2,1)S(1)} %get-tuple-element.156), channel_id=1, source_target_pairs={{0,1},{1,0},{2,3},{3,2},{4,5},{5,4},{6,7},{7,6},{8,9},{9,8},{10,11... | collective-permute-start | bytes 21512 | tf_op jit(solution)/shard_map/ppermute | solution.py:33
  206.3 14.2 %all-to-all-start.14 = ((bf16[16,16,128]{2,1,0:T(8,128)(2,1)}), bf16[16,16,128]{2,1,0:T(8,128)(2,1)S(1)}, u32[]{:S(2)}, u32[]{:S(2)}) async-start(bf16[16,16,128]{2,1,0:T(8,128)(2,1)} %shard_map.121), calls=%async_computation.14 | async-start | bytes 131072 | tf_op jit(solution)/shard_map/all_to_all | solution.py:413
Sparse Core Ops, SparseCore 0:
  10.1 44.4 all-gather.4
  56.7 39.4 all-gather.6

commit v11 on v10

--- a/solution.py
+++ b/solution.py
@@ -105,23 +105,25 @@
                 self.anc[a, u] = anc_count + len(self.anc)
 
 
-def sub_leaf_solve(there, other, own, here, rhs, out, near, near_rhs, sems):
-    first, count = LEAVES[0], len(LEAVES)
+def sub_leaf_load(own, here, near, near_rhs, sems):
     copies = [
-        pltpu.make_async_copy(own.at[pl.ds(first, count)], near, sems.at[0]),
+        pltpu.make_async_copy(own.at[pl.ds(LEAVES[0], len(LEAVES))], near, sems.at[0]),
         pltpu.make_async_copy(here, near_rhs, sems.at[1]),
     ]
     for copy in copies:
         copy.start()
     for copy in copies:
         copy.wait()
+
+
+def sub_leaf_solve(there, other, near, near_rhs, rhs, out):
     core = lax.axis_index("core")
     cols = rhs.shape[1]
     for m in range(SUB_NODES):
         flipped = jnp.concatenate([near_rhs[m], there[m]], 0).astype(F32).T
         rhs[m] = jnp.where(core == 0, flipped[:cols], flipped[cols:]).astype(BF16)
     for m in LEAVES:
-        both = jnp.concatenate([near[m - first], other[m]], 0)
+        both = jnp.concatenate([near[m - LEAVES[0]], other[m]], 0)
         part = times(rhs[m], both).astype(BF16)
         for i in range(out.shape[0]):
             out[i, m - 1] = part
@@ -446,17 +448,19 @@
     acc_shape = shape(F32, ROWS8, pair_rows)
     row_shape = shape(F32, ROWS8, size)
 
+    first = run(
+        sub_leaf_load,
+        (shape(BF16, len(LEAVES), own, wide), shape(BF16, *sub_rhs.shape)),
+        (),
+        (),
+        (pltpu.SemaphoreType.DMA((2,)),),
+        (sub_lower, sub_rhs),
+    )
     rhs, tiles = run(
         sub_leaf_solve,
         (shape(BF16, SUB_NODES, cols, pair_rows), shape(BF16, nz, 2, cols, wide)),
         (),
-        (rhs_there, low[1]),
-        (
-            pltpu.VMEM((len(LEAVES), own, wide), BF16),
-            pltpu.VMEM(sub_rhs.shape, BF16),
-            pltpu.SemaphoreType.DMA((2,)),
-        ),
-        (sub_lower, sub_rhs),
+        (rhs_there, low[1], *first),
     )
     tiles, anc_rhs = tied(tiles, anc_rhs)
     anc_there = swapped(anc_rhs)
@@ -521,9 +525,6 @@
         if depth < levels - 1:
             near = loaded(step_blocks(depth), anc_low)
             tiles, *near = tied(tiles, *near)
-        if depth == 1:
-            near_root = loaded(diagonal(0), anc_up)
-            tiles, *near_root = tied(tiles, *near_root)
         y8, acc, tiles = run(
             part(anc_forward, depth),
             (row_shape, acc_shape, level_shape(depth - 1)),
@@ -536,6 +537,8 @@
         if depth > 1:
             acc = others(depth, True, y8, acc, anc_low)
             tiles, acc = tied(tiles, acc)
+    near_root = loaded(diagonal(0), anc_up)
+    tiles, *near_root = tied(tiles, *near_root)
     y8, tiles = run(anc_turn, (row_shape, level_shape(0)), (), (tiles, *near_root), (scr8,))
     y_parts.append(y8)
     tiles = exchange(tiles, "z")

time: 230 us -> 228 us (level)
  blocking collectives: 84.6 us -> 74.2 us
  waiting for transfers between devices: 32.1 us -> 36.4 us
  starting transfers between devices: 62.2 us -> 65.8 us
    all_to_all x8 -> x7, blocking collectives: 84.6 us -> 74.2 us  [exchange(): return lax.all_to_all(array, axes, 0, 0, tiled=True)]
    all_to_all x7 -> x8, waiting for transfers between devices: 29.5 us -> 34.7 us  [exchange(): return lax.all_to_all(array, axes, 0, 0, tiled=True)]
    all_to_all x7 -> x8, starting transfers between devices: 31.9 us -> 35.7 us  [exchange(): return lax.all_to_all(array, axes, 0, 0, tiled=True)]
    pallas_call x27 -> x28, Pallas kernels: 31 us -> 31.4 us  [run(): pl.pallas_call(body, out_shape=outs, in_specs=in_specs, out_specs=spec if...]
  transfers between devices with their start and end apart: 14 -> 15, of which waited for: 8 -> 9; matrix products, arithmetic and copies ran while one was open for 1% -> 1% of each run, Pallas kernels for 10% -> 12%
where the time goes in v11:
time: 228 us; the launch traced here: 226 us
  blocking collectives  74.2 us (33%)
  starting transfers between devices  65.8 us (29%)
  waiting for transfers between devices  36.4 us (16%)
  Pallas kernels  31.4 us (14%)
  between operations  14.4 us (6%)
  local copies, waits for them, and re-layouts  3.25 us (1%)
    all_to_all x7, blocking collectives, exchange(): return lax.all_to_all(array, axes, 0, 0, tiled=True)  74.2 us
    all_to_all x8, starting transfers between devices, exchange(): return lax.all_to_all(array, axes, 0, 0, tiled=True)  35.7 us
    all_to_all x8, waiting for transfers between devices, exchange(): return lax.all_to_all(array, axes, 0, 0, tiled=True)  34.7 us
    pallas_call x28, Pallas kernels, run(): pl.pallas_call(body, out_shape=outs, in_specs=in_specs, out_specs=spec if...  31.4 us
    ppermute x5, starting transfers between devices, swapped(): return lax.ppermute(array, 'core', [(0, 1), (1, 0)])  30 us
  transfers between devices with their start and end apart: 15, of which 9 were waited for; matrix products, arithmetic and copies ran while one was open for 1% of the time, Pallas kernels for 12%

profile of v11, /device:TPU:1, one launch (start us, length us, event | category | flops | bytes accessed | tf_op | source)
XLA Modules:
  0.0 226.2 jit_solution(17878408834559115113)
XLA Ops:
  8.0 8.7 %collective-permute-start.1 = (bf16[14,64,256]{2,1,0:T(8,128)(2,1)}, bf16[14,64,256]{2,1,0:T(8,128)(2,1)S(1)}, u32[]{:S(2)}, u32[]{:S(2)}) collective-permute-start(bf16[14,64,256]{2,1,0:T(8,128)(2,1)} %own.5), channel_id=1, source_target_pairs={{0,1},{1,0},{2,3},{3,2},{4,5},{5,4},{6,7},{7,6},{8,9},{9,8},{10,11... | collective-permute-start | bytes 1376264 | tf_op jit(solution)/shard_map/ppermute | solution.py:33
  16.7 1.9 collective-permute-start
  20.3 2.1 collective-permute-start.2
  26.8 16.7 %all_to_all.75.tiles = bf16[8,2,32,256]{3,2,1,0:T(8,128)(2,1)S(1)} all-to-all(bf16[8,2,32,256]{3,2,1,0:T(8,128)(2,1)S(1)} %get-tuple-element.89), channel_id=1, replica_groups=mesh['gz'=8,'row'=4,'z'=8,'core'=2] {'z'}, dimensions={0} | all-to-all | bytes 524288 | tf_op jit(solution)/shard_map/all_to_all | solution.py:415
  43.7 8.6 %all_to_all.76.tiles = bf16[4,32,128]{2,1,0:T(8,128)(2,1)S(1)} all-to-all(bf16[4,32,128]{2,1,0:T(8,128)(2,1)S(1)} %get-tuple-element.99), channel_id=1, replica_groups=mesh['gz'=8,'row'=4,'z'=8,'core'=2] {'row'}, dimensions={0} | all-to-all | bytes 65536 | tf_op jit(solution)/shard_map/all_to_all | solution.py:415
  52.5 10.3 %all_to_all.77.tiles = bf16[8,32,256]{2,1,0:T(8,128)(2,1)S(1)} all-to-all(bf16[8,32,256]{2,1,0:T(8,128)(2,1)S(1)} %shard_map.99), channel_id=1, replica_groups=mesh['gz'=8,'row'=4,'z'=8,'core'=2] {'z'}, dimensions={0} | all-to-all | bytes 262144 | tf_op jit(solution)/shard_map/all_to_all | solution.py:415
  63.8 8.0 %all-to-all-start.3 = ((bf16[32,8,128]{2,1,0:T(8,128)(2,1)}), bf16[32,8,128]{2,1,0:T(8,128)(2,1)S(1)}, u32[]{:S(2)}, u32[]{:S(2)}) async-start(bf16[32,8,128]{2,1,0:T(8,128)(2,1)} %get-tuple-element.102), calls=%async_computation.3 | async-start | bytes 131072 | tf_op jit(solution)/shard_map/all_to_all | solution.py:415
  71.8 2.6 %shard_map.102 = (bf16[6,64,1024]{2,1,0:T(8,128)(2,1)S(1)}, bf16[6,64,1024]{2,1,0:T(8,128)(2,1)S(1)}) custom-call(s32[6]{0:T(128)S(1)} %stack.31.where, bf16[8,17,64,256]{3,2,1,0:T(8,128)(2,1)} %bitcast.12), custom_call_target="tpu_custom_call" | custom-call | tf_op jit(solution)/shard_map/pallas_call | solution.py:47
  74.5 2.1 shard_map.101
  76.6 4.1 %all-to-all-done.3.tiles = bf16[32,8,128]{2,1,0:T(8,128)(2,1)S(1)} async-done(((bf16[32,8,128]{2,1,0:T(8,128)(2,1)}), bf16[32,8,128]{2,1,0:T(8,128)(2,1)S(1)}, u32[]{:S(2)}, u32[]{:S(2)}) %all-to-all-start.3) | async-done | bytes 65568 | tf_op jit(solution)/shard_map/all_to_all | solution.py:415
  81.1 9.6 %all_to_all.78.tiles = bf16[8,4,1024]{2,1,0:T(4,128)(2,1)S(1)} all-to-all(bf16[8,4,1024]{2,1,0:T(4,128)(2,1)S(1)} %get-tuple-element.112), channel_id=1, replica_groups=mesh['gz'=8,'row'=4,'z'=8,'core'=2] {'z'}, dimensions={0} | all-to-all | bytes 131072 | tf_op jit(solution)/shard_map/all_to_all | solution.py:415
  92.1 3.3 %all-to-all-start.5 = ((bf16[8,2,1024]{2,1,0:T(2,128)(2,1)}), bf16[8,2,1024]{2,1,0:T(2,128)(2,1)S(1)}, u32[]{:S(2)}, u32[]{:S(2)}) async-start(bf16[8,2,1024]{2,1,0:T(2,128)(2,1)} %get-tuple-element.116), calls=%async_computation.5 | async-start | bytes 65536 | tf_op jit(solution)/shard_map/all_to_all | solution.py:415
  97.3 2.4 %shard_map.105.acc_in = f32[8,128]{1,0:T(8,128)S(1)} custom-call(s32[6]{0:T(128)S(1)} %stack.31.where, f32[8,1024]{1,0:T(8,128)S(1)} %get-tuple-element.117.values.refs_0_, f32[8,128]{1,0:T(8,128)S(1)} %get-tuple-element.118.acc_in, bf16[8,17,64,256]{3,2,1,0:T(8,128)(2,1)} %bitcast.15), custom_call_target="tpu_custom_call" | custom-call | tf_op jit(solution)/shard_map/pallas_call | solution.py:47
  99.7 2.6 %all-to-all-done.5.tiles = bf16[8,2,1024]{2,1,0:T(2,128)(2,1)S(1)} async-done(((bf16[8,2,1024]{2,1,0:T(2,128)(2,1)}), bf16[8,2,1024]{2,1,0:T(2,128)(2,1)S(1)}, u32[]{:S(2)}, u32[]{:S(2)}) %all-to-all-start.5) | async-done | bytes 32800 | tf_op jit(solution)/shard_map/all_to_all | solution.py:415
  103.3 4.0 %all-to-all-start.6 = ((bf16[8,2,1024]{2,1,0:T(2,128)(2,1)}), bf16[8,2,1024]{2,1,0:T(2,128)(2,1)S(1)}, u32[]{:S(2)}, u32[]{:S(2)}) async-start(bf16[8,2,1024]{2,1,0:T(2,128)(2,1)} %get-tuple-element.126), calls=%async_computation.6 | async-start | bytes 65536 | tf_op jit(solution)/shard_map/all_to_all | solution.py:415
  108.8 5.4 %all-to-all-done.6.tiles = bf16[8,2,1024]{2,1,0:T(2,128)(2,1)S(1)} async-done(((bf16[8,2,1024]{2,1,0:T(2,128)(2,1)}), bf16[8,2,1024]{2,1,0:T(2,128)(2,1)S(1)}, u32[]{:S(2)}, u32[]{:S(2)}) %all-to-all-start.6) | async-done | bytes 32800 | tf_op jit(solution)/shard_map/all_to_all | solution.py:415
  115.0 3.3 %all-to-all-start.7 = ((bf16[8,2,1024]{2,1,0:T(2,128)(2,1)}), bf16[8,2,1024]{2,1,0:T(2,128)(2,1)S(1)}, u32[]{:S(2)}, u32[]{:S(2)}) async-start(bf16[8,2,1024]{2,1,0:T(2,128)(2,1)} %get-tuple-element.133), calls=%async_computation.7 | async-start | bytes 65536 | tf_op jit(solution)/shard_map/all_to_all | solution.py:415
  118.4 2.1 shard_map.111
  120.6 4.6 %all-to-all-done.7.tiles = bf16[8,2,1024]{2,1,0:T(2,128)(2,1)S(1)} async-done(((bf16[8,2,1024]{2,1,0:T(2,128)(2,1)}), bf16[8,2,1024]{2,1,0:T(2,128)(2,1)S(1)}, u32[]{:S(2)}, u32[]{:S(2)}) %all-to-all-start.7) | async-done | bytes 32800 | tf_op jit(solution)/shard_map/all_to_all | solution.py:415
  126.4 3.3 %all-to-all-start.8 = ((bf16[8,2,1024]{2,1,0:T(2,128)(2,1)}), bf16[8,2,1024]{2,1,0:T(2,128)(2,1)S(1)}, u32[]{:S(2)}, u32[]{:S(2)}) async-start(bf16[8,2,1024]{2,1,0:T(2,128)(2,1)} %get-tuple-element.143), calls=%async_computation.8 | async-start | bytes 65536 | tf_op jit(solution)/shard_map/all_to_all | solution.py:415
  129.7 2.7 %shard_map.113 = (bf16[8,64,1024]{2,1,0:T(8,128)(2,1)S(1)}, bf16[8,64,1024]{2,1,0:T(8,128)(2,1)S(1)}) custom-call(s32[6]{0:T(128)S(1)} %stack.31.where, bf16[8,17,64,256]{3,2,1,0:T(8,128)(2,1)} %bitcast.18), custom_call_target="tpu_custom_call" | custom-call | tf_op jit(solution)/shard_map/pallas_call | solution.py:47
  132.5 2.4 %shard_map.114.acc_in = f32[8,128]{1,0:T(8,128)S(1)} custom-call(s32[6]{0:T(128)S(1)} %stack.31.where, f32[8,1024]{1,0:T(8,128)S(1)} %get-tuple-element.147.values.refs_0_, f32[8,128]{1,0:T(8,128)S(1)} %shard_map.110.acc_in, bf16[8,17,64,256]{3,2,1,0:T(8,128)(2,1)} %bitcast.19), custom_call_target="tpu_custom_call" | custom-call | tf_op jit(solution)/shard_map/pallas_call | solution.py:47
  137.4 11.9 %all_to_all.79.tiles = bf16[8,4,1024]{2,1,0:T(4,128)(2,1)S(1)} all-to-all(bf16[8,4,1024]{2,1,0:T(4,128)(2,1)S(1)} %get-tuple-element.152), channel_id=1, replica_groups=mesh['gz'=8,'row'=4,'z'=8,'core'=2] {'z'}, dimensions={0} | all-to-all | bytes 131072 | tf_op jit(solution)/shard_map/all_to_all | solution.py:415
  150.1 11.5 %collective-permute-start.3 = (bf16[14,64,256]{2,1,0:T(8,128)(2,1)S(1)}, bf16[14,64,256]{2,1,0:T(8,128)(2,1)S(1)}, u32[]{:S(2)}, u32[]{:S(2)}) collective-permute-start(bf16[14,64,256]{2,1,0:T(8,128)(2,1)S(1)} %copy-done), channel_id=1, source_target_pairs={{0,1},{1,0},{2,3},{3,2},{4,5},{5,4},{6,7},{7,6},{8,9},{9,8},{10,11... | collective-permute-start | bytes 1376264 | tf_op jit(solution)/shard_map/ppermute | solution.py:33
  161.5 4.1 %all-to-all-start.10 = ((bf16[32,8,256]{2,1,0:T(8,128)(2,1)}), bf16[32,8,256]{2,1,0:T(8,128)(2,1)S(1)}, u32[]{:S(2)}, u32[]{:S(2)}) async-start(bf16[32,8,256]{2,1,0:T(8,128)(2,1)} %shard_map.116), calls=%async_computation.10 | async-start | bytes 262144 | tf_op jit(solution)/shard_map/all_to_all | solution.py:415
  166.3 9.3 %all-to-all-done.10.tiles = bf16[32,8,256]{2,1,0:T(8,128)(2,1)S(1)} async-done(((bf16[32,8,256]{2,1,0:T(8,128)(2,1)}), bf16[32,8,256]{2,1,0:T(8,128)(2,1)S(1)}, u32[]{:S(2)}, u32[]{:S(2)}) %all-to-all-start.10) | async-done | bytes 131104 | tf_op jit(solution)/shard_map/all_to_all | solution.py:415
  175.9 6.6 %all_to_all.80.tiles = bf16[4,32,128]{2,1,0:T(8,128)(2,1)S(1)} all-to-all(bf16[4,32,128]{2,1,0:T(8,128)(2,1)S(1)} %get-tuple-element.166), channel_id=1, replica_groups=mesh['gz'=8,'row'=4,'z'=8,'core'=2] {'row'}, dimensions={0} | all-to-all | bytes 65536 | tf_op jit(solution)/shard_map/all_to_all | solution.py:415
  182.7 10.3 %all_to_all.81.tiles = bf16[8,32,256]{2,1,0:T(8,128)(2,1)S(1)} all-to-all(bf16[8,32,256]{2,1,0:T(8,128)(2,1)S(1)} %get-tuple-element.167), channel_id=1, replica_groups=mesh['gz'=8,'row'=4,'z'=8,'core'=2] {'z'}, dimensions={0} | all-to-all | bytes 262144 | tf_op jit(solution)/shard_map/all_to_all | solution.py:415
  193.8 3.3 %all-to-all-start.13 = ((bf16[4,2,32,128]{3,2,1,0:T(8,128)(2,1)}), bf16[4,2,32,128]{3,2,1,0:T(8,128)(2,1)S(1)}, u32[]{:S(2)}, u32[]{:S(2)}) async-start(bf16[4,2,32,128]{3,2,1,0:T(8,128)(2,1)} %shard_map.121), calls=%async_computation.13 | async-start | bytes 131072 | tf_op jit(solution)/shard_map/all_to_all | solution.py:415
  197.6 5.8 %collective-permute-start.4 = (bf16[7,16,32]{2,1,0:T(8,128)(2,1)S(1)}, bf16[7,16,32]{2,1,0:T(8,128)(2,1)S(1)}, u32[]{:S(2)}, u32[]{:S(2)}) collective-permute-start(bf16[7,16,32]{2,1,0:T(8,128)(2,1)S(1)} %get-tuple-element.160), channel_id=1, source_target_pairs={{0,1},{1,0},{2,3},{3,2},{4,5},{5,4},{6,7},{7,6},{8,9},{9,8},{10,11... | collective-permute-start | bytes 21512 | tf_op jit(solution)/shard_map/ppermute | solution.py:33
  204.3 6.4 %all-to-all-start.14 = ((bf16[16,16,128]{2,1,0:T(8,128)(2,1)}), bf16[16,16,128]{2,1,0:T(8,128)(2,1)S(1)}, u32[]{:S(2)}, u32[]{:S(2)}) async-start(bf16[16,16,128]{2,1,0:T(8,128)(2,1)} %shard_map.122), calls=%async_computation.14 | async-start | bytes 131072 | tf_op jit(solution)/shard_map/all_to_all | solution.py:415
  211.4 7.1 %all-to-all-done.14 = bf16[16,16,128]{2,1,0:T(8,128)(2,1)S(1)} async-done(((bf16[16,16,128]{2,1,0:T(8,128)(2,1)}), bf16[16,16,128]{2,1,0:T(8,128)(2,1)S(1)}, u32[]{:S(2)}, u32[]{:S(2)}) %all-to-all-start.14) | async-done | bytes 65568 | tf_op jit(solution)/shard_map/all_to_all | solution.py:415
  (51 shorter events, 24.5 us)
Async XLA Ops:
  7.2 45.2 %copy-start.1 = (bf16[14,64,256]{2,1,0:T(8,128)(2,1)S(1)}, bf16[14,64,256]{2,1,0:T(8,128)(2,1)}, u32[]{:S(2)}) copy-start(bf16[14,64,256]{2,1,0:T(8,128)(2,1)} %own.5) | copy-start | bytes 1376260
  7.2 64.6 %all-gather.5.cloned.1.call-start = ((), (), s32[]{:S(2)}) async-start(), calls=%async_computation.15 | async-start | bytes 5013504 | tf_op jit(solution)/shard_map/all_gather | solution.py:412
  7.9 99.4 %all-gather.7.cloned.1.call-start = ((), (), s32[]{:S(2)}) async-start(), calls=%async_computation.16 | async-start | bytes 5013504 | tf_op jit(solution)/shard_map/all_gather | solution.py:412
  8.0 12.1 %collective-permute-start.1 = (bf16[14,64,256]{2,1,0:T(8,128)(2,1)}, bf16[14,64,256]{2,1,0:T(8,128)(2,1)S(1)}, u32[]{:S(2)}, u32[]{:S(2)}) collective-permute-start(bf16[14,64,256]{2,1,0:T(8,128)(2,1)} %own.5), channel_id=1, source_target_pairs={{0,1},{1,0},{2,3},{3,2},{4,5},{5,4},{6,7},{7,6},{8,9},{9,8},{10,11... | collective-permute-start | bytes 1376264 | tf_op jit(solution)/shard_map/ppermute | solution.py:33
  16.7 3.3 %collective-permute-start = (bf16[3,64,64]{2,1,0:T(8,128)(2,1)}, bf16[3,64,64]{2,1,0:T(8,128)(2,1)S(1)}, u32[]{:S(2)}, u32[]{:S(2)}) collective-permute-start(bf16[3,64,64]{2,1,0:T(8,128)(2,1)} %here.1), channel_id=1, source_target_pairs={{0,1},{1,0},{2,3},{3,2},{4,5},{5,4},{6,7},{7,6},{8,9},{9,8},{10,11... | collective-permute-start | bytes 73736 | tf_op jit(solution)/shard_map/ppermute | solution.py:33
  20.3 3.4 %collective-permute-start.2 = (bf16[7,64,64]{2,1,0:T(8,128)(2,1)}, bf16[7,64,64]{2,1,0:T(8,128)(2,1)S(1)}, u32[]{:S(2)}, u32[]{:S(2)}) collective-permute-start(bf16[7,64,64]{2,1,0:T(8,128)(2,1)} %here.2), channel_id=1, source_target_pairs={{0,1},{1,0},{2,3},{3,2},{4,5},{5,4},{6,7},{7,6},{8,9},{9,8},{10,11... | collective-permute-start | bytes 172040 | tf_op jit(solution)/shard_map/ppermute | solution.py:33
  23.7 0.9 copy-start.2
  24.6 0.7 copy-start.3
  63.8 16.9 %all-to-all-start.3 = ((bf16[32,8,128]{2,1,0:T(8,128)(2,1)}), bf16[32,8,128]{2,1,0:T(8,128)(2,1)S(1)}, u32[]{:S(2)}, u32[]{:S(2)}) async-start(bf16[32,8,128]{2,1,0:T(8,128)(2,1)} %get-tuple-element.102), calls=%async_computation.3 | async-start | bytes 131072 | tf_op jit(solution)/shard_map/all_to_all | solution.py:415
  92.1 10.1 %all-to-all-start.5 = ((bf16[8,2,1024]{2,1,0:T(2,128)(2,1)}), bf16[8,2,1024]{2,1,0:T(2,128)(2,1)S(1)}, u32[]{:S(2)}, u32[]{:S(2)}) async-start(bf16[8,2,1024]{2,1,0:T(2,128)(2,1)} %get-tuple-element.116), calls=%async_computation.5 | async-start | bytes 65536 | tf_op jit(solution)/shard_map/all_to_all | solution.py:415
  103.3 10.9 %all-to-all-start.6 = ((bf16[8,2,1024]{2,1,0:T(2,128)(2,1)}), bf16[8,2,1024]{2,1,0:T(2,128)(2,1)S(1)}, u32[]{:S(2)}, u32[]{:S(2)}) async-start(bf16[8,2,1024]{2,1,0:T(2,128)(2,1)} %get-tuple-element.126), calls=%async_computation.6 | async-start | bytes 65536 | tf_op jit(solution)/shard_map/all_to_all | solution.py:415
  115.0 10.1 %all-to-all-start.7 = ((bf16[8,2,1024]{2,1,0:T(2,128)(2,1)}), bf16[8,2,1024]{2,1,0:T(2,128)(2,1)S(1)}, u32[]{:S(2)}, u32[]{:S(2)}) async-start(bf16[8,2,1024]{2,1,0:T(2,128)(2,1)} %get-tuple-element.133), calls=%async_computation.7 | async-start | bytes 65536 | tf_op jit(solution)/shard_map/all_to_all | solution.py:415
  126.4 10.1 %all-to-all-start.8 = ((bf16[8,2,1024]{2,1,0:T(2,128)(2,1)}), bf16[8,2,1024]{2,1,0:T(2,128)(2,1)S(1)}, u32[]{:S(2)}, u32[]{:S(2)}) async-start(bf16[8,2,1024]{2,1,0:T(2,128)(2,1)} %get-tuple-element.143), calls=%async_computation.8 | async-start | bytes 65536 | tf_op jit(solution)/shard_map/all_to_all | solution.py:415
  132.5 17.6 %copy-start = (bf16[14,64,256]{2,1,0:T(8,128)(2,1)S(1)}, bf16[14,64,256]{2,1,0:T(8,128)(2,1)}, u32[]{:S(2)}) copy-start(bf16[14,64,256]{2,1,0:T(8,128)(2,1)} %own.9) | copy-start | bytes 1376260
  150.1 25.5 %collective-permute-start.3 = (bf16[14,64,256]{2,1,0:T(8,128)(2,1)S(1)}, bf16[14,64,256]{2,1,0:T(8,128)(2,1)S(1)}, u32[]{:S(2)}, u32[]{:S(2)}) collective-permute-start(bf16[14,64,256]{2,1,0:T(8,128)(2,1)S(1)} %copy-done), channel_id=1, source_target_pairs={{0,1},{1,0},{2,3},{3,2},{4,5},{5,4},{6,7},{7,6},{8,9},{9,8},{10,11... | collective-permute-start | bytes 1376264 | tf_op jit(solution)/shard_map/ppermute | solution.py:33
  161.5 14.0 %all-to-all-start.10 = ((bf16[32,8,256]{2,1,0:T(8,128)(2,1)}), bf16[32,8,256]{2,1,0:T(8,128)(2,1)S(1)}, u32[]{:S(2)}, u32[]{:S(2)}) async-start(bf16[32,8,256]{2,1,0:T(8,128)(2,1)} %shard_map.116), calls=%async_computation.10 | async-start | bytes 262144 | tf_op jit(solution)/shard_map/all_to_all | solution.py:415
  193.8 9.7 %all-to-all-start.13 = ((bf16[4,2,32,128]{3,2,1,0:T(8,128)(2,1)}), bf16[4,2,32,128]{3,2,1,0:T(8,128)(2,1)S(1)}, u32[]{:S(2)}, u32[]{:S(2)}) async-start(bf16[4,2,32,128]{3,2,1,0:T(8,128)(2,1)} %shard_map.121), calls=%async_computation.13 | async-start | bytes 131072 | tf_op jit(solution)/shard_map/all_to_all | solution.py:415
  197.6 13.0 %collective-permute-start.4 = (bf16[7,16,32]{2,1,0:T(8,128)(2,1)S(1)}, bf16[7,16,32]{2,1,0:T(8,128)(2,1)S(1)}, u32[]{:S(2)}, u32[]{:S(2)}) collective-permute-start(bf16[7,16,32]{2,1,0:T(8,128)(2,1)S(1)} %get-tuple-element.160), channel_id=1, source_target_pairs={{0,1},{1,0},{2,3},{3,2},{4,5},{5,4},{6,7},{7,6},{8,9},{9,8},{10,11... | collective-permute-start | bytes 21512 | tf_op jit(solution)/shard_map/ppermute | solution.py:33
  204.3 14.2 %all-to-all-start.14 = ((bf16[16,16,128]{2,1,0:T(8,128)(2,1)}), bf16[16,16,128]{2,1,0:T(8,128)(2,1)S(1)}, u32[]{:S(2)}, u32[]{:S(2)}) async-start(bf16[16,16,128]{2,1,0:T(8,128)(2,1)} %shard_map.122), calls=%async_computation.14 | async-start | bytes 131072 | tf_op jit(solution)/shard_map/all_to_all | solution.py:415
Sparse Core Ops, SparseCore 0:
  10.1 44.5 all-gather.4
  56.8 39.3 all-gather.6
